TPU v7x, 256 devices: a whole 4x4x8 slice. The times are simulated.
256 devices in a mesh: lat: 128 (over x, z, y), lev: 2 (over core).
Axes of the slice: x: 4, y: 4, z: 8, core: 2. Of those that a mesh axis runs over, the one named last changes fastest.
Arguments:
- fields: float32 [1280, 3, 16, 2560], P('lat', None, 'lev'), may hold values from 0.1 to 5
- lat_fraction: float32 [1280], P('lat'), may hold values from 0 to 1
- lon_fraction: float32 [1280], P('lat'), may hold values from 0 to 1
- lon_shift: int32 [1280], P('lat'), may hold values from 0 to 2559
- departure_row: int32 [1280], P('lat'), may hold values from 1 to 1277, as said below
- extents: int32 [128, 2], P('lat'), may hold values from 1 to 4
Outputs:
- advected: float32 [1280, 3, 16, 2560], P('lat', None, 'lev')
Inputs may be any that keep to these rules, and one draw needn't show every extreme that they name: departure_row[r] lies within 39 rows of r.
All inputs are finite; a program needn't handle non-finite values.
Results may differ from a plain program's by a relative error of at most 0.0003.
Values sent between devices are 32-bit elements; how exact they have to be, the bound alone decides.
No kernel may reach another device: no remote copies, remote signals or barrier semaphores. Data moves between devices by JAX's collectives and lax.ppermute only.
A program may use at most 128 MiB of HBM per device.

v0:
```python
import math

import jax
import jax.numpy as jnp
from jax import lax
from jax.sharding import Mesh
from jax.sharding import PartitionSpec as P

REACH = 4
LAT = ("lat_0", "lat_1", "lat_2")
LAT_LEV = ("lat_0", "lat_1", "lat_2", "lev")


def from_behind(block, axis, distance):
    devices = range(lax.axis_size(axis))
    route = [(i - distance, i) for i in devices if i - distance in devices]
    return lax.ppermute(block, axis, route)


def one_axis_at_a_time(array, axes):
    for axis in axes:
        array = lax.psum(array, axis)
    return array


def cubic_weights(fraction):
    return jnp.stack(
        [
            -fraction * (fraction - 1.0) * (fraction - 2.0) / 6.0,
            (fraction + 1.0) * (fraction - 1.0) * (fraction - 2.0) / 2.0,
            -(fraction + 1.0) * fraction * (fraction - 2.0) / 2.0,
            (fraction + 1.0) * fraction * (fraction - 1.0) / 6.0,
        ]
    )


def along_lon(column, lon_w, shift_value):
    lon_count = column.shape[-1]
    doubled = jnp.concatenate([column, column], axis=-1)
    result = jnp.zeros_like(column)
    for offset in range(4):
        first = (shift_value + offset - 1) % lon_count
        result = result + lon_w[offset] * lax.dynamic_slice_in_dim(doubled, first, lon_count, 2)
    return result


def per_device(fields, lat_fraction, lon_fraction, lon_shift, departure_row, extents):
    row_count = fields.shape[0]
    band_index = lax.axis_index(LAT)
    total_rows = lax.axis_size(LAT) * row_count
    first_row = band_index * row_count
    north_bands = []
    south_bands = []
    band_piece = fields
    for distance in range(REACH):
        band_piece = from_behind(band_piece, LAT, 1)
        north_bands.insert(0, band_piece)
    band_piece = fields
    for distance in range(REACH):
        band_piece = from_behind(band_piece, LAT, -1)
        south_bands.append(band_piece)
    padded = jnp.concatenate(north_bands + [fields] + south_bands, axis=0)
    low_bound = first_row - extents[0, 0] * row_count + 1
    high_bound = first_row + row_count - 3 + extents[0, 1] * row_count
    departure = jnp.clip(jnp.clip(departure_row, low_bound, high_bound), 1, total_rows - 3)
    local_start = departure - 1 - (first_row - REACH * row_count)

    def one_row(inputs):
        start_value, lat_t, lon_t, shift_value = inputs
        row_block = lax.dynamic_slice_in_dim(padded, start_value, 4, 0)
        lat_w = cubic_weights(lat_t)
        column = (
            lat_w[0] * row_block[0]
            + lat_w[1] * row_block[1]
            + lat_w[2] * row_block[2]
            + lat_w[3] * row_block[3]
        )
        return along_lon(column, cubic_weights(lon_t), shift_value)

    moved = lax.map(one_row, (local_start, lat_fraction, lon_fraction, lon_shift))
    row_ids = first_row + jnp.arange(row_count, dtype=jnp.int32)
    area = jnp.cos(math.pi * (row_ids.astype(jnp.float32) + 0.5) / total_rows - math.pi / 2.0)
    local_before = jnp.sum(area[:, None, None, None] * fields, axis=(0, 2, 3))
    local_after = jnp.sum(area[:, None, None, None] * moved, axis=(0, 2, 3))
    mass_before, mass_after = (
        one_axis_at_a_time(local_before, LAT_LEV),
        one_axis_at_a_time(local_after, LAT_LEV),
    )
    return moved * (mass_before / mass_after)[None, :, None, None]


def solution(mesh):
    finer = Mesh(
        mesh.devices.reshape(4, 8, 4, mesh.shape["lev"]), ("lat_0", "lat_1", "lat_2", "lev")
    )
    placed = (P(LAT, None, "lev", None), P(LAT), P(LAT), P(LAT), P(LAT), P(LAT, None))
    return jax.shard_map(
        per_device,
        mesh=finer,
        in_specs=placed,
        out_specs=P(LAT, None, "lev", None),
        check_vma=False,
    )
```

profile of v0, /device:TPU:1, one launch (start us, length us, event | category | flops | bytes accessed | tf_op | source)
XLA Modules:
  0.0 472.4 jit_solution(14239120991809122161)
XLA Ops:
  0.0 4.2 collective-permute-start
  5.5 50.9 %collective-permute-done = f32[10,3,8,2560]{3,2,1,0:T(8,128)S(1)} collective-permute-done((f32[10,3,8,2560]{3,2,1,0:T(8,128)}, f32[10,3,8,2560]{3,2,1,0:T(8,128)S(1)}, u32[]{:S(2)}, u32[]{:S(2)}) %collective-permute-start) | collective-permute-done | bytes 2457632 | tf_op jit(solution)/shard_map/ppermute | solution.py:17
  56.4 4.1 collective-permute-start.1
  61.8 49.7 %collective-permute-done.1 = f32[10,3,8,2560]{3,2,1,0:T(8,128)S(1)} collective-permute-done((f32[10,3,8,2560]{3,2,1,0:T(8,128)S(1)}, f32[10,3,8,2560]{3,2,1,0:T(8,128)S(1)}, u32[]{:S(2)}, u32[]{:S(2)}) %collective-permute-start.1) | collective-permute-done | bytes 2457632 | tf_op jit(solution)/shard_map/ppermute | solution.py:17
  111.5 5.6 %collective-permute-start.2 = (f32[10,3,8,2560]{3,2,1,0:T(8,128)S(1)}, f32[10,3,8,2560]{3,2,1,0:T(8,128)}, u32[]{:S(2)}, u32[]{:S(2)}) collective-permute-start(f32[10,3,8,2560]{3,2,1,0:T(8,128)S(1)} %collective-permute-done.1), channel_id=1, source_target_pairs={{0,2},{2,4},{4,6},{6,8},{8,10},{10,12},{12,14},{14,16},{16,18},{18... | collective-permute-start | bytes 7372808 | tf_op jit(solution)/shard_map/ppermute | solution.py:17
  118.4 47.7 %collective-permute-done.2 = f32[10,3,8,2560]{3,2,1,0:T(8,128)} collective-permute-done((f32[10,3,8,2560]{3,2,1,0:T(8,128)S(1)}, f32[10,3,8,2560]{3,2,1,0:T(8,128)}, u32[]{:S(2)}, u32[]{:S(2)}) %collective-permute-start.2) | collective-permute-done | bytes 2457632 | tf_op jit(solution)/shard_map/ppermute | solution.py:17
  166.1 5.7 %collective-permute-start.3 = (f32[10,3,8,2560]{3,2,1,0:T(8,128)}, f32[10,3,8,2560]{3,2,1,0:T(8,128)}, u32[]{:S(2)}, u32[]{:S(2)}) collective-permute-start(f32[10,3,8,2560]{3,2,1,0:T(8,128)} %collective-permute-done.2), channel_id=1, source_target_pairs={{0,2},{2,4},{4,6},{6,8},{8,10},{10,12},{12,14},{14,16},{16,18},{18... | collective-permute-start | bytes 7372808 | tf_op jit(solution)/shard_map/ppermute | solution.py:17
  171.8 1.4 fusion.17
  176.6 43.7 %collective-permute-done.3 = f32[10,3,8,2560]{3,2,1,0:T(8,128)} collective-permute-done((f32[10,3,8,2560]{3,2,1,0:T(8,128)}, f32[10,3,8,2560]{3,2,1,0:T(8,128)}, u32[]{:S(2)}, u32[]{:S(2)}) %collective-permute-start.3) | collective-permute-done | bytes 2457632 | tf_op jit(solution)/shard_map/ppermute | solution.py:17
  220.2 1.9 constant_dynamic-update-slice_fusion.8
  222.1 2.0 constant_dynamic-update-slice_fusion.7
  224.7 1.5 copy-done.5
  226.4 1.5 copy-done
  228.1 1.5 copy-done.3
  229.8 1.9 constant_dynamic-update-slice_fusion.2
  231.7 1.9 constant_dynamic-update-slice_fusion.1
  233.8 7.3 %copy-done.1 = f32[90,3,8,2560]{3,2,1,0:T(8,128)} copy-done((f32[90,3,8,2560]{3,2,1,0:T(8,128)}, f32[90,3,8,2560]{3,2,1,0:T(8,128)S(1)}, u32[]{:S(2)}) %copy-start.1) | copy-done | bytes 22118424
  241.1 167.7 %while.15 = (s32[]{:T(128)}, f32[10,3,8,2560]{3,2,1,0:T(8,128)S(1)}, f32[10]{0:T(128)S(1)}, f32[10]{0:T(128)S(1)}, s32[10]{0:T(128)S(1)}, /*index=5*/f32[90,3,8,...) while((s32[]{:T(128)}, ...), condition=%wide.region_1.2_spmd, body=%wide.region_0.1_spmd.sunk | while | flops 1106001 | bytes 1721515 | solution.py:80
  408.8 2.3 multiply_reduce_fusion
  411.1 29.6 %all-reduce.2 = (f32[3]{0:T(128)S(1)}, f32[3]{0:T(128)S(1)}) all-reduce(f32[3]{0:T(128)S(1)} %get-tuple-element.190, f32[3]{0:T(128)S(1)} %get-tuple-element.189), channel_id=1, replica_groups=mesh['lat_0'=4,'lat_1'=8,'lat_2'=4,'lev'=2] {'lat_0'}, use_global_device_ids=true, to_apply=%region_3.4 | all-reduce | flops 6 | bytes 48 | tf_op jit(solution)/shard_map/psum | solution.py:22
  440.8 10.7 %all-reduce = (f32[3]{0:T(128)S(1)}, f32[3]{0:T(128)S(1)}) all-reduce(f32[3]{0:T(128)S(1)} %get-tuple-element.209, f32[3]{0:T(128)S(1)} %get-tuple-element.210), channel_id=1, replica_groups=mesh['lat_0'=4,'lat_1'=8,'lat_2'=4,'lev'=2] {'lat_1'}, use_global_device_ids=true, to_apply=%region_4.5 | all-reduce | flops 6 | bytes 48 | tf_op jit(solution)/shard_map/psum | solution.py:22
  451.4 6.0 %all-reduce.1 = (f32[3]{0:T(128)S(1)}, f32[3]{0:T(128)S(1)}) all-reduce(f32[3]{0:T(128)S(1)} %get-tuple-element.205, f32[3]{0:T(128)S(1)} %get-tuple-element.206), channel_id=1, replica_groups=mesh['lat_0'=4,'lat_1'=8,'lat_2'=4,'lev'=2] {'lat_2'}, use_global_device_ids=true, to_apply=%region_5.6 | all-reduce | flops 6 | bytes 48 | tf_op jit(solution)/shard_map/psum | solution.py:22
  457.4 13.2 %all-reduce.3 = (f32[3]{0:T(128)S(1)}, f32[3]{0:T(128)S(1)}) all-reduce(f32[3]{0:T(128)S(1)} %get-tuple-element.207, f32[3]{0:T(128)S(1)} %get-tuple-element.208), channel_id=1, replica_groups=mesh['lat_0'=4,'lat_1'=8,'lat_2'=4,'lev'=2] {'lev'}, use_global_device_ids=true, to_apply=%region_6.7 | all-reduce | flops 6 | bytes 48 | tf_op jit(solution)/shard_map/psum | solution.py:22
  470.6 1.8 broadcast_multiply_fusion
  (95 shorter events, 50.8 us)
Async XLA Ops:
  0.0 56.4 %collective-permute-start = (f32[10,3,8,2560]{3,2,1,0:T(8,128)}, f32[10,3,8,2560]{3,2,1,0:T(8,128)S(1)}, u32[]{:S(2)}, u32[]{:S(2)}) collective-permute-start(f32[10,3,8,2560]{3,2,1,0:T(8,128)} %param.8), channel_id=1, source_target_pairs={{0,2},{2,4},{4,6},{6,8},{8,10},{10,12},{12,14},{14,16},{16,18},{18... | collective-permute-start | bytes 7372808 | tf_op jit(solution)/shard_map/ppermute | solution.py:17
  4.2 56.3 %collective-permute-start.4 = (f32[10,3,8,2560]{3,2,1,0:T(8,128)}, f32[10,3,8,2560]{3,2,1,0:T(8,128)S(1)}, u32[]{:S(2)}, u32[]{:S(2)}) collective-permute-start(f32[10,3,8,2560]{3,2,1,0:T(8,128)} %param.8), channel_id=1, source_target_pairs={{2,0},{4,2},{6,4},{8,6},{10,8},{12,10},{14,12},{16,14},{18,16},{20... | collective-permute-start | bytes 7372808 | tf_op jit(solution)/shard_map/ppermute | solution.py:17
  56.4 115.4 %copy-start.4 = (f32[10,3,8,2560]{3,2,1,0:T(8,128)}, f32[10,3,8,2560]{3,2,1,0:T(8,128)S(1)}, u32[]{:S(2)}) copy-start(f32[10,3,8,2560]{3,2,1,0:T(8,128)S(1)} %collective-permute-done) | copy-start | bytes 7372804
  56.4 55.2 %collective-permute-start.1 = (f32[10,3,8,2560]{3,2,1,0:T(8,128)S(1)}, f32[10,3,8,2560]{3,2,1,0:T(8,128)S(1)}, u32[]{:S(2)}, u32[]{:S(2)}) collective-permute-start(f32[10,3,8,2560]{3,2,1,0:T(8,128)S(1)} %collective-permute-done), channel_id=1, source_target_pairs={{0,2},{2,4},{4,6},{6,8},{8,10},{10,12},{12,14},{14,16},{16,18},{18... | collective-permute-start | bytes 7372808 | tf_op jit(solution)/shard_map/ppermute | solution.py:17
  60.5 111.3 %copy-start.2 = (f32[10,3,8,2560]{3,2,1,0:T(8,128)}, f32[10,3,8,2560]{3,2,1,0:T(8,128)S(1)}, u32[]{:S(2)}) copy-start(f32[10,3,8,2560]{3,2,1,0:T(8,128)S(1)} %collective-permute-done.4) | copy-start | bytes 7372804
  60.5 56.6 %collective-permute-start.5 = (f32[10,3,8,2560]{3,2,1,0:T(8,128)S(1)}, f32[10,3,8,2560]{3,2,1,0:T(8,128)}, u32[]{:S(2)}, u32[]{:S(2)}) collective-permute-start(f32[10,3,8,2560]{3,2,1,0:T(8,128)S(1)} %collective-permute-done.4), channel_id=1, source_target_pairs={{2,0},{4,2},{6,4},{8,6},{10,8},{12,10},{14,12},{16,14},{18,16},{20... | collective-permute-start | bytes 7372808 | tf_op jit(solution)/shard_map/ppermute | solution.py:17
  111.5 60.3 %copy-start.6 = (f32[10,3,8,2560]{3,2,1,0:T(8,128)}, f32[10,3,8,2560]{3,2,1,0:T(8,128)S(1)}, u32[]{:S(2)}) copy-start(f32[10,3,8,2560]{3,2,1,0:T(8,128)S(1)} %collective-permute-done.1) | copy-start | bytes 7372804
  111.5 54.6 %collective-permute-start.2 = (f32[10,3,8,2560]{3,2,1,0:T(8,128)S(1)}, f32[10,3,8,2560]{3,2,1,0:T(8,128)}, u32[]{:S(2)}, u32[]{:S(2)}) collective-permute-start(f32[10,3,8,2560]{3,2,1,0:T(8,128)S(1)} %collective-permute-done.1), channel_id=1, source_target_pairs={{0,2},{2,4},{4,6},{6,8},{8,10},{10,12},{12,14},{14,16},{16,18},{18... | collective-permute-start | bytes 7372808 | tf_op jit(solution)/shard_map/ppermute | solution.py:17
  117.1 58.1 %collective-permute-start.6 = (f32[10,3,8,2560]{3,2,1,0:T(8,128)}, f32[10,3,8,2560]{3,2,1,0:T(8,128)}, u32[]{:S(2)}, u32[]{:S(2)}) collective-permute-start(f32[10,3,8,2560]{3,2,1,0:T(8,128)} %collective-permute-done.5), channel_id=1, source_target_pairs={{2,0},{4,2},{6,4},{8,6},{10,8},{12,10},{14,12},{16,14},{18,16},{20... | collective-permute-start | bytes 7372808 | tf_op jit(solution)/shard_map/ppermute | solution.py:17
  166.1 54.1 %collective-permute-start.3 = (f32[10,3,8,2560]{3,2,1,0:T(8,128)}, f32[10,3,8,2560]{3,2,1,0:T(8,128)}, u32[]{:S(2)}, u32[]{:S(2)}) collective-permute-start(f32[10,3,8,2560]{3,2,1,0:T(8,128)} %collective-permute-done.2), channel_id=1, source_target_pairs={{0,2},{2,4},{4,6},{6,8},{8,10},{10,12},{12,14},{14,16},{16,18},{18... | collective-permute-start | bytes 7372808 | tf_op jit(solution)/shard_map/ppermute | solution.py:17
  175.3 58.3 %collective-permute-start.7 = (f32[10,3,8,2560]{3,2,1,0:T(8,128)}, f32[10,3,8,2560]{3,2,1,0:T(8,128)S(1)}, u32[]{:S(2)}, u32[]{:S(2)}) collective-permute-start(f32[10,3,8,2560]{3,2,1,0:T(8,128)} %collective-permute-done.6), channel_id=1, source_target_pairs={{2,0},{4,2},{6,4},{8,6},{10,8},{12,10},{14,12},{16,14},{18,16},{20... | collective-permute-start | bytes 7372808 | tf_op jit(solution)/shard_map/ppermute | solution.py:17
  222.1 2.4 copy-start.7
  224.5 1.7 copy-start.5
  226.2 1.7 copy-start
  227.9 1.7 copy-start.3
  233.5 7.6 %copy-start.8 = (f32[10]{0:T(128)S(1)}, f32[10]{0:T(128)}, u32[]{:S(2)}) copy-start(f32[10]{0:T(128)} %param.10) | copy-start | bytes 124
  233.5 7.6 %copy-start.9 = (f32[10]{0:T(128)S(1)}, f32[10]{0:T(128)}, u32[]{:S(2)}) copy-start(f32[10]{0:T(128)} %param.9) | copy-start | bytes 124
  233.5 7.6 %copy-start.10 = (s32[10]{0:T(128)S(1)}, s32[10]{0:T(128)}, u32[]{:S(2)}) copy-start(s32[10]{0:T(128)} %param.11) | copy-start | bytes 124
  233.8 7.3 %copy-start.1 = (f32[90,3,8,2560]{3,2,1,0:T(8,128)}, f32[90,3,8,2560]{3,2,1,0:T(8,128)S(1)}, u32[]{:S(2)}) copy-start(f32[90,3,8,2560]{3,2,1,0:T(8,128)S(1)} %constant_dynamic-update-slice_fusion) | copy-start | bytes 66355204
where the time goes:
time: 475 us; the launch traced here: 472 us
  waiting for transfers between devices  192 us (40%)
  loops' own time  124 us (26%)
  blocking collectives  59.5 us (13%)
  local copies, waits for them, and re-layouts  45.7 us (10%)
  other arithmetic  24.8 us (5%)
  starting transfers between devices  24.7 us (5%)
    ppermute x8, waiting for transfers between devices, from_behind(): return lax.ppermute(block, axis, route)  192 us
    another operation x1, loops' own time, per_device(): lax.map(one_row, (local_start, lat_fraction, lon_fraction, lon_shift))  124 us
    psum x4, blocking collectives, one_axis_at_a_time(): array = lax.psum(array, axis)  59.5 us
    ppermute x8, starting transfers between devices, from_behind(): return lax.ppermute(block, axis, route)  24.7 us
    dynamic_slice x40, local copies, waits for them, and re-layouts, per_device(): lax.map(one_row, (local_start, lat_fraction, lon_fraction, lon_shift))  23.5 us
    unnamed x30, local copies, waits for them, and re-layouts  20.6 us
    add x10, other arithmetic, one_row(): lat_w[0] * row_block[0] + lat_w[1] * row_block[1] + lat_w[2] * row_block[2]  13.8 us
  transfers between devices with their start and end apart: 8, of which 4 were waited for; matrix products, arithmetic and copies ran while one was open for 2% of the time, Pallas kernels for 0%

commit v1 on v0

v1 whole, which is shorter than its diff:
```python
import math
from functools import partial

import jax
import jax.numpy as jnp
from jax import lax
from jax.experimental import pallas as pl
from jax.experimental.pallas import tpu as pltpu
from jax.sharding import Mesh
from jax.sharding import PartitionSpec as P


LAT = ("lat_0", "lat_1", "lat_2")
ROWS = 10
RING = 4
GROUP = RING * ROWS
FIELDS = 3
LANES = 128
QUARTER = 5
TILES = RING * QUARTER
LON = TILES * LANES
CUTS = (0, 2, 6, 12, 15)
CHUNKS = tuple(zip(CUTS[:-1], CUTS[1:]))
INFO_CHUNK = 1
VMEM_LIMIT = 14 * 1024 * 1024


VMEM = pl.BlockSpec(memory_space=pltpu.VMEM)
SMEM = pl.BlockSpec(memory_space=pltpu.SMEM)
ANY = pl.BlockSpec(memory_space=pl.ANY)


def cubic_weights(fraction):
    return (
        -fraction * (fraction - 1.0) * (fraction - 2.0) / 6.0,
        (fraction + 1.0) * (fraction - 1.0) * (fraction - 2.0) / 2.0,
        -(fraction + 1.0) * fraction * (fraction - 2.0) / 2.0,
        (fraction + 1.0) * fraction * (fraction - 1.0) / 6.0,
    )


def around(place, distance):
    return lax.rem(place + RING + distance, RING)


def tile_count(chunk):
    first, last = CHUNKS[chunk]
    return ROWS * (last - first) + (1 if chunk == INFO_CHUNK else 0)


def copy_units(fields_ref, field_base, chunk, piece_refs):
    first, last = CHUNKS[chunk]
    width = last - first
    place = lax.axis_index(LAT[2])
    for distance in range(RING):
        owner = around(place, distance)
        for unit in range(first, last):
            field, tile = divmod(unit, QUARTER)
            start = pl.multiple_of((owner * QUARTER + tile) * LANES, LANES)
            for row in range(ROWS):
                piece_refs[distance][row * width + unit - first] = fields_ref[
                    row, field - field_base, :, pl.ds(start, LANES)
                ]


def pack_first(fields_ref, *piece_refs):
    copy_units(fields_ref, 0, 0, piece_refs)


def pack_rest(departure_ref, extents_ref, lat_ref, lon_ref, fields_ref, *piece_refs):
    band = lax.axis_index(LAT)
    first_row = band * ROWS
    group_row = lax.axis_index(LAT[:2]) * GROUP
    low_bound = first_row - extents_ref[0, 0] * ROWS + 1
    high_bound = first_row + ROWS - 3 + extents_ref[0, 1] * ROWS
    info_sub = lax.broadcasted_iota(jnp.int32, (8, LANES), 0)
    info_lane = lax.broadcasted_iota(jnp.int32, (8, LANES), 1)
    starts = jnp.zeros((8, LANES), jnp.int32)
    info = jnp.zeros((8, LANES), jnp.float32)
    for row in range(ROWS):
        departure = jnp.clip(departure_ref[row], low_bound, high_bound)
        departure = jnp.clip(departure, 1, RING * 32 * ROWS - 3)
        here = info_lane == row
        starts = jnp.where(here, departure - 1 - (group_row - GROUP), starts)
        info = jnp.where(here & (info_sub == 1), lat_ref[row], info)
        info = jnp.where(here & (info_sub == 2), lon_ref[row], info)
    info = jnp.where(info_sub == 0, starts.astype(jnp.float32), info)
    sub = lax.broadcasted_iota(jnp.int32, (ROWS, LANES), 0)
    lane = lax.broadcasted_iota(jnp.int32, (ROWS, LANES), 1)
    for field in range(FIELDS):
        total = fields_ref[:, field, :, 0:LANES]
        for tile in range(1, TILES):
            total = total + fields_ref[:, field, :, tile * LANES : (tile + 1) * LANES]
        by_row = jnp.sum(jnp.sum(total, axis=1), axis=1, keepdims=True)
        in_lanes = jnp.sum(jnp.where(sub == lane, by_row, 0.0), axis=0, keepdims=True)
        info = jnp.where(info_sub == 3 + field, in_lanes, info)
    for chunk in range(1, len(CHUNKS)):
        refs = piece_refs[(chunk - 1) * RING : chunk * RING]
        copy_units(fields_ref, 0, chunk, refs)
        if chunk == INFO_CHUNK:
            for ref in refs:
                ref[tile_count(chunk) - 1] = info


def join_kernel(*refs):
    for distance in range(RING):
        refs[RING][distance] = refs[distance][...]


def column_kernel(width, start_ref, weight_ref, north_ref, own_ref, south_ref, *refs):
    out_refs, rows_ref = refs[:RING], refs[RING]
    count = width * ROWS
    place = lax.axis_index(LAT[2])
    for distance in range(RING):
        band = around(place, -distance)
        for side, ref in enumerate((north_ref, own_ref, south_ref)):
            rows_ref[pl.ds((side * RING + band) * count, count)] = ref[distance, :count]

    def one_row(row, carry):
        for distance in range(RING):
            source = (RING - distance) % RING
            first = start_ref[source, row]
            total = weight_ref[0, source, row] * rows_ref[pl.ds(first * width, width)]
            for step in range(1, 4):
                total = total + weight_ref[step, source, row] * rows_ref[pl.ds((first + step) * width, width)]
            out_refs[distance][pl.ds(row * width, width)] = total
        return carry

    lax.fori_loop(0, ROWS, one_row, 0)


def field_units(field):
    found = []
    for tile in range(QUARTER):
        unit = field * QUARTER + tile
        for chunk, (first, last) in enumerate(CHUNKS):
            if first <= unit < last:
                found.append((chunk, unit - first, last - first))
    return found


def field_chunks(field):
    return sorted({chunk for chunk, _, _ in field_units(field)})


def finish_kernel(field, rows, shift_ref, weight_ref, ratio_ref, *refs):
    out_ref, turned_ref = refs[-2], refs[-1]
    chunks = field_chunks(field)
    place = lax.axis_index(LAT[2])
    owners = [around(place, -distance) for distance in range(RING)]
    lane = lax.broadcasted_iota(jnp.int32, (8, LANES), 1)
    row_base = pl.program_id(0) * rows
    scale = ratio_ref[field]

    def one_row(step_row, carry):
        row = row_base + step_row
        base = shift_ref[row]
        base = jnp.where(base == 0, LON - 1, base - 1)
        whole = base // LANES
        back = LANES - (base - whole * LANES)
        for distance in range(RING):
            for tile, (chunk, at, width) in enumerate(field_units(field)):
                piece = refs[chunks.index(chunk) * RING + distance][row * width + at]
                turned_ref[owners[distance] * QUARTER + tile] = piece
                turned_ref[TILES + owners[distance] * QUARTER + tile] = piece
        weights = [weight_ref[step, row] * scale for step in range(4)]
        rolled = [pltpu.roll(turned_ref[whole + tile], back, 1) for tile in range(TILES)]
        rolled.append(rolled[0])
        lined = [jnp.where(lane < back, rolled[tile], rolled[tile + 1]) for tile in range(TILES)]
        lined.append(lined[0])
        total = [weights[0] * lined[tile] for tile in range(TILES)]
        for step in range(1, 4):
            moved = [pltpu.roll(lined[tile], LANES - step, 1) for tile in range(TILES)]
            moved.append(moved[0])
            for tile in range(TILES):
                near = jnp.where(lane < LANES - step, moved[tile], moved[tile + 1])
                total[tile] = total[tile] + weights[step] * near
        for tile in range(TILES):
            out_ref[step_row, 0, :, tile * LANES : (tile + 1) * LANES] = total[tile]
        return carry

    lax.fori_loop(0, rows, one_row, 0)


def turn(array, axis, distance):
    count = lax.axis_size(axis)
    return lax.ppermute(array, axis, [(i, (i + distance) % count) for i in range(count)])


def exchange(pieces):
    return [pieces[0]] + [turn(pieces[distance], LAT[2], distance) for distance in range(1, RING)]


def tiles(*shape):
    return jax.ShapeDtypeStruct((*shape, 8, LANES), jnp.float32)


def per_device(fields, lat_fraction, lon_fraction, lon_shift, departure_row, extents):
    params = pltpu.CompilerParams(vmem_limit_bytes=VMEM_LIMIT)
    last_chunk = len(CHUNKS)

    width = CHUNKS[0][1]
    first_pieces = pl.pallas_call(
        pack_first,
        grid=(1,),
        out_shape=[tiles(ROWS * width)] * RING,
        in_specs=[pl.BlockSpec((ROWS, 1, 8, LON), lambda i: (0, 0, 0, 0))],
        out_specs=[pl.BlockSpec((ROWS * width, 8, LANES), lambda i: (0, 0, 0))] * RING,
        compiler_params=params,
        name="pack_a",
    )(fields)
    rest = pl.pallas_call(
        pack_rest,
        out_shape=[tiles(tile_count(chunk)) for chunk in range(1, last_chunk) for _ in range(RING)],
        in_specs=[SMEM] * 4 + [VMEM],
        out_specs=[VMEM] * (RING * (last_chunk - 1)),
        compiler_params=params,
        name="pack_b",
    )(departure_row, extents, lat_fraction, lon_fraction, fields)
    pieces = [first_pieces] + [rest[i * RING : (i + 1) * RING] for i in range(last_chunk - 1)]

    own, north, south = [], [], []
    for chunk in range(last_chunk):
        received = exchange(pieces[chunk])
        joined = pl.pallas_call(
            join_kernel,
            out_shape=tiles(RING, tile_count(chunk)),
            in_specs=[VMEM] * RING,
            out_specs=VMEM,
            compiler_params=params,
            name="join",
        )(*received)
        north.append(turn(joined, LAT[:2], 1))
        south.append(turn(joined, LAT[:2], -1))
        own.append(joined)

    ring_info = own[INFO_CHUNK][:, -1, :, :ROWS]
    ring_start = ring_info[:, 0].astype(jnp.int32)
    ring_weight = jnp.stack(cubic_weights(ring_info[:, 1]))

    gathered = []
    for chunk, (first, last) in enumerate(CHUNKS):
        width = last - first
        columns = pl.pallas_call(
            partial(column_kernel, width),
            out_shape=[tiles(ROWS * width)] * RING,
            in_specs=[SMEM, SMEM, VMEM, VMEM, VMEM],
            out_specs=[VMEM] * RING,
            scratch_shapes=[pltpu.VMEM((3 * GROUP * width, 8, LANES), jnp.float32)],
            compiler_params=params,
            name="column",
        )(ring_start, ring_weight, north[chunk], own[chunk], south[chunk])
        gathered.append(exchange(columns))

    total_rows = lax.axis_size(LAT) * ROWS
    group_row = lax.axis_index(LAT[:2]) * GROUP
    bands = around(lax.axis_index(LAT[2]), -jnp.arange(RING, dtype=jnp.int32))
    ring_rows = bands[:, None] * ROWS + jnp.arange(ROWS, dtype=jnp.int32)[None]
    area = jnp.cos(math.pi * ((group_row + ring_rows).astype(jnp.float32) + 0.5) / total_rows - math.pi / 2.0)
    sums = [part[INFO_CHUNK][:, -1, 3 : 3 + FIELDS, :ROWS] for part in (north, own, south)]
    lon_total = sum(cubic_weights(ring_info[:, 2]))
    before = jnp.sum(area[:, None, :] * sums[1], axis=(0, 2))
    after = jnp.zeros((FIELDS,), jnp.float32)
    for side in range(3):
        spots = side * GROUP + ring_rows
        factor = jnp.zeros((RING, ROWS), jnp.float32)
        for step in range(4):
            hit = (ring_start + step)[None, None] == spots[..., None, None]
            share = area * lon_total * ring_weight[step]
            factor = factor + jnp.sum(jnp.where(hit, share[None, None], 0.0), axis=(2, 3))
        after = after + jnp.sum(factor[:, None, :] * sums[side], axis=(0, 2))
    mass = jnp.pad(jnp.concatenate([before, after]), (0, LANES - 2 * FIELDS))
    parties = (LAT[0], LAT[1], "lev")
    spread = jnp.broadcast_to(mass[None, None], (lax.axis_size(parties), 1, LANES))
    spread = lax.all_to_all(spread, parties, 0, 0)
    mass = jnp.sum(spread, axis=(0, 1))
    ratio = mass[:FIELDS] / mass[FIELDS : 2 * FIELDS]
    lon_w = jnp.stack(cubic_weights(lon_fraction))

    result = None
    half = ROWS // 2
    for field in range(FIELDS):
        operands = [piece for chunk in field_chunks(field) for piece in gathered[chunk]]
        in_specs = [SMEM, SMEM, SMEM] + [VMEM] * len(operands)
        aliases = {}
        if result is not None:
            operands.append(result)
            in_specs.append(ANY)
            aliases = {len(in_specs) - 1: 0}
        result = pl.pallas_call(
            partial(finish_kernel, field, half),
            grid=(2,),
            out_shape=jax.ShapeDtypeStruct(fields.shape, jnp.float32),
            in_specs=in_specs,
            out_specs=pl.BlockSpec((half, 1, 8, LON), lambda i, field=field: (i, field, 0, 0)),
            scratch_shapes=[pltpu.VMEM((2 * TILES, 8, LANES), jnp.float32)],
            input_output_aliases=aliases,
            compiler_params=params,
            name="finish",
        )(lon_shift, lon_w, ratio, *operands)
    return result


def solution(mesh):
    finer = Mesh(mesh.devices.reshape(4, 8, 4, mesh.shape["lev"]), LAT + ("lev",))
    placed = (P(LAT, None, "lev", None), P(LAT), P(LAT), P(LAT), P(LAT), P(LAT, None))
    return jax.shard_map(
        per_device,
        mesh=finer,
        in_specs=placed,
        out_specs=P(LAT, None, "lev", None),
        check_vma=False,
    )
```

time: 475 us -> 136 us (0.29)
  waiting for transfers between devices: 192 us -> 48.9 us
  loops' own time: 124 us -> 0 us
  blocking collectives: 59.5 us -> 0 us
  local copies, waits for them, and re-layouts: 45.7 us -> 5.19 us
  starting transfers between devices: 24.7 us -> 61.5 us
  other arithmetic: 24.8 us -> 1.92 us
  Pallas kernels: 0 us -> 18.1 us
    ppermute x8 -> x32, waiting for transfers between devices: 192 us -> 46.3 us  [turn(): lax.ppermute(array, axis, [(i, (i + distance) % count) for i in range(cou...]
    another operation x1 -> x0, loops' own time: 124 us -> none  [per_device(): lax.map(one_row, (local_start, lat_fraction, lon_fraction, lon_shift))]
    psum x4 -> x0, blocking collectives: 59.5 us -> none  [one_axis_at_a_time(): array = lax.psum(array, axis)]
    ppermute x8 -> x32, starting transfers between devices: 24.7 us -> 50.3 us  [turn(): lax.ppermute(array, axis, [(i, (i + distance) % count) for i in range(cou...]
    dynamic_slice x40 -> x0, local copies, waits for them, and re-layouts: 23.5 us -> none  [per_device(): lax.map(one_row, (local_start, lat_fraction, lon_fraction, lon_shift))]
    pallas_call x0 -> x13, Pallas kernels: none -> 18.1 us  [the longest x3 10.9 us: per_device(): pl.pallas_call(partial(finish_kernel, field, half), grid=(2,), out_shape=...]
    unnamed x30 -> x26, local copies, waits for them, and re-layouts: 20.6 us -> 4.55 us
    add x10 -> x5, other arithmetic: 13.8 us -> 0.09 us  [the longest x1 0.07 us: per_device(): ring_rows = bands[:, None] * ROWS + jnp.arange(ROWS, dtype=jnp.int32)[None]]
  transfers between devices with their start and end apart: 8 -> 33, of which waited for: 4 -> 5; matrix products, arithmetic and copies ran while one was open for 2% -> 2% of each run, Pallas kernels for 0% -> 11%
where the time goes in v1:
time: 136 us
  starting transfers between devices  61.5 us (45%)
  waiting for transfers between devices  48.9 us (36%)
  Pallas kernels  18.1 us (13%)
  local copies, waits for them, and re-layouts  5.19 us (4%)
  other arithmetic  1.92 us (1%)
    ppermute x32, starting transfers between devices, turn(): lax.ppermute(array, axis, [(i, (i + distance) % count) for i in range(cou...  50.3 us
    ppermute x32, waiting for transfers between devices, turn(): lax.ppermute(array, axis, [(i, (i + distance) % count) for i in range(cou...  46.3 us
    all_to_all x1, starting transfers between devices, per_device(): spread = lax.all_to_all(spread, parties, 0, 0)  11.3 us
    pallas_call x3, Pallas kernels, per_device(): pl.pallas_call(partial(finish_kernel, field, half), grid=(2,), out_shape=...  10.9 us
    pallas_call x4, Pallas kernels, per_device(): pl.pallas_call(partial(column_kernel, width), out_shape=[tiles(ROWS * wid...  5.95 us
    unnamed x26, local copies, waits for them, and re-layouts  4.55 us
  transfers between devices with their start and end apart: 33, of which 5 were waited for; matrix products, arithmetic and copies ran while one was open for 2% of the time, Pallas kernels for 11%

profile of v1, /device:TPU:1, one launch (start us, length us, event | category | flops | bytes accessed | tf_op | source)
XLA Modules:
  0.0 135.9 jit_solution(1546451993368336437)
XLA Ops:
  0.0 1.7 %copy-done = f32[10,3,8,2560]{3,2,1,0:T(8,128)S(1)} copy-done((f32[10,3,8,2560]{3,2,1,0:T(8,128)S(1)}, f32[10,3,8,2560]{3,2,1,0:T(8,128)}, u32[]{:S(2)}) %copy-start) | copy-done | bytes 2457624
  1.8 2.2 %collective-permute-start.24 = (f32[20,8,128]{2,1,0:T(8,128)S(1)}, f32[20,8,128]{2,1,0:T(8,128)S(1)}, u32[]{:S(2)}, u32[]{:S(2)}) collective-permute-start(f32[20,8,128]{2,1,0:T(8,128)S(1)} %get-tuple-element.62), channel_id=1, source_target_pairs={{0,2},{2,4},{4,6},{6,0},{1,3},{3,5},{5,7},{7,1},{8,10},{10,12},{12... | collective-permute-start | bytes 245768 | tf_op jit(solution)/shard_map/ppermute | solution.py:187
  4.0 2.6 %collective-permute-start.25 = (f32[20,8,128]{2,1,0:T(8,128)S(1)}, f32[20,8,128]{2,1,0:T(8,128)S(1)}, u32[]{:S(2)}, u32[]{:S(2)}) collective-permute-start(f32[20,8,128]{2,1,0:T(8,128)S(1)} %get-tuple-element.63), channel_id=1, source_target_pairs={{0,4},{2,6},{4,0},{6,2},{1,5},{3,7},{5,1},{7,3},{8,12},{10,14},{12... | collective-permute-start | bytes 245768 | tf_op jit(solution)/shard_map/ppermute | solution.py:187
  10.1 1.7 %collective-permute-start.15 = (f32[30,8,128]{2,1,0:T(8,128)S(1)}, f32[30,8,128]{2,1,0:T(8,128)S(1)}, u32[]{:S(2)}, u32[]{:S(2)}) collective-permute-start(f32[30,8,128]{2,1,0:T(8,128)S(1)} %get-tuple-element.52), channel_id=1, source_target_pairs={{0,6},{2,0},{4,2},{6,4},{1,7},{3,1},{5,3},{7,5},{8,14},{10,8},{12,... | collective-permute-start | bytes 368648 | tf_op jit(solution)/shard_map/ppermute | solution.py:187
  12.3 1.8 %collective-permute-start.1 = (f32[41,8,128]{2,1,0:T(8,128)S(1)}, f32[41,8,128]{2,1,0:T(8,128)S(1)}, u32[]{:S(2)}, u32[]{:S(2)}) collective-permute-start(f32[41,8,128]{2,1,0:T(8,128)S(1)} %get-tuple-element.39), channel_id=1, source_target_pairs={{0,4},{2,6},{4,0},{6,2},{1,5},{3,7},{5,1},{7,3},{8,12},{10,14},{12... | collective-permute-start | bytes 503816 | tf_op jit(solution)/shard_map/ppermute | solution.py:187
  16.4 1.6 %collective-permute-start.6 = (f32[60,8,128]{2,1,0:T(8,128)S(1)}, f32[60,8,128]{2,1,0:T(8,128)S(1)}, u32[]{:S(2)}, u32[]{:S(2)}) collective-permute-start(f32[60,8,128]{2,1,0:T(8,128)S(1)} %get-tuple-element.43), channel_id=1, source_target_pairs={{0,4},{2,6},{4,0},{6,2},{1,5},{3,7},{5,1},{7,3},{8,12},{10,14},{12... | collective-permute-start | bytes 737288 | tf_op jit(solution)/shard_map/ppermute | solution.py:187
  18.0 2.6 %collective-permute-done.refs_1_ = f32[41,8,128]{2,1,0:T(8,128)S(1)} collective-permute-done((f32[41,8,128]{2,1,0:T(8,128)S(1)}, f32[41,8,128]{2,1,0:T(8,128)S(1)}, u32[]{:S(2)}, u32[]{:S(2)}) %collective-permute-start) | collective-permute-done | bytes 167968 | tf_op jit(solution)/shard_map/ppermute | solution.py:187
  20.6 2.5 %collective-permute-done.1.refs_2_ = f32[41,8,128]{2,1,0:T(8,128)S(1)} collective-permute-done((f32[41,8,128]{2,1,0:T(8,128)S(1)}, f32[41,8,128]{2,1,0:T(8,128)S(1)}, u32[]{:S(2)}, u32[]{:S(2)}) %collective-permute-start.1) | collective-permute-done | bytes 167968 | tf_op jit(solution)/shard_map/ppermute | solution.py:187
  23.1 7.5 %collective-permute-start.28 = (f32[4,20,8,128]{3,2,1,0:T(8,128)S(1)}, f32[4,20,8,128]{3,2,1,0:T(8,128)S(1)}, u32[]{:S(2)}, u32[]{:S(2)}) collective-permute-start(f32[4,20,8,128]{3,2,1,0:T(8,128)S(1)} %join.7.own_ref), channel_id=1, source_target_pairs={{0,248},{8,0},{16,8},{24,16},{32,24},{40,32},{48,40},{56,48},{64,5... | collective-permute-start | bytes 983048 | tf_op jit(solution)/shard_map/ppermute | solution.py:187
  30.8 1.7 %collective-permute-start.4 = (f32[4,41,8,128]{3,2,1,0:T(8,128)S(1)}, f32[4,41,8,128]{3,2,1,0:T(8,128)S(1)}, u32[]{:S(2)}, u32[]{:S(2)}) collective-permute-start(f32[4,41,8,128]{3,2,1,0:T(8,128)S(1)} %join.4.own_ref), channel_id=1, source_target_pairs={{0,248},{8,0},{16,8},{24,16},{32,24},{40,32},{48,40},{56,48},{64,5... | collective-permute-start | bytes 2015240 | tf_op jit(solution)/shard_map/ppermute | solution.py:187
  32.7 3.7 %collective-permute-start.3 = (f32[4,41,8,128]{3,2,1,0:T(8,128)S(1)}, f32[4,41,8,128]{3,2,1,0:T(8,128)S(1)}, u32[]{:S(2)}, u32[]{:S(2)}) collective-permute-start(f32[4,41,8,128]{3,2,1,0:T(8,128)S(1)} %join.4.own_ref), channel_id=1, source_target_pairs={{0,8},{8,16},{16,24},{24,32},{32,40},{40,48},{48,56},{56,64},{64,7... | collective-permute-start | bytes 2015240 | tf_op jit(solution)/shard_map/ppermute | solution.py:187
  36.5 6.4 %collective-permute-start.9 = (f32[4,60,8,128]{3,2,1,0:T(8,128)S(1)}, f32[4,60,8,128]{3,2,1,0:T(8,128)S(1)}, u32[]{:S(2)}, u32[]{:S(2)}) collective-permute-start(f32[4,60,8,128]{3,2,1,0:T(8,128)S(1)} %join.5.own_ref), channel_id=1, source_target_pairs={{0,248},{8,0},{16,8},{24,16},{32,24},{40,32},{48,40},{56,48},{64,5... | collective-permute-start | bytes 2949128 | tf_op jit(solution)/shard_map/ppermute | solution.py:187
  44.3 40.4 %collective-permute-done.27.north_ref = f32[4,20,8,128]{3,2,1,0:T(8,128)S(1)} collective-permute-done((f32[4,20,8,128]{3,2,1,0:T(8,128)S(1)}, f32[4,20,8,128]{3,2,1,0:T(8,128)S(1)}, u32[]{:S(2)}, u32[]{:S(2)}) %collective-permute-start.27) | collective-permute-done | bytes 327712 | tf_op jit(solution)/shard_map/ppermute | solution.py:187
  87.5 1.8 %column.6 = (f32[40,8,128]{2,1,0:T(8,128)S(1)}, f32[40,8,128]{2,1,0:T(8,128)S(1)}, f32[40,8,128]{2,1,0:T(8,128)}, f32[40,8,128]{2,1,0:T(8,128)}) custom-call(s32[4,10]{1,0:T(4,128)S(1)} %bitcast.33, f32[4,4,10]{2,1,0:T(4,128)S(1)} %pad_maximum_fusion.weight_ref, f32[4,41,8,128]{3,2,1,0:T(8,128)S(1)} %collective-permute-done.3.north_ref, ...), custom_call_target="tpu_custom_call" | custom-call | tf_op jit(solution)/shard_map/column/pallas_call | solution.py:244
  89.5 2.7 %collective-permute-start.31 = (f32[20,8,128]{2,1,0:T(8,128)S(1)}, f32[20,8,128]{2,1,0:T(8,128)S(1)}, u32[]{:S(2)}, u32[]{:S(2)}) collective-permute-start(f32[20,8,128]{2,1,0:T(8,128)S(1)} %get-tuple-element.68), channel_id=1, source_target_pairs={{0,6},{2,0},{4,2},{6,4},{1,7},{3,1},{5,3},{7,5},{8,14},{10,8},{12,... | collective-permute-start | bytes 245768 | tf_op jit(solution)/shard_map/ppermute | solution.py:187
  92.3 2.0 %column.4 = (f32[60,8,128]{2,1,0:T(8,128)S(1)}, f32[60,8,128]{2,1,0:T(8,128)}, f32[60,8,128]{2,1,0:T(8,128)}, f32[60,8,128]{2,1,0:T(8,128)S(1)}) custom-call(s32[4,10]{1,0:T(4,128)S(1)} %bitcast.34, f32[4,4,10]{2,1,0:T(4,128)S(1)} %pad_maximum_fusion.weight_ref, f32[4,60,8,128]{3,2,1,0:T(8,128)S(1)} %collective-permute-done.8.north_ref, ...), custom_call_target="tpu_custom_call" | custom-call | tf_op jit(solution)/shard_map/column/pallas_call | solution.py:244
  96.4 2.1 %collective-permute-start.22 = (f32[40,8,128]{2,1,0:T(8,128)}, f32[40,8,128]{2,1,0:T(8,128)S(1)}, u32[]{:S(2)}, u32[]{:S(2)}) collective-permute-start(f32[40,8,128]{2,1,0:T(8,128)} %get-tuple-element.59), channel_id=1, source_target_pairs={{0,4},{2,6},{4,0},{6,2},{1,5},{3,7},{5,1},{7,3},{8,12},{10,14},{12... | collective-permute-start | bytes 491528 | tf_op jit(solution)/shard_map/ppermute | solution.py:187
  99.6 11.3 %all-to-all-start = ((f32[64,1,128]{2,1,0:T(1,128)}), f32[64,1,128]{2,1,0:T(1,128)S(1)}, u32[]{:S(2)}, u32[]{:S(2)}) async-start(f32[64,1,128]{2,1,0:T(1,128)} %broadcast_in_dim.115), calls=%async_computation | async-start | bytes 65536 | tf_op jit(solution)/shard_map/all_to_all | solution.py:275
  112.2 2.4 %collective-permute-start.12 = (f32[60,8,128]{2,1,0:T(8,128)}, f32[60,8,128]{2,1,0:T(8,128)S(1)}, u32[]{:S(2)}, u32[]{:S(2)}) collective-permute-start(f32[60,8,128]{2,1,0:T(8,128)} %copy-done.9), channel_id=1, source_target_pairs={{0,6},{2,0},{4,2},{6,4},{1,7},{3,1},{5,3},{7,5},{8,14},{10,8},{12,... | collective-permute-start | bytes 737288 | tf_op jit(solution)/shard_map/ppermute | solution.py:187
  117.6 2.6 %all-to-all-done = f32[64,1,128]{2,1,0:T(1,128)S(1)} async-done(((f32[64,1,128]{2,1,0:T(1,128)}), f32[64,1,128]{2,1,0:T(1,128)S(1)}, u32[]{:S(2)}, u32[]{:S(2)}) %all-to-all-start) | async-done | bytes 32800 | tf_op jit(solution)/shard_map/all_to_all | solution.py:275
  122.4 1.7 %collective-permute-start.20 = (f32[30,8,128]{2,1,0:T(8,128)}, f32[30,8,128]{2,1,0:T(8,128)S(1)}, u32[]{:S(2)}, u32[]{:S(2)}) collective-permute-start(f32[30,8,128]{2,1,0:T(8,128)} %copy-done.10), channel_id=1, source_target_pairs={{0,6},{2,0},{4,2},{6,4},{1,7},{3,1},{5,3},{7,5},{8,14},{10,8},{12,... | collective-permute-start | bytes 368648 | tf_op jit(solution)/shard_map/ppermute | solution.py:187
  125.0 3.6 %finish.3.refs_8_ = f32[10,3,8,2560]{3,2,1,0:T(8,128)} custom-call(s32[10]{0:T(128)S(1)} %copy-done.4, f32[4,10]{1,0:T(4,128)S(1)} %pad_maximum_fusion.1.weight_ref, f32[3]{0:T(128)S(1)} %slice_divide_fusion.ratio_ref, f32[20,8,128]{2,1,0:T(8,128)S(1)} %get-tuple-element.65.refs_0_, f32[20,8,128]{2,1,0:T(8,128)S(1)} %collective-permute-done.29.refs_1_, ...), custom_call_target="tpu_custom_call" | custom-call | tf_op jit(solution)/shard_map/finish/pallas_call | solution.py:290
  128.6 3.6 %finish.4.refs_8_ = f32[10,3,8,2560]{3,2,1,0:T(8,128)} custom-call(s32[10]{0:T(128)S(1)} %copy-done.4, f32[4,10]{1,0:T(4,128)S(1)} %pad_maximum_fusion.1.weight_ref, f32[3]{0:T(128)S(1)} %slice_divide_fusion.ratio_ref, f32[40,8,128]{2,1,0:T(8,128)S(1)} %get-tuple-element.57.refs_4_.refs_0_, ...), custom_call_target="tpu_custom_call", output_to_operand_aliasing={{}: (11, {})} | custom-call | tf_op jit(solution)/shard_map/finish/pallas_call | solution.py:290
  132.3 3.6 %finish.5 = f32[10,3,8,2560]{3,2,1,0:T(8,128)} custom-call(s32[10]{0:T(128)S(1)} %copy-done.4, f32[4,10]{1,0:T(4,128)S(1)} %pad_maximum_fusion.1.weight_ref, f32[3]{0:T(128)S(1)} %slice_divide_fusion.ratio_ref, f32[60,8,128]{2,1,0:T(8,128)S(1)} %get-tuple-element.45.refs_4_.refs_0_, ...), custom_call_target="tpu_custom_call", output_to_operand_aliasing={{}: (11, {})} | custom-call | tf_op jit(solution)/shard_map/finish/pallas_call | solution.py:290
  (106 shorter events, 21.7 us)
Async XLA Ops:
  11.8 8.8 %collective-permute-start = (f32[41,8,128]{2,1,0:T(8,128)S(1)}, f32[41,8,128]{2,1,0:T(8,128)S(1)}, u32[]{:S(2)}, u32[]{:S(2)}) collective-permute-start(f32[41,8,128]{2,1,0:T(8,128)S(1)} %get-tuple-element.38), channel_id=1, source_target_pairs={{0,2},{2,4},{4,6},{6,0},{1,3},{3,5},{5,7},{7,1},{8,10},{10,12},{12... | collective-permute-start | bytes 503816 | tf_op jit(solution)/shard_map/ppermute | solution.py:187
  12.3 10.9 %collective-permute-start.1 = (f32[41,8,128]{2,1,0:T(8,128)S(1)}, f32[41,8,128]{2,1,0:T(8,128)S(1)}, u32[]{:S(2)}, u32[]{:S(2)}) collective-permute-start(f32[41,8,128]{2,1,0:T(8,128)S(1)} %get-tuple-element.39), channel_id=1, source_target_pairs={{0,4},{2,6},{4,0},{6,2},{1,5},{3,7},{5,1},{7,3},{8,12},{10,14},{12... | collective-permute-start | bytes 503816 | tf_op jit(solution)/shard_map/ppermute | solution.py:187
  14.8 15.9 %collective-permute-start.2 = (f32[41,8,128]{2,1,0:T(8,128)S(1)}, f32[41,8,128]{2,1,0:T(8,128)S(1)}, u32[]{:S(2)}, u32[]{:S(2)}) collective-permute-start(f32[41,8,128]{2,1,0:T(8,128)S(1)} %get-tuple-element.40), channel_id=1, source_target_pairs={{0,6},{2,0},{4,2},{6,4},{1,7},{3,1},{5,3},{7,5},{8,14},{10,8},{12,... | collective-permute-start | bytes 503816 | tf_op jit(solution)/shard_map/ppermute | solution.py:187
  16.1 16.6 %collective-permute-start.5 = (f32[60,8,128]{2,1,0:T(8,128)S(1)}, f32[60,8,128]{2,1,0:T(8,128)S(1)}, u32[]{:S(2)}, u32[]{:S(2)}) collective-permute-start(f32[60,8,128]{2,1,0:T(8,128)S(1)} %get-tuple-element.42), channel_id=1, source_target_pairs={{0,2},{2,4},{4,6},{6,0},{1,3},{3,5},{5,7},{7,1},{8,10},{10,12},{12... | collective-permute-start | bytes 737288 | tf_op jit(solution)/shard_map/ppermute | solution.py:187
  16.4 20.0 %collective-permute-start.6 = (f32[60,8,128]{2,1,0:T(8,128)S(1)}, f32[60,8,128]{2,1,0:T(8,128)S(1)}, u32[]{:S(2)}, u32[]{:S(2)}) collective-permute-start(f32[60,8,128]{2,1,0:T(8,128)S(1)} %get-tuple-element.43), channel_id=1, source_target_pairs={{0,4},{2,6},{4,0},{6,2},{1,5},{3,7},{5,1},{7,3},{8,12},{10,14},{12... | collective-permute-start | bytes 737288 | tf_op jit(solution)/shard_map/ppermute | solution.py:187
  20.6 15.8 %collective-permute-start.7 = (f32[60,8,128]{2,1,0:T(8,128)S(1)}, f32[60,8,128]{2,1,0:T(8,128)S(1)}, u32[]{:S(2)}, u32[]{:S(2)}) collective-permute-start(f32[60,8,128]{2,1,0:T(8,128)S(1)} %get-tuple-element.44), channel_id=1, source_target_pairs={{0,6},{2,0},{4,2},{6,4},{1,7},{3,1},{5,3},{7,5},{8,14},{10,8},{12,... | collective-permute-start | bytes 737288 | tf_op jit(solution)/shard_map/ppermute | solution.py:187
  23.1 20.9 %collective-permute-start.28 = (f32[4,20,8,128]{3,2,1,0:T(8,128)S(1)}, f32[4,20,8,128]{3,2,1,0:T(8,128)S(1)}, u32[]{:S(2)}, u32[]{:S(2)}) collective-permute-start(f32[4,20,8,128]{3,2,1,0:T(8,128)S(1)} %join.7.own_ref), channel_id=1, source_target_pairs={{0,248},{8,0},{16,8},{24,16},{32,24},{40,32},{48,40},{56,48},{64,5... | collective-permute-start | bytes 983048 | tf_op jit(solution)/shard_map/ppermute | solution.py:187
  30.8 56.1 %collective-permute-start.4 = (f32[4,41,8,128]{3,2,1,0:T(8,128)S(1)}, f32[4,41,8,128]{3,2,1,0:T(8,128)S(1)}, u32[]{:S(2)}, u32[]{:S(2)}) collective-permute-start(f32[4,41,8,128]{3,2,1,0:T(8,128)S(1)} %join.4.own_ref), channel_id=1, source_target_pairs={{0,248},{8,0},{16,8},{24,16},{32,24},{40,32},{48,40},{56,48},{64,5... | collective-permute-start | bytes 2015240 | tf_op jit(solution)/shard_map/ppermute | solution.py:187
  32.7 54.7 %collective-permute-start.3 = (f32[4,41,8,128]{3,2,1,0:T(8,128)S(1)}, f32[4,41,8,128]{3,2,1,0:T(8,128)S(1)}, u32[]{:S(2)}, u32[]{:S(2)}) collective-permute-start(f32[4,41,8,128]{3,2,1,0:T(8,128)S(1)} %join.4.own_ref), channel_id=1, source_target_pairs={{0,8},{8,16},{16,24},{24,32},{32,40},{40,48},{48,56},{56,64},{64,7... | collective-permute-start | bytes 2015240 | tf_op jit(solution)/shard_map/ppermute | solution.py:187
  36.5 52.9 %collective-permute-start.9 = (f32[4,60,8,128]{3,2,1,0:T(8,128)S(1)}, f32[4,60,8,128]{3,2,1,0:T(8,128)S(1)}, u32[]{:S(2)}, u32[]{:S(2)}) collective-permute-start(f32[4,60,8,128]{3,2,1,0:T(8,128)S(1)} %join.5.own_ref), channel_id=1, source_target_pairs={{0,248},{8,0},{16,8},{24,16},{32,24},{40,32},{48,40},{56,48},{64,5... | collective-permute-start | bytes 2949128 | tf_op jit(solution)/shard_map/ppermute | solution.py:187
  42.9 46.7 %collective-permute-start.8 = (f32[4,60,8,128]{3,2,1,0:T(8,128)S(1)}, f32[4,60,8,128]{3,2,1,0:T(8,128)S(1)}, u32[]{:S(2)}, u32[]{:S(2)}) collective-permute-start(f32[4,60,8,128]{3,2,1,0:T(8,128)S(1)} %join.5.own_ref), channel_id=1, source_target_pairs={{0,8},{8,16},{16,24},{24,32},{32,40},{40,48},{48,56},{56,64},{64,7... | collective-permute-start | bytes 2949128 | tf_op jit(solution)/shard_map/ppermute | solution.py:187
  44.0 40.6 %collective-permute-start.27 = (f32[4,20,8,128]{3,2,1,0:T(8,128)S(1)}, f32[4,20,8,128]{3,2,1,0:T(8,128)S(1)}, u32[]{:S(2)}, u32[]{:S(2)}) collective-permute-start(f32[4,20,8,128]{3,2,1,0:T(8,128)S(1)} %join.7.own_ref), channel_id=1, source_target_pairs={{0,8},{8,16},{16,24},{24,32},{32,40},{40,48},{48,56},{56,64},{64,7... | collective-permute-start | bytes 983048 | tf_op jit(solution)/shard_map/ppermute | solution.py:187
  84.7 13.8 %collective-permute-start.17 = (f32[4,30,8,128]{3,2,1,0:T(8,128)S(1)}, f32[4,30,8,128]{3,2,1,0:T(8,128)S(1)}, u32[]{:S(2)}, u32[]{:S(2)}) collective-permute-start(f32[4,30,8,128]{3,2,1,0:T(8,128)S(1)} %join.6.own_ref), channel_id=1, source_target_pairs={{0,248},{8,0},{16,8},{24,16},{32,24},{40,32},{48,40},{56,48},{64,5... | collective-permute-start | bytes 1474568 | tf_op jit(solution)/shard_map/ppermute | solution.py:187
  86.9 24.0 %collective-permute-start.16 = (f32[4,30,8,128]{3,2,1,0:T(8,128)S(1)}, f32[4,30,8,128]{3,2,1,0:T(8,128)S(1)}, u32[]{:S(2)}, u32[]{:S(2)}) collective-permute-start(f32[4,30,8,128]{3,2,1,0:T(8,128)S(1)} %join.6.own_ref), channel_id=1, source_target_pairs={{0,8},{8,16},{16,24},{24,32},{32,40},{40,48},{48,56},{56,64},{64,7... | collective-permute-start | bytes 1474568 | tf_op jit(solution)/shard_map/ppermute | solution.py:187
  94.3 17.9 %collective-permute-start.21 = (f32[40,8,128]{2,1,0:T(8,128)S(1)}, f32[40,8,128]{2,1,0:T(8,128)S(1)}, u32[]{:S(2)}, u32[]{:S(2)}) collective-permute-start(f32[40,8,128]{2,1,0:T(8,128)S(1)} %get-tuple-element.58), channel_id=1, source_target_pairs={{0,2},{2,4},{4,6},{6,0},{1,3},{3,5},{5,7},{7,1},{8,10},{10,12},{12... | collective-permute-start | bytes 491528 | tf_op jit(solution)/shard_map/ppermute | solution.py:187
  94.9 27.5 %collective-permute-start.10 = (f32[60,8,128]{2,1,0:T(8,128)}, f32[60,8,128]{2,1,0:T(8,128)S(1)}, u32[]{:S(2)}, u32[]{:S(2)}) collective-permute-start(f32[60,8,128]{2,1,0:T(8,128)} %get-tuple-element.46), channel_id=1, source_target_pairs={{0,2},{2,4},{4,6},{6,0},{1,3},{3,5},{5,7},{7,1},{8,10},{10,12},{12... | collective-permute-start | bytes 737288 | tf_op jit(solution)/shard_map/ppermute | solution.py:187
  96.4 23.9 %collective-permute-start.22 = (f32[40,8,128]{2,1,0:T(8,128)}, f32[40,8,128]{2,1,0:T(8,128)S(1)}, u32[]{:S(2)}, u32[]{:S(2)}) collective-permute-start(f32[40,8,128]{2,1,0:T(8,128)} %get-tuple-element.59), channel_id=1, source_target_pairs={{0,4},{2,6},{4,0},{6,2},{1,5},{3,7},{5,1},{7,3},{8,12},{10,14},{12... | collective-permute-start | bytes 491528 | tf_op jit(solution)/shard_map/ppermute | solution.py:187
  98.4 23.1 %collective-permute-start.23 = (f32[40,8,128]{2,1,0:T(8,128)}, f32[40,8,128]{2,1,0:T(8,128)S(1)}, u32[]{:S(2)}, u32[]{:S(2)}) collective-permute-start(f32[40,8,128]{2,1,0:T(8,128)} %get-tuple-element.60), channel_id=1, source_target_pairs={{0,6},{2,0},{4,2},{6,4},{1,7},{3,1},{5,3},{7,5},{8,14},{10,8},{12,... | collective-permute-start | bytes 491528 | tf_op jit(solution)/shard_map/ppermute | solution.py:187
  99.6 20.6 %all-to-all-start = ((f32[64,1,128]{2,1,0:T(1,128)}), f32[64,1,128]{2,1,0:T(1,128)S(1)}, u32[]{:S(2)}, u32[]{:S(2)}) async-start(f32[64,1,128]{2,1,0:T(1,128)} %broadcast_in_dim.115), calls=%async_computation | async-start | bytes 65536 | tf_op jit(solution)/shard_map/all_to_all | solution.py:275
  110.9 17.7 %collective-permute-start.11 = (f32[60,8,128]{2,1,0:T(8,128)}, f32[60,8,128]{2,1,0:T(8,128)S(1)}, u32[]{:S(2)}, u32[]{:S(2)}) collective-permute-start(f32[60,8,128]{2,1,0:T(8,128)} %get-tuple-element.47), channel_id=1, source_target_pairs={{0,4},{2,6},{4,0},{6,2},{1,5},{3,7},{5,1},{7,3},{8,12},{10,14},{12... | collective-permute-start | bytes 737288 | tf_op jit(solution)/shard_map/ppermute | solution.py:187
  112.2 16.4 %collective-permute-start.12 = (f32[60,8,128]{2,1,0:T(8,128)}, f32[60,8,128]{2,1,0:T(8,128)S(1)}, u32[]{:S(2)}, u32[]{:S(2)}) collective-permute-start(f32[60,8,128]{2,1,0:T(8,128)} %copy-done.9), channel_id=1, source_target_pairs={{0,6},{2,0},{4,2},{6,4},{1,7},{3,1},{5,3},{7,5},{8,14},{10,8},{12,... | collective-permute-start | bytes 737288 | tf_op jit(solution)/shard_map/ppermute | solution.py:187
  120.3 12.0 %collective-permute-start.18 = (f32[30,8,128]{2,1,0:T(8,128)}, f32[30,8,128]{2,1,0:T(8,128)S(1)}, u32[]{:S(2)}, u32[]{:S(2)}) collective-permute-start(f32[30,8,128]{2,1,0:T(8,128)} %copy-done.12), channel_id=1, source_target_pairs={{0,2},{2,4},{4,6},{6,0},{1,3},{3,5},{5,7},{7,1},{8,10},{10,12},{12... | collective-permute-start | bytes 368648 | tf_op jit(solution)/shard_map/ppermute | solution.py:187
  121.5 10.7 %collective-permute-start.19 = (f32[30,8,128]{2,1,0:T(8,128)}, f32[30,8,128]{2,1,0:T(8,128)S(1)}, u32[]{:S(2)}, u32[]{:S(2)}) collective-permute-start(f32[30,8,128]{2,1,0:T(8,128)} %copy-done.11), channel_id=1, source_target_pairs={{0,4},{2,6},{4,0},{6,2},{1,5},{3,7},{5,1},{7,3},{8,12},{10,14},{12... | collective-permute-start | bytes 368648 | tf_op jit(solution)/shard_map/ppermute | solution.py:187
  122.4 9.9 %collective-permute-start.20 = (f32[30,8,128]{2,1,0:T(8,128)}, f32[30,8,128]{2,1,0:T(8,128)S(1)}, u32[]{:S(2)}, u32[]{:S(2)}) collective-permute-start(f32[30,8,128]{2,1,0:T(8,128)} %copy-done.10), channel_id=1, source_target_pairs={{0,6},{2,0},{4,2},{6,4},{1,7},{3,1},{5,3},{7,5},{8,14},{10,8},{12,... | collective-permute-start | bytes 368648 | tf_op jit(solution)/shard_map/ppermute | solution.py:187
  (22 other events, 152.1 us)

commit v2 on v1

--- a/solution.py
+++ b/solution.py
@@ -19,10 +19,11 @@
 QUARTER = 5
 TILES = RING * QUARTER
 LON = TILES * LANES
-CUTS = (0, 2, 6, 12, 15)
+CUTS = (0, 2, 7, 12, 15)
 CHUNKS = tuple(zip(CUTS[:-1], CUTS[1:]))
 INFO_CHUNK = 1
-VMEM_LIMIT = 14 * 1024 * 1024
+TOGETHER = 2
+VMEM_LIMIT = 10 * 1024 * 1024
 
 
 VMEM = pl.BlockSpec(memory_space=pltpu.VMEM)
@@ -48,7 +49,7 @@
     return ROWS * (last - first) + (1 if chunk == INFO_CHUNK else 0)
 
 
-def copy_units(fields_ref, field_base, chunk, piece_refs):
+def copy_units(fields_ref, chunk, piece_refs):
     first, last = CHUNKS[chunk]
     width = last - first
     place = lax.axis_index(LAT[2])
@@ -59,12 +60,12 @@
             start = pl.multiple_of((owner * QUARTER + tile) * LANES, LANES)
             for row in range(ROWS):
                 piece_refs[distance][row * width + unit - first] = fields_ref[
-                    row, field - field_base, :, pl.ds(start, LANES)
+                    row, field, :, pl.ds(start, LANES)
                 ]
 
 
 def pack_first(fields_ref, *piece_refs):
-    copy_units(fields_ref, 0, 0, piece_refs)
+    copy_units(fields_ref, 0, piece_refs)
 
 
 def pack_rest(departure_ref, extents_ref, lat_ref, lon_ref, fields_ref, *piece_refs):
@@ -96,7 +97,7 @@
         info = jnp.where(info_sub == 3 + field, in_lanes, info)
     for chunk in range(1, len(CHUNKS)):
         refs = piece_refs[(chunk - 1) * RING : chunk * RING]
-        copy_units(fields_ref, 0, chunk, refs)
+        copy_units(fields_ref, chunk, refs)
         if chunk == INFO_CHUNK:
             for ref in refs:
                 ref[tile_count(chunk) - 1] = info
@@ -105,12 +106,17 @@
 def join_kernel(*refs):
     for distance in range(RING):
         refs[RING][distance] = refs[distance][...]
+        for info_ref in refs[RING + 1 :]:
+            info_ref[distance] = refs[distance][tile_count(INFO_CHUNK) - 1]
 
 
 def column_kernel(width, start_ref, weight_ref, north_ref, own_ref, south_ref, *refs):
-    out_refs, rows_ref = refs[:RING], refs[RING]
+    out_refs, rows_ref = refs[:RING], refs[-1]
     count = width * ROWS
     place = lax.axis_index(LAT[2])
+    for info_ref in refs[RING:-1]:
+        for side, ref in enumerate((north_ref, own_ref, south_ref)):
+            info_ref[side] = ref[:, count]
     for distance in range(RING):
         band = around(place, -distance)
         for side, ref in enumerate((north_ref, own_ref, south_ref)):
@@ -143,43 +149,44 @@
     return sorted({chunk for chunk, _, _ in field_units(field)})
 
 
-def finish_kernel(field, rows, shift_ref, weight_ref, ratio_ref, *refs):
+def finish_kernel(field, shift_ref, weight_ref, ratio_ref, *refs):
     out_ref, turned_ref = refs[-2], refs[-1]
     chunks = field_chunks(field)
     place = lax.axis_index(LAT[2])
     owners = [around(place, -distance) for distance in range(RING)]
     lane = lax.broadcasted_iota(jnp.int32, (8, LANES), 1)
-    row_base = pl.program_id(0) * rows
     scale = ratio_ref[field]
 
-    def one_row(step_row, carry):
-        row = row_base + step_row
-        base = shift_ref[row]
-        base = jnp.where(base == 0, LON - 1, base - 1)
-        whole = base // LANES
-        back = LANES - (base - whole * LANES)
-        for distance in range(RING):
-            for tile, (chunk, at, width) in enumerate(field_units(field)):
-                piece = refs[chunks.index(chunk) * RING + distance][row * width + at]
-                turned_ref[owners[distance] * QUARTER + tile] = piece
-                turned_ref[TILES + owners[distance] * QUARTER + tile] = piece
-        weights = [weight_ref[step, row] * scale for step in range(4)]
-        rolled = [pltpu.roll(turned_ref[whole + tile], back, 1) for tile in range(TILES)]
-        rolled.append(rolled[0])
-        lined = [jnp.where(lane < back, rolled[tile], rolled[tile + 1]) for tile in range(TILES)]
-        lined.append(lined[0])
-        total = [weights[0] * lined[tile] for tile in range(TILES)]
-        for step in range(1, 4):
-            moved = [pltpu.roll(lined[tile], LANES - step, 1) for tile in range(TILES)]
-            moved.append(moved[0])
+    def ahead(values, step):
+        moved = [pltpu.roll(value, LANES - step, 1) for value in values]
+        following = moved[1:] + moved[:1]
+        return [jnp.where(lane < LANES - step, here, then) for here, then in zip(moved, following)]
+
+    def some_rows(pair, carry):
+        for member in range(TOGETHER):
+            row = pair * TOGETHER + member
+            slot = member * 2 * TILES
+            base = shift_ref[row]
+            base = jnp.where(base == 0, LON - 1, base - 1)
+            whole = base // LANES
+            back = LANES - (base - whole * LANES)
+            for distance in range(RING):
+                for tile, (chunk, at, width) in enumerate(field_units(field)):
+                    piece = refs[chunks.index(chunk) * RING + distance][row * width + at]
+                    turned_ref[slot + owners[distance] * QUARTER + tile] = piece
+                    turned_ref[slot + TILES + owners[distance] * QUARTER + tile] = piece
+            weights = [weight_ref[step, row] * scale for step in range(4)]
+            rolled = [pltpu.roll(turned_ref[slot + whole + tile], back, 1) for tile in range(TILES)]
+            lined = [jnp.where(lane < back, here, then) for here, then in zip(rolled, rolled[1:] + rolled[:1])]
+            next_one = ahead(lined, 1)
+            far = ahead([weights[2] * here + weights[3] * then for here, then in zip(lined, next_one)], 2)
             for tile in range(TILES):
-                near = jnp.where(lane < LANES - step, moved[tile], moved[tile + 1])
-                total[tile] = total[tile] + weights[step] * near
-        for tile in range(TILES):
-            out_ref[step_row, 0, :, tile * LANES : (tile + 1) * LANES] = total[tile]
+                out_ref[row, 0, :, tile * LANES : (tile + 1) * LANES] = (
+                    weights[0] * lined[tile] + weights[1] * next_one[tile] + far[tile]
+                )
         return carry
 
-    lax.fori_loop(0, rows, one_row, 0)
+    lax.fori_loop(0, ROWS // TOGETHER, some_rows, 0)
 
 
 def turn(array, axis, distance):
@@ -202,10 +209,9 @@
     width = CHUNKS[0][1]
     first_pieces = pl.pallas_call(
         pack_first,
-        grid=(1,),
         out_shape=[tiles(ROWS * width)] * RING,
-        in_specs=[pl.BlockSpec((ROWS, 1, 8, LON), lambda i: (0, 0, 0, 0))],
-        out_specs=[pl.BlockSpec((ROWS * width, 8, LANES), lambda i: (0, 0, 0))] * RING,
+        in_specs=[VMEM],
+        out_specs=[VMEM] * RING,
         compiler_params=params,
         name="pack_a",
     )(fields)
@@ -224,17 +230,19 @@
         received = exchange(pieces[chunk])
         joined = pl.pallas_call(
             join_kernel,
-            out_shape=tiles(RING, tile_count(chunk)),
+            out_shape=[tiles(RING, tile_count(chunk))] + [tiles(RING)] * (chunk == INFO_CHUNK),
             in_specs=[VMEM] * RING,
-            out_specs=VMEM,
+            out_specs=[VMEM] * (2 if chunk == INFO_CHUNK else 1),
             compiler_params=params,
             name="join",
         )(*received)
+        if chunk == INFO_CHUNK:
+            ring_info = joined[1][:, :, :ROWS]
+        joined = joined[0]
         north.append(turn(joined, LAT[:2], 1))
         south.append(turn(joined, LAT[:2], -1))
         own.append(joined)
 
-    ring_info = own[INFO_CHUNK][:, -1, :, :ROWS]
     ring_start = ring_info[:, 0].astype(jnp.int32)
     ring_weight = jnp.stack(cubic_weights(ring_info[:, 1]))
 
@@ -243,21 +251,23 @@
         width = last - first
         columns = pl.pallas_call(
             partial(column_kernel, width),
-            out_shape=[tiles(ROWS * width)] * RING,
+            out_shape=[tiles(ROWS * width)] * RING + [tiles(3, RING)] * (chunk == INFO_CHUNK),
             in_specs=[SMEM, SMEM, VMEM, VMEM, VMEM],
-            out_specs=[VMEM] * RING,
+            out_specs=[VMEM] * (RING + (chunk == INFO_CHUNK)),
             scratch_shapes=[pltpu.VMEM((3 * GROUP * width, 8, LANES), jnp.float32)],
             compiler_params=params,
             name="column",
         )(ring_start, ring_weight, north[chunk], own[chunk], south[chunk])
-        gathered.append(exchange(columns))
+        if chunk == INFO_CHUNK:
+            all_info = columns[RING]
+        gathered.append(exchange(columns[:RING]))
 
     total_rows = lax.axis_size(LAT) * ROWS
     group_row = lax.axis_index(LAT[:2]) * GROUP
     bands = around(lax.axis_index(LAT[2]), -jnp.arange(RING, dtype=jnp.int32))
     ring_rows = bands[:, None] * ROWS + jnp.arange(ROWS, dtype=jnp.int32)[None]
     area = jnp.cos(math.pi * ((group_row + ring_rows).astype(jnp.float32) + 0.5) / total_rows - math.pi / 2.0)
-    sums = [part[INFO_CHUNK][:, -1, 3 : 3 + FIELDS, :ROWS] for part in (north, own, south)]
+    sums = all_info[:, :, 3 : 3 + FIELDS, :ROWS]
     lon_total = sum(cubic_weights(ring_info[:, 2]))
     before = jnp.sum(area[:, None, :] * sums[1], axis=(0, 2))
     after = jnp.zeros((FIELDS,), jnp.float32)
@@ -278,7 +288,6 @@
     lon_w = jnp.stack(cubic_weights(lon_fraction))
 
     result = None
-    half = ROWS // 2
     for field in range(FIELDS):
         operands = [piece for chunk in field_chunks(field) for piece in gathered[chunk]]
         in_specs = [SMEM, SMEM, SMEM] + [VMEM] * len(operands)
@@ -288,12 +297,12 @@
             in_specs.append(ANY)
             aliases = {len(in_specs) - 1: 0}
         result = pl.pallas_call(
-            partial(finish_kernel, field, half),
-            grid=(2,),
+            partial(finish_kernel, field),
+            grid=(1,),
             out_shape=jax.ShapeDtypeStruct(fields.shape, jnp.float32),
             in_specs=in_specs,
-            out_specs=pl.BlockSpec((half, 1, 8, LON), lambda i, field=field: (i, field, 0, 0)),
-            scratch_shapes=[pltpu.VMEM((2 * TILES, 8, LANES), jnp.float32)],
+            out_specs=pl.BlockSpec((ROWS, 1, 8, LON), lambda i, field=field: (0, field, 0, 0)),
+            scratch_shapes=[pltpu.VMEM((TOGETHER * 2 * TILES, 8, LANES), jnp.float32)],
             input_output_aliases=aliases,
             compiler_params=params,
             name="finish",

time: 136 us -> 141 us (1.037)
  waiting for transfers between devices: 48.9 us -> 57 us
  Pallas kernels: 18.1 us -> 16.3 us
    ppermute x32, waiting for transfers between devices: 46.3 us -> 50.5 us  [turn(): lax.ppermute(array, axis, [(i, (i + distance) % count) for i in range(cou...]
    all_to_all x1, waiting for transfers between devices: 2.59 us -> 6.48 us  [per_device(): spread = lax.all_to_all(spread, parties, 0, 0)]
    pallas_call x8, Pallas kernels: 11.1 us -> 8.74 us  [the longest x3 8.51 us: per_device(): pl.pallas_call(partial(finish_kernel, field), grid=(1,), out_shape=jax.Sh...]
    ppermute x32, starting transfers between devices: 50.3 us -> 48 us  [turn(): lax.ppermute(array, axis, [(i, (i + distance) % count) for i in range(cou...]
    unnamed x26 -> x20, local copies, waits for them, and re-layouts: 4.55 us -> 3.68 us
  transfers between devices with their start and end apart: 33 -> 33, of which waited for: 5 -> 8; matrix products, arithmetic and copies ran while one was open for 2% -> 2% of each run, Pallas kernels for 11% -> 10%
where the time goes in v2:
time: 141 us; the launch traced here: 140 us
  starting transfers between devices  60.5 us (43%)
  waiting for transfers between devices  57 us (40%)
  Pallas kernels  16.3 us (12%)
  local copies, waits for them, and re-layouts  4.33 us (3%)
  other arithmetic  1.83 us (1%)
    ppermute x32, waiting for transfers between devices, turn(): lax.ppermute(array, axis, [(i, (i + distance) % count) for i in range(cou...  50.5 us
    ppermute x32, starting transfers between devices, turn(): lax.ppermute(array, axis, [(i, (i + distance) % count) for i in range(cou...  48 us
    all_to_all x1, starting transfers between devices, per_device(): spread = lax.all_to_all(spread, parties, 0, 0)  12.5 us
    pallas_call x3, Pallas kernels, per_device(): pl.pallas_call(partial(finish_kernel, field), grid=(1,), out_shape=jax.Sh...  8.51 us
    pallas_call x4, Pallas kernels, per_device(): pl.pallas_call(partial(column_kernel, width), out_shape=[tiles(ROWS * wid...  6.56 us
    all_to_all x1, waiting for transfers between devices, per_device(): spread = lax.all_to_all(spread, parties, 0, 0)  6.48 us
    unnamed x20, local copies, waits for them, and re-layouts  3.68 us
  transfers between devices with their start and end apart: 33, of which 8 were waited for; matrix products, arithmetic and copies ran while one was open for 2% of the time, Pallas kernels for 10%

profile of v2, /device:TPU:1, one launch (start us, length us, event | category | flops | bytes accessed | tf_op | source)
XLA Modules:
  0.0 140.1 jit_solution(12222070014145117958)
XLA Ops:
  0.0 1.7 %copy-done = f32[10,3,8,2560]{3,2,1,0:T(8,128)S(1)} copy-done((f32[10,3,8,2560]{3,2,1,0:T(8,128)S(1)}, f32[10,3,8,2560]{3,2,1,0:T(8,128)}, u32[]{:S(2)}) %copy-start) | copy-done | bytes 2457624
  1.8 2.2 %collective-permute-start.24 = (f32[20,8,128]{2,1,0:T(8,128)S(1)}, f32[20,8,128]{2,1,0:T(8,128)S(1)}, u32[]{:S(2)}, u32[]{:S(2)}) collective-permute-start(f32[20,8,128]{2,1,0:T(8,128)S(1)} %get-tuple-element.68), channel_id=1, source_target_pairs={{0,2},{2,4},{4,6},{6,0},{1,3},{3,5},{5,7},{7,1},{8,10},{10,12},{12... | collective-permute-start | bytes 245768 | tf_op jit(solution)/shard_map/ppermute | solution.py:194
  4.0 2.6 %collective-permute-start.25 = (f32[20,8,128]{2,1,0:T(8,128)S(1)}, f32[20,8,128]{2,1,0:T(8,128)S(1)}, u32[]{:S(2)}, u32[]{:S(2)}) collective-permute-start(f32[20,8,128]{2,1,0:T(8,128)S(1)} %get-tuple-element.69), channel_id=1, source_target_pairs={{0,4},{2,6},{4,0},{6,2},{1,5},{3,7},{5,1},{7,3},{8,12},{10,14},{12... | collective-permute-start | bytes 245768 | tf_op jit(solution)/shard_map/ppermute | solution.py:194
  10.0 1.8 %collective-permute-start.15 = (f32[30,8,128]{2,1,0:T(8,128)S(1)}, f32[30,8,128]{2,1,0:T(8,128)S(1)}, u32[]{:S(2)}, u32[]{:S(2)}) collective-permute-start(f32[30,8,128]{2,1,0:T(8,128)S(1)} %get-tuple-element.58), channel_id=1, source_target_pairs={{0,6},{2,0},{4,2},{6,4},{1,7},{3,1},{5,3},{7,5},{8,14},{10,8},{12,... | collective-permute-start | bytes 368648 | tf_op jit(solution)/shard_map/ppermute | solution.py:194
  12.3 1.7 %collective-permute-start.6 = (f32[50,8,128]{2,1,0:T(8,128)S(1)}, f32[50,8,128]{2,1,0:T(8,128)S(1)}, u32[]{:S(2)}, u32[]{:S(2)}) collective-permute-start(f32[50,8,128]{2,1,0:T(8,128)S(1)} %get-tuple-element.49), channel_id=1, source_target_pairs={{0,4},{2,6},{4,0},{6,2},{1,5},{3,7},{5,1},{7,3},{8,12},{10,14},{12... | collective-permute-start | bytes 614408 | tf_op jit(solution)/shard_map/ppermute | solution.py:194
  16.3 1.7 %collective-permute-start.1 = (f32[51,8,128]{2,1,0:T(8,128)S(1)}, f32[51,8,128]{2,1,0:T(8,128)S(1)}, u32[]{:S(2)}, u32[]{:S(2)}) collective-permute-start(f32[51,8,128]{2,1,0:T(8,128)S(1)} %get-tuple-element.42), channel_id=1, source_target_pairs={{0,4},{2,6},{4,0},{6,2},{1,5},{3,7},{5,1},{7,3},{8,12},{10,14},{12... | collective-permute-start | bytes 626696 | tf_op jit(solution)/shard_map/ppermute | solution.py:194
  18.0 3.4 %collective-permute-done.5.refs_1_ = f32[50,8,128]{2,1,0:T(8,128)S(1)} collective-permute-done((f32[50,8,128]{2,1,0:T(8,128)S(1)}, f32[50,8,128]{2,1,0:T(8,128)S(1)}, u32[]{:S(2)}, u32[]{:S(2)}) %collective-permute-start.5) | collective-permute-done | bytes 204832 | tf_op jit(solution)/shard_map/ppermute | solution.py:194
  21.5 3.2 %collective-permute-done.6.refs_2_ = f32[50,8,128]{2,1,0:T(8,128)S(1)} collective-permute-done((f32[50,8,128]{2,1,0:T(8,128)S(1)}, f32[50,8,128]{2,1,0:T(8,128)S(1)}, u32[]{:S(2)}, u32[]{:S(2)}) %collective-permute-start.6) | collective-permute-done | bytes 204832 | tf_op jit(solution)/shard_map/ppermute | solution.py:194
  24.7 7.6 %collective-permute-start.28 = (f32[4,20,8,128]{3,2,1,0:T(8,128)S(1)}, f32[4,20,8,128]{3,2,1,0:T(8,128)S(1)}, u32[]{:S(2)}, u32[]{:S(2)}) collective-permute-start(f32[4,20,8,128]{3,2,1,0:T(8,128)S(1)} %join.7.own_ref), channel_id=1, source_target_pairs={{0,248},{8,0},{16,8},{24,16},{32,24},{40,32},{48,40},{56,48},{64,5... | collective-permute-start | bytes 983048 | tf_op jit(solution)/shard_map/ppermute | solution.py:194
  34.1 7.9 %collective-permute-start.4 = (f32[4,51,8,128]{3,2,1,0:T(8,128)S(1)}, f32[4,51,8,128]{3,2,1,0:T(8,128)S(1)}, u32[]{:S(2)}, u32[]{:S(2)}) collective-permute-start(f32[4,51,8,128]{3,2,1,0:T(8,128)S(1)} %get-tuple-element.45.own_ref), channel_id=1, source_target_pairs={{0,248},{8,0},{16,8},{24,16},{32,24},{40,32},{48,40},{56,48},{64,5... | collective-permute-start | bytes 2506760 | tf_op jit(solution)/shard_map/ppermute | solution.py:194
  43.5 35.0 %collective-permute-done.27.north_ref = f32[4,20,8,128]{3,2,1,0:T(8,128)S(1)} collective-permute-done((f32[4,20,8,128]{3,2,1,0:T(8,128)S(1)}, f32[4,20,8,128]{3,2,1,0:T(8,128)S(1)}, u32[]{:S(2)}, u32[]{:S(2)}) %collective-permute-start.27) | collective-permute-done | bytes 327712 | tf_op jit(solution)/shard_map/ppermute | solution.py:194
  82.4 1.8 %column.5 = (f32[50,8,128]{2,1,0:T(8,128)S(1)}, f32[50,8,128]{2,1,0:T(8,128)}, f32[50,8,128]{2,1,0:T(8,128)S(1)}, f32[50,8,128]{2,1,0:T(8,128)S(1)}) custom-call(s32[4,10]{1,0:T(4,128)S(1)} %bitcast.31, f32[4,4,10]{2,1,0:T(4,128)S(1)} %pad_maximum_fusion.weight_ref, f32[4,50,8,128]{3,2,1,0:T(8,128)S(1)} %collective-permute-done.8.north_ref, ...), custom_call_target="tpu_custom_call" | custom-call | tf_op jit(solution)/shard_map/column/pallas_call | solution.py:252
  84.9 3.3 %collective-permute-start.30 = (f32[20,8,128]{2,1,0:T(8,128)S(1)}, f32[20,8,128]{2,1,0:T(8,128)S(1)}, u32[]{:S(2)}, u32[]{:S(2)}) collective-permute-start(f32[20,8,128]{2,1,0:T(8,128)S(1)} %get-tuple-element.73), channel_id=1, source_target_pairs={{0,4},{2,6},{4,0},{6,2},{1,5},{3,7},{5,1},{7,3},{8,12},{10,14},{12... | collective-permute-start | bytes 245768 | tf_op jit(solution)/shard_map/ppermute | solution.py:194
  88.3 2.0 %column.4 = (f32[50,8,128]{2,1,0:T(8,128)S(1)}, f32[50,8,128]{2,1,0:T(8,128)}, f32[50,8,128]{2,1,0:T(8,128)}, f32[50,8,128]{2,1,0:T(8,128)}, f32[3,4,8,128]{3,2,1,0:T(8,128)S(1)}) custom-call(s32[4,10]{1,0:T(4,128)S(1)} %bitcast.32, f32[4,4,10]{2,1,0:T(4,128)S(1)} %pad_maximum_fusion.weight_ref, f32[4,51,8,128]{3,2,1,0:T(8,128)S(1)} %collective-permute-done.3.north_ref, ...), custom_call_target="tpu_custom_call" | custom-call | tf_op jit(solution)/shard_map/column/pallas_call | solution.py:252
  90.6 3.8 %collective-permute-start.22 = (f32[50,8,128]{2,1,0:T(8,128)}, f32[50,8,128]{2,1,0:T(8,128)S(1)}, u32[]{:S(2)}, u32[]{:S(2)}) collective-permute-start(f32[50,8,128]{2,1,0:T(8,128)} %get-tuple-element.65), channel_id=1, source_target_pairs={{0,4},{2,6},{4,0},{6,2},{1,5},{3,7},{5,1},{7,3},{8,12},{10,14},{12... | collective-permute-start | bytes 614408 | tf_op jit(solution)/shard_map/ppermute | solution.py:194
  95.2 12.5 %all-to-all-start = ((f32[64,1,128]{2,1,0:T(1,128)}), f32[64,1,128]{2,1,0:T(1,128)S(1)}, u32[]{:S(2)}, u32[]{:S(2)}) async-start(f32[64,1,128]{2,1,0:T(1,128)} %broadcast_in_dim.115), calls=%async_computation | async-start | bytes 65536 | tf_op jit(solution)/shard_map/all_to_all | solution.py:285
  110.5 6.5 %all-to-all-done = f32[64,1,128]{2,1,0:T(1,128)S(1)} async-done(((f32[64,1,128]{2,1,0:T(1,128)}), f32[64,1,128]{2,1,0:T(1,128)S(1)}, u32[]{:S(2)}, u32[]{:S(2)}) %all-to-all-start) | async-done | bytes 32800 | tf_op jit(solution)/shard_map/all_to_all | solution.py:285
  117.0 1.8 %collective-permute-start.18 = (f32[30,8,128]{2,1,0:T(8,128)}, f32[30,8,128]{2,1,0:T(8,128)S(1)}, u32[]{:S(2)}, u32[]{:S(2)}) collective-permute-start(f32[30,8,128]{2,1,0:T(8,128)} %copy-done.9), channel_id=1, source_target_pairs={{0,2},{2,4},{4,6},{6,0},{1,3},{3,5},{5,7},{7,1},{8,10},{10,12},{12... | collective-permute-start | bytes 368648 | tf_op jit(solution)/shard_map/ppermute | solution.py:194
  119.7 2.0 %collective-permute-start.20 = (f32[30,8,128]{2,1,0:T(8,128)S(1)}, f32[30,8,128]{2,1,0:T(8,128)S(1)}, u32[]{:S(2)}, u32[]{:S(2)}) collective-permute-start(f32[30,8,128]{2,1,0:T(8,128)S(1)} %get-tuple-element.62), channel_id=1, source_target_pairs={{0,6},{2,0},{4,2},{6,4},{1,7},{3,1},{5,3},{7,5},{8,14},{10,8},{12,... | collective-permute-start | bytes 368648 | tf_op jit(solution)/shard_map/ppermute | solution.py:194
  123.6 2.8 %finish.3.refs_8_ = f32[10,3,8,2560]{3,2,1,0:T(8,128)} custom-call(s32[10]{0:T(128)S(1)} %copy-done.2, f32[4,10]{1,0:T(4,128)S(1)} %pad_maximum_fusion.1.weight_ref, f32[3]{0:T(128)S(1)} %slice_divide_fusion.ratio_ref, f32[20,8,128]{2,1,0:T(8,128)S(1)} %get-tuple-element.71.refs_0_, f32[20,8,128]{2,1,0:T(8,128)S(1)} %collective-permute-done.29.refs_1_, ...), custom_call_target="tpu_custom_call" | custom-call | tf_op jit(solution)/shard_map/finish/pallas_call | solution.py:299
  126.5 2.6 %collective-permute-done.11.refs_6_.refs_2_ = f32[50,8,128]{2,1,0:T(8,128)S(1)} collective-permute-done((f32[50,8,128]{2,1,0:T(8,128)}, f32[50,8,128]{2,1,0:T(8,128)S(1)}, u32[]{:S(2)}, u32[]{:S(2)}) %collective-permute-start.11) | collective-permute-done | bytes 204832 | tf_op jit(solution)/shard_map/ppermute | solution.py:194
  129.0 5.4 %collective-permute-done.12.refs_7_.refs_3_ = f32[50,8,128]{2,1,0:T(8,128)S(1)} collective-permute-done((f32[50,8,128]{2,1,0:T(8,128)S(1)}, f32[50,8,128]{2,1,0:T(8,128)S(1)}, u32[]{:S(2)}, u32[]{:S(2)}) %collective-permute-start.12) | collective-permute-done | bytes 204832 | tf_op jit(solution)/shard_map/ppermute | solution.py:194
  134.4 2.8 %finish.4.refs_8_ = f32[10,3,8,2560]{3,2,1,0:T(8,128)} custom-call(s32[10]{0:T(128)S(1)} %copy-done.2, f32[4,10]{1,0:T(4,128)S(1)} %pad_maximum_fusion.1.weight_ref, f32[3]{0:T(128)S(1)} %slice_divide_fusion.ratio_ref, f32[50,8,128]{2,1,0:T(8,128)S(1)} %get-tuple-element.63.refs_4_.refs_0_, ...), custom_call_target="tpu_custom_call", output_to_operand_aliasing={{}: (11, {})} | custom-call | tf_op jit(solution)/shard_map/finish/pallas_call | solution.py:299
  137.3 2.8 %finish.5 = f32[10,3,8,2560]{3,2,1,0:T(8,128)} custom-call(s32[10]{0:T(128)S(1)} %copy-done.2, f32[4,10]{1,0:T(4,128)S(1)} %pad_maximum_fusion.1.weight_ref, f32[3]{0:T(128)S(1)} %slice_divide_fusion.ratio_ref, f32[50,8,128]{2,1,0:T(8,128)S(1)} %get-tuple-element.51.refs_4_.refs_0_, ...), custom_call_target="tpu_custom_call", output_to_operand_aliasing={{}: (11, {})} | custom-call | tf_op jit(solution)/shard_map/finish/pallas_call | solution.py:299
  (97 shorter events, 20.8 us)
Async XLA Ops:
  11.7 9.7 %collective-permute-start.5 = (f32[50,8,128]{2,1,0:T(8,128)S(1)}, f32[50,8,128]{2,1,0:T(8,128)S(1)}, u32[]{:S(2)}, u32[]{:S(2)}) collective-permute-start(f32[50,8,128]{2,1,0:T(8,128)S(1)} %get-tuple-element.48), channel_id=1, source_target_pairs={{0,2},{2,4},{4,6},{6,0},{1,3},{3,5},{5,7},{7,1},{8,10},{10,12},{12... | collective-permute-start | bytes 614408 | tf_op jit(solution)/shard_map/ppermute | solution.py:194
  12.3 12.4 %collective-permute-start.6 = (f32[50,8,128]{2,1,0:T(8,128)S(1)}, f32[50,8,128]{2,1,0:T(8,128)S(1)}, u32[]{:S(2)}, u32[]{:S(2)}) collective-permute-start(f32[50,8,128]{2,1,0:T(8,128)S(1)} %get-tuple-element.49), channel_id=1, source_target_pairs={{0,4},{2,6},{4,0},{6,2},{1,5},{3,7},{5,1},{7,3},{8,12},{10,14},{12... | collective-permute-start | bytes 614408 | tf_op jit(solution)/shard_map/ppermute | solution.py:194
  14.8 17.6 %collective-permute-start.7 = (f32[50,8,128]{2,1,0:T(8,128)S(1)}, f32[50,8,128]{2,1,0:T(8,128)S(1)}, u32[]{:S(2)}, u32[]{:S(2)}) collective-permute-start(f32[50,8,128]{2,1,0:T(8,128)S(1)} %get-tuple-element.50), channel_id=1, source_target_pairs={{0,6},{2,0},{4,2},{6,4},{1,7},{3,1},{5,3},{7,5},{8,14},{10,8},{12,... | collective-permute-start | bytes 614408 | tf_op jit(solution)/shard_map/ppermute | solution.py:194
  16.1 17.9 %collective-permute-start = (f32[51,8,128]{2,1,0:T(8,128)S(1)}, f32[51,8,128]{2,1,0:T(8,128)S(1)}, u32[]{:S(2)}, u32[]{:S(2)}) collective-permute-start(f32[51,8,128]{2,1,0:T(8,128)S(1)} %get-tuple-element.41), channel_id=1, source_target_pairs={{0,2},{2,4},{4,6},{6,0},{1,3},{3,5},{5,7},{7,1},{8,10},{10,12},{12... | collective-permute-start | bytes 626696 | tf_op jit(solution)/shard_map/ppermute | solution.py:194
  16.3 17.7 %collective-permute-start.1 = (f32[51,8,128]{2,1,0:T(8,128)S(1)}, f32[51,8,128]{2,1,0:T(8,128)S(1)}, u32[]{:S(2)}, u32[]{:S(2)}) collective-permute-start(f32[51,8,128]{2,1,0:T(8,128)S(1)} %get-tuple-element.42), channel_id=1, source_target_pairs={{0,4},{2,6},{4,0},{6,2},{1,5},{3,7},{5,1},{7,3},{8,12},{10,14},{12... | collective-permute-start | bytes 626696 | tf_op jit(solution)/shard_map/ppermute | solution.py:194
  21.4 12.7 %collective-permute-start.2 = (f32[51,8,128]{2,1,0:T(8,128)S(1)}, f32[51,8,128]{2,1,0:T(8,128)S(1)}, u32[]{:S(2)}, u32[]{:S(2)}) collective-permute-start(f32[51,8,128]{2,1,0:T(8,128)S(1)} %get-tuple-element.43), channel_id=1, source_target_pairs={{0,6},{2,0},{4,2},{6,4},{1,7},{3,1},{5,3},{7,5},{8,14},{10,8},{12,... | collective-permute-start | bytes 626696 | tf_op jit(solution)/shard_map/ppermute | solution.py:194
  24.7 18.7 %collective-permute-start.28 = (f32[4,20,8,128]{3,2,1,0:T(8,128)S(1)}, f32[4,20,8,128]{3,2,1,0:T(8,128)S(1)}, u32[]{:S(2)}, u32[]{:S(2)}) collective-permute-start(f32[4,20,8,128]{3,2,1,0:T(8,128)S(1)} %join.7.own_ref), channel_id=1, source_target_pairs={{0,248},{8,0},{16,8},{24,16},{32,24},{40,32},{48,40},{56,48},{64,5... | collective-permute-start | bytes 983048 | tf_op jit(solution)/shard_map/ppermute | solution.py:194
  32.4 48.9 %collective-permute-start.9 = (f32[4,50,8,128]{3,2,1,0:T(8,128)S(1)}, f32[4,50,8,128]{3,2,1,0:T(8,128)S(1)}, u32[]{:S(2)}, u32[]{:S(2)}) collective-permute-start(f32[4,50,8,128]{3,2,1,0:T(8,128)S(1)} %join.5.own_ref), channel_id=1, source_target_pairs={{0,248},{8,0},{16,8},{24,16},{32,24},{40,32},{48,40},{56,48},{64,5... | collective-permute-start | bytes 2457608 | tf_op jit(solution)/shard_map/ppermute | solution.py:194
  34.0 47.6 %collective-permute-start.8 = (f32[4,50,8,128]{3,2,1,0:T(8,128)S(1)}, f32[4,50,8,128]{3,2,1,0:T(8,128)S(1)}, u32[]{:S(2)}, u32[]{:S(2)}) collective-permute-start(f32[4,50,8,128]{3,2,1,0:T(8,128)S(1)} %join.5.own_ref), channel_id=1, source_target_pairs={{0,8},{8,16},{16,24},{24,32},{32,40},{40,48},{48,56},{56,64},{64,7... | collective-permute-start | bytes 2457608 | tf_op jit(solution)/shard_map/ppermute | solution.py:194
  34.1 50.8 %collective-permute-start.4 = (f32[4,51,8,128]{3,2,1,0:T(8,128)S(1)}, f32[4,51,8,128]{3,2,1,0:T(8,128)S(1)}, u32[]{:S(2)}, u32[]{:S(2)}) collective-permute-start(f32[4,51,8,128]{3,2,1,0:T(8,128)S(1)} %get-tuple-element.45.own_ref), channel_id=1, source_target_pairs={{0,248},{8,0},{16,8},{24,16},{32,24},{40,32},{48,40},{56,48},{64,5... | collective-permute-start | bytes 2506760 | tf_op jit(solution)/shard_map/ppermute | solution.py:194
  42.1 46.2 %collective-permute-start.3 = (f32[4,51,8,128]{3,2,1,0:T(8,128)S(1)}, f32[4,51,8,128]{3,2,1,0:T(8,128)S(1)}, u32[]{:S(2)}, u32[]{:S(2)}) collective-permute-start(f32[4,51,8,128]{3,2,1,0:T(8,128)S(1)} %get-tuple-element.45.own_ref), channel_id=1, source_target_pairs={{0,8},{8,16},{16,24},{24,32},{32,40},{40,48},{48,56},{56,64},{64,7... | collective-permute-start | bytes 2506760 | tf_op jit(solution)/shard_map/ppermute | solution.py:194
  43.4 35.1 %collective-permute-start.27 = (f32[4,20,8,128]{3,2,1,0:T(8,128)S(1)}, f32[4,20,8,128]{3,2,1,0:T(8,128)S(1)}, u32[]{:S(2)}, u32[]{:S(2)}) collective-permute-start(f32[4,20,8,128]{3,2,1,0:T(8,128)S(1)} %join.7.own_ref), channel_id=1, source_target_pairs={{0,8},{8,16},{16,24},{24,32},{32,40},{40,48},{48,56},{56,64},{64,7... | collective-permute-start | bytes 983048 | tf_op jit(solution)/shard_map/ppermute | solution.py:194
  78.5 16.0 %collective-permute-start.17 = (f32[4,30,8,128]{3,2,1,0:T(8,128)S(1)}, f32[4,30,8,128]{3,2,1,0:T(8,128)S(1)}, u32[]{:S(2)}, u32[]{:S(2)}) collective-permute-start(f32[4,30,8,128]{3,2,1,0:T(8,128)S(1)} %join.6.own_ref), channel_id=1, source_target_pairs={{0,248},{8,0},{16,8},{24,16},{32,24},{40,32},{48,40},{56,48},{64,5... | collective-permute-start | bytes 1474568 | tf_op jit(solution)/shard_map/ppermute | solution.py:194
  81.3 26.4 %collective-permute-start.16 = (f32[4,30,8,128]{3,2,1,0:T(8,128)S(1)}, f32[4,30,8,128]{3,2,1,0:T(8,128)S(1)}, u32[]{:S(2)}, u32[]{:S(2)}) collective-permute-start(f32[4,30,8,128]{3,2,1,0:T(8,128)S(1)} %join.6.own_ref), channel_id=1, source_target_pairs={{0,8},{8,16},{16,24},{24,32},{32,40},{40,48},{48,56},{56,64},{64,7... | collective-permute-start | bytes 1474568 | tf_op jit(solution)/shard_map/ppermute | solution.py:194
  88.3 30.6 %collective-permute-start.10 = (f32[50,8,128]{2,1,0:T(8,128)}, f32[50,8,128]{2,1,0:T(8,128)S(1)}, u32[]{:S(2)}, u32[]{:S(2)}) collective-permute-start(f32[50,8,128]{2,1,0:T(8,128)} %get-tuple-element.52), channel_id=1, source_target_pairs={{0,2},{2,4},{4,6},{6,0},{1,3},{3,5},{5,7},{7,1},{8,10},{10,12},{12... | collective-permute-start | bytes 614408 | tf_op jit(solution)/shard_map/ppermute | solution.py:194
  90.5 29.2 %collective-permute-start.21 = (f32[50,8,128]{2,1,0:T(8,128)}, f32[50,8,128]{2,1,0:T(8,128)S(1)}, u32[]{:S(2)}, u32[]{:S(2)}) collective-permute-start(f32[50,8,128]{2,1,0:T(8,128)} %get-tuple-element.64), channel_id=1, source_target_pairs={{0,2},{2,4},{4,6},{6,0},{1,3},{3,5},{5,7},{7,1},{8,10},{10,12},{12... | collective-permute-start | bytes 614408 | tf_op jit(solution)/shard_map/ppermute | solution.py:194
  90.6 31.0 %collective-permute-start.22 = (f32[50,8,128]{2,1,0:T(8,128)}, f32[50,8,128]{2,1,0:T(8,128)S(1)}, u32[]{:S(2)}, u32[]{:S(2)}) collective-permute-start(f32[50,8,128]{2,1,0:T(8,128)} %get-tuple-element.65), channel_id=1, source_target_pairs={{0,4},{2,6},{4,0},{6,2},{1,5},{3,7},{5,1},{7,3},{8,12},{10,14},{12... | collective-permute-start | bytes 614408 | tf_op jit(solution)/shard_map/ppermute | solution.py:194
  94.5 27.7 %collective-permute-start.23 = (f32[50,8,128]{2,1,0:T(8,128)}, f32[50,8,128]{2,1,0:T(8,128)S(1)}, u32[]{:S(2)}, u32[]{:S(2)}) collective-permute-start(f32[50,8,128]{2,1,0:T(8,128)} %get-tuple-element.66), channel_id=1, source_target_pairs={{0,6},{2,0},{4,2},{6,4},{1,7},{3,1},{5,3},{7,5},{8,14},{10,8},{12,... | collective-permute-start | bytes 614408 | tf_op jit(solution)/shard_map/ppermute | solution.py:194
  95.2 21.8 %all-to-all-start = ((f32[64,1,128]{2,1,0:T(1,128)}), f32[64,1,128]{2,1,0:T(1,128)S(1)}, u32[]{:S(2)}, u32[]{:S(2)}) async-start(f32[64,1,128]{2,1,0:T(1,128)} %broadcast_in_dim.115), calls=%async_computation | async-start | bytes 65536 | tf_op jit(solution)/shard_map/all_to_all | solution.py:285
  107.7 9.3 %collective-permute-start.31 = (f32[20,8,128]{2,1,0:T(8,128)}, f32[20,8,128]{2,1,0:T(8,128)S(1)}, u32[]{:S(2)}, u32[]{:S(2)}) collective-permute-start(f32[20,8,128]{2,1,0:T(8,128)} %get-tuple-element.74), channel_id=1, source_target_pairs={{0,6},{2,0},{4,2},{6,4},{1,7},{3,1},{5,3},{7,5},{8,14},{10,8},{12,... | collective-permute-start | bytes 245768 | tf_op jit(solution)/shard_map/ppermute | solution.py:194
  117.0 20.3 %collective-permute-start.18 = (f32[30,8,128]{2,1,0:T(8,128)}, f32[30,8,128]{2,1,0:T(8,128)S(1)}, u32[]{:S(2)}, u32[]{:S(2)}) collective-permute-start(f32[30,8,128]{2,1,0:T(8,128)} %copy-done.9), channel_id=1, source_target_pairs={{0,2},{2,4},{4,6},{6,0},{1,3},{3,5},{5,7},{7,1},{8,10},{10,12},{12... | collective-permute-start | bytes 368648 | tf_op jit(solution)/shard_map/ppermute | solution.py:194
  118.8 18.4 %collective-permute-start.19 = (f32[30,8,128]{2,1,0:T(8,128)}, f32[30,8,128]{2,1,0:T(8,128)S(1)}, u32[]{:S(2)}, u32[]{:S(2)}) collective-permute-start(f32[30,8,128]{2,1,0:T(8,128)} %copy-done.8), channel_id=1, source_target_pairs={{0,4},{2,6},{4,0},{6,2},{1,5},{3,7},{5,1},{7,3},{8,12},{10,14},{12... | collective-permute-start | bytes 368648 | tf_op jit(solution)/shard_map/ppermute | solution.py:194
  119.7 17.6 %collective-permute-start.20 = (f32[30,8,128]{2,1,0:T(8,128)S(1)}, f32[30,8,128]{2,1,0:T(8,128)S(1)}, u32[]{:S(2)}, u32[]{:S(2)}) collective-permute-start(f32[30,8,128]{2,1,0:T(8,128)S(1)} %get-tuple-element.62), channel_id=1, source_target_pairs={{0,6},{2,0},{4,2},{6,4},{1,7},{3,1},{5,3},{7,5},{8,14},{10,8},{12,... | collective-permute-start | bytes 368648 | tf_op jit(solution)/shard_map/ppermute | solution.py:194
  122.2 12.3 %collective-permute-start.12 = (f32[50,8,128]{2,1,0:T(8,128)S(1)}, f32[50,8,128]{2,1,0:T(8,128)S(1)}, u32[]{:S(2)}, u32[]{:S(2)}) collective-permute-start(f32[50,8,128]{2,1,0:T(8,128)S(1)} %get-tuple-element.54), channel_id=1, source_target_pairs={{0,6},{2,0},{4,2},{6,4},{1,7},{3,1},{5,3},{7,5},{8,14},{10,8},{12,... | collective-permute-start | bytes 614408 | tf_op jit(solution)/shard_map/ppermute | solution.py:194
  (19 other events, 135.1 us)

commit v3 on v2

--- a/solution.py
+++ b/solution.py
@@ -19,11 +19,12 @@
 QUARTER = 5
 TILES = RING * QUARTER
 LON = TILES * LANES
-CUTS = (0, 2, 7, 12, 15)
-CHUNKS = tuple(zip(CUTS[:-1], CUTS[1:]))
+CHUNKS = ((0, 2), (2, 8), (8, 13), (13, 15))
+OWN = ((0,), (1,), (2, 3))
+BACK = ((0, 1), (2,), (3,))
 INFO_CHUNK = 1
 TOGETHER = 2
-VMEM_LIMIT = 10 * 1024 * 1024
+VMEM_LIMIT = 12 * 1024 * 1024
 
 
 VMEM = pl.BlockSpec(memory_space=pltpu.VMEM)
@@ -44,28 +45,42 @@
     return lax.rem(place + RING + distance, RING)
 
 
+def width_of(chunk):
+    first, last = CHUNKS[chunk]
+    return last - first
+
+
 def tile_count(chunk):
-    first, last = CHUNKS[chunk]
-    return ROWS * (last - first) + (1 if chunk == INFO_CHUNK else 0)
-
-
-def copy_units(fields_ref, chunk, piece_refs):
-    first, last = CHUNKS[chunk]
-    width = last - first
+    return ROWS * width_of(chunk) + (1 if chunk == INFO_CHUNK else 0)
+
+
+def batch_tiles(batch):
+    return sum(tile_count(chunk) for chunk in batch)
+
+
+def column_tiles(batch):
+    return sum(ROWS * width_of(chunk) for chunk in batch)
+
+
+def copy_units(fields_ref, batch, piece_refs):
     place = lax.axis_index(LAT[2])
     for distance in range(RING):
         owner = around(place, distance)
-        for unit in range(first, last):
-            field, tile = divmod(unit, QUARTER)
-            start = pl.multiple_of((owner * QUARTER + tile) * LANES, LANES)
-            for row in range(ROWS):
-                piece_refs[distance][row * width + unit - first] = fields_ref[
-                    row, field, :, pl.ds(start, LANES)
-                ]
+        base = 0
+        for chunk in batch:
+            first, last = CHUNKS[chunk]
+            for unit in range(first, last):
+                field, tile = divmod(unit, QUARTER)
+                start = pl.multiple_of((owner * QUARTER + tile) * LANES, LANES)
+                for row in range(ROWS):
+                    piece_refs[distance][base + row * (last - first) + unit - first] = fields_ref[
+                        row, field, :, pl.ds(start, LANES)
+                    ]
+            base += tile_count(chunk)
 
 
 def pack_first(fields_ref, *piece_refs):
-    copy_units(fields_ref, 0, piece_refs)
+    copy_units(fields_ref, OWN[0], piece_refs)
 
 
 def pack_rest(departure_ref, extents_ref, lat_ref, lon_ref, fields_ref, *piece_refs):
@@ -95,41 +110,53 @@
         by_row = jnp.sum(jnp.sum(total, axis=1), axis=1, keepdims=True)
         in_lanes = jnp.sum(jnp.where(sub == lane, by_row, 0.0), axis=0, keepdims=True)
         info = jnp.where(info_sub == 3 + field, in_lanes, info)
-    for chunk in range(1, len(CHUNKS)):
-        refs = piece_refs[(chunk - 1) * RING : chunk * RING]
-        copy_units(fields_ref, chunk, refs)
+    for number, batch in enumerate(OWN[1:]):
+        refs = piece_refs[number * RING : (number + 1) * RING]
+        copy_units(fields_ref, batch, refs)
+        if INFO_CHUNK in batch:
+            for ref in refs:
+                ref[batch_tiles(batch) - 1] = info
+
+
+def join_kernel(batch, *refs):
+    out_refs = refs[RING:]
+    for distance in range(RING):
+        base = 0
+        for out_ref, chunk in zip(out_refs, batch):
+            out_ref[distance] = refs[distance][base : base + tile_count(chunk)]
+            base += tile_count(chunk)
+        if INFO_CHUNK in batch:
+            out_refs[-1][distance] = refs[distance][batch_tiles(batch) - 1]
+
+
+def column_kernel(batch, start_ref, weight_ref, *refs):
+    sides = [refs[3 * number : 3 * number + 3] for number in range(len(batch))]
+    refs = refs[3 * len(batch) :]
+    out_refs, rows_refs = refs[:RING], refs[len(refs) - len(batch) :]
+    place = lax.axis_index(LAT[2])
+    for chunk, side_refs, rows_ref in zip(batch, sides, rows_refs):
+        count = width_of(chunk) * ROWS
         if chunk == INFO_CHUNK:
-            for ref in refs:
-                ref[tile_count(chunk) - 1] = info
-
-
-def join_kernel(*refs):
-    for distance in range(RING):
-        refs[RING][distance] = refs[distance][...]
-        for info_ref in refs[RING + 1 :]:
-            info_ref[distance] = refs[distance][tile_count(INFO_CHUNK) - 1]
-
-
-def column_kernel(width, start_ref, weight_ref, north_ref, own_ref, south_ref, *refs):
-    out_refs, rows_ref = refs[:RING], refs[-1]
-    count = width * ROWS
-    place = lax.axis_index(LAT[2])
-    for info_ref in refs[RING:-1]:
-        for side, ref in enumerate((north_ref, own_ref, south_ref)):
-            info_ref[side] = ref[:, count]
-    for distance in range(RING):
-        band = around(place, -distance)
-        for side, ref in enumerate((north_ref, own_ref, south_ref)):
-            rows_ref[pl.ds((side * RING + band) * count, count)] = ref[distance, :count]
+            for side, ref in enumerate(side_refs):
+                refs[RING][side] = ref[:, count]
+        for distance in range(RING):
+            band = around(place, -distance)
+            for side, ref in enumerate(side_refs):
+                rows_ref[pl.ds((side * RING + band) * count, count)] = ref[distance, :count]
 
     def one_row(row, carry):
         for distance in range(RING):
             source = (RING - distance) % RING
             first = start_ref[source, row]
-            total = weight_ref[0, source, row] * rows_ref[pl.ds(first * width, width)]
-            for step in range(1, 4):
-                total = total + weight_ref[step, source, row] * rows_ref[pl.ds((first + step) * width, width)]
-            out_refs[distance][pl.ds(row * width, width)] = total
+            weights = [weight_ref[step, source, row] for step in range(4)]
+            base = 0
+            for chunk, rows_ref in zip(batch, rows_refs):
+                width = width_of(chunk)
+                total = weights[0] * rows_ref[pl.ds(first * width, width)]
+                for step in range(1, 4):
+                    total = total + weights[step] * rows_ref[pl.ds((first + step) * width, width)]
+                out_refs[distance][pl.ds(base + row * width, width)] = total
+                base += ROWS * width
         return carry
 
     lax.fori_loop(0, ROWS, one_row, 0)
@@ -139,19 +166,23 @@
     found = []
     for tile in range(QUARTER):
         unit = field * QUARTER + tile
-        for chunk, (first, last) in enumerate(CHUNKS):
-            if first <= unit < last:
-                found.append((chunk, unit - first, last - first))
+        for number, batch in enumerate(BACK):
+            base = 0
+            for chunk in batch:
+                first, last = CHUNKS[chunk]
+                if first <= unit < last:
+                    found.append((number, base + unit - first, last - first))
+                base += ROWS * (last - first)
     return found
 
 
-def field_chunks(field):
-    return sorted({chunk for chunk, _, _ in field_units(field)})
+def field_batches(field):
+    return sorted({number for number, _, _ in field_units(field)})
 
 
 def finish_kernel(field, shift_ref, weight_ref, ratio_ref, *refs):
     out_ref, turned_ref = refs[-2], refs[-1]
-    chunks = field_chunks(field)
+    batches = field_batches(field)
     place = lax.axis_index(LAT[2])
     owners = [around(place, -distance) for distance in range(RING)]
     lane = lax.broadcasted_iota(jnp.int32, (8, LANES), 1)
@@ -171,8 +202,8 @@
             whole = base // LANES
             back = LANES - (base - whole * LANES)
             for distance in range(RING):
-                for tile, (chunk, at, width) in enumerate(field_units(field)):
-                    piece = refs[chunks.index(chunk) * RING + distance][row * width + at]
+                for tile, (number, at, width) in enumerate(field_units(field)):
+                    piece = refs[batches.index(number) * RING + distance][row * width + at]
                     turned_ref[slot + owners[distance] * QUARTER + tile] = piece
                     turned_ref[slot + TILES + owners[distance] * QUARTER + tile] = piece
             weights = [weight_ref[step, row] * scale for step in range(4)]
@@ -204,61 +235,64 @@
 
 def per_device(fields, lat_fraction, lon_fraction, lon_shift, departure_row, extents):
     params = pltpu.CompilerParams(vmem_limit_bytes=VMEM_LIMIT)
-    last_chunk = len(CHUNKS)
-
-    width = CHUNKS[0][1]
-    first_pieces = pl.pallas_call(
-        pack_first,
-        out_shape=[tiles(ROWS * width)] * RING,
-        in_specs=[VMEM],
-        out_specs=[VMEM] * RING,
-        compiler_params=params,
-        name="pack_a",
-    )(fields)
+    pieces = [
+        pl.pallas_call(
+            pack_first,
+            out_shape=[tiles(batch_tiles(OWN[0]))] * RING,
+            in_specs=[VMEM],
+            out_specs=[VMEM] * RING,
+            compiler_params=params,
+            name="pack_a",
+        )(fields)
+    ]
     rest = pl.pallas_call(
         pack_rest,
-        out_shape=[tiles(tile_count(chunk)) for chunk in range(1, last_chunk) for _ in range(RING)],
+        out_shape=[tiles(batch_tiles(batch)) for batch in OWN[1:] for _ in range(RING)],
         in_specs=[SMEM] * 4 + [VMEM],
-        out_specs=[VMEM] * (RING * (last_chunk - 1)),
+        out_specs=[VMEM] * (RING * (len(OWN) - 1)),
         compiler_params=params,
         name="pack_b",
     )(departure_row, extents, lat_fraction, lon_fraction, fields)
-    pieces = [first_pieces] + [rest[i * RING : (i + 1) * RING] for i in range(last_chunk - 1)]
-
-    own, north, south = [], [], []
-    for chunk in range(last_chunk):
-        received = exchange(pieces[chunk])
+    pieces += [rest[number * RING : (number + 1) * RING] for number in range(len(OWN) - 1)]
+
+    own, north, south = {}, {}, {}
+    for number, batch in enumerate(OWN):
+        received = exchange(pieces[number])
+        shapes = [tiles(RING, tile_count(chunk)) for chunk in batch] + [tiles(RING)] * (INFO_CHUNK in batch)
         joined = pl.pallas_call(
-            join_kernel,
-            out_shape=[tiles(RING, tile_count(chunk))] + [tiles(RING)] * (chunk == INFO_CHUNK),
+            partial(join_kernel, batch),
+            out_shape=shapes,
             in_specs=[VMEM] * RING,
-            out_specs=[VMEM] * (2 if chunk == INFO_CHUNK else 1),
+            out_specs=[VMEM] * len(shapes),
             compiler_params=params,
             name="join",
         )(*received)
-        if chunk == INFO_CHUNK:
-            ring_info = joined[1][:, :, :ROWS]
-        joined = joined[0]
-        north.append(turn(joined, LAT[:2], 1))
-        south.append(turn(joined, LAT[:2], -1))
-        own.append(joined)
+        if INFO_CHUNK in batch:
+            ring_info = joined[-1][:, :, :ROWS]
+        for chunk, block in zip(batch, joined):
+            own[chunk] = block
+            north[chunk] = turn(block, LAT[:2], 1)
+            south[chunk] = turn(block, LAT[:2], -1)
 
     ring_start = ring_info[:, 0].astype(jnp.int32)
     ring_weight = jnp.stack(cubic_weights(ring_info[:, 1]))
 
     gathered = []
-    for chunk, (first, last) in enumerate(CHUNKS):
-        width = last - first
+    for batch in BACK:
+        shapes = [tiles(column_tiles(batch))] * RING + [tiles(3, RING)] * (INFO_CHUNK in batch)
+        operands = [part[chunk] for chunk in batch for part in (north, own, south)]
         columns = pl.pallas_call(
-            partial(column_kernel, width),
-            out_shape=[tiles(ROWS * width)] * RING + [tiles(3, RING)] * (chunk == INFO_CHUNK),
-            in_specs=[SMEM, SMEM, VMEM, VMEM, VMEM],
-            out_specs=[VMEM] * (RING + (chunk == INFO_CHUNK)),
-            scratch_shapes=[pltpu.VMEM((3 * GROUP * width, 8, LANES), jnp.float32)],
+            partial(column_kernel, batch),
+            out_shape=shapes,
+            in_specs=[SMEM, SMEM] + [VMEM] * len(operands),
+            out_specs=[VMEM] * len(shapes),
+            scratch_shapes=[
+                pltpu.VMEM((3 * GROUP * width_of(chunk), 8, LANES), jnp.float32) for chunk in batch
+            ],
             compiler_params=params,
             name="column",
-        )(ring_start, ring_weight, north[chunk], own[chunk], south[chunk])
-        if chunk == INFO_CHUNK:
+        )(ring_start, ring_weight, *operands)
+        if INFO_CHUNK in batch:
             all_info = columns[RING]
         gathered.append(exchange(columns[:RING]))
 
@@ -289,7 +323,7 @@
 
     result = None
     for field in range(FIELDS):
-        operands = [piece for chunk in field_chunks(field) for piece in gathered[chunk]]
+        operands = [piece for number in field_batches(field) for piece in gathered[number]]
         in_specs = [SMEM, SMEM, SMEM] + [VMEM] * len(operands)
         aliases = {}
         if result is not None:

time: 141 us -> 140 us (level)
  starting transfers between devices: 60.5 us -> 56.6 us
  waiting for transfers between devices: 57 us -> 60.3 us
    ppermute x32 -> x26, waiting for transfers between devices: 50.5 us -> 54.9 us  [turn(): lax.ppermute(array, axis, [(i, (i + distance) % count) for i in range(cou...]
    all_to_all x1, starting transfers between devices: 12.5 us -> 9.63 us  [per_device(): spread = lax.all_to_all(spread, parties, 0, 0)]
    pallas_call x10 -> x8, Pallas kernels: 7.77 us -> 6.78 us  [the longest x3 5.58 us: per_device(): pl.pallas_call(partial(column_kernel, batch), out_shape=shapes, in_specs=...]
    ppermute x32 -> x26, starting transfers between devices: 48 us -> 47 us  [turn(): lax.ppermute(array, axis, [(i, (i + distance) % count) for i in range(cou...]
  transfers between devices with their start and end apart: 33 -> 27, of which waited for: 8 -> 7; matrix products, arithmetic and copies ran while one was open for 2% -> 2% of each run, Pallas kernels for 10% -> 9%
where the time goes in v3:
time: 140 us; the launch traced here: 139 us
  waiting for transfers between devices  60.3 us (43%)
  starting transfers between devices  56.6 us (40%)
  Pallas kernels  15.3 us (11%)
  local copies, waits for them, and re-layouts  4.34 us (3%)
  other arithmetic  2.58 us (2%)
    ppermute x26, waiting for transfers between devices, turn(): lax.ppermute(array, axis, [(i, (i + distance) % count) for i in range(cou...  54.9 us
    ppermute x26, starting transfers between devices, turn(): lax.ppermute(array, axis, [(i, (i + distance) % count) for i in range(cou...  47 us
    all_to_all x1, starting transfers between devices, per_device(): spread = lax.all_to_all(spread, parties, 0, 0)  9.63 us
    pallas_call x3, Pallas kernels, per_device(): pl.pallas_call(partial(finish_kernel, field), grid=(1,), out_shape=jax.Sh...  8.51 us
    pallas_call x3, Pallas kernels, per_device(): pl.pallas_call(partial(column_kernel, batch), out_shape=shapes, in_specs=...  5.58 us
    all_to_all x1, waiting for transfers between devices, per_device(): spread = lax.all_to_all(spread, parties, 0, 0)  5.36 us
    unnamed x20, local copies, waits for them, and re-layouts  3.69 us
  transfers between devices with their start and end apart: 27, of which 7 were waited for; matrix products, arithmetic and copies ran while one was open for 2% of the time, Pallas kernels for 9%

profile of v3, /device:TPU:1, one launch (start us, length us, event | category | flops | bytes accessed | tf_op | source)
XLA Modules:
  0.0 139.3 jit_solution(12013314395439762484)
XLA Ops:
  0.0 1.7 %copy-done = f32[10,3,8,2560]{3,2,1,0:T(8,128)S(1)} copy-done((f32[10,3,8,2560]{3,2,1,0:T(8,128)S(1)}, f32[10,3,8,2560]{3,2,1,0:T(8,128)}, u32[]{:S(2)}) %copy-start) | copy-done | bytes 2457624
  1.8 2.2 %collective-permute-start.3 = (f32[20,8,128]{2,1,0:T(8,128)S(1)}, f32[20,8,128]{2,1,0:T(8,128)S(1)}, u32[]{:S(2)}, u32[]{:S(2)}) collective-permute-start(f32[20,8,128]{2,1,0:T(8,128)S(1)} %get-tuple-element.40), channel_id=1, source_target_pairs={{0,2},{2,4},{4,6},{6,0},{1,3},{3,5},{5,7},{7,1},{8,10},{10,12},{12... | collective-permute-start | bytes 245768 | tf_op jit(solution)/shard_map/ppermute | solution.py:225
  4.0 2.6 %collective-permute-start.4 = (f32[20,8,128]{2,1,0:T(8,128)S(1)}, f32[20,8,128]{2,1,0:T(8,128)S(1)}, u32[]{:S(2)}, u32[]{:S(2)}) collective-permute-start(f32[20,8,128]{2,1,0:T(8,128)S(1)} %get-tuple-element.41), channel_id=1, source_target_pairs={{0,4},{2,6},{4,0},{6,2},{1,5},{3,7},{5,1},{7,3},{8,12},{10,14},{12... | collective-permute-start | bytes 245768 | tf_op jit(solution)/shard_map/ppermute | solution.py:225
  7.7 2.2 %collective-permute-start.1 = (f32[61,8,128]{2,1,0:T(8,128)S(1)}, f32[61,8,128]{2,1,0:T(8,128)S(1)}, u32[]{:S(2)}, u32[]{:S(2)}) collective-permute-start(f32[61,8,128]{2,1,0:T(8,128)S(1)} %get-tuple-element.36), channel_id=1, source_target_pairs={{0,4},{2,6},{4,0},{6,2},{1,5},{3,7},{5,1},{7,3},{8,12},{10,14},{12... | collective-permute-start | bytes 749576 | tf_op jit(solution)/shard_map/ppermute | solution.py:225
  12.0 10.9 %collective-permute-done.5.refs_3_ = f32[20,8,128]{2,1,0:T(8,128)S(1)} collective-permute-done((f32[20,8,128]{2,1,0:T(8,128)S(1)}, f32[20,8,128]{2,1,0:T(8,128)S(1)}, u32[]{:S(2)}, u32[]{:S(2)}) %collective-permute-start.5) | collective-permute-done | bytes 81952 | tf_op jit(solution)/shard_map/ppermute | solution.py:225
  23.8 2.9 %collective-permute-start.12 = (f32[70,8,128]{2,1,0:T(8,128)S(1)}, f32[70,8,128]{2,1,0:T(8,128)S(1)}, u32[]{:S(2)}, u32[]{:S(2)}) collective-permute-start(f32[70,8,128]{2,1,0:T(8,128)S(1)} %get-tuple-element.48), channel_id=1, source_target_pairs={{0,6},{2,0},{4,2},{6,4},{1,7},{3,1},{5,3},{7,5},{8,14},{10,8},{12,... | collective-permute-start | bytes 860168 | tf_op jit(solution)/shard_map/ppermute | solution.py:225
  26.7 8.1 %collective-permute-start.7 = (f32[4,20,8,128]{3,2,1,0:T(8,128)S(1)}, f32[4,20,8,128]{3,2,1,0:T(8,128)S(1)}, u32[]{:S(2)}, u32[]{:S(2)}) collective-permute-start(f32[4,20,8,128]{3,2,1,0:T(8,128)S(1)} %join.4.refs_1_), channel_id=1, source_target_pairs={{0,248},{8,0},{16,8},{24,16},{32,24},{40,32},{48,40},{56,48},{64,5... | collective-permute-start | bytes 983048 | tf_op jit(solution)/shard_map/ppermute | solution.py:225
  36.7 2.7 %collective-permute-done.12.refs_3_ = f32[70,8,128]{2,1,0:T(8,128)S(1)} collective-permute-done((f32[70,8,128]{2,1,0:T(8,128)S(1)}, f32[70,8,128]{2,1,0:T(8,128)S(1)}, u32[]{:S(2)}, u32[]{:S(2)}) %collective-permute-start.12) | collective-permute-done | bytes 286752 | tf_op jit(solution)/shard_map/ppermute | solution.py:225
  39.4 7.8 %collective-permute-start.14 = (f32[4,50,8,128]{3,2,1,0:T(8,128)S(1)}, f32[4,50,8,128]{3,2,1,0:T(8,128)S(1)}, u32[]{:S(2)}, u32[]{:S(2)}) collective-permute-start(f32[4,50,8,128]{3,2,1,0:T(8,128)S(1)} %get-tuple-element.49.refs_1_), channel_id=1, source_target_pairs={{0,248},{8,0},{16,8},{24,16},{32,24},{40,32},{48,40},{56,48},{64,5... | collective-permute-start | bytes 2457608 | tf_op jit(solution)/shard_map/ppermute | solution.py:225
  48.5 31.4 %collective-permute-done.14.refs_2_ = f32[4,50,8,128]{3,2,1,0:T(8,128)S(1)} collective-permute-done((f32[4,50,8,128]{3,2,1,0:T(8,128)S(1)}, f32[4,50,8,128]{3,2,1,0:T(8,128)S(1)}, u32[]{:S(2)}, u32[]{:S(2)}) %collective-permute-start.14) | collective-permute-done | bytes 819232 | tf_op jit(solution)/shard_map/ppermute | solution.py:225
  79.9 5.6 %collective-permute-start.19 = (f32[4,20,8,128]{3,2,1,0:T(8,128)S(1)}, f32[4,20,8,128]{3,2,1,0:T(8,128)S(1)}, u32[]{:S(2)}, u32[]{:S(2)}) collective-permute-start(f32[4,20,8,128]{3,2,1,0:T(8,128)S(1)} %get-tuple-element.54.refs_1_), channel_id=1, source_target_pairs={{0,248},{8,0},{16,8},{24,16},{32,24},{40,32},{48,40},{56,48},{64,5... | collective-permute-start | bytes 983048 | tf_op jit(solution)/shard_map/ppermute | solution.py:225
  85.5 1.9 %column.4 = (f32[50,8,128]{2,1,0:T(8,128)S(1)}, f32[50,8,128]{2,1,0:T(8,128)}, f32[50,8,128]{2,1,0:T(8,128)S(1)}, f32[50,8,128]{2,1,0:T(8,128)S(1)}) custom-call(s32[4,10]{1,0:T(4,128)S(1)} %bitcast.30, f32[4,4,10]{2,1,0:T(4,128)S(1)} %pad_maximum_fusion.weight_ref, f32[4,50,8,128]{3,2,1,0:T(8,128)S(1)} %collective-permute-done.13.refs_0_, ...), custom_call_target="tpu_custom_call" | custom-call | tf_op jit(solution)/shard_map/column/pallas_call | solution.py:284
  88.7 2.9 %collective-permute-done.6.refs_0_ = f32[4,20,8,128]{3,2,1,0:T(8,128)S(1)} collective-permute-done((f32[4,20,8,128]{3,2,1,0:T(8,128)S(1)}, f32[4,20,8,128]{3,2,1,0:T(8,128)S(1)}, u32[]{:S(2)}, u32[]{:S(2)}) %collective-permute-start.6) | collective-permute-done | bytes 327712 | tf_op jit(solution)/shard_map/ppermute | solution.py:225
  91.5 2.1 %column.3 = (f32[80,8,128]{2,1,0:T(8,128)S(1)}, f32[80,8,128]{2,1,0:T(8,128)}, f32[80,8,128]{2,1,0:T(8,128)S(1)}, f32[80,8,128]{2,1,0:T(8,128)S(1)}, f32[3,4,8,128]{3,2,1,0:T(8,128)S(1)}) custom-call(s32[4,10]{1,0:T(4,128)S(1)} %bitcast.31, f32[4,4,10]{2,1,0:T(4,128)S(1)} %pad_maximum_fusion.weight_ref, ...), custom_call_target="tpu_custom_call" | custom-call | tf_op jit(solution)/shard_map/column/pallas_call | solution.py:284
  95.0 2.0 %collective-permute-start.25 = (f32[80,8,128]{2,1,0:T(8,128)S(1)}, f32[80,8,128]{2,1,0:T(8,128)S(1)}, u32[]{:S(2)}, u32[]{:S(2)}) collective-permute-start(f32[80,8,128]{2,1,0:T(8,128)S(1)} %get-tuple-element.62), channel_id=1, source_target_pairs={{0,6},{2,0},{4,2},{6,4},{1,7},{3,1},{5,3},{7,5},{8,14},{10,8},{12,... | collective-permute-start | bytes 983048 | tf_op jit(solution)/shard_map/ppermute | solution.py:225
  98.0 9.6 %all-to-all-start = ((f32[64,1,128]{2,1,0:T(1,128)}), f32[64,1,128]{2,1,0:T(1,128)}, u32[]{:S(2)}, u32[]{:S(2)}) async-start(f32[64,1,128]{2,1,0:T(1,128)} %broadcast_in_dim.115), calls=%async_computation | async-start | bytes 65536 | tf_op jit(solution)/shard_map/all_to_all | solution.py:319
  107.7 1.6 %column.5 = (f32[20,8,128]{2,1,0:T(8,128)S(1)}, f32[20,8,128]{2,1,0:T(8,128)}, f32[20,8,128]{2,1,0:T(8,128)S(1)}, f32[20,8,128]{2,1,0:T(8,128)S(1)}) custom-call(s32[4,10]{1,0:T(4,128)S(1)} %bitcast.32, f32[4,4,10]{2,1,0:T(4,128)S(1)} %pad_maximum_fusion.weight_ref, f32[4,20,8,128]{3,2,1,0:T(8,128)S(1)} %collective-permute-done.18.refs_0_, ...), custom_call_target="tpu_custom_call" | custom-call | tf_op jit(solution)/shard_map/column/pallas_call | solution.py:284
  111.4 5.4 %all-to-all-done = f32[64,1,128]{2,1,0:T(1,128)} async-done(((f32[64,1,128]{2,1,0:T(1,128)}), f32[64,1,128]{2,1,0:T(1,128)}, u32[]{:S(2)}, u32[]{:S(2)}) %all-to-all-start) | async-done | bytes 32800 | tf_op jit(solution)/shard_map/all_to_all | solution.py:319
  119.1 2.3 %collective-permute-start.22 = (f32[20,8,128]{2,1,0:T(8,128)S(1)}, f32[20,8,128]{2,1,0:T(8,128)S(1)}, u32[]{:S(2)}, u32[]{:S(2)}) collective-permute-start(f32[20,8,128]{2,1,0:T(8,128)S(1)} %get-tuple-element.58), channel_id=1, source_target_pairs={{0,6},{2,0},{4,2},{6,4},{1,7},{3,1},{5,3},{7,5},{8,14},{10,8},{12,... | collective-permute-start | bytes 245768 | tf_op jit(solution)/shard_map/ppermute | solution.py:225
  123.7 2.8 %finish.3.refs_8_ = f32[10,3,8,2560]{3,2,1,0:T(8,128)} custom-call(s32[10]{0:T(128)S(1)} %copy-done.2, f32[4,10]{1,0:T(4,128)S(1)} %pad_maximum_fusion.1.weight_ref, f32[3]{0:T(128)S(1)} %slice_divide_fusion.ratio_ref, f32[80,8,128]{2,1,0:T(8,128)S(1)} %get-tuple-element.59.refs_0_, f32[80,8,128]{2,1,0:T(8,128)S(1)} %collective-permute-done.23.refs_1_, ...), custom_call_target="tpu_custom_call" | custom-call | tf_op jit(solution)/shard_map/finish/pallas_call | solution.py:333
  126.5 1.9 %collective-permute-done.16.refs_6_.refs_2_ = f32[50,8,128]{2,1,0:T(8,128)S(1)} collective-permute-done((f32[50,8,128]{2,1,0:T(8,128)}, f32[50,8,128]{2,1,0:T(8,128)S(1)}, u32[]{:S(2)}, u32[]{:S(2)}) %collective-permute-start.16) | collective-permute-done | bytes 204832 | tf_op jit(solution)/shard_map/ppermute | solution.py:225
  128.4 5.2 %collective-permute-done.17.refs_7_.refs_3_ = f32[50,8,128]{2,1,0:T(8,128)S(1)} collective-permute-done((f32[50,8,128]{2,1,0:T(8,128)}, f32[50,8,128]{2,1,0:T(8,128)S(1)}, u32[]{:S(2)}, u32[]{:S(2)}) %collective-permute-start.17) | collective-permute-done | bytes 204832 | tf_op jit(solution)/shard_map/ppermute | solution.py:225
  133.6 2.8 %finish.4.refs_8_ = f32[10,3,8,2560]{3,2,1,0:T(8,128)} custom-call(s32[10]{0:T(128)S(1)} %copy-done.2, f32[4,10]{1,0:T(4,128)S(1)} %pad_maximum_fusion.1.weight_ref, f32[3]{0:T(128)S(1)} %slice_divide_fusion.ratio_ref, f32[80,8,128]{2,1,0:T(8,128)S(1)} %get-tuple-element.59.refs_0_, ...), custom_call_target="tpu_custom_call", output_to_operand_aliasing={{}: (11, {})} | custom-call | tf_op jit(solution)/shard_map/finish/pallas_call | solution.py:333
  136.5 2.8 %finish.5 = f32[10,3,8,2560]{3,2,1,0:T(8,128)} custom-call(s32[10]{0:T(128)S(1)} %copy-done.2, f32[4,10]{1,0:T(4,128)S(1)} %pad_maximum_fusion.1.weight_ref, f32[3]{0:T(128)S(1)} %slice_divide_fusion.ratio_ref, f32[50,8,128]{2,1,0:T(8,128)S(1)} %get-tuple-element.50.refs_4_.refs_0_, ...), custom_call_target="tpu_custom_call", output_to_operand_aliasing={{}: (11, {})} | custom-call | tf_op jit(solution)/shard_map/finish/pallas_call | solution.py:333
  (83 shorter events, 17.6 us)
Async XLA Ops:
  7.6 16.2 %collective-permute-start = (f32[61,8,128]{2,1,0:T(8,128)S(1)}, f32[61,8,128]{2,1,0:T(8,128)S(1)}, u32[]{:S(2)}, u32[]{:S(2)}) collective-permute-start(f32[61,8,128]{2,1,0:T(8,128)S(1)} %get-tuple-element.35), channel_id=1, source_target_pairs={{0,2},{2,4},{4,6},{6,0},{1,3},{3,5},{5,7},{7,1},{8,10},{10,12},{12... | collective-permute-start | bytes 749576 | tf_op jit(solution)/shard_map/ppermute | solution.py:225
  7.7 19.0 %collective-permute-start.1 = (f32[61,8,128]{2,1,0:T(8,128)S(1)}, f32[61,8,128]{2,1,0:T(8,128)S(1)}, u32[]{:S(2)}, u32[]{:S(2)}) collective-permute-start(f32[61,8,128]{2,1,0:T(8,128)S(1)} %get-tuple-element.36), channel_id=1, source_target_pairs={{0,4},{2,6},{4,0},{6,2},{1,5},{3,7},{5,1},{7,3},{8,12},{10,14},{12... | collective-permute-start | bytes 749576 | tf_op jit(solution)/shard_map/ppermute | solution.py:225
  9.9 24.9 %collective-permute-start.2 = (f32[61,8,128]{2,1,0:T(8,128)S(1)}, f32[61,8,128]{2,1,0:T(8,128)S(1)}, u32[]{:S(2)}, u32[]{:S(2)}) collective-permute-start(f32[61,8,128]{2,1,0:T(8,128)S(1)} %get-tuple-element.37), channel_id=1, source_target_pairs={{0,6},{2,0},{4,2},{6,4},{1,7},{3,1},{5,3},{7,5},{8,14},{10,8},{12,... | collective-permute-start | bytes 749576 | tf_op jit(solution)/shard_map/ppermute | solution.py:225
  10.5 12.5 %collective-permute-start.5 = (f32[20,8,128]{2,1,0:T(8,128)S(1)}, f32[20,8,128]{2,1,0:T(8,128)S(1)}, u32[]{:S(2)}, u32[]{:S(2)}) collective-permute-start(f32[20,8,128]{2,1,0:T(8,128)S(1)} %get-tuple-element.42), channel_id=1, source_target_pairs={{0,6},{2,0},{4,2},{6,4},{1,7},{3,1},{5,3},{7,5},{8,14},{10,8},{12,... | collective-permute-start | bytes 245768 | tf_op jit(solution)/shard_map/ppermute | solution.py:225
  11.2 24.7 %collective-permute-start.10 = (f32[70,8,128]{2,1,0:T(8,128)S(1)}, f32[70,8,128]{2,1,0:T(8,128)S(1)}, u32[]{:S(2)}, u32[]{:S(2)}) collective-permute-start(f32[70,8,128]{2,1,0:T(8,128)S(1)} %get-tuple-element.46), channel_id=1, source_target_pairs={{0,2},{2,4},{4,6},{6,0},{1,3},{3,5},{5,7},{7,1},{8,10},{10,12},{12... | collective-permute-start | bytes 860168 | tf_op jit(solution)/shard_map/ppermute | solution.py:225
  22.9 13.7 %collective-permute-start.11 = (f32[70,8,128]{2,1,0:T(8,128)S(1)}, f32[70,8,128]{2,1,0:T(8,128)S(1)}, u32[]{:S(2)}, u32[]{:S(2)}) collective-permute-start(f32[70,8,128]{2,1,0:T(8,128)S(1)} %get-tuple-element.47), channel_id=1, source_target_pairs={{0,4},{2,6},{4,0},{6,2},{1,5},{3,7},{5,1},{7,3},{8,12},{10,14},{12... | collective-permute-start | bytes 860168 | tf_op jit(solution)/shard_map/ppermute | solution.py:225
  23.8 15.5 %collective-permute-start.12 = (f32[70,8,128]{2,1,0:T(8,128)S(1)}, f32[70,8,128]{2,1,0:T(8,128)S(1)}, u32[]{:S(2)}, u32[]{:S(2)}) collective-permute-start(f32[70,8,128]{2,1,0:T(8,128)S(1)} %get-tuple-element.48), channel_id=1, source_target_pairs={{0,6},{2,0},{4,2},{6,4},{1,7},{3,1},{5,3},{7,5},{8,14},{10,8},{12,... | collective-permute-start | bytes 860168 | tf_op jit(solution)/shard_map/ppermute | solution.py:225
  26.7 62.0 %collective-permute-start.7 = (f32[4,20,8,128]{3,2,1,0:T(8,128)S(1)}, f32[4,20,8,128]{3,2,1,0:T(8,128)S(1)}, u32[]{:S(2)}, u32[]{:S(2)}) collective-permute-start(f32[4,20,8,128]{3,2,1,0:T(8,128)S(1)} %join.4.refs_1_), channel_id=1, source_target_pairs={{0,248},{8,0},{16,8},{24,16},{32,24},{40,32},{48,40},{56,48},{64,5... | collective-permute-start | bytes 983048 | tf_op jit(solution)/shard_map/ppermute | solution.py:225
  35.1 56.5 %collective-permute-start.9 = (f32[4,61,8,128]{3,2,1,0:T(8,128)S(1)}, f32[4,61,8,128]{3,2,1,0:T(8,128)S(1)}, u32[]{:S(2)}, u32[]{:S(2)}) collective-permute-start(f32[4,61,8,128]{3,2,1,0:T(8,128)S(1)} %get-tuple-element.43.refs_4_), channel_id=1, source_target_pairs={{0,248},{8,0},{16,8},{24,16},{32,24},{40,32},{48,40},{56,48},{64,5... | collective-permute-start | bytes 2998280 | tf_op jit(solution)/shard_map/ppermute | solution.py:225
  35.9 55.7 %collective-permute-start.8 = (f32[4,61,8,128]{3,2,1,0:T(8,128)S(1)}, f32[4,61,8,128]{3,2,1,0:T(8,128)S(1)}, u32[]{:S(2)}, u32[]{:S(2)}) collective-permute-start(f32[4,61,8,128]{3,2,1,0:T(8,128)S(1)} %get-tuple-element.43.refs_4_), channel_id=1, source_target_pairs={{0,8},{8,16},{16,24},{24,32},{32,40},{40,48},{48,56},{56,64},{64,7... | collective-permute-start | bytes 2998280 | tf_op jit(solution)/shard_map/ppermute | solution.py:225
  39.4 40.4 %collective-permute-start.14 = (f32[4,50,8,128]{3,2,1,0:T(8,128)S(1)}, f32[4,50,8,128]{3,2,1,0:T(8,128)S(1)}, u32[]{:S(2)}, u32[]{:S(2)}) collective-permute-start(f32[4,50,8,128]{3,2,1,0:T(8,128)S(1)} %get-tuple-element.49.refs_1_), channel_id=1, source_target_pairs={{0,248},{8,0},{16,8},{24,16},{32,24},{40,32},{48,40},{56,48},{64,5... | collective-permute-start | bytes 2457608 | tf_op jit(solution)/shard_map/ppermute | solution.py:225
  47.3 32.6 %collective-permute-start.13 = (f32[4,50,8,128]{3,2,1,0:T(8,128)S(1)}, f32[4,50,8,128]{3,2,1,0:T(8,128)S(1)}, u32[]{:S(2)}, u32[]{:S(2)}) collective-permute-start(f32[4,50,8,128]{3,2,1,0:T(8,128)S(1)} %get-tuple-element.49.refs_1_), channel_id=1, source_target_pairs={{0,8},{8,16},{16,24},{24,32},{32,40},{40,48},{48,56},{56,64},{64,7... | collective-permute-start | bytes 2457608 | tf_op jit(solution)/shard_map/ppermute | solution.py:225
  79.8 11.7 %collective-permute-start.6 = (f32[4,20,8,128]{3,2,1,0:T(8,128)S(1)}, f32[4,20,8,128]{3,2,1,0:T(8,128)S(1)}, u32[]{:S(2)}, u32[]{:S(2)}) collective-permute-start(f32[4,20,8,128]{3,2,1,0:T(8,128)S(1)} %join.4.refs_1_), channel_id=1, source_target_pairs={{0,8},{8,16},{16,24},{24,32},{32,40},{40,48},{48,56},{56,64},{64,7... | collective-permute-start | bytes 983048 | tf_op jit(solution)/shard_map/ppermute | solution.py:225
  79.9 17.4 %collective-permute-start.19 = (f32[4,20,8,128]{3,2,1,0:T(8,128)S(1)}, f32[4,20,8,128]{3,2,1,0:T(8,128)S(1)}, u32[]{:S(2)}, u32[]{:S(2)}) collective-permute-start(f32[4,20,8,128]{3,2,1,0:T(8,128)S(1)} %get-tuple-element.54.refs_1_), channel_id=1, source_target_pairs={{0,248},{8,0},{16,8},{24,16},{32,24},{40,32},{48,40},{56,48},{64,5... | collective-permute-start | bytes 983048 | tf_op jit(solution)/shard_map/ppermute | solution.py:225
  88.7 19.0 %collective-permute-start.18 = (f32[4,20,8,128]{3,2,1,0:T(8,128)S(1)}, f32[4,20,8,128]{3,2,1,0:T(8,128)S(1)}, u32[]{:S(2)}, u32[]{:S(2)}) collective-permute-start(f32[4,20,8,128]{3,2,1,0:T(8,128)S(1)} %get-tuple-element.54.refs_1_), channel_id=1, source_target_pairs={{0,8},{8,16},{16,24},{24,32},{32,40},{40,48},{48,56},{56,64},{64,7... | collective-permute-start | bytes 983048 | tf_op jit(solution)/shard_map/ppermute | solution.py:225
  93.6 25.5 %collective-permute-start.23 = (f32[80,8,128]{2,1,0:T(8,128)}, f32[80,8,128]{2,1,0:T(8,128)S(1)}, u32[]{:S(2)}, u32[]{:S(2)}) collective-permute-start(f32[80,8,128]{2,1,0:T(8,128)} %get-tuple-element.60), channel_id=1, source_target_pairs={{0,2},{2,4},{4,6},{6,0},{1,3},{3,5},{5,7},{7,1},{8,10},{10,12},{12... | collective-permute-start | bytes 983048 | tf_op jit(solution)/shard_map/ppermute | solution.py:225
  93.8 27.7 %collective-permute-start.24 = (f32[80,8,128]{2,1,0:T(8,128)S(1)}, f32[80,8,128]{2,1,0:T(8,128)S(1)}, u32[]{:S(2)}, u32[]{:S(2)}) collective-permute-start(f32[80,8,128]{2,1,0:T(8,128)S(1)} %get-tuple-element.61), channel_id=1, source_target_pairs={{0,4},{2,6},{4,0},{6,2},{1,5},{3,7},{5,1},{7,3},{8,12},{10,14},{12... | collective-permute-start | bytes 983048 | tf_op jit(solution)/shard_map/ppermute | solution.py:225
  95.0 27.9 %collective-permute-start.25 = (f32[80,8,128]{2,1,0:T(8,128)S(1)}, f32[80,8,128]{2,1,0:T(8,128)S(1)}, u32[]{:S(2)}, u32[]{:S(2)}) collective-permute-start(f32[80,8,128]{2,1,0:T(8,128)S(1)} %get-tuple-element.62), channel_id=1, source_target_pairs={{0,6},{2,0},{4,2},{6,4},{1,7},{3,1},{5,3},{7,5},{8,14},{10,8},{12,... | collective-permute-start | bytes 983048 | tf_op jit(solution)/shard_map/ppermute | solution.py:225
  97.2 20.3 %collective-permute-start.15 = (f32[50,8,128]{2,1,0:T(8,128)}, f32[50,8,128]{2,1,0:T(8,128)S(1)}, u32[]{:S(2)}, u32[]{:S(2)}) collective-permute-start(f32[50,8,128]{2,1,0:T(8,128)} %get-tuple-element.51), channel_id=1, source_target_pairs={{0,2},{2,4},{4,6},{6,0},{1,3},{3,5},{5,7},{7,1},{8,10},{10,12},{12... | collective-permute-start | bytes 614408 | tf_op jit(solution)/shard_map/ppermute | solution.py:225
  98.0 18.7 %all-to-all-start = ((f32[64,1,128]{2,1,0:T(1,128)}), f32[64,1,128]{2,1,0:T(1,128)}, u32[]{:S(2)}, u32[]{:S(2)}) async-start(f32[64,1,128]{2,1,0:T(1,128)} %broadcast_in_dim.115), calls=%async_computation | async-start | bytes 65536 | tf_op jit(solution)/shard_map/all_to_all | solution.py:319
  110.0 26.5 %collective-permute-start.20 = (f32[20,8,128]{2,1,0:T(8,128)}, f32[20,8,128]{2,1,0:T(8,128)S(1)}, u32[]{:S(2)}, u32[]{:S(2)}) collective-permute-start(f32[20,8,128]{2,1,0:T(8,128)} %get-tuple-element.56), channel_id=1, source_target_pairs={{0,2},{2,4},{4,6},{6,0},{1,3},{3,5},{5,7},{7,1},{8,10},{10,12},{12... | collective-permute-start | bytes 245768 | tf_op jit(solution)/shard_map/ppermute | solution.py:225
  117.5 18.9 %collective-permute-start.21 = (f32[20,8,128]{2,1,0:T(8,128)}, f32[20,8,128]{2,1,0:T(8,128)S(1)}, u32[]{:S(2)}, u32[]{:S(2)}) collective-permute-start(f32[20,8,128]{2,1,0:T(8,128)} %copy-done.9), channel_id=1, source_target_pairs={{0,4},{2,6},{4,0},{6,2},{1,5},{3,7},{5,1},{7,3},{8,12},{10,14},{12... | collective-permute-start | bytes 245768 | tf_op jit(solution)/shard_map/ppermute | solution.py:225
  119.1 17.4 %collective-permute-start.22 = (f32[20,8,128]{2,1,0:T(8,128)S(1)}, f32[20,8,128]{2,1,0:T(8,128)S(1)}, u32[]{:S(2)}, u32[]{:S(2)}) collective-permute-start(f32[20,8,128]{2,1,0:T(8,128)S(1)} %get-tuple-element.58), channel_id=1, source_target_pairs={{0,6},{2,0},{4,2},{6,4},{1,7},{3,1},{5,3},{7,5},{8,14},{10,8},{12,... | collective-permute-start | bytes 245768 | tf_op jit(solution)/shard_map/ppermute | solution.py:225
  122.9 10.7 %collective-permute-start.17 = (f32[50,8,128]{2,1,0:T(8,128)}, f32[50,8,128]{2,1,0:T(8,128)S(1)}, u32[]{:S(2)}, u32[]{:S(2)}) collective-permute-start(f32[50,8,128]{2,1,0:T(8,128)} %copy-done.7), channel_id=1, source_target_pairs={{0,6},{2,0},{4,2},{6,4},{1,7},{3,1},{5,3},{7,5},{8,14},{10,8},{12,... | collective-permute-start | bytes 614408 | tf_op jit(solution)/shard_map/ppermute | solution.py:225
  (13 other events, 86.1 us)

commit v4 on v3

--- a/solution.py
+++ b/solution.py
@@ -20,7 +20,8 @@
 TILES = RING * QUARTER
 LON = TILES * LANES
 CHUNKS = ((0, 2), (2, 8), (8, 13), (13, 15))
-OWN = ((0,), (1,), (2, 3))
+EARLY = 0
+OWN = ((1,), (2, 3))
 BACK = ((0, 1), (2,), (3,))
 INFO_CHUNK = 1
 TOGETHER = 2
@@ -62,29 +63,18 @@
     return sum(ROWS * width_of(chunk) for chunk in batch)
 
 
-def copy_units(fields_ref, batch, piece_refs):
+def copy_units(fields_ref, chunk, owner, piece_ref, base):
+    first, last = CHUNKS[chunk]
+    for unit in range(first, last):
+        field, tile = divmod(unit, QUARTER)
+        start = pl.multiple_of((owner * QUARTER + tile) * LANES, LANES)
+        for row in range(ROWS):
+            piece_ref[base + row * (last - first) + unit - first] = fields_ref[row, field, :, pl.ds(start, LANES)]
+
+
+def pack_kernel(departure_ref, extents_ref, lat_ref, lon_ref, fields_ref, early_ref, *piece_refs):
+    band = lax.axis_index(LAT)
     place = lax.axis_index(LAT[2])
-    for distance in range(RING):
-        owner = around(place, distance)
-        base = 0
-        for chunk in batch:
-            first, last = CHUNKS[chunk]
-            for unit in range(first, last):
-                field, tile = divmod(unit, QUARTER)
-                start = pl.multiple_of((owner * QUARTER + tile) * LANES, LANES)
-                for row in range(ROWS):
-                    piece_refs[distance][base + row * (last - first) + unit - first] = fields_ref[
-                        row, field, :, pl.ds(start, LANES)
-                    ]
-            base += tile_count(chunk)
-
-
-def pack_first(fields_ref, *piece_refs):
-    copy_units(fields_ref, OWN[0], piece_refs)
-
-
-def pack_rest(departure_ref, extents_ref, lat_ref, lon_ref, fields_ref, *piece_refs):
-    band = lax.axis_index(LAT)
     first_row = band * ROWS
     group_row = lax.axis_index(LAT[:2]) * GROUP
     low_bound = first_row - extents_ref[0, 0] * ROWS + 1
@@ -110,12 +100,24 @@
         by_row = jnp.sum(jnp.sum(total, axis=1), axis=1, keepdims=True)
         in_lanes = jnp.sum(jnp.where(sub == lane, by_row, 0.0), axis=0, keepdims=True)
         info = jnp.where(info_sub == 3 + field, in_lanes, info)
-    for number, batch in enumerate(OWN[1:]):
-        refs = piece_refs[number * RING : (number + 1) * RING]
-        copy_units(fields_ref, batch, refs)
-        if INFO_CHUNK in batch:
-            for ref in refs:
-                ref[batch_tiles(batch) - 1] = info
+    for distance in range(RING):
+        owner = around(place, distance)
+        copy_units(fields_ref, EARLY, owner, early_ref.at[distance], 0)
+        for number, batch in enumerate(OWN):
+            piece_ref = piece_refs[number * RING + distance]
+            base = 0
+            for chunk in batch:
+                copy_units(fields_ref, chunk, owner, piece_ref, base)
+                base += tile_count(chunk)
+            if INFO_CHUNK in batch:
+                piece_ref[base - 1] = info
+
+
+def bundle_kernel(north_ref, own_ref, south_ref, *out_refs):
+    count = tile_count(EARLY)
+    for distance in range(RING):
+        for side, ref in enumerate((north_ref, own_ref, south_ref)):
+            out_refs[distance][side * count : (side + 1) * count] = ref[distance]
 
 
 def join_kernel(batch, *refs):
@@ -130,8 +132,11 @@
 
 
 def column_kernel(batch, start_ref, weight_ref, *refs):
-    sides = [refs[3 * number : 3 * number + 3] for number in range(len(batch))]
-    refs = refs[3 * len(batch) :]
+    sides = []
+    for chunk in batch:
+        taken = RING if chunk == EARLY else 3
+        sides.append(refs[:taken])
+        refs = refs[taken:]
     out_refs, rows_refs = refs[:RING], refs[len(refs) - len(batch) :]
     place = lax.axis_index(LAT[2])
     for chunk, side_refs, rows_ref in zip(batch, sides, rows_refs):
@@ -141,8 +146,12 @@
                 refs[RING][side] = ref[:, count]
         for distance in range(RING):
             band = around(place, -distance)
-            for side, ref in enumerate(side_refs):
-                rows_ref[pl.ds((side * RING + band) * count, count)] = ref[distance, :count]
+            for side in range(3):
+                if chunk == EARLY:
+                    block = side_refs[distance][side * count : (side + 1) * count]
+                else:
+                    block = side_refs[side][distance, :count]
+                rows_ref[pl.ds((side * RING + band) * count, count)] = block
 
     def one_row(row, carry):
         for distance in range(RING):
@@ -235,25 +244,27 @@
 
 def per_device(fields, lat_fraction, lon_fraction, lon_shift, departure_row, extents):
     params = pltpu.CompilerParams(vmem_limit_bytes=VMEM_LIMIT)
-    pieces = [
-        pl.pallas_call(
-            pack_first,
-            out_shape=[tiles(batch_tiles(OWN[0]))] * RING,
-            in_specs=[VMEM],
-            out_specs=[VMEM] * RING,
-            compiler_params=params,
-            name="pack_a",
-        )(fields)
-    ]
-    rest = pl.pallas_call(
-        pack_rest,
-        out_shape=[tiles(batch_tiles(batch)) for batch in OWN[1:] for _ in range(RING)],
+    early, *rest = pl.pallas_call(
+        pack_kernel,
+        out_shape=[tiles(RING, tile_count(EARLY))]
+        + [tiles(batch_tiles(batch)) for batch in OWN for _ in range(RING)],
         in_specs=[SMEM] * 4 + [VMEM],
-        out_specs=[VMEM] * (RING * (len(OWN) - 1)),
+        out_specs=[VMEM] * (1 + RING * len(OWN)),
         compiler_params=params,
-        name="pack_b",
+        name="pack",
     )(departure_row, extents, lat_fraction, lon_fraction, fields)
-    pieces += [rest[number * RING : (number + 1) * RING] for number in range(len(OWN) - 1)]
+    pieces = [rest[number * RING : (number + 1) * RING] for number in range(len(OWN))]
+    early_north = turn(early, LAT[:2], 1)
+    early_south = turn(early, LAT[:2], -1)
+    bundles = pl.pallas_call(
+        bundle_kernel,
+        out_shape=[tiles(3 * tile_count(EARLY))] * RING,
+        in_specs=[VMEM] * 3,
+        out_specs=[VMEM] * RING,
+        compiler_params=params,
+        name="bundle",
+    )(early_north, early, early_south)
+    bundles = exchange(bundles)
 
     own, north, south = {}, {}, {}
     for number, batch in enumerate(OWN):
@@ -280,7 +291,9 @@
     gathered = []
     for batch in BACK:
         shapes = [tiles(column_tiles(batch))] * RING + [tiles(3, RING)] * (INFO_CHUNK in batch)
-        operands = [part[chunk] for chunk in batch for part in (north, own, south)]
+        operands = []
+        for chunk in batch:
+            operands += bundles if chunk == EARLY else [north[chunk], own[chunk], south[chunk]]
         columns = pl.pallas_call(
             partial(column_kernel, batch),
             out_shape=shapes,

time: 140 us -> 144 us (1.029)
  waiting for transfers between devices: 60.3 us -> 63.8 us
    ppermute x26, waiting for transfers between devices: 54.9 us -> 58.7 us  [turn(): lax.ppermute(array, axis, [(i, (i + distance) % count) for i in range(cou...]
    all_to_all x1, starting transfers between devices: 9.63 us -> 7.58 us  [per_device(): spread = lax.all_to_all(spread, parties, 0, 0)]
    unnamed x20 -> x18, local copies, waits for them, and re-layouts: 3.69 us -> 4.95 us
  transfers between devices with their start and end apart: 27 -> 27, of which waited for: 7 -> 10; matrix products, arithmetic and copies ran while one was open for 2% -> 2% of each run, Pallas kernels for 9% -> 8%
where the time goes in v4:
time: 144 us
  waiting for transfers between devices  63.8 us (44%)
  starting transfers between devices  55.8 us (39%)
  Pallas kernels  16.1 us (11%)
  local copies, waits for them, and re-layouts  5.58 us (4%)
  other arithmetic  2.58 us (2%)
    ppermute x26, waiting for transfers between devices, turn(): lax.ppermute(array, axis, [(i, (i + distance) % count) for i in range(cou...  58.7 us
    ppermute x26, starting transfers between devices, turn(): lax.ppermute(array, axis, [(i, (i + distance) % count) for i in range(cou...  48.2 us
    pallas_call x3, Pallas kernels, per_device(): pl.pallas_call(partial(finish_kernel, field), grid=(1,), out_shape=jax.Sh...  8.5 us
    all_to_all x1, starting transfers between devices, per_device(): spread = lax.all_to_all(spread, parties, 0, 0)  7.58 us
    pallas_call x3, Pallas kernels, per_device(): pl.pallas_call(partial(column_kernel, batch), out_shape=shapes, in_specs=...  5.59 us
    all_to_all x1, waiting for transfers between devices, per_device(): spread = lax.all_to_all(spread, parties, 0, 0)  5.05 us
    unnamed x18, local copies, waits for them, and re-layouts  4.95 us
  transfers between devices with their start and end apart: 27, of which 10 were waited for; matrix products, arithmetic and copies ran while one was open for 2% of the time, Pallas kernels for 8%

profile of v4, /device:TPU:1, one launch (start us, length us, event | category | flops | bytes accessed | tf_op | source)
XLA Modules:
  0.0 144.0 jit_solution(9059641892469678454)
XLA Ops:
  4.3 1.8 %pack.1 = (f32[4,20,8,128]{3,2,1,0:T(8,128)S(1)}, f32[61,8,128]{2,1,0:T(8,128)S(1)}, f32[61,8,128]{2,1,0:T(8,128)S(1)}, f32[61,8,128]{2,1,0:T(8,128)}, f32[61,8,...) custom-call(s32[10]{0:T(128)S(1)} %copy-done.3, ...), custom_call_target="tpu_custom_call" | custom-call | tf_op jit(solution)/shard_map/pack/pallas_call | solution.py:247
  6.1 2.1 %collective-permute-start = (f32[61,8,128]{2,1,0:T(8,128)S(1)}, f32[61,8,128]{2,1,0:T(8,128)S(1)}, u32[]{:S(2)}, u32[]{:S(2)}) collective-permute-start(f32[61,8,128]{2,1,0:T(8,128)S(1)} %get-tuple-element.36), channel_id=1, source_target_pairs={{0,2},{2,4},{4,6},{6,0},{1,3},{3,5},{5,7},{7,1},{8,10},{10,12},{12... | collective-permute-start | bytes 749576 | tf_op jit(solution)/shard_map/ppermute | solution.py:234
  8.2 2.6 %collective-permute-start.1 = (f32[61,8,128]{2,1,0:T(8,128)}, f32[61,8,128]{2,1,0:T(8,128)S(1)}, u32[]{:S(2)}, u32[]{:S(2)}) collective-permute-start(f32[61,8,128]{2,1,0:T(8,128)} %get-tuple-element.37), channel_id=1, source_target_pairs={{0,4},{2,6},{4,0},{6,2},{1,5},{3,7},{5,1},{7,3},{8,12},{10,14},{12... | collective-permute-start | bytes 749576 | tf_op jit(solution)/shard_map/ppermute | solution.py:234
  13.3 3.3 %collective-permute-start.12 = (f32[70,8,128]{2,1,0:T(8,128)S(1)}, f32[70,8,128]{2,1,0:T(8,128)S(1)}, u32[]{:S(2)}, u32[]{:S(2)}) collective-permute-start(f32[70,8,128]{2,1,0:T(8,128)S(1)} %get-tuple-element.50), channel_id=1, source_target_pairs={{0,6},{2,0},{4,2},{6,4},{1,7},{3,1},{5,3},{7,5},{8,14},{10,8},{12,... | collective-permute-start | bytes 860168 | tf_op jit(solution)/shard_map/ppermute | solution.py:234
  16.6 5.1 %collective-permute-done.1.refs_2_ = f32[61,8,128]{2,1,0:T(8,128)S(1)} collective-permute-done((f32[61,8,128]{2,1,0:T(8,128)}, f32[61,8,128]{2,1,0:T(8,128)S(1)}, u32[]{:S(2)}, u32[]{:S(2)}) %collective-permute-start.1) | collective-permute-done | bytes 249888 | tf_op jit(solution)/shard_map/ppermute | solution.py:234
  21.7 7.8 %collective-permute-start.4 = (f32[4,20,8,128]{3,2,1,0:T(8,128)S(1)}, f32[4,20,8,128]{3,2,1,0:T(8,128)S(1)}, u32[]{:S(2)}, u32[]{:S(2)}) collective-permute-start(f32[4,20,8,128]{3,2,1,0:T(8,128)S(1)} %get-tuple-element.40.own_ref), channel_id=1, source_target_pairs={{0,248},{8,0},{16,8},{24,16},{32,24},{40,32},{48,40},{56,48},{64,5... | collective-permute-start | bytes 983048 | tf_op jit(solution)/shard_map/ppermute | solution.py:234
  31.3 2.6 %collective-permute-done.11.refs_2_ = f32[70,8,128]{2,1,0:T(8,128)S(1)} collective-permute-done((f32[70,8,128]{2,1,0:T(8,128)S(1)}, f32[70,8,128]{2,1,0:T(8,128)S(1)}, u32[]{:S(2)}, u32[]{:S(2)}) %collective-permute-start.11) | collective-permute-done | bytes 286752 | tf_op jit(solution)/shard_map/ppermute | solution.py:234
  34.1 7.9 %collective-permute-start.14 = (f32[4,50,8,128]{3,2,1,0:T(8,128)S(1)}, f32[4,50,8,128]{3,2,1,0:T(8,128)S(1)}, u32[]{:S(2)}, u32[]{:S(2)}) collective-permute-start(f32[4,50,8,128]{3,2,1,0:T(8,128)S(1)} %get-tuple-element.51.refs_1_), channel_id=1, source_target_pairs={{0,248},{8,0},{16,8},{24,16},{32,24},{40,32},{48,40},{56,48},{64,5... | collective-permute-start | bytes 2457608 | tf_op jit(solution)/shard_map/ppermute | solution.py:234
  43.2 35.7 %collective-permute-done.3.north_ref = f32[4,20,8,128]{3,2,1,0:T(8,128)S(1)} collective-permute-done((f32[4,20,8,128]{3,2,1,0:T(8,128)S(1)}, f32[4,20,8,128]{3,2,1,0:T(8,128)S(1)}, u32[]{:S(2)}, u32[]{:S(2)}) %collective-permute-start.3) | collective-permute-done | bytes 327712 | tf_op jit(solution)/shard_map/ppermute | solution.py:234
  79.1 6.8 %collective-permute-start.6 = (f32[60,8,128]{2,1,0:T(8,128)S(1)}, f32[60,8,128]{2,1,0:T(8,128)S(1)}, u32[]{:S(2)}, u32[]{:S(2)}) collective-permute-start(f32[60,8,128]{2,1,0:T(8,128)S(1)} %get-tuple-element.43), channel_id=1, source_target_pairs={{0,4},{2,6},{4,0},{6,2},{1,5},{3,7},{5,1},{7,3},{8,12},{10,14},{12... | collective-permute-start | bytes 737288 | tf_op jit(solution)/shard_map/ppermute | solution.py:234
  86.0 1.9 %column.4 = (f32[50,8,128]{2,1,0:T(8,128)S(1)}, f32[50,8,128]{2,1,0:T(8,128)}, f32[50,8,128]{2,1,0:T(8,128)S(1)}, f32[50,8,128]{2,1,0:T(8,128)S(1)}) custom-call(s32[4,10]{1,0:T(4,128)S(1)} %bitcast.30, f32[4,4,10]{2,1,0:T(4,128)S(1)} %pad_maximum_fusion.weight_ref, f32[4,50,8,128]{3,2,1,0:T(8,128)S(1)} %collective-permute-done.13.refs_0_, ...), custom_call_target="tpu_custom_call" | custom-call | tf_op jit(solution)/shard_map/column/pallas_call | solution.py:297
  89.2 6.2 %collective-permute-done.6.refs_2_ = f32[60,8,128]{2,1,0:T(8,128)S(1)} collective-permute-done((f32[60,8,128]{2,1,0:T(8,128)S(1)}, f32[60,8,128]{2,1,0:T(8,128)S(1)}, u32[]{:S(2)}, u32[]{:S(2)}) %collective-permute-start.6) | collective-permute-done | bytes 245792 | tf_op jit(solution)/shard_map/ppermute | solution.py:234
  95.9 2.1 %column.3 = (f32[80,8,128]{2,1,0:T(8,128)S(1)}, f32[80,8,128]{2,1,0:T(8,128)}, f32[80,8,128]{2,1,0:T(8,128)S(1)}, f32[80,8,128]{2,1,0:T(8,128)S(1)}, f32[3,4,8,128]{3,2,1,0:T(8,128)S(1)}) custom-call(s32[4,10]{1,0:T(4,128)S(1)} %bitcast.31, f32[4,4,10]{2,1,0:T(4,128)S(1)} %pad_maximum_fusion.weight_ref, f32[60,8,128]{2,1,0:T(8,128)S(1)} %get-tuple-element.41.refs_0_, ...), custom_call_target="tpu_custom_call" | custom-call | tf_op jit(solution)/shard_map/column/pallas_call | solution.py:297
  98.7 4.0 %collective-permute-start.24 = (f32[80,8,128]{2,1,0:T(8,128)S(1)}, f32[80,8,128]{2,1,0:T(8,128)S(1)}, u32[]{:S(2)}, u32[]{:S(2)}) collective-permute-start(f32[80,8,128]{2,1,0:T(8,128)S(1)} %get-tuple-element.63), channel_id=1, source_target_pairs={{0,4},{2,6},{4,0},{6,2},{1,5},{3,7},{5,1},{7,3},{8,12},{10,14},{12... | collective-permute-start | bytes 983048 | tf_op jit(solution)/shard_map/ppermute | solution.py:234
  105.2 7.6 %all-to-all-start = ((f32[64,1,128]{2,1,0:T(1,128)}), f32[64,1,128]{2,1,0:T(1,128)}, u32[]{:S(2)}, u32[]{:S(2)}) async-start(f32[64,1,128]{2,1,0:T(1,128)} %broadcast_in_dim.115), calls=%async_computation | async-start | bytes 65536 | tf_op jit(solution)/shard_map/all_to_all | solution.py:332
  115.1 1.7 %collective-permute-start.20 = (f32[20,8,128]{2,1,0:T(8,128)}, f32[20,8,128]{2,1,0:T(8,128)S(1)}, u32[]{:S(2)}, u32[]{:S(2)}) collective-permute-start(f32[20,8,128]{2,1,0:T(8,128)} %get-tuple-element.58), channel_id=1, source_target_pairs={{0,2},{2,4},{4,6},{6,0},{1,3},{3,5},{5,7},{7,1},{8,10},{10,12},{12... | collective-permute-start | bytes 245768 | tf_op jit(solution)/shard_map/ppermute | solution.py:234
  116.9 5.0 %all-to-all-done = f32[64,1,128]{2,1,0:T(1,128)} async-done(((f32[64,1,128]{2,1,0:T(1,128)}), f32[64,1,128]{2,1,0:T(1,128)}, u32[]{:S(2)}, u32[]{:S(2)}) %all-to-all-start) | async-done | bytes 32800 | tf_op jit(solution)/shard_map/all_to_all | solution.py:332
  122.7 1.9 %collective-permute-start.21 = (f32[20,8,128]{2,1,0:T(8,128)}, f32[20,8,128]{2,1,0:T(8,128)S(1)}, u32[]{:S(2)}, u32[]{:S(2)}) collective-permute-start(f32[20,8,128]{2,1,0:T(8,128)} %copy-done.8), channel_id=1, source_target_pairs={{0,4},{2,6},{4,0},{6,2},{1,5},{3,7},{5,1},{7,3},{8,12},{10,14},{12... | collective-permute-start | bytes 245768 | tf_op jit(solution)/shard_map/ppermute | solution.py:234
  124.6 2.3 %collective-permute-start.22 = (f32[20,8,128]{2,1,0:T(8,128)S(1)}, f32[20,8,128]{2,1,0:T(8,128)S(1)}, u32[]{:S(2)}, u32[]{:S(2)}) collective-permute-start(f32[20,8,128]{2,1,0:T(8,128)S(1)} %get-tuple-element.60), channel_id=1, source_target_pairs={{0,6},{2,0},{4,2},{6,4},{1,7},{3,1},{5,3},{7,5},{8,14},{10,8},{12,... | collective-permute-start | bytes 245768 | tf_op jit(solution)/shard_map/ppermute | solution.py:234
  128.5 2.8 %finish.3.refs_8_ = f32[10,3,8,2560]{3,2,1,0:T(8,128)} custom-call(s32[10]{0:T(128)S(1)} %copy-done.1, f32[4,10]{1,0:T(4,128)S(1)} %pad_maximum_fusion.1.weight_ref, f32[3]{0:T(128)S(1)} %slice_divide_fusion.ratio_ref, f32[80,8,128]{2,1,0:T(8,128)S(1)} %get-tuple-element.61.refs_0_, f32[80,8,128]{2,1,0:T(8,128)S(1)} %collective-permute-done.23.refs_1_, ...), custom_call_target="tpu_custom_call" | custom-call | tf_op jit(solution)/shard_map/finish/pallas_call | solution.py:346
  131.3 2.5 %collective-permute-done.16.refs_6_.refs_2_ = f32[50,8,128]{2,1,0:T(8,128)S(1)} collective-permute-done((f32[50,8,128]{2,1,0:T(8,128)}, f32[50,8,128]{2,1,0:T(8,128)S(1)}, u32[]{:S(2)}, u32[]{:S(2)}) %collective-permute-start.16) | collective-permute-done | bytes 204832 | tf_op jit(solution)/shard_map/ppermute | solution.py:234
  133.9 4.5 %collective-permute-done.17.refs_7_.refs_3_ = f32[50,8,128]{2,1,0:T(8,128)S(1)} collective-permute-done((f32[50,8,128]{2,1,0:T(8,128)}, f32[50,8,128]{2,1,0:T(8,128)S(1)}, u32[]{:S(2)}, u32[]{:S(2)}) %collective-permute-start.17) | collective-permute-done | bytes 204832 | tf_op jit(solution)/shard_map/ppermute | solution.py:234
  138.4 2.8 %finish.4.refs_8_ = f32[10,3,8,2560]{3,2,1,0:T(8,128)} custom-call(s32[10]{0:T(128)S(1)} %copy-done.1, f32[4,10]{1,0:T(4,128)S(1)} %pad_maximum_fusion.1.weight_ref, f32[3]{0:T(128)S(1)} %slice_divide_fusion.ratio_ref, f32[80,8,128]{2,1,0:T(8,128)S(1)} %get-tuple-element.61.refs_0_, ...), custom_call_target="tpu_custom_call", output_to_operand_aliasing={{}: (11, {})} | custom-call | tf_op jit(solution)/shard_map/finish/pallas_call | solution.py:346
  141.2 2.8 %finish.5 = f32[10,3,8,2560]{3,2,1,0:T(8,128)} custom-call(s32[10]{0:T(128)S(1)} %copy-done.1, f32[4,10]{1,0:T(4,128)S(1)} %pad_maximum_fusion.1.weight_ref, f32[3]{0:T(128)S(1)} %slice_divide_fusion.ratio_ref, f32[50,8,128]{2,1,0:T(8,128)S(1)} %get-tuple-element.52.refs_4_.refs_0_, ...), custom_call_target="tpu_custom_call", output_to_operand_aliasing={{}: (11, {})} | custom-call | tf_op jit(solution)/shard_map/finish/pallas_call | solution.py:346
  (80 shorter events, 19.9 us)
Async XLA Ops:
  8.2 13.5 %collective-permute-start.1 = (f32[61,8,128]{2,1,0:T(8,128)}, f32[61,8,128]{2,1,0:T(8,128)S(1)}, u32[]{:S(2)}, u32[]{:S(2)}) collective-permute-start(f32[61,8,128]{2,1,0:T(8,128)} %get-tuple-element.37), channel_id=1, source_target_pairs={{0,4},{2,6},{4,0},{6,2},{1,5},{3,7},{5,1},{7,3},{8,12},{10,14},{12... | collective-permute-start | bytes 749576 | tf_op jit(solution)/shard_map/ppermute | solution.py:234
  10.8 18.6 %collective-permute-start.2 = (f32[61,8,128]{2,1,0:T(8,128)}, f32[61,8,128]{2,1,0:T(8,128)S(1)}, u32[]{:S(2)}, u32[]{:S(2)}) collective-permute-start(f32[61,8,128]{2,1,0:T(8,128)} %get-tuple-element.38), channel_id=1, source_target_pairs={{0,6},{2,0},{4,2},{6,4},{1,7},{3,1},{5,3},{7,5},{8,14},{10,8},{12,... | collective-permute-start | bytes 749576 | tf_op jit(solution)/shard_map/ppermute | solution.py:234
  11.9 18.6 %collective-permute-start.10 = (f32[70,8,128]{2,1,0:T(8,128)S(1)}, f32[70,8,128]{2,1,0:T(8,128)S(1)}, u32[]{:S(2)}, u32[]{:S(2)}) collective-permute-start(f32[70,8,128]{2,1,0:T(8,128)S(1)} %get-tuple-element.48), channel_id=1, source_target_pairs={{0,2},{2,4},{4,6},{6,0},{1,3},{3,5},{5,7},{7,1},{8,10},{10,12},{12... | collective-permute-start | bytes 860168 | tf_op jit(solution)/shard_map/ppermute | solution.py:234
  12.3 21.7 %collective-permute-start.11 = (f32[70,8,128]{2,1,0:T(8,128)S(1)}, f32[70,8,128]{2,1,0:T(8,128)S(1)}, u32[]{:S(2)}, u32[]{:S(2)}) collective-permute-start(f32[70,8,128]{2,1,0:T(8,128)S(1)} %get-tuple-element.49), channel_id=1, source_target_pairs={{0,4},{2,6},{4,0},{6,2},{1,5},{3,7},{5,1},{7,3},{8,12},{10,14},{12... | collective-permute-start | bytes 860168 | tf_op jit(solution)/shard_map/ppermute | solution.py:234
  13.3 20.7 %collective-permute-start.12 = (f32[70,8,128]{2,1,0:T(8,128)S(1)}, f32[70,8,128]{2,1,0:T(8,128)S(1)}, u32[]{:S(2)}, u32[]{:S(2)}) collective-permute-start(f32[70,8,128]{2,1,0:T(8,128)S(1)} %get-tuple-element.50), channel_id=1, source_target_pairs={{0,6},{2,0},{4,2},{6,4},{1,7},{3,1},{5,3},{7,5},{8,14},{10,8},{12,... | collective-permute-start | bytes 860168 | tf_op jit(solution)/shard_map/ppermute | solution.py:234
  21.7 21.4 %collective-permute-start.4 = (f32[4,20,8,128]{3,2,1,0:T(8,128)S(1)}, f32[4,20,8,128]{3,2,1,0:T(8,128)S(1)}, u32[]{:S(2)}, u32[]{:S(2)}) collective-permute-start(f32[4,20,8,128]{3,2,1,0:T(8,128)S(1)} %get-tuple-element.40.own_ref), channel_id=1, source_target_pairs={{0,248},{8,0},{16,8},{24,16},{32,24},{40,32},{48,40},{56,48},{64,5... | collective-permute-start | bytes 983048 | tf_op jit(solution)/shard_map/ppermute | solution.py:234
  29.6 66.4 %collective-permute-start.9 = (f32[4,61,8,128]{3,2,1,0:T(8,128)S(1)}, f32[4,61,8,128]{3,2,1,0:T(8,128)S(1)}, u32[]{:S(2)}, u32[]{:S(2)}) collective-permute-start(f32[4,61,8,128]{3,2,1,0:T(8,128)S(1)} %get-tuple-element.45.refs_5_), channel_id=1, source_target_pairs={{0,248},{8,0},{16,8},{24,16},{32,24},{40,32},{48,40},{56,48},{64,5... | collective-permute-start | bytes 2998280 | tf_op jit(solution)/shard_map/ppermute | solution.py:234
  30.5 65.4 %collective-permute-start.8 = (f32[4,61,8,128]{3,2,1,0:T(8,128)S(1)}, f32[4,61,8,128]{3,2,1,0:T(8,128)S(1)}, u32[]{:S(2)}, u32[]{:S(2)}) collective-permute-start(f32[4,61,8,128]{3,2,1,0:T(8,128)S(1)} %get-tuple-element.45.refs_5_), channel_id=1, source_target_pairs={{0,8},{8,16},{16,24},{24,32},{32,40},{40,48},{48,56},{56,64},{64,7... | collective-permute-start | bytes 2998280 | tf_op jit(solution)/shard_map/ppermute | solution.py:234
  34.1 45.0 %collective-permute-start.14 = (f32[4,50,8,128]{3,2,1,0:T(8,128)S(1)}, f32[4,50,8,128]{3,2,1,0:T(8,128)S(1)}, u32[]{:S(2)}, u32[]{:S(2)}) collective-permute-start(f32[4,50,8,128]{3,2,1,0:T(8,128)S(1)} %get-tuple-element.51.refs_1_), channel_id=1, source_target_pairs={{0,248},{8,0},{16,8},{24,16},{32,24},{40,32},{48,40},{56,48},{64,5... | collective-permute-start | bytes 2457608 | tf_op jit(solution)/shard_map/ppermute | solution.py:234
  41.9 44.0 %collective-permute-start.13 = (f32[4,50,8,128]{3,2,1,0:T(8,128)S(1)}, f32[4,50,8,128]{3,2,1,0:T(8,128)S(1)}, u32[]{:S(2)}, u32[]{:S(2)}) collective-permute-start(f32[4,50,8,128]{3,2,1,0:T(8,128)S(1)} %get-tuple-element.51.refs_1_), channel_id=1, source_target_pairs={{0,8},{8,16},{16,24},{24,32},{32,40},{40,48},{48,56},{56,64},{64,7... | collective-permute-start | bytes 2457608 | tf_op jit(solution)/shard_map/ppermute | solution.py:234
  43.1 35.8 %collective-permute-start.3 = (f32[4,20,8,128]{3,2,1,0:T(8,128)S(1)}, f32[4,20,8,128]{3,2,1,0:T(8,128)S(1)}, u32[]{:S(2)}, u32[]{:S(2)}) collective-permute-start(f32[4,20,8,128]{3,2,1,0:T(8,128)S(1)} %get-tuple-element.40.own_ref), channel_id=1, source_target_pairs={{0,8},{8,16},{16,24},{24,32},{32,40},{40,48},{48,56},{56,64},{64,7... | collective-permute-start | bytes 983048 | tf_op jit(solution)/shard_map/ppermute | solution.py:234
  79.0 10.2 %collective-permute-start.5 = (f32[60,8,128]{2,1,0:T(8,128)S(1)}, f32[60,8,128]{2,1,0:T(8,128)S(1)}, u32[]{:S(2)}, u32[]{:S(2)}) collective-permute-start(f32[60,8,128]{2,1,0:T(8,128)S(1)} %get-tuple-element.42), channel_id=1, source_target_pairs={{0,2},{2,4},{4,6},{6,0},{1,3},{3,5},{5,7},{7,1},{8,10},{10,12},{12... | collective-permute-start | bytes 737288 | tf_op jit(solution)/shard_map/ppermute | solution.py:234
  79.1 16.3 %collective-permute-start.6 = (f32[60,8,128]{2,1,0:T(8,128)S(1)}, f32[60,8,128]{2,1,0:T(8,128)S(1)}, u32[]{:S(2)}, u32[]{:S(2)}) collective-permute-start(f32[60,8,128]{2,1,0:T(8,128)S(1)} %get-tuple-element.43), channel_id=1, source_target_pairs={{0,4},{2,6},{4,0},{6,2},{1,5},{3,7},{5,1},{7,3},{8,12},{10,14},{12... | collective-permute-start | bytes 737288 | tf_op jit(solution)/shard_map/ppermute | solution.py:234
  89.2 13.8 %collective-permute-start.19 = (f32[4,20,8,128]{3,2,1,0:T(8,128)S(1)}, f32[4,20,8,128]{3,2,1,0:T(8,128)S(1)}, u32[]{:S(2)}, u32[]{:S(2)}) collective-permute-start(f32[4,20,8,128]{3,2,1,0:T(8,128)S(1)} %get-tuple-element.56.refs_1_), channel_id=1, source_target_pairs={{0,248},{8,0},{16,8},{24,16},{32,24},{40,32},{48,40},{56,48},{64,5... | collective-permute-start | bytes 983048 | tf_op jit(solution)/shard_map/ppermute | solution.py:234
  95.4 17.5 %collective-permute-start.18 = (f32[4,20,8,128]{3,2,1,0:T(8,128)S(1)}, f32[4,20,8,128]{3,2,1,0:T(8,128)S(1)}, u32[]{:S(2)}, u32[]{:S(2)}) collective-permute-start(f32[4,20,8,128]{3,2,1,0:T(8,128)S(1)} %get-tuple-element.56.refs_1_), channel_id=1, source_target_pairs={{0,8},{8,16},{16,24},{24,32},{32,40},{40,48},{48,56},{56,64},{64,7... | collective-permute-start | bytes 983048 | tf_op jit(solution)/shard_map/ppermute | solution.py:234
  98.0 26.5 %collective-permute-start.23 = (f32[80,8,128]{2,1,0:T(8,128)}, f32[80,8,128]{2,1,0:T(8,128)S(1)}, u32[]{:S(2)}, u32[]{:S(2)}) collective-permute-start(f32[80,8,128]{2,1,0:T(8,128)} %get-tuple-element.62), channel_id=1, source_target_pairs={{0,2},{2,4},{4,6},{6,0},{1,3},{3,5},{5,7},{7,1},{8,10},{10,12},{12... | collective-permute-start | bytes 983048 | tf_op jit(solution)/shard_map/ppermute | solution.py:234
  98.7 28.2 %collective-permute-start.24 = (f32[80,8,128]{2,1,0:T(8,128)S(1)}, f32[80,8,128]{2,1,0:T(8,128)S(1)}, u32[]{:S(2)}, u32[]{:S(2)}) collective-permute-start(f32[80,8,128]{2,1,0:T(8,128)S(1)} %get-tuple-element.63), channel_id=1, source_target_pairs={{0,4},{2,6},{4,0},{6,2},{1,5},{3,7},{5,1},{7,3},{8,12},{10,14},{12... | collective-permute-start | bytes 983048 | tf_op jit(solution)/shard_map/ppermute | solution.py:234
  102.7 24.5 %collective-permute-start.25 = (f32[80,8,128]{2,1,0:T(8,128)S(1)}, f32[80,8,128]{2,1,0:T(8,128)S(1)}, u32[]{:S(2)}, u32[]{:S(2)}) collective-permute-start(f32[80,8,128]{2,1,0:T(8,128)S(1)} %get-tuple-element.64), channel_id=1, source_target_pairs={{0,6},{2,0},{4,2},{6,4},{1,7},{3,1},{5,3},{7,5},{8,14},{10,8},{12,... | collective-permute-start | bytes 983048 | tf_op jit(solution)/shard_map/ppermute | solution.py:234
  103.0 19.7 %collective-permute-start.15 = (f32[50,8,128]{2,1,0:T(8,128)}, f32[50,8,128]{2,1,0:T(8,128)S(1)}, u32[]{:S(2)}, u32[]{:S(2)}) collective-permute-start(f32[50,8,128]{2,1,0:T(8,128)} %get-tuple-element.53), channel_id=1, source_target_pairs={{0,2},{2,4},{4,6},{6,0},{1,3},{3,5},{5,7},{7,1},{8,10},{10,12},{12... | collective-permute-start | bytes 614408 | tf_op jit(solution)/shard_map/ppermute | solution.py:234
  105.2 16.7 %all-to-all-start = ((f32[64,1,128]{2,1,0:T(1,128)}), f32[64,1,128]{2,1,0:T(1,128)}, u32[]{:S(2)}, u32[]{:S(2)}) async-start(f32[64,1,128]{2,1,0:T(1,128)} %broadcast_in_dim.115), calls=%async_computation | async-start | bytes 65536 | tf_op jit(solution)/shard_map/all_to_all | solution.py:332
  115.1 26.1 %collective-permute-start.20 = (f32[20,8,128]{2,1,0:T(8,128)}, f32[20,8,128]{2,1,0:T(8,128)S(1)}, u32[]{:S(2)}, u32[]{:S(2)}) collective-permute-start(f32[20,8,128]{2,1,0:T(8,128)} %get-tuple-element.58), channel_id=1, source_target_pairs={{0,2},{2,4},{4,6},{6,0},{1,3},{3,5},{5,7},{7,1},{8,10},{10,12},{12... | collective-permute-start | bytes 245768 | tf_op jit(solution)/shard_map/ppermute | solution.py:234
  122.7 18.5 %collective-permute-start.21 = (f32[20,8,128]{2,1,0:T(8,128)}, f32[20,8,128]{2,1,0:T(8,128)S(1)}, u32[]{:S(2)}, u32[]{:S(2)}) collective-permute-start(f32[20,8,128]{2,1,0:T(8,128)} %copy-done.8), channel_id=1, source_target_pairs={{0,4},{2,6},{4,0},{6,2},{1,5},{3,7},{5,1},{7,3},{8,12},{10,14},{12... | collective-permute-start | bytes 245768 | tf_op jit(solution)/shard_map/ppermute | solution.py:234
  124.6 16.6 %collective-permute-start.22 = (f32[20,8,128]{2,1,0:T(8,128)S(1)}, f32[20,8,128]{2,1,0:T(8,128)S(1)}, u32[]{:S(2)}, u32[]{:S(2)}) collective-permute-start(f32[20,8,128]{2,1,0:T(8,128)S(1)} %get-tuple-element.60), channel_id=1, source_target_pairs={{0,6},{2,0},{4,2},{6,4},{1,7},{3,1},{5,3},{7,5},{8,14},{10,8},{12,... | collective-permute-start | bytes 245768 | tf_op jit(solution)/shard_map/ppermute | solution.py:234
  127.2 11.1 %collective-permute-start.17 = (f32[50,8,128]{2,1,0:T(8,128)}, f32[50,8,128]{2,1,0:T(8,128)S(1)}, u32[]{:S(2)}, u32[]{:S(2)}) collective-permute-start(f32[50,8,128]{2,1,0:T(8,128)} %copy-done.6), channel_id=1, source_target_pairs={{0,6},{2,0},{4,2},{6,4},{1,7},{3,1},{5,3},{7,5},{8,14},{10,8},{12,... | collective-permute-start | bytes 614408 | tf_op jit(solution)/shard_map/ppermute | solution.py:234
  (12 other events, 92.0 us)

commit v5 on v3

--- a/solution.py
+++ b/solution.py
@@ -19,7 +19,8 @@
 QUARTER = 5
 TILES = RING * QUARTER
 LON = TILES * LANES
-CHUNKS = ((0, 2), (2, 8), (8, 13), (13, 15))
+CHUNKS = ((0, 3), (3, 9), (9, 13), (13, 15))
+PARTNERS = (2, 1, 3)
 OWN = ((0,), (1,), (2, 3))
 BACK = ((0, 1), (2,), (3,))
 INFO_CHUNK = 1
@@ -41,8 +42,13 @@
     )
 
 
-def around(place, distance):
-    return lax.rem(place + RING + distance, RING)
+def across(place, step):
+    return jnp.bitwise_xor(place, step)
+
+
+def side_places(group):
+    even = 1 - lax.rem(group, 2)
+    return 2 * even, 1, 2 - 2 * even
 
 
 def width_of(chunk):
@@ -65,7 +71,7 @@
 def copy_units(fields_ref, batch, piece_refs):
     place = lax.axis_index(LAT[2])
     for distance in range(RING):
-        owner = around(place, distance)
+        owner = across(place, distance)
         base = 0
         for chunk in batch:
             first, last = CHUNKS[chunk]
@@ -134,21 +140,21 @@
     refs = refs[3 * len(batch) :]
     out_refs, rows_refs = refs[:RING], refs[len(refs) - len(batch) :]
     place = lax.axis_index(LAT[2])
+    positions = side_places(lax.axis_index(LAT[:2]))
     for chunk, side_refs, rows_ref in zip(batch, sides, rows_refs):
         count = width_of(chunk) * ROWS
         if chunk == INFO_CHUNK:
-            for side, ref in enumerate(side_refs):
+            for side, ref in zip(positions, side_refs):
                 refs[RING][side] = ref[:, count]
         for distance in range(RING):
-            band = around(place, -distance)
-            for side, ref in enumerate(side_refs):
+            band = across(place, distance)
+            for side, ref in zip(positions, side_refs):
                 rows_ref[pl.ds((side * RING + band) * count, count)] = ref[distance, :count]
 
     def one_row(row, carry):
         for distance in range(RING):
-            source = (RING - distance) % RING
-            first = start_ref[source, row]
-            weights = [weight_ref[step, source, row] for step in range(4)]
+            first = start_ref[distance, row]
+            weights = [weight_ref[step, distance, row] for step in range(4)]
             base = 0
             for chunk, rows_ref in zip(batch, rows_refs):
                 width = width_of(chunk)
@@ -184,7 +190,7 @@
     out_ref, turned_ref = refs[-2], refs[-1]
     batches = field_batches(field)
     place = lax.axis_index(LAT[2])
-    owners = [around(place, -distance) for distance in range(RING)]
+    owners = [across(place, distance) for distance in range(RING)]
     lane = lax.broadcasted_iota(jnp.int32, (8, LANES), 1)
     scale = ratio_ref[field]
 
@@ -220,13 +226,22 @@
     lax.fori_loop(0, ROWS // TOGETHER, some_rows, 0)
 
 
-def turn(array, axis, distance):
-    count = lax.axis_size(axis)
-    return lax.ppermute(array, axis, [(i, (i + distance) % count) for i in range(count)])
+def swap(array, axis, partner):
+    return lax.ppermute(array, axis, [(i, partner(i)) for i in range(lax.axis_size(axis))])
 
 
 def exchange(pieces):
-    return [pieces[0]] + [turn(pieces[distance], LAT[2], distance) for distance in range(1, RING)]
+    received = {0: pieces[0]}
+    for step in PARTNERS:
+        received[step] = swap(pieces[step], LAT[2], lambda i, step=step: i ^ step)
+    return [received[step] for step in range(RING)]
+
+
+def both_sides(block):
+    groups = lax.axis_size(LAT[:2])
+    inner = swap(block, LAT[:2], lambda i: i ^ 1)
+    outer = swap(block, LAT[:2], lambda i: (i + 1 if i % 2 else i - 1) % groups)
+    return inner, outer
 
 
 def tiles(*shape):
@@ -255,7 +270,7 @@
     )(departure_row, extents, lat_fraction, lon_fraction, fields)
     pieces += [rest[number * RING : (number + 1) * RING] for number in range(len(OWN) - 1)]
 
-    own, north, south = {}, {}, {}
+    own, inner, outer = {}, {}, {}
     for number, batch in enumerate(OWN):
         received = exchange(pieces[number])
         shapes = [tiles(RING, tile_count(chunk)) for chunk in batch] + [tiles(RING)] * (INFO_CHUNK in batch)
@@ -271,8 +286,7 @@
             ring_info = joined[-1][:, :, :ROWS]
         for chunk, block in zip(batch, joined):
             own[chunk] = block
-            north[chunk] = turn(block, LAT[:2], 1)
-            south[chunk] = turn(block, LAT[:2], -1)
+            inner[chunk], outer[chunk] = both_sides(block)
 
     ring_start = ring_info[:, 0].astype(jnp.int32)
     ring_weight = jnp.stack(cubic_weights(ring_info[:, 1]))
@@ -280,7 +294,7 @@
     gathered = []
     for batch in BACK:
         shapes = [tiles(column_tiles(batch))] * RING + [tiles(3, RING)] * (INFO_CHUNK in batch)
-        operands = [part[chunk] for chunk in batch for part in (north, own, south)]
+        operands = [part[chunk] for chunk in batch for part in (inner, own, outer)]
         columns = pl.pallas_call(
             partial(column_kernel, batch),
             out_shape=shapes,
@@ -298,7 +312,7 @@
 
     total_rows = lax.axis_size(LAT) * ROWS
     group_row = lax.axis_index(LAT[:2]) * GROUP
-    bands = around(lax.axis_index(LAT[2]), -jnp.arange(RING, dtype=jnp.int32))
+    bands = across(lax.axis_index(LAT[2]), jnp.arange(RING, dtype=jnp.int32))
     ring_rows = bands[:, None] * ROWS + jnp.arange(ROWS, dtype=jnp.int32)[None]
     area = jnp.cos(math.pi * ((group_row + ring_rows).astype(jnp.float32) + 0.5) / total_rows - math.pi / 2.0)
     sums = all_info[:, :, 3 : 3 + FIELDS, :ROWS]

time: 140 us -> 135 us (0.964)
  waiting for transfers between devices: 60.3 us -> 47.6 us
  starting transfers between devices: 56.6 us -> 63.1 us
  local copies, waits for them, and re-layouts: 4.34 us -> 6.25 us
    ppermute x26, waiting for transfers between devices: 54.9 us -> 42.2 us  [swap(): lax.ppermute(array, axis, [(i, partner(i)) for i in range(lax.axis_size(a...]
    ppermute x26, starting transfers between devices: 47 us -> 53.1 us  [swap(): lax.ppermute(array, axis, [(i, partner(i)) for i in range(lax.axis_size(a...]
    unnamed x20, local copies, waits for them, and re-layouts: 3.69 us -> 5.61 us
  transfers between devices with their start and end apart: 27 -> 27, of which waited for: 7 -> 9; matrix products, arithmetic and copies ran while one was open for 2% -> 2% of each run, Pallas kernels for 9% -> 9%
where the time goes in v5:
time: 135 us
  starting transfers between devices  63.1 us (47%)
  waiting for transfers between devices  47.6 us (35%)
  Pallas kernels  16.2 us (12%)
  local copies, waits for them, and re-layouts  6.25 us (5%)
  other arithmetic  1.83 us (1%)
    ppermute x26, starting transfers between devices, swap(): lax.ppermute(array, axis, [(i, partner(i)) for i in range(lax.axis_size(a...  53.1 us
    ppermute x26, waiting for transfers between devices, swap(): lax.ppermute(array, axis, [(i, partner(i)) for i in range(lax.axis_size(a...  42.2 us
    all_to_all x1, starting transfers between devices, per_device(): spread = lax.all_to_all(spread, parties, 0, 0)  9.99 us
    pallas_call x3, Pallas kernels, per_device(): pl.pallas_call(partial(finish_kernel, field), grid=(1,), out_shape=jax.Sh...  8.52 us
    pallas_call x3, Pallas kernels, per_device(): pl.pallas_call(partial(column_kernel, batch), out_shape=shapes, in_specs=...  5.73 us
    unnamed x20, local copies, waits for them, and re-layouts  5.61 us
    all_to_all x1, waiting for transfers between devices, per_device(): spread = lax.all_to_all(spread, parties, 0, 0)  5.39 us
  transfers between devices with their start and end apart: 27, of which 9 were waited for; matrix products, arithmetic and copies ran while one was open for 2% of the time, Pallas kernels for 9%

profile of v5, /device:TPU:1, one launch (start us, length us, event | category | flops | bytes accessed | tf_op | source)
XLA Modules:
  0.0 135.2 jit_solution(8937020620676348969)
XLA Ops:
  6.0 2.1 %collective-permute-start.10 = (f32[60,8,128]{2,1,0:T(8,128)S(1)}, f32[60,8,128]{2,1,0:T(8,128)S(1)}, u32[]{:S(2)}, u32[]{:S(2)}) collective-permute-start(f32[60,8,128]{2,1,0:T(8,128)S(1)} %get-tuple-element.46), channel_id=1, source_target_pairs={{0,2},{2,0},{4,6},{6,4},{1,3},{3,1},{5,7},{7,5},{8,10},{10,8},{12,... | collective-permute-start | bytes 737288 | tf_op jit(solution)/shard_map/ppermute | solution.py:230
  8.3 3.1 %collective-permute-start.4 = (f32[30,8,128]{2,1,0:T(8,128)S(1)}, f32[30,8,128]{2,1,0:T(8,128)S(1)}, u32[]{:S(2)}, u32[]{:S(2)}) collective-permute-start(f32[30,8,128]{2,1,0:T(8,128)S(1)} %get-tuple-element.41), channel_id=1, source_target_pairs={{0,4},{2,6},{4,0},{6,2},{1,5},{3,7},{5,1},{7,3},{8,12},{10,14},{12... | collective-permute-start | bytes 368648 | tf_op jit(solution)/shard_map/ppermute | solution.py:230
  15.3 3.8 %collective-permute-start.12 = (f32[60,8,128]{2,1,0:T(8,128)}, f32[60,8,128]{2,1,0:T(8,128)S(1)}, u32[]{:S(2)}, u32[]{:S(2)}) collective-permute-start(f32[60,8,128]{2,1,0:T(8,128)} %get-tuple-element.48), channel_id=1, source_target_pairs={{0,6},{2,4},{4,2},{6,0},{1,7},{3,5},{5,3},{7,1},{8,14},{10,12},{12... | collective-permute-start | bytes 737288 | tf_op jit(solution)/shard_map/ppermute | solution.py:230
  19.1 2.3 %collective-permute-done.4.refs_2_ = f32[30,8,128]{2,1,0:T(8,128)S(1)} collective-permute-done((f32[30,8,128]{2,1,0:T(8,128)S(1)}, f32[30,8,128]{2,1,0:T(8,128)S(1)}, u32[]{:S(2)}, u32[]{:S(2)}) %collective-permute-start.4) | collective-permute-done | bytes 122912 | tf_op jit(solution)/shard_map/ppermute | solution.py:230
  21.6 3.6 %collective-permute-start.2 = (f32[61,8,128]{2,1,0:T(8,128)S(1)}, f32[61,8,128]{2,1,0:T(8,128)S(1)}, u32[]{:S(2)}, u32[]{:S(2)}) collective-permute-start(f32[61,8,128]{2,1,0:T(8,128)S(1)} %get-tuple-element.37), channel_id=1, source_target_pairs={{0,6},{2,4},{4,2},{6,0},{1,7},{3,5},{5,3},{7,1},{8,14},{10,12},{12... | collective-permute-start | bytes 749576 | tf_op jit(solution)/shard_map/ppermute | solution.py:230
  26.7 7.8 %collective-permute-start.7 = (f32[4,30,8,128]{3,2,1,0:T(8,128)S(1)}, f32[4,30,8,128]{3,2,1,0:T(8,128)S(1)}, u32[]{:S(2)}, u32[]{:S(2)}) collective-permute-start(f32[4,30,8,128]{3,2,1,0:T(8,128)S(1)} %join.4.refs_1_), channel_id=1, source_target_pairs={{0,248},{8,16},{16,8},{24,32},{32,24},{40,48},{48,40},{56,64},{64,... | collective-permute-start | bytes 1474568 | tf_op jit(solution)/shard_map/ppermute | solution.py:230
  34.6 6.2 %collective-permute-start.14 = (f32[4,40,8,128]{3,2,1,0:T(8,128)S(1)}, f32[4,40,8,128]{3,2,1,0:T(8,128)S(1)}, u32[]{:S(2)}, u32[]{:S(2)}) collective-permute-start(f32[4,40,8,128]{3,2,1,0:T(8,128)S(1)} %get-tuple-element.49.refs_1_), channel_id=1, source_target_pairs={{0,248},{8,16},{16,8},{24,32},{32,24},{40,48},{48,40},{56,64},{64,... | collective-permute-start | bytes 1966088 | tf_op jit(solution)/shard_map/ppermute | solution.py:230
  40.8 2.4 %collective-permute-done.2.refs_3_ = f32[61,8,128]{2,1,0:T(8,128)S(1)} collective-permute-done((f32[61,8,128]{2,1,0:T(8,128)S(1)}, f32[61,8,128]{2,1,0:T(8,128)S(1)}, u32[]{:S(2)}, u32[]{:S(2)}) %collective-permute-start.2) | collective-permute-done | bytes 249888 | tf_op jit(solution)/shard_map/ppermute | solution.py:230
  43.2 7.9 %collective-permute-start.9 = (f32[4,61,8,128]{3,2,1,0:T(8,128)S(1)}, f32[4,61,8,128]{3,2,1,0:T(8,128)S(1)}, u32[]{:S(2)}, u32[]{:S(2)}) collective-permute-start(f32[4,61,8,128]{3,2,1,0:T(8,128)S(1)} %get-tuple-element.43.refs_4_), channel_id=1, source_target_pairs={{0,248},{8,16},{16,8},{24,32},{32,24},{40,48},{48,40},{56,64},{64,... | collective-permute-start | bytes 2998280 | tf_op jit(solution)/shard_map/ppermute | solution.py:230
  52.4 5.0 %collective-permute-done.14.refs_2_ = f32[4,40,8,128]{3,2,1,0:T(8,128)S(1)} collective-permute-done((f32[4,40,8,128]{3,2,1,0:T(8,128)S(1)}, f32[4,40,8,128]{3,2,1,0:T(8,128)S(1)}, u32[]{:S(2)}, u32[]{:S(2)}) %collective-permute-start.14) | collective-permute-done | bytes 655392 | tf_op jit(solution)/shard_map/ppermute | solution.py:230
  57.5 4.6 %collective-permute-start.19 = (f32[4,20,8,128]{3,2,1,0:T(8,128)S(1)}, f32[4,20,8,128]{3,2,1,0:T(8,128)S(1)}, u32[]{:S(2)}, u32[]{:S(2)}) collective-permute-start(f32[4,20,8,128]{3,2,1,0:T(8,128)S(1)} %get-tuple-element.54.refs_1_), channel_id=1, source_target_pairs={{0,248},{8,16},{16,8},{24,32},{32,24},{40,48},{48,40},{56,64},{64,... | collective-permute-start | bytes 983048 | tf_op jit(solution)/shard_map/ppermute | solution.py:230
  62.1 1.8 %column.4 = (f32[40,8,128]{2,1,0:T(8,128)S(1)}, f32[40,8,128]{2,1,0:T(8,128)}, f32[40,8,128]{2,1,0:T(8,128)S(1)}, f32[40,8,128]{2,1,0:T(8,128)S(1)}) custom-call(s32[4,10]{1,0:T(4,128)S(1)} %bitcast.30, f32[4,4,10]{2,1,0:T(4,128)S(1)} %pad_maximum_fusion.weight_ref, f32[4,40,8,128]{3,2,1,0:T(8,128)S(1)} %collective-permute-done.13.refs_0_, ...), custom_call_target="tpu_custom_call" | custom-call | tf_op jit(solution)/shard_map/column/pallas_call | solution.py:298
  64.6 22.3 %collective-permute-done.6.refs_0_ = f32[4,30,8,128]{3,2,1,0:T(8,128)S(1)} collective-permute-done((f32[4,30,8,128]{3,2,1,0:T(8,128)S(1)}, f32[4,30,8,128]{3,2,1,0:T(8,128)S(1)}, u32[]{:S(2)}, u32[]{:S(2)}) %collective-permute-start.6) | collective-permute-done | bytes 491552 | tf_op jit(solution)/shard_map/ppermute | solution.py:230
  86.9 2.3 %column.3 = (f32[90,8,128]{2,1,0:T(8,128)S(1)}, f32[90,8,128]{2,1,0:T(8,128)}, f32[90,8,128]{2,1,0:T(8,128)}, f32[90,8,128]{2,1,0:T(8,128)S(1)}, f32[3,4,8,128]{3,2,1,0:T(8,128)S(1)}) custom-call(s32[4,10]{1,0:T(4,128)S(1)} %bitcast.31, f32[4,4,10]{2,1,0:T(4,128)S(1)} %pad_maximum_fusion.weight_ref, f32[4,30,8,128]{3,2,1,0:T(8,128)S(1)} %collective-permute-done.6.refs_0_, ...), custom_call_target="tpu_custom_call" | custom-call | tf_op jit(solution)/shard_map/column/pallas_call | solution.py:298
  90.0 3.7 %collective-permute-start.24 = (f32[90,8,128]{2,1,0:T(8,128)}, f32[90,8,128]{2,1,0:T(8,128)S(1)}, u32[]{:S(2)}, u32[]{:S(2)}) collective-permute-start(f32[90,8,128]{2,1,0:T(8,128)} %get-tuple-element.61), channel_id=1, source_target_pairs={{0,4},{2,6},{4,0},{6,2},{1,5},{3,7},{5,1},{7,3},{8,12},{10,14},{12... | collective-permute-start | bytes 1105928 | tf_op jit(solution)/shard_map/ppermute | solution.py:230
  94.8 10.0 %all-to-all-start = ((f32[64,1,128]{2,1,0:T(1,128)}), f32[64,1,128]{2,1,0:T(1,128)S(1)}, u32[]{:S(2)}, u32[]{:S(2)}) async-start(f32[64,1,128]{2,1,0:T(1,128)} %broadcast_in_dim.115), calls=%async_computation | async-start | bytes 65536 | tf_op jit(solution)/shard_map/all_to_all | solution.py:333
  107.1 1.7 %collective-permute-start.20 = (f32[20,8,128]{2,1,0:T(8,128)}, f32[20,8,128]{2,1,0:T(8,128)S(1)}, u32[]{:S(2)}, u32[]{:S(2)}) collective-permute-start(f32[20,8,128]{2,1,0:T(8,128)} %get-tuple-element.56), channel_id=1, source_target_pairs={{0,2},{2,0},{4,6},{6,4},{1,3},{3,1},{5,7},{7,5},{8,10},{10,8},{12,... | collective-permute-start | bytes 245768 | tf_op jit(solution)/shard_map/ppermute | solution.py:230
  108.8 5.4 %all-to-all-done = f32[64,1,128]{2,1,0:T(1,128)S(1)} async-done(((f32[64,1,128]{2,1,0:T(1,128)}), f32[64,1,128]{2,1,0:T(1,128)S(1)}, u32[]{:S(2)}, u32[]{:S(2)}) %all-to-all-start) | async-done | bytes 32800 | tf_op jit(solution)/shard_map/all_to_all | solution.py:333
  114.2 2.5 %collective-permute-start.21 = (f32[20,8,128]{2,1,0:T(8,128)}, f32[20,8,128]{2,1,0:T(8,128)S(1)}, u32[]{:S(2)}, u32[]{:S(2)}) collective-permute-start(f32[20,8,128]{2,1,0:T(8,128)} %copy-done.9), channel_id=1, source_target_pairs={{0,4},{2,6},{4,0},{6,2},{1,5},{3,7},{5,1},{7,3},{8,12},{10,14},{12... | collective-permute-start | bytes 245768 | tf_op jit(solution)/shard_map/ppermute | solution.py:230
  119.6 2.8 %finish.3.refs_8_ = f32[10,3,8,2560]{3,2,1,0:T(8,128)} custom-call(s32[10]{0:T(128)S(1)} %copy-done.2, f32[4,10]{1,0:T(4,128)S(1)} %pad_maximum_fusion.1.weight_ref, f32[3]{0:T(128)S(1)} %slice_divide_fusion.ratio_ref, f32[90,8,128]{2,1,0:T(8,128)S(1)} %get-tuple-element.59.refs_0_, f32[90,8,128]{2,1,0:T(8,128)S(1)} %collective-permute-done.23.refs_1_, ...), custom_call_target="tpu_custom_call" | custom-call | tf_op jit(solution)/shard_map/finish/pallas_call | solution.py:347
  122.4 2.4 %collective-permute-done.16.refs_6_.refs_2_ = f32[40,8,128]{2,1,0:T(8,128)S(1)} collective-permute-done((f32[40,8,128]{2,1,0:T(8,128)}, f32[40,8,128]{2,1,0:T(8,128)S(1)}, u32[]{:S(2)}, u32[]{:S(2)}) %collective-permute-start.16) | collective-permute-done | bytes 163872 | tf_op jit(solution)/shard_map/ppermute | solution.py:230
  124.8 4.7 %collective-permute-done.17.refs_7_.refs_3_ = f32[40,8,128]{2,1,0:T(8,128)S(1)} collective-permute-done((f32[40,8,128]{2,1,0:T(8,128)S(1)}, f32[40,8,128]{2,1,0:T(8,128)S(1)}, u32[]{:S(2)}, u32[]{:S(2)}) %collective-permute-start.17) | collective-permute-done | bytes 163872 | tf_op jit(solution)/shard_map/ppermute | solution.py:230
  129.5 2.8 %finish.4.refs_8_ = f32[10,3,8,2560]{3,2,1,0:T(8,128)} custom-call(s32[10]{0:T(128)S(1)} %copy-done.2, f32[4,10]{1,0:T(4,128)S(1)} %pad_maximum_fusion.1.weight_ref, f32[3]{0:T(128)S(1)} %slice_divide_fusion.ratio_ref, f32[90,8,128]{2,1,0:T(8,128)S(1)} %get-tuple-element.59.refs_0_, ...), custom_call_target="tpu_custom_call", output_to_operand_aliasing={{}: (11, {})} | custom-call | tf_op jit(solution)/shard_map/finish/pallas_call | solution.py:347
  132.3 2.8 %finish.5 = f32[10,3,8,2560]{3,2,1,0:T(8,128)} custom-call(s32[10]{0:T(128)S(1)} %copy-done.2, f32[4,10]{1,0:T(4,128)S(1)} %pad_maximum_fusion.1.weight_ref, f32[3]{0:T(128)S(1)} %slice_divide_fusion.ratio_ref, f32[40,8,128]{2,1,0:T(8,128)S(1)} %get-tuple-element.50.refs_4_.refs_0_, ...), custom_call_target="tpu_custom_call", output_to_operand_aliasing={{}: (11, {})} | custom-call | tf_op jit(solution)/shard_map/finish/pallas_call | solution.py:347
  (83 shorter events, 20.9 us)
Async XLA Ops:
  6.0 15.6 %collective-permute-start.10 = (f32[60,8,128]{2,1,0:T(8,128)S(1)}, f32[60,8,128]{2,1,0:T(8,128)S(1)}, u32[]{:S(2)}, u32[]{:S(2)}) collective-permute-start(f32[60,8,128]{2,1,0:T(8,128)S(1)} %get-tuple-element.46), channel_id=1, source_target_pairs={{0,2},{2,0},{4,6},{6,4},{1,3},{3,1},{5,7},{7,5},{8,10},{10,8},{12,... | collective-permute-start | bytes 737288 | tf_op jit(solution)/shard_map/ppermute | solution.py:230
  8.3 13.1 %collective-permute-start.4 = (f32[30,8,128]{2,1,0:T(8,128)S(1)}, f32[30,8,128]{2,1,0:T(8,128)S(1)}, u32[]{:S(2)}, u32[]{:S(2)}) collective-permute-start(f32[30,8,128]{2,1,0:T(8,128)S(1)} %get-tuple-element.41), channel_id=1, source_target_pairs={{0,4},{2,6},{4,0},{6,2},{1,5},{3,7},{5,1},{7,3},{8,12},{10,14},{12... | collective-permute-start | bytes 368648 | tf_op jit(solution)/shard_map/ppermute | solution.py:230
  12.2 14.6 %collective-permute-start.11 = (f32[60,8,128]{2,1,0:T(8,128)S(1)}, f32[60,8,128]{2,1,0:T(8,128)S(1)}, u32[]{:S(2)}, u32[]{:S(2)}) collective-permute-start(f32[60,8,128]{2,1,0:T(8,128)S(1)} %get-tuple-element.47), channel_id=1, source_target_pairs={{0,4},{2,6},{4,0},{6,2},{1,5},{3,7},{5,1},{7,3},{8,12},{10,14},{12... | collective-permute-start | bytes 737288 | tf_op jit(solution)/shard_map/ppermute | solution.py:230
  15.3 19.2 %collective-permute-start.12 = (f32[60,8,128]{2,1,0:T(8,128)}, f32[60,8,128]{2,1,0:T(8,128)S(1)}, u32[]{:S(2)}, u32[]{:S(2)}) collective-permute-start(f32[60,8,128]{2,1,0:T(8,128)} %get-tuple-element.48), channel_id=1, source_target_pairs={{0,6},{2,4},{4,2},{6,0},{1,7},{3,5},{5,3},{7,1},{8,14},{10,12},{12... | collective-permute-start | bytes 737288 | tf_op jit(solution)/shard_map/ppermute | solution.py:230
  21.4 19.3 %collective-permute-start = (f32[61,8,128]{2,1,0:T(8,128)}, f32[61,8,128]{2,1,0:T(8,128)S(1)}, u32[]{:S(2)}, u32[]{:S(2)}) collective-permute-start(f32[61,8,128]{2,1,0:T(8,128)} %get-tuple-element.35), channel_id=1, source_target_pairs={{0,2},{2,0},{4,6},{6,4},{1,3},{3,1},{5,7},{7,5},{8,10},{10,8},{12,... | collective-permute-start | bytes 749576 | tf_op jit(solution)/shard_map/ppermute | solution.py:230
  21.4 19.3 %collective-permute-start.1 = (f32[61,8,128]{2,1,0:T(8,128)}, f32[61,8,128]{2,1,0:T(8,128)S(1)}, u32[]{:S(2)}, u32[]{:S(2)}) collective-permute-start(f32[61,8,128]{2,1,0:T(8,128)} %get-tuple-element.36), channel_id=1, source_target_pairs={{0,4},{2,6},{4,0},{6,2},{1,5},{3,7},{5,1},{7,3},{8,12},{10,14},{12... | collective-permute-start | bytes 749576 | tf_op jit(solution)/shard_map/ppermute | solution.py:230
  21.6 21.5 %collective-permute-start.2 = (f32[61,8,128]{2,1,0:T(8,128)S(1)}, f32[61,8,128]{2,1,0:T(8,128)S(1)}, u32[]{:S(2)}, u32[]{:S(2)}) collective-permute-start(f32[61,8,128]{2,1,0:T(8,128)S(1)} %get-tuple-element.37), channel_id=1, source_target_pairs={{0,6},{2,4},{4,2},{6,0},{1,7},{3,5},{5,3},{7,1},{8,14},{10,12},{12... | collective-permute-start | bytes 749576 | tf_op jit(solution)/shard_map/ppermute | solution.py:230
  26.7 37.8 %collective-permute-start.7 = (f32[4,30,8,128]{3,2,1,0:T(8,128)S(1)}, f32[4,30,8,128]{3,2,1,0:T(8,128)S(1)}, u32[]{:S(2)}, u32[]{:S(2)}) collective-permute-start(f32[4,30,8,128]{3,2,1,0:T(8,128)S(1)} %join.4.refs_1_), channel_id=1, source_target_pairs={{0,248},{8,16},{16,8},{24,32},{32,24},{40,48},{48,40},{56,64},{64,... | collective-permute-start | bytes 1474568 | tf_op jit(solution)/shard_map/ppermute | solution.py:230
  34.6 22.9 %collective-permute-start.14 = (f32[4,40,8,128]{3,2,1,0:T(8,128)S(1)}, f32[4,40,8,128]{3,2,1,0:T(8,128)S(1)}, u32[]{:S(2)}, u32[]{:S(2)}) collective-permute-start(f32[4,40,8,128]{3,2,1,0:T(8,128)S(1)} %get-tuple-element.49.refs_1_), channel_id=1, source_target_pairs={{0,248},{8,16},{16,8},{24,32},{32,24},{40,48},{48,40},{56,64},{64,... | collective-permute-start | bytes 1966088 | tf_op jit(solution)/shard_map/ppermute | solution.py:230
  40.8 16.8 %collective-permute-start.13 = (f32[4,40,8,128]{3,2,1,0:T(8,128)S(1)}, f32[4,40,8,128]{3,2,1,0:T(8,128)S(1)}, u32[]{:S(2)}, u32[]{:S(2)}) collective-permute-start(f32[4,40,8,128]{3,2,1,0:T(8,128)S(1)} %get-tuple-element.49.refs_1_), channel_id=1, source_target_pairs={{0,8},{8,0},{16,24},{24,16},{32,40},{40,32},{48,56},{56,48},{64,72... | collective-permute-start | bytes 1966088 | tf_op jit(solution)/shard_map/ppermute | solution.py:230
  43.2 43.7 %collective-permute-start.9 = (f32[4,61,8,128]{3,2,1,0:T(8,128)S(1)}, f32[4,61,8,128]{3,2,1,0:T(8,128)S(1)}, u32[]{:S(2)}, u32[]{:S(2)}) collective-permute-start(f32[4,61,8,128]{3,2,1,0:T(8,128)S(1)} %get-tuple-element.43.refs_4_), channel_id=1, source_target_pairs={{0,248},{8,16},{16,8},{24,32},{32,24},{40,48},{48,40},{56,64},{64,... | collective-permute-start | bytes 2998280 | tf_op jit(solution)/shard_map/ppermute | solution.py:230
  51.1 35.8 %collective-permute-start.8 = (f32[4,61,8,128]{3,2,1,0:T(8,128)S(1)}, f32[4,61,8,128]{3,2,1,0:T(8,128)S(1)}, u32[]{:S(2)}, u32[]{:S(2)}) collective-permute-start(f32[4,61,8,128]{3,2,1,0:T(8,128)S(1)} %get-tuple-element.43.refs_4_), channel_id=1, source_target_pairs={{0,8},{8,0},{16,24},{24,16},{32,40},{40,32},{48,56},{56,48},{64,72... | collective-permute-start | bytes 2998280 | tf_op jit(solution)/shard_map/ppermute | solution.py:230
  57.5 29.4 %collective-permute-start.6 = (f32[4,30,8,128]{3,2,1,0:T(8,128)S(1)}, f32[4,30,8,128]{3,2,1,0:T(8,128)S(1)}, u32[]{:S(2)}, u32[]{:S(2)}) collective-permute-start(f32[4,30,8,128]{3,2,1,0:T(8,128)S(1)} %join.4.refs_1_), channel_id=1, source_target_pairs={{0,8},{8,0},{16,24},{24,16},{32,40},{40,32},{48,56},{56,48},{64,72... | collective-permute-start | bytes 1474568 | tf_op jit(solution)/shard_map/ppermute | solution.py:230
  57.5 36.4 %collective-permute-start.19 = (f32[4,20,8,128]{3,2,1,0:T(8,128)S(1)}, f32[4,20,8,128]{3,2,1,0:T(8,128)S(1)}, u32[]{:S(2)}, u32[]{:S(2)}) collective-permute-start(f32[4,20,8,128]{3,2,1,0:T(8,128)S(1)} %get-tuple-element.54.refs_1_), channel_id=1, source_target_pairs={{0,248},{8,16},{16,8},{24,32},{32,24},{40,48},{48,40},{56,64},{64,... | collective-permute-start | bytes 983048 | tf_op jit(solution)/shard_map/ppermute | solution.py:230
  64.6 40.2 %collective-permute-start.18 = (f32[4,20,8,128]{3,2,1,0:T(8,128)S(1)}, f32[4,20,8,128]{3,2,1,0:T(8,128)S(1)}, u32[]{:S(2)}, u32[]{:S(2)}) collective-permute-start(f32[4,20,8,128]{3,2,1,0:T(8,128)S(1)} %get-tuple-element.54.refs_1_), channel_id=1, source_target_pairs={{0,8},{8,0},{16,24},{24,16},{32,40},{40,32},{48,56},{56,48},{64,72... | collective-permute-start | bytes 983048 | tf_op jit(solution)/shard_map/ppermute | solution.py:230
  89.2 27.5 %collective-permute-start.23 = (f32[90,8,128]{2,1,0:T(8,128)}, f32[90,8,128]{2,1,0:T(8,128)S(1)}, u32[]{:S(2)}, u32[]{:S(2)}) collective-permute-start(f32[90,8,128]{2,1,0:T(8,128)} %get-tuple-element.60), channel_id=1, source_target_pairs={{0,2},{2,0},{4,6},{6,4},{1,3},{3,1},{5,7},{7,5},{8,10},{10,8},{12,... | collective-permute-start | bytes 1105928 | tf_op jit(solution)/shard_map/ppermute | solution.py:230
  90.0 28.4 %collective-permute-start.24 = (f32[90,8,128]{2,1,0:T(8,128)}, f32[90,8,128]{2,1,0:T(8,128)S(1)}, u32[]{:S(2)}, u32[]{:S(2)}) collective-permute-start(f32[90,8,128]{2,1,0:T(8,128)} %get-tuple-element.61), channel_id=1, source_target_pairs={{0,4},{2,6},{4,0},{6,2},{1,5},{3,7},{5,1},{7,3},{8,12},{10,14},{12... | collective-permute-start | bytes 1105928 | tf_op jit(solution)/shard_map/ppermute | solution.py:230
  93.7 24.7 %collective-permute-start.25 = (f32[90,8,128]{2,1,0:T(8,128)S(1)}, f32[90,8,128]{2,1,0:T(8,128)S(1)}, u32[]{:S(2)}, u32[]{:S(2)}) collective-permute-start(f32[90,8,128]{2,1,0:T(8,128)S(1)} %get-tuple-element.62), channel_id=1, source_target_pairs={{0,6},{2,4},{4,2},{6,0},{1,7},{3,5},{5,3},{7,1},{8,14},{10,12},{12... | collective-permute-start | bytes 1105928 | tf_op jit(solution)/shard_map/ppermute | solution.py:230
  94.0 20.3 %collective-permute-start.15 = (f32[40,8,128]{2,1,0:T(8,128)}, f32[40,8,128]{2,1,0:T(8,128)S(1)}, u32[]{:S(2)}, u32[]{:S(2)}) collective-permute-start(f32[40,8,128]{2,1,0:T(8,128)} %get-tuple-element.51), channel_id=1, source_target_pairs={{0,2},{2,0},{4,6},{6,4},{1,3},{3,1},{5,7},{7,5},{8,10},{10,8},{12,... | collective-permute-start | bytes 491528 | tf_op jit(solution)/shard_map/ppermute | solution.py:230
  94.8 19.4 %all-to-all-start = ((f32[64,1,128]{2,1,0:T(1,128)}), f32[64,1,128]{2,1,0:T(1,128)S(1)}, u32[]{:S(2)}, u32[]{:S(2)}) async-start(f32[64,1,128]{2,1,0:T(1,128)} %broadcast_in_dim.115), calls=%async_computation | async-start | bytes 65536 | tf_op jit(solution)/shard_map/all_to_all | solution.py:333
  107.1 25.2 %collective-permute-start.20 = (f32[20,8,128]{2,1,0:T(8,128)}, f32[20,8,128]{2,1,0:T(8,128)S(1)}, u32[]{:S(2)}, u32[]{:S(2)}) collective-permute-start(f32[20,8,128]{2,1,0:T(8,128)} %get-tuple-element.56), channel_id=1, source_target_pairs={{0,2},{2,0},{4,6},{6,4},{1,3},{3,1},{5,7},{7,5},{8,10},{10,8},{12,... | collective-permute-start | bytes 245768 | tf_op jit(solution)/shard_map/ppermute | solution.py:230
  114.2 18.1 %collective-permute-start.21 = (f32[20,8,128]{2,1,0:T(8,128)}, f32[20,8,128]{2,1,0:T(8,128)S(1)}, u32[]{:S(2)}, u32[]{:S(2)}) collective-permute-start(f32[20,8,128]{2,1,0:T(8,128)} %copy-done.9), channel_id=1, source_target_pairs={{0,4},{2,6},{4,0},{6,2},{1,5},{3,7},{5,1},{7,3},{8,12},{10,14},{12... | collective-permute-start | bytes 245768 | tf_op jit(solution)/shard_map/ppermute | solution.py:230
  116.7 15.6 %collective-permute-start.22 = (f32[20,8,128]{2,1,0:T(8,128)S(1)}, f32[20,8,128]{2,1,0:T(8,128)S(1)}, u32[]{:S(2)}, u32[]{:S(2)}) collective-permute-start(f32[20,8,128]{2,1,0:T(8,128)S(1)} %get-tuple-element.58), channel_id=1, source_target_pairs={{0,6},{2,4},{4,2},{6,0},{1,7},{3,5},{5,3},{7,1},{8,14},{10,12},{12... | collective-permute-start | bytes 245768 | tf_op jit(solution)/shard_map/ppermute | solution.py:230
  118.5 11.0 %collective-permute-start.17 = (f32[40,8,128]{2,1,0:T(8,128)S(1)}, f32[40,8,128]{2,1,0:T(8,128)S(1)}, u32[]{:S(2)}, u32[]{:S(2)}) collective-permute-start(f32[40,8,128]{2,1,0:T(8,128)S(1)} %get-tuple-element.53), channel_id=1, source_target_pairs={{0,6},{2,4},{4,2},{6,0},{1,7},{3,5},{5,3},{7,1},{8,14},{10,12},{12... | collective-permute-start | bytes 491528 | tf_op jit(solution)/shard_map/ppermute | solution.py:230
  (13 other events, 97.2 us)

commit v6 on v5

--- a/solution.py
+++ b/solution.py
@@ -22,8 +22,8 @@
 CHUNKS = ((0, 3), (3, 9), (9, 13), (13, 15))
 PARTNERS = (2, 1, 3)
 OWN = ((0,), (1,), (2, 3))
-BACK = ((0, 1), (2,), (3,))
-INFO_CHUNK = 1
+BACK = ((0,), (1,), (2,), (3,))
+INFO_CHUNK = 0
 TOGETHER = 2
 VMEM_LIMIT = 12 * 1024 * 1024
 
@@ -85,28 +85,23 @@
             base += tile_count(chunk)
 
 
-def pack_first(fields_ref, *piece_refs):
-    copy_units(fields_ref, OWN[0], piece_refs)
-
-
-def pack_rest(departure_ref, extents_ref, lat_ref, lon_ref, fields_ref, *piece_refs):
-    band = lax.axis_index(LAT)
-    first_row = band * ROWS
-    group_row = lax.axis_index(LAT[:2]) * GROUP
-    low_bound = first_row - extents_ref[0, 0] * ROWS + 1
-    high_bound = first_row + ROWS - 3 + extents_ref[0, 1] * ROWS
+def pack_first(scalar_ref, fields_ref, *piece_refs):
+    first_row = (lax.axis_index(LAT) * ROWS).astype(jnp.float32)
+    group_row = (lax.axis_index(LAT[:2]) * GROUP).astype(jnp.float32)
     info_sub = lax.broadcasted_iota(jnp.int32, (8, LANES), 0)
     info_lane = lax.broadcasted_iota(jnp.int32, (8, LANES), 1)
-    starts = jnp.zeros((8, LANES), jnp.int32)
+    departure = jnp.zeros((8, LANES), jnp.float32)
     info = jnp.zeros((8, LANES), jnp.float32)
     for row in range(ROWS):
-        departure = jnp.clip(departure_ref[row], low_bound, high_bound)
-        departure = jnp.clip(departure, 1, RING * 32 * ROWS - 3)
         here = info_lane == row
-        starts = jnp.where(here, departure - 1 - (group_row - GROUP), starts)
-        info = jnp.where(here & (info_sub == 1), lat_ref[row], info)
-        info = jnp.where(here & (info_sub == 2), lon_ref[row], info)
-    info = jnp.where(info_sub == 0, starts.astype(jnp.float32), info)
+        departure = jnp.where(here, scalar_ref[row], departure)
+        info = jnp.where(here & (info_sub == 1), scalar_ref[ROWS + row], info)
+        info = jnp.where(here & (info_sub == 2), scalar_ref[2 * ROWS + row], info)
+    low_bound = first_row - scalar_ref[3 * ROWS] * ROWS + 1.0
+    high_bound = first_row + (ROWS - 3.0) + scalar_ref[3 * ROWS + 1] * ROWS
+    departure = jnp.minimum(jnp.maximum(departure, low_bound), high_bound)
+    departure = jnp.minimum(jnp.maximum(departure, 1.0), RING * 32 * ROWS - 3.0)
+    info = jnp.where(info_sub == 0, departure - 1.0 - (group_row - GROUP), info)
     sub = lax.broadcasted_iota(jnp.int32, (ROWS, LANES), 0)
     lane = lax.broadcasted_iota(jnp.int32, (ROWS, LANES), 1)
     for field in range(FIELDS):
@@ -116,12 +111,14 @@
         by_row = jnp.sum(jnp.sum(total, axis=1), axis=1, keepdims=True)
         in_lanes = jnp.sum(jnp.where(sub == lane, by_row, 0.0), axis=0, keepdims=True)
         info = jnp.where(info_sub == 3 + field, in_lanes, info)
+    copy_units(fields_ref, OWN[0], piece_refs)
+    for ref in piece_refs:
+        ref[batch_tiles(OWN[0]) - 1] = info
+
+
+def pack_rest(fields_ref, *piece_refs):
     for number, batch in enumerate(OWN[1:]):
-        refs = piece_refs[number * RING : (number + 1) * RING]
-        copy_units(fields_ref, batch, refs)
-        if INFO_CHUNK in batch:
-            for ref in refs:
-                ref[batch_tiles(batch) - 1] = info
+        copy_units(fields_ref, batch, piece_refs[number * RING : (number + 1) * RING])
 
 
 def join_kernel(batch, *refs):
@@ -250,24 +247,27 @@
 
 def per_device(fields, lat_fraction, lon_fraction, lon_shift, departure_row, extents):
     params = pltpu.CompilerParams(vmem_limit_bytes=VMEM_LIMIT)
+    scalars = jnp.concatenate(
+        [departure_row.astype(jnp.float32), lat_fraction, lon_fraction, extents[0].astype(jnp.float32)]
+    )
     pieces = [
         pl.pallas_call(
             pack_first,
             out_shape=[tiles(batch_tiles(OWN[0]))] * RING,
-            in_specs=[VMEM],
+            in_specs=[SMEM, VMEM],
             out_specs=[VMEM] * RING,
             compiler_params=params,
             name="pack_a",
-        )(fields)
+        )(scalars, fields)
     ]
     rest = pl.pallas_call(
         pack_rest,
         out_shape=[tiles(batch_tiles(batch)) for batch in OWN[1:] for _ in range(RING)],
-        in_specs=[SMEM] * 4 + [VMEM],
+        in_specs=[VMEM],
         out_specs=[VMEM] * (RING * (len(OWN) - 1)),
         compiler_params=params,
         name="pack_b",
-    )(departure_row, extents, lat_fraction, lon_fraction, fields)
+    )(fields)
     pieces += [rest[number * RING : (number + 1) * RING] for number in range(len(OWN) - 1)]
 
     own, inner, outer = {}, {}, {}

time: 135 us -> 150 us (1.11)
  waiting for transfers between devices: 47.6 us -> 69.5 us
  starting transfers between devices: 63.1 us -> 53.6 us
  other arithmetic: 1.83 us -> 5.21 us
  local copies, waits for them, and re-layouts: 6.25 us -> 4.71 us
    ppermute x26 -> x29, waiting for transfers between devices: 42.2 us -> 63.4 us  [swap(): lax.ppermute(array, axis, [(i, partner(i)) for i in range(lax.axis_size(a...]
    ppermute x26 -> x29, starting transfers between devices: 53.1 us -> 42.9 us  [swap(): lax.ppermute(array, axis, [(i, partner(i)) for i in range(lax.axis_size(a...]
    unnamed x20 -> x18, local copies, waits for them, and re-layouts: 5.61 us -> 4.08 us
    pallas_call x3 -> x4, Pallas kernels: 5.73 us -> 6.46 us  [per_device(): pl.pallas_call(partial(column_kernel, batch), out_shape=shapes, in_specs=...]
  transfers between devices with their start and end apart: 27 -> 30, of which waited for: 9 -> 10; matrix products, arithmetic and copies ran while one was open for 2% -> 3% of each run, Pallas kernels for 9% -> 8%
where the time goes in v6:
time: 150 us; the launch traced here: 149 us
  waiting for transfers between devices  69.5 us (46%)
  starting transfers between devices  53.6 us (36%)
  Pallas kernels  16.1 us (11%)
  other arithmetic  5.21 us (3%)
  local copies, waits for them, and re-layouts  4.71 us (3%)
    ppermute x29, waiting for transfers between devices, swap(): lax.ppermute(array, axis, [(i, partner(i)) for i in range(lax.axis_size(a...  63.4 us
    ppermute x29, starting transfers between devices, swap(): lax.ppermute(array, axis, [(i, partner(i)) for i in range(lax.axis_size(a...  42.9 us
    all_to_all x1, starting transfers between devices, per_device(): spread = lax.all_to_all(spread, parties, 0, 0)  10.7 us
    pallas_call x3, Pallas kernels, per_device(): pl.pallas_call(partial(finish_kernel, field), grid=(1,), out_shape=jax.Sh...  8.51 us
    pallas_call x4, Pallas kernels, per_device(): pl.pallas_call(partial(column_kernel, batch), out_shape=shapes, in_specs=...  6.46 us
    all_to_all x1, waiting for transfers between devices, per_device(): spread = lax.all_to_all(spread, parties, 0, 0)  6.15 us
    unnamed x18, local copies, waits for them, and re-layouts  4.08 us
  transfers between devices with their start and end apart: 30, of which 10 were waited for; matrix products, arithmetic and copies ran while one was open for 3% of the time, Pallas kernels for 8%

profile of v6, /device:TPU:1, one launch (start us, length us, event | category | flops | bytes accessed | tf_op | source)
XLA Modules:
  0.0 149.4 jit_solution(5885216203664213637)
XLA Ops:
  4.5 2.2 %collective-permute-start = (f32[31,8,128]{2,1,0:T(8,128)S(1)}, f32[31,8,128]{2,1,0:T(8,128)S(1)}, u32[]{:S(2)}, u32[]{:S(2)}) collective-permute-start(f32[31,8,128]{2,1,0:T(8,128)S(1)} %get-tuple-element.39), channel_id=1, source_target_pairs={{0,2},{2,0},{4,6},{6,4},{1,3},{3,1},{5,7},{7,5},{8,10},{10,8},{12,... | collective-permute-start | bytes 380936 | tf_op jit(solution)/shard_map/ppermute | solution.py:227
  6.7 2.6 %collective-permute-start.1 = (f32[31,8,128]{2,1,0:T(8,128)S(1)}, f32[31,8,128]{2,1,0:T(8,128)S(1)}, u32[]{:S(2)}, u32[]{:S(2)}) collective-permute-start(f32[31,8,128]{2,1,0:T(8,128)S(1)} %get-tuple-element.40), channel_id=1, source_target_pairs={{0,4},{2,6},{4,0},{6,2},{1,5},{3,7},{5,1},{7,3},{8,12},{10,14},{12... | collective-permute-start | bytes 380936 | tf_op jit(solution)/shard_map/ppermute | solution.py:227
  9.7 3.8 %collective-permute-start.6 = (f32[60,8,128]{2,1,0:T(8,128)S(1)}, f32[60,8,128]{2,1,0:T(8,128)S(1)}, u32[]{:S(2)}, u32[]{:S(2)}) collective-permute-start(f32[60,8,128]{2,1,0:T(8,128)S(1)} %get-tuple-element.47), channel_id=1, source_target_pairs={{0,4},{2,6},{4,0},{6,2},{1,5},{3,7},{5,1},{7,3},{8,12},{10,14},{12... | collective-permute-start | bytes 737288 | tf_op jit(solution)/shard_map/ppermute | solution.py:227
  15.4 2.1 %collective-permute-done.2.refs_3_ = f32[31,8,128]{2,1,0:T(8,128)S(1)} collective-permute-done((f32[31,8,128]{2,1,0:T(8,128)S(1)}, f32[31,8,128]{2,1,0:T(8,128)S(1)}, u32[]{:S(2)}, u32[]{:S(2)}) %collective-permute-start.2) | collective-permute-done | bytes 127008 | tf_op jit(solution)/shard_map/ppermute | solution.py:227
  18.3 10.2 %collective-permute-done.18.refs_1_ = f32[60,8,128]{2,1,0:T(8,128)S(1)} collective-permute-done((f32[60,8,128]{2,1,0:T(8,128)S(1)}, f32[60,8,128]{2,1,0:T(8,128)S(1)}, u32[]{:S(2)}, u32[]{:S(2)}) %collective-permute-start.18) | collective-permute-done | bytes 245792 | tf_op jit(solution)/shard_map/ppermute | solution.py:227
  28.5 2.5 %collective-permute-start.7 = (f32[60,8,128]{2,1,0:T(8,128)S(1)}, f32[60,8,128]{2,1,0:T(8,128)S(1)}, u32[]{:S(2)}, u32[]{:S(2)}) collective-permute-start(f32[60,8,128]{2,1,0:T(8,128)S(1)} %get-tuple-element.48), channel_id=1, source_target_pairs={{0,6},{2,4},{4,2},{6,0},{1,7},{3,5},{5,3},{7,1},{8,14},{10,12},{12... | collective-permute-start | bytes 737288 | tf_op jit(solution)/shard_map/ppermute | solution.py:227
  31.0 5.0 %collective-permute-done.19.refs_2_ = f32[60,8,128]{2,1,0:T(8,128)S(1)} collective-permute-done((f32[60,8,128]{2,1,0:T(8,128)S(1)}, f32[60,8,128]{2,1,0:T(8,128)S(1)}, u32[]{:S(2)}, u32[]{:S(2)}) %collective-permute-start.19) | collective-permute-done | bytes 245792 | tf_op jit(solution)/shard_map/ppermute | solution.py:227
  36.1 7.9 %collective-permute-start.22 = (f32[4,60,8,128]{3,2,1,0:T(8,128)S(1)}, f32[4,60,8,128]{3,2,1,0:T(8,128)S(1)}, u32[]{:S(2)}, u32[]{:S(2)}) collective-permute-start(f32[4,60,8,128]{3,2,1,0:T(8,128)S(1)} %join.5.refs_1_), channel_id=1, source_target_pairs={{0,248},{8,16},{16,8},{24,32},{32,24},{40,48},{48,40},{56,64},{64,... | collective-permute-start | bytes 2949128 | tf_op jit(solution)/shard_map/ppermute | solution.py:227
  46.9 4.8 %collective-permute-start.9 = (f32[4,40,8,128]{3,2,1,0:T(8,128)S(1)}, f32[4,40,8,128]{3,2,1,0:T(8,128)S(1)}, u32[]{:S(2)}, u32[]{:S(2)}) collective-permute-start(f32[4,40,8,128]{3,2,1,0:T(8,128)S(1)} %get-tuple-element.49.refs_1_), channel_id=1, source_target_pairs={{0,248},{8,16},{16,8},{24,32},{32,24},{40,48},{48,40},{56,64},{64,... | collective-permute-start | bytes 1966088 | tf_op jit(solution)/shard_map/ppermute | solution.py:227
  51.7 23.7 %collective-permute-done.4.refs_2_ = f32[4,31,8,128]{3,2,1,0:T(8,128)S(1)} collective-permute-done((f32[4,31,8,128]{3,2,1,0:T(8,128)S(1)}, f32[4,31,8,128]{3,2,1,0:T(8,128)S(1)}, u32[]{:S(2)}, u32[]{:S(2)}) %collective-permute-start.4) | collective-permute-done | bytes 507936 | tf_op jit(solution)/shard_map/ppermute | solution.py:227
  75.4 4.6 %collective-permute-start.14 = (f32[4,20,8,128]{3,2,1,0:T(8,128)S(1)}, f32[4,20,8,128]{3,2,1,0:T(8,128)S(1)}, u32[]{:S(2)}, u32[]{:S(2)}) collective-permute-start(f32[4,20,8,128]{3,2,1,0:T(8,128)S(1)} %get-tuple-element.54.refs_1_), channel_id=1, source_target_pairs={{0,248},{8,16},{16,8},{24,32},{32,24},{40,48},{48,40},{56,64},{64,... | collective-permute-start | bytes 983048 | tf_op jit(solution)/shard_map/ppermute | solution.py:227
  82.3 1.9 %column.7 = (f32[60,8,128]{2,1,0:T(8,128)S(1)}, f32[60,8,128]{2,1,0:T(8,128)}, f32[60,8,128]{2,1,0:T(8,128)S(1)}, f32[60,8,128]{2,1,0:T(8,128)S(1)}) custom-call(s32[4,10]{1,0:T(4,128)S(1)} %bitcast.33, f32[4,4,10]{2,1,0:T(4,128)S(1)} %pad_maximum_fusion.weight_ref, f32[4,60,8,128]{3,2,1,0:T(8,128)S(1)} %collective-permute-done.21.refs_0_, ...), custom_call_target="tpu_custom_call" | custom-call | tf_op jit(solution)/shard_map/column/pallas_call | solution.py:298
  84.2 12.2 %collective-permute-done.14.refs_2_ = f32[4,20,8,128]{3,2,1,0:T(8,128)S(1)} collective-permute-done((f32[4,20,8,128]{3,2,1,0:T(8,128)S(1)}, f32[4,20,8,128]{3,2,1,0:T(8,128)S(1)}, u32[]{:S(2)}, u32[]{:S(2)}) %collective-permute-start.14) | collective-permute-done | bytes 327712 | tf_op jit(solution)/shard_map/ppermute | solution.py:227
  96.6 2.0 %collective-permute-done.13.refs_0_ = f32[4,20,8,128]{3,2,1,0:T(8,128)S(1)} collective-permute-done((f32[4,20,8,128]{3,2,1,0:T(8,128)S(1)}, f32[4,20,8,128]{3,2,1,0:T(8,128)S(1)}, u32[]{:S(2)}, u32[]{:S(2)}) %collective-permute-start.13) | collective-permute-done | bytes 327712 | tf_op jit(solution)/shard_map/ppermute | solution.py:227
  99.9 2.5 %collective-permute-start.25 = (f32[60,8,128]{2,1,0:T(8,128)S(1)}, f32[60,8,128]{2,1,0:T(8,128)S(1)}, u32[]{:S(2)}, u32[]{:S(2)}) collective-permute-start(f32[60,8,128]{2,1,0:T(8,128)S(1)} %get-tuple-element.66), channel_id=1, source_target_pairs={{0,6},{2,4},{4,2},{6,0},{1,7},{3,5},{5,3},{7,1},{8,14},{10,12},{12... | collective-permute-start | bytes 737288 | tf_op jit(solution)/shard_map/ppermute | solution.py:227
  105.6 10.7 %all-to-all-start = ((f32[64,1,128]{2,1,0:T(1,128)}), f32[64,1,128]{2,1,0:T(1,128)}, u32[]{:S(2)}, u32[]{:S(2)}) async-start(f32[64,1,128]{2,1,0:T(1,128)} %broadcast_in_dim.115), calls=%async_computation | async-start | bytes 65536 | tf_op jit(solution)/shard_map/all_to_all | solution.py:333
  119.2 6.1 %all-to-all-done = f32[64,1,128]{2,1,0:T(1,128)} async-done(((f32[64,1,128]{2,1,0:T(1,128)}), f32[64,1,128]{2,1,0:T(1,128)}, u32[]{:S(2)}, u32[]{:S(2)}) %all-to-all-start) | async-done | bytes 32800 | tf_op jit(solution)/shard_map/all_to_all | solution.py:333
  126.2 1.8 %collective-permute-start.15 = (f32[20,8,128]{2,1,0:T(8,128)}, f32[20,8,128]{2,1,0:T(8,128)S(1)}, u32[]{:S(2)}, u32[]{:S(2)}) collective-permute-start(f32[20,8,128]{2,1,0:T(8,128)} %copy-done.6), channel_id=1, source_target_pairs={{0,2},{2,0},{4,6},{6,4},{1,3},{3,1},{5,7},{7,5},{8,10},{10,8},{12,... | collective-permute-start | bytes 245768 | tf_op jit(solution)/shard_map/ppermute | solution.py:227
  128.0 2.1 %collective-permute-start.16 = (f32[20,8,128]{2,1,0:T(8,128)}, f32[20,8,128]{2,1,0:T(8,128)S(1)}, u32[]{:S(2)}, u32[]{:S(2)}) collective-permute-start(f32[20,8,128]{2,1,0:T(8,128)} %copy-done.5), channel_id=1, source_target_pairs={{0,4},{2,6},{4,0},{6,2},{1,5},{3,7},{5,1},{7,3},{8,12},{10,14},{12... | collective-permute-start | bytes 245768 | tf_op jit(solution)/shard_map/ppermute | solution.py:227
  130.5 2.2 %collective-permute-start.11 = (f32[40,8,128]{2,1,0:T(8,128)}, f32[40,8,128]{2,1,0:T(8,128)S(1)}, u32[]{:S(2)}, u32[]{:S(2)}) collective-permute-start(f32[40,8,128]{2,1,0:T(8,128)} %copy-done.3), channel_id=1, source_target_pairs={{0,4},{2,6},{4,0},{6,2},{1,5},{3,7},{5,1},{7,3},{8,12},{10,14},{12... | collective-permute-start | bytes 491528 | tf_op jit(solution)/shard_map/ppermute | solution.py:227
  133.4 2.8 %finish.3.refs_8_ = f32[10,3,8,2560]{3,2,1,0:T(8,128)} custom-call(s32[10]{0:T(128)S(1)} %copy-done.2, f32[4,10]{1,0:T(4,128)S(1)} %pad_maximum_fusion.1.weight_ref, f32[3]{0:T(128)S(1)} %slice_divide_fusion.ratio_ref, f32[30,8,128]{2,1,0:T(8,128)S(1)} %get-tuple-element.67.refs_0_, f32[30,8,128]{2,1,0:T(8,128)S(1)} %collective-permute-done.26.refs_1_, ...), custom_call_target="tpu_custom_call" | custom-call | tf_op jit(solution)/shard_map/finish/pallas_call | solution.py:347
  136.9 6.8 %collective-permute-done.12.refs_7_.refs_3_ = f32[40,8,128]{2,1,0:T(8,128)S(1)} collective-permute-done((f32[40,8,128]{2,1,0:T(8,128)S(1)}, f32[40,8,128]{2,1,0:T(8,128)S(1)}, u32[]{:S(2)}, u32[]{:S(2)}) %collective-permute-start.12) | collective-permute-done | bytes 163872 | tf_op jit(solution)/shard_map/ppermute | solution.py:227
  143.7 2.8 %finish.4.refs_8_ = f32[10,3,8,2560]{3,2,1,0:T(8,128)} custom-call(s32[10]{0:T(128)S(1)} %copy-done.2, f32[4,10]{1,0:T(4,128)S(1)} %pad_maximum_fusion.1.weight_ref, f32[3]{0:T(128)S(1)} %slice_divide_fusion.ratio_ref, f32[60,8,128]{2,1,0:T(8,128)S(1)} %get-tuple-element.63.refs_4_.refs_0_, ...), custom_call_target="tpu_custom_call", output_to_operand_aliasing={{}: (11, {})} | custom-call | tf_op jit(solution)/shard_map/finish/pallas_call | solution.py:347
  146.6 2.8 %finish.5 = f32[10,3,8,2560]{3,2,1,0:T(8,128)} custom-call(s32[10]{0:T(128)S(1)} %copy-done.2, f32[4,10]{1,0:T(4,128)S(1)} %pad_maximum_fusion.1.weight_ref, f32[3]{0:T(128)S(1)} %slice_divide_fusion.ratio_ref, f32[40,8,128]{2,1,0:T(8,128)S(1)} %get-tuple-element.50.refs_4_.refs_0_, ...), custom_call_target="tpu_custom_call", output_to_operand_aliasing={{}: (11, {})} | custom-call | tf_op jit(solution)/shard_map/finish/pallas_call | solution.py:347
  (91 shorter events, 22.9 us)
Async XLA Ops:
  9.6 35.6 %collective-permute-start.5 = (f32[60,8,128]{2,1,0:T(8,128)S(1)}, f32[60,8,128]{2,1,0:T(8,128)S(1)}, u32[]{:S(2)}, u32[]{:S(2)}) collective-permute-start(f32[60,8,128]{2,1,0:T(8,128)S(1)} %get-tuple-element.46), channel_id=1, source_target_pairs={{0,2},{2,0},{4,6},{6,4},{1,3},{3,1},{5,7},{7,5},{8,10},{10,8},{12,... | collective-permute-start | bytes 737288 | tf_op jit(solution)/shard_map/ppermute | solution.py:227
  9.7 35.6 %collective-permute-start.6 = (f32[60,8,128]{2,1,0:T(8,128)S(1)}, f32[60,8,128]{2,1,0:T(8,128)S(1)}, u32[]{:S(2)}, u32[]{:S(2)}) collective-permute-start(f32[60,8,128]{2,1,0:T(8,128)S(1)} %get-tuple-element.47), channel_id=1, source_target_pairs={{0,4},{2,6},{4,0},{6,2},{1,5},{3,7},{5,1},{7,3},{8,12},{10,14},{12... | collective-permute-start | bytes 737288 | tf_op jit(solution)/shard_map/ppermute | solution.py:227
  14.2 14.3 %collective-permute-start.18 = (f32[60,8,128]{2,1,0:T(8,128)S(1)}, f32[60,8,128]{2,1,0:T(8,128)S(1)}, u32[]{:S(2)}, u32[]{:S(2)}) collective-permute-start(f32[60,8,128]{2,1,0:T(8,128)S(1)} %get-tuple-element.60), channel_id=1, source_target_pairs={{0,2},{2,0},{4,6},{6,4},{1,3},{3,1},{5,7},{7,5},{8,10},{10,8},{12,... | collective-permute-start | bytes 737288 | tf_op jit(solution)/shard_map/ppermute | solution.py:227
  14.9 21.2 %collective-permute-start.19 = (f32[60,8,128]{2,1,0:T(8,128)S(1)}, f32[60,8,128]{2,1,0:T(8,128)S(1)}, u32[]{:S(2)}, u32[]{:S(2)}) collective-permute-start(f32[60,8,128]{2,1,0:T(8,128)S(1)} %get-tuple-element.61), channel_id=1, source_target_pairs={{0,4},{2,6},{4,0},{6,2},{1,5},{3,7},{5,1},{7,3},{8,12},{10,14},{12... | collective-permute-start | bytes 737288 | tf_op jit(solution)/shard_map/ppermute | solution.py:227
  17.5 18.6 %collective-permute-start.20 = (f32[60,8,128]{2,1,0:T(8,128)S(1)}, f32[60,8,128]{2,1,0:T(8,128)S(1)}, u32[]{:S(2)}, u32[]{:S(2)}) collective-permute-start(f32[60,8,128]{2,1,0:T(8,128)S(1)} %get-tuple-element.62), channel_id=1, source_target_pairs={{0,6},{2,4},{4,2},{6,0},{1,7},{3,5},{5,3},{7,1},{8,14},{10,12},{12... | collective-permute-start | bytes 737288 | tf_op jit(solution)/shard_map/ppermute | solution.py:227
  28.5 18.4 %collective-permute-start.7 = (f32[60,8,128]{2,1,0:T(8,128)S(1)}, f32[60,8,128]{2,1,0:T(8,128)S(1)}, u32[]{:S(2)}, u32[]{:S(2)}) collective-permute-start(f32[60,8,128]{2,1,0:T(8,128)S(1)} %get-tuple-element.48), channel_id=1, source_target_pairs={{0,6},{2,4},{4,2},{6,0},{1,7},{3,5},{5,3},{7,1},{8,14},{10,12},{12... | collective-permute-start | bytes 737288 | tf_op jit(solution)/shard_map/ppermute | solution.py:227
  36.1 45.6 %collective-permute-start.22 = (f32[4,60,8,128]{3,2,1,0:T(8,128)S(1)}, f32[4,60,8,128]{3,2,1,0:T(8,128)S(1)}, u32[]{:S(2)}, u32[]{:S(2)}) collective-permute-start(f32[4,60,8,128]{3,2,1,0:T(8,128)S(1)} %join.5.refs_1_), channel_id=1, source_target_pairs={{0,248},{8,16},{16,8},{24,32},{32,24},{40,48},{48,40},{56,64},{64,... | collective-permute-start | bytes 2949128 | tf_op jit(solution)/shard_map/ppermute | solution.py:227
  44.0 31.4 %collective-permute-start.4 = (f32[4,31,8,128]{3,2,1,0:T(8,128)S(1)}, f32[4,31,8,128]{3,2,1,0:T(8,128)S(1)}, u32[]{:S(2)}, u32[]{:S(2)}) collective-permute-start(f32[4,31,8,128]{3,2,1,0:T(8,128)S(1)} %get-tuple-element.43.refs_1_), channel_id=1, source_target_pairs={{0,248},{8,16},{16,8},{24,32},{32,24},{40,48},{48,40},{56,64},{64,... | collective-permute-start | bytes 1523720 | tf_op jit(solution)/shard_map/ppermute | solution.py:227
  45.2 30.2 %collective-permute-start.3 = (f32[4,31,8,128]{3,2,1,0:T(8,128)S(1)}, f32[4,31,8,128]{3,2,1,0:T(8,128)S(1)}, u32[]{:S(2)}, u32[]{:S(2)}) collective-permute-start(f32[4,31,8,128]{3,2,1,0:T(8,128)S(1)} %get-tuple-element.43.refs_1_), channel_id=1, source_target_pairs={{0,8},{8,0},{16,24},{24,16},{32,40},{40,32},{48,56},{56,48},{64,72... | collective-permute-start | bytes 1523720 | tf_op jit(solution)/shard_map/ppermute | solution.py:227
  45.4 36.6 %collective-permute-start.21 = (f32[4,60,8,128]{3,2,1,0:T(8,128)S(1)}, f32[4,60,8,128]{3,2,1,0:T(8,128)S(1)}, u32[]{:S(2)}, u32[]{:S(2)}) collective-permute-start(f32[4,60,8,128]{3,2,1,0:T(8,128)S(1)} %join.5.refs_1_), channel_id=1, source_target_pairs={{0,8},{8,0},{16,24},{24,16},{32,40},{40,32},{48,56},{56,48},{64,72... | collective-permute-start | bytes 2949128 | tf_op jit(solution)/shard_map/ppermute | solution.py:227
  46.9 51.7 %collective-permute-start.9 = (f32[4,40,8,128]{3,2,1,0:T(8,128)S(1)}, f32[4,40,8,128]{3,2,1,0:T(8,128)S(1)}, u32[]{:S(2)}, u32[]{:S(2)}) collective-permute-start(f32[4,40,8,128]{3,2,1,0:T(8,128)S(1)} %get-tuple-element.49.refs_1_), channel_id=1, source_target_pairs={{0,248},{8,16},{16,8},{24,32},{32,24},{40,48},{48,40},{56,64},{64,... | collective-permute-start | bytes 1966088 | tf_op jit(solution)/shard_map/ppermute | solution.py:227
  75.4 24.5 %collective-permute-start.8 = (f32[4,40,8,128]{3,2,1,0:T(8,128)S(1)}, f32[4,40,8,128]{3,2,1,0:T(8,128)S(1)}, u32[]{:S(2)}, u32[]{:S(2)}) collective-permute-start(f32[4,40,8,128]{3,2,1,0:T(8,128)S(1)} %get-tuple-element.49.refs_1_), channel_id=1, source_target_pairs={{0,8},{8,0},{16,24},{24,16},{32,40},{40,32},{48,56},{56,48},{64,72... | collective-permute-start | bytes 1966088 | tf_op jit(solution)/shard_map/ppermute | solution.py:227
  75.4 21.0 %collective-permute-start.14 = (f32[4,20,8,128]{3,2,1,0:T(8,128)S(1)}, f32[4,20,8,128]{3,2,1,0:T(8,128)S(1)}, u32[]{:S(2)}, u32[]{:S(2)}) collective-permute-start(f32[4,20,8,128]{3,2,1,0:T(8,128)S(1)} %get-tuple-element.54.refs_1_), channel_id=1, source_target_pairs={{0,248},{8,16},{16,8},{24,32},{32,24},{40,48},{48,40},{56,64},{64,... | collective-permute-start | bytes 983048 | tf_op jit(solution)/shard_map/ppermute | solution.py:227
  81.8 16.8 %collective-permute-start.13 = (f32[4,20,8,128]{3,2,1,0:T(8,128)S(1)}, f32[4,20,8,128]{3,2,1,0:T(8,128)S(1)}, u32[]{:S(2)}, u32[]{:S(2)}) collective-permute-start(f32[4,20,8,128]{3,2,1,0:T(8,128)S(1)} %get-tuple-element.54.refs_1_), channel_id=1, source_target_pairs={{0,8},{8,0},{16,24},{24,16},{32,40},{40,32},{48,56},{56,48},{64,72... | collective-permute-start | bytes 983048 | tf_op jit(solution)/shard_map/ppermute | solution.py:227
  82.0 22.2 %collective-permute-start.26 = (f32[30,8,128]{2,1,0:T(8,128)S(1)}, f32[30,8,128]{2,1,0:T(8,128)S(1)}, u32[]{:S(2)}, u32[]{:S(2)}) collective-permute-start(f32[30,8,128]{2,1,0:T(8,128)S(1)} %get-tuple-element.68), channel_id=1, source_target_pairs={{0,2},{2,0},{4,6},{6,4},{1,3},{3,1},{5,7},{7,5},{8,10},{10,8},{12,... | collective-permute-start | bytes 368648 | tf_op jit(solution)/shard_map/ppermute | solution.py:227
  98.6 31.6 %collective-permute-start.23 = (f32[60,8,128]{2,1,0:T(8,128)}, f32[60,8,128]{2,1,0:T(8,128)S(1)}, u32[]{:S(2)}, u32[]{:S(2)}) collective-permute-start(f32[60,8,128]{2,1,0:T(8,128)} %get-tuple-element.64), channel_id=1, source_target_pairs={{0,2},{2,0},{4,6},{6,4},{1,3},{3,1},{5,7},{7,5},{8,10},{10,8},{12,... | collective-permute-start | bytes 737288 | tf_op jit(solution)/shard_map/ppermute | solution.py:227
  98.6 31.9 %collective-permute-start.24 = (f32[60,8,128]{2,1,0:T(8,128)S(1)}, f32[60,8,128]{2,1,0:T(8,128)S(1)}, u32[]{:S(2)}, u32[]{:S(2)}) collective-permute-start(f32[60,8,128]{2,1,0:T(8,128)S(1)} %get-tuple-element.65), channel_id=1, source_target_pairs={{0,4},{2,6},{4,0},{6,2},{1,5},{3,7},{5,1},{7,3},{8,12},{10,14},{12... | collective-permute-start | bytes 737288 | tf_op jit(solution)/shard_map/ppermute | solution.py:227
  99.9 32.8 %collective-permute-start.25 = (f32[60,8,128]{2,1,0:T(8,128)S(1)}, f32[60,8,128]{2,1,0:T(8,128)S(1)}, u32[]{:S(2)}, u32[]{:S(2)}) collective-permute-start(f32[60,8,128]{2,1,0:T(8,128)S(1)} %get-tuple-element.66), channel_id=1, source_target_pairs={{0,6},{2,4},{4,2},{6,0},{1,7},{3,5},{5,3},{7,1},{8,14},{10,12},{12... | collective-permute-start | bytes 737288 | tf_op jit(solution)/shard_map/ppermute | solution.py:227
  104.2 22.0 %collective-permute-start.28 = (f32[30,8,128]{2,1,0:T(8,128)}, f32[30,8,128]{2,1,0:T(8,128)S(1)}, u32[]{:S(2)}, u32[]{:S(2)}) collective-permute-start(f32[30,8,128]{2,1,0:T(8,128)} %get-tuple-element.70), channel_id=1, source_target_pairs={{0,6},{2,4},{4,2},{6,0},{1,7},{3,5},{5,3},{7,1},{8,14},{10,12},{12... | collective-permute-start | bytes 368648 | tf_op jit(solution)/shard_map/ppermute | solution.py:227
  104.9 23.1 %collective-permute-start.10 = (f32[40,8,128]{2,1,0:T(8,128)}, f32[40,8,128]{2,1,0:T(8,128)S(1)}, u32[]{:S(2)}, u32[]{:S(2)}) collective-permute-start(f32[40,8,128]{2,1,0:T(8,128)} %get-tuple-element.51), channel_id=1, source_target_pairs={{0,2},{2,0},{4,6},{6,4},{1,3},{3,1},{5,7},{7,5},{8,10},{10,8},{12,... | collective-permute-start | bytes 491528 | tf_op jit(solution)/shard_map/ppermute | solution.py:227
  105.6 19.8 %all-to-all-start = ((f32[64,1,128]{2,1,0:T(1,128)}), f32[64,1,128]{2,1,0:T(1,128)}, u32[]{:S(2)}, u32[]{:S(2)}) async-start(f32[64,1,128]{2,1,0:T(1,128)} %broadcast_in_dim.115), calls=%async_computation | async-start | bytes 65536 | tf_op jit(solution)/shard_map/all_to_all | solution.py:333
  126.2 20.4 %collective-permute-start.15 = (f32[20,8,128]{2,1,0:T(8,128)}, f32[20,8,128]{2,1,0:T(8,128)S(1)}, u32[]{:S(2)}, u32[]{:S(2)}) collective-permute-start(f32[20,8,128]{2,1,0:T(8,128)} %copy-done.6), channel_id=1, source_target_pairs={{0,2},{2,0},{4,6},{6,4},{1,3},{3,1},{5,7},{7,5},{8,10},{10,8},{12,... | collective-permute-start | bytes 245768 | tf_op jit(solution)/shard_map/ppermute | solution.py:227
  128.0 18.6 %collective-permute-start.16 = (f32[20,8,128]{2,1,0:T(8,128)}, f32[20,8,128]{2,1,0:T(8,128)S(1)}, u32[]{:S(2)}, u32[]{:S(2)}) collective-permute-start(f32[20,8,128]{2,1,0:T(8,128)} %copy-done.5), channel_id=1, source_target_pairs={{0,4},{2,6},{4,0},{6,2},{1,5},{3,7},{5,1},{7,3},{8,12},{10,14},{12... | collective-permute-start | bytes 245768 | tf_op jit(solution)/shard_map/ppermute | solution.py:227
  130.1 16.4 %collective-permute-start.17 = (f32[20,8,128]{2,1,0:T(8,128)}, f32[20,8,128]{2,1,0:T(8,128)S(1)}, u32[]{:S(2)}, u32[]{:S(2)}) collective-permute-start(f32[20,8,128]{2,1,0:T(8,128)} %copy-done.4), channel_id=1, source_target_pairs={{0,6},{2,4},{4,2},{6,0},{1,7},{3,5},{5,3},{7,1},{8,14},{10,12},{12... | collective-permute-start | bytes 245768 | tf_op jit(solution)/shard_map/ppermute | solution.py:227
  (15 other events, 156.8 us)

commit v7 on v6

--- a/solution.py
+++ b/solution.py
@@ -24,7 +24,7 @@
 OWN = ((0,), (1,), (2, 3))
 BACK = ((0,), (1,), (2,), (3,))
 INFO_CHUNK = 0
-TOGETHER = 2
+TOGETHER = 5
 VMEM_LIMIT = 12 * 1024 * 1024
 
 
@@ -85,7 +85,7 @@
             base += tile_count(chunk)
 
 
-def pack_first(scalar_ref, fields_ref, *piece_refs):
+def pack_first(extents_ref, scalar_ref, fields_ref, *piece_refs):
     first_row = (lax.axis_index(LAT) * ROWS).astype(jnp.float32)
     group_row = (lax.axis_index(LAT[:2]) * GROUP).astype(jnp.float32)
     info_sub = lax.broadcasted_iota(jnp.int32, (8, LANES), 0)
@@ -97,8 +97,8 @@
         departure = jnp.where(here, scalar_ref[row], departure)
         info = jnp.where(here & (info_sub == 1), scalar_ref[ROWS + row], info)
         info = jnp.where(here & (info_sub == 2), scalar_ref[2 * ROWS + row], info)
-    low_bound = first_row - scalar_ref[3 * ROWS] * ROWS + 1.0
-    high_bound = first_row + (ROWS - 3.0) + scalar_ref[3 * ROWS + 1] * ROWS
+    low_bound = first_row - (extents_ref[0, 0] * ROWS).astype(jnp.float32) + 1.0
+    high_bound = first_row + (extents_ref[0, 1] * ROWS).astype(jnp.float32) + (ROWS - 3.0)
     departure = jnp.minimum(jnp.maximum(departure, low_bound), high_bound)
     departure = jnp.minimum(jnp.maximum(departure, 1.0), RING * 32 * ROWS - 3.0)
     info = jnp.where(info_sub == 0, departure - 1.0 - (group_row - GROUP), info)
@@ -247,18 +247,16 @@
 
 def per_device(fields, lat_fraction, lon_fraction, lon_shift, departure_row, extents):
     params = pltpu.CompilerParams(vmem_limit_bytes=VMEM_LIMIT)
-    scalars = jnp.concatenate(
-        [departure_row.astype(jnp.float32), lat_fraction, lon_fraction, extents[0].astype(jnp.float32)]
-    )
+    scalars = jnp.concatenate([departure_row.astype(jnp.float32), lat_fraction, lon_fraction])
     pieces = [
         pl.pallas_call(
             pack_first,
             out_shape=[tiles(batch_tiles(OWN[0]))] * RING,
-            in_specs=[SMEM, VMEM],
+            in_specs=[SMEM, SMEM, VMEM],
             out_specs=[VMEM] * RING,
             compiler_params=params,
             name="pack_a",
-        )(scalars, fields)
+        )(extents, scalars, fields)
     ]
     rest = pl.pallas_call(
         pack_rest,

time: 150 us -> 149 us (level)
    unnamed x18 -> x20, local copies, waits for them, and re-layouts: 4.08 us -> 4.72 us
where the time goes in v7:
time: 149 us
  waiting for transfers between devices  69.7 us (47%)
  starting transfers between devices  53.6 us (36%)
  Pallas kernels  15.6 us (10%)
  local copies, waits for them, and re-layouts  5.36 us (4%)
  other arithmetic  4.55 us (3%)
    ppermute x29, waiting for transfers between devices, swap(): lax.ppermute(array, axis, [(i, partner(i)) for i in range(lax.axis_size(a...  63.6 us
    ppermute x29, starting transfers between devices, swap(): lax.ppermute(array, axis, [(i, partner(i)) for i in range(lax.axis_size(a...  42.9 us
    all_to_all x1, starting transfers between devices, per_device(): spread = lax.all_to_all(spread, parties, 0, 0)  10.7 us
    pallas_call x3, Pallas kernels, per_device(): pl.pallas_call(partial(finish_kernel, field), grid=(1,), out_shape=jax.Sh...  7.95 us
    pallas_call x4, Pallas kernels, per_device(): pl.pallas_call(partial(column_kernel, batch), out_shape=shapes, in_specs=...  6.45 us
    all_to_all x1, waiting for transfers between devices, per_device(): spread = lax.all_to_all(spread, parties, 0, 0)  6.15 us
    unnamed x20, local copies, waits for them, and re-layouts  4.72 us
  transfers between devices with their start and end apart: 30, of which 10 were waited for; matrix products, arithmetic and copies ran while one was open for 3% of the time, Pallas kernels for 8%

profile of v7, /device:TPU:1, one launch (start us, length us, event | category | flops | bytes accessed | tf_op | source)
XLA Modules:
  0.0 149.0 jit_solution(5855923391576362263)
XLA Ops:
  4.5 2.2 %collective-permute-start = (f32[31,8,128]{2,1,0:T(8,128)S(1)}, f32[31,8,128]{2,1,0:T(8,128)S(1)}, u32[]{:S(2)}, u32[]{:S(2)}) collective-permute-start(f32[31,8,128]{2,1,0:T(8,128)S(1)} %get-tuple-element.39), channel_id=1, source_target_pairs={{0,2},{2,0},{4,6},{6,4},{1,3},{3,1},{5,7},{7,5},{8,10},{10,8},{12,... | collective-permute-start | bytes 380936 | tf_op jit(solution)/shard_map/ppermute | solution.py:227
  6.7 2.6 %collective-permute-start.1 = (f32[31,8,128]{2,1,0:T(8,128)S(1)}, f32[31,8,128]{2,1,0:T(8,128)S(1)}, u32[]{:S(2)}, u32[]{:S(2)}) collective-permute-start(f32[31,8,128]{2,1,0:T(8,128)S(1)} %get-tuple-element.40), channel_id=1, source_target_pairs={{0,4},{2,6},{4,0},{6,2},{1,5},{3,7},{5,1},{7,3},{8,12},{10,14},{12... | collective-permute-start | bytes 380936 | tf_op jit(solution)/shard_map/ppermute | solution.py:227
  9.7 3.8 %collective-permute-start.6 = (f32[60,8,128]{2,1,0:T(8,128)S(1)}, f32[60,8,128]{2,1,0:T(8,128)S(1)}, u32[]{:S(2)}, u32[]{:S(2)}) collective-permute-start(f32[60,8,128]{2,1,0:T(8,128)S(1)} %get-tuple-element.47), channel_id=1, source_target_pairs={{0,4},{2,6},{4,0},{6,2},{1,5},{3,7},{5,1},{7,3},{8,12},{10,14},{12... | collective-permute-start | bytes 737288 | tf_op jit(solution)/shard_map/ppermute | solution.py:227
  15.4 2.1 %collective-permute-done.2.refs_3_ = f32[31,8,128]{2,1,0:T(8,128)S(1)} collective-permute-done((f32[31,8,128]{2,1,0:T(8,128)S(1)}, f32[31,8,128]{2,1,0:T(8,128)S(1)}, u32[]{:S(2)}, u32[]{:S(2)}) %collective-permute-start.2) | collective-permute-done | bytes 127008 | tf_op jit(solution)/shard_map/ppermute | solution.py:227
  18.3 10.2 %collective-permute-done.18.refs_1_ = f32[60,8,128]{2,1,0:T(8,128)S(1)} collective-permute-done((f32[60,8,128]{2,1,0:T(8,128)S(1)}, f32[60,8,128]{2,1,0:T(8,128)S(1)}, u32[]{:S(2)}, u32[]{:S(2)}) %collective-permute-start.18) | collective-permute-done | bytes 245792 | tf_op jit(solution)/shard_map/ppermute | solution.py:227
  28.5 2.5 %collective-permute-start.7 = (f32[60,8,128]{2,1,0:T(8,128)S(1)}, f32[60,8,128]{2,1,0:T(8,128)S(1)}, u32[]{:S(2)}, u32[]{:S(2)}) collective-permute-start(f32[60,8,128]{2,1,0:T(8,128)S(1)} %get-tuple-element.48), channel_id=1, source_target_pairs={{0,6},{2,4},{4,2},{6,0},{1,7},{3,5},{5,3},{7,1},{8,14},{10,12},{12... | collective-permute-start | bytes 737288 | tf_op jit(solution)/shard_map/ppermute | solution.py:227
  31.0 5.0 %collective-permute-done.19.refs_2_ = f32[60,8,128]{2,1,0:T(8,128)S(1)} collective-permute-done((f32[60,8,128]{2,1,0:T(8,128)S(1)}, f32[60,8,128]{2,1,0:T(8,128)S(1)}, u32[]{:S(2)}, u32[]{:S(2)}) %collective-permute-start.19) | collective-permute-done | bytes 245792 | tf_op jit(solution)/shard_map/ppermute | solution.py:227
  36.1 7.9 %collective-permute-start.22 = (f32[4,60,8,128]{3,2,1,0:T(8,128)S(1)}, f32[4,60,8,128]{3,2,1,0:T(8,128)S(1)}, u32[]{:S(2)}, u32[]{:S(2)}) collective-permute-start(f32[4,60,8,128]{3,2,1,0:T(8,128)S(1)} %join.5.refs_1_), channel_id=1, source_target_pairs={{0,248},{8,16},{16,8},{24,32},{32,24},{40,48},{48,40},{56,64},{64,... | collective-permute-start | bytes 2949128 | tf_op jit(solution)/shard_map/ppermute | solution.py:227
  46.9 4.8 %collective-permute-start.9 = (f32[4,40,8,128]{3,2,1,0:T(8,128)S(1)}, f32[4,40,8,128]{3,2,1,0:T(8,128)S(1)}, u32[]{:S(2)}, u32[]{:S(2)}) collective-permute-start(f32[4,40,8,128]{3,2,1,0:T(8,128)S(1)} %get-tuple-element.49.refs_1_), channel_id=1, source_target_pairs={{0,248},{8,16},{16,8},{24,32},{32,24},{40,48},{48,40},{56,64},{64,... | collective-permute-start | bytes 1966088 | tf_op jit(solution)/shard_map/ppermute | solution.py:227
  51.7 23.7 %collective-permute-done.4.refs_2_ = f32[4,31,8,128]{3,2,1,0:T(8,128)S(1)} collective-permute-done((f32[4,31,8,128]{3,2,1,0:T(8,128)S(1)}, f32[4,31,8,128]{3,2,1,0:T(8,128)S(1)}, u32[]{:S(2)}, u32[]{:S(2)}) %collective-permute-start.4) | collective-permute-done | bytes 507936 | tf_op jit(solution)/shard_map/ppermute | solution.py:227
  75.4 4.6 %collective-permute-start.14 = (f32[4,20,8,128]{3,2,1,0:T(8,128)S(1)}, f32[4,20,8,128]{3,2,1,0:T(8,128)S(1)}, u32[]{:S(2)}, u32[]{:S(2)}) collective-permute-start(f32[4,20,8,128]{3,2,1,0:T(8,128)S(1)} %get-tuple-element.54.refs_1_), channel_id=1, source_target_pairs={{0,248},{8,16},{16,8},{24,32},{32,24},{40,48},{48,40},{56,64},{64,... | collective-permute-start | bytes 983048 | tf_op jit(solution)/shard_map/ppermute | solution.py:227
  82.3 1.9 %column.7 = (f32[60,8,128]{2,1,0:T(8,128)S(1)}, f32[60,8,128]{2,1,0:T(8,128)}, f32[60,8,128]{2,1,0:T(8,128)S(1)}, f32[60,8,128]{2,1,0:T(8,128)S(1)}) custom-call(s32[4,10]{1,0:T(4,128)S(1)} %bitcast.31, f32[4,4,10]{2,1,0:T(4,128)S(1)} %pad_maximum_fusion.weight_ref, f32[4,60,8,128]{3,2,1,0:T(8,128)S(1)} %collective-permute-done.21.refs_0_, ...), custom_call_target="tpu_custom_call" | custom-call | tf_op jit(solution)/shard_map/column/pallas_call | solution.py:296
  84.2 12.2 %collective-permute-done.14.refs_2_ = f32[4,20,8,128]{3,2,1,0:T(8,128)S(1)} collective-permute-done((f32[4,20,8,128]{3,2,1,0:T(8,128)S(1)}, f32[4,20,8,128]{3,2,1,0:T(8,128)S(1)}, u32[]{:S(2)}, u32[]{:S(2)}) %collective-permute-start.14) | collective-permute-done | bytes 327712 | tf_op jit(solution)/shard_map/ppermute | solution.py:227
  96.6 2.0 %collective-permute-done.13.refs_0_ = f32[4,20,8,128]{3,2,1,0:T(8,128)S(1)} collective-permute-done((f32[4,20,8,128]{3,2,1,0:T(8,128)S(1)}, f32[4,20,8,128]{3,2,1,0:T(8,128)S(1)}, u32[]{:S(2)}, u32[]{:S(2)}) %collective-permute-start.13) | collective-permute-done | bytes 327712 | tf_op jit(solution)/shard_map/ppermute | solution.py:227
  99.9 2.5 %collective-permute-start.25 = (f32[60,8,128]{2,1,0:T(8,128)S(1)}, f32[60,8,128]{2,1,0:T(8,128)S(1)}, u32[]{:S(2)}, u32[]{:S(2)}) collective-permute-start(f32[60,8,128]{2,1,0:T(8,128)S(1)} %get-tuple-element.66), channel_id=1, source_target_pairs={{0,6},{2,4},{4,2},{6,0},{1,7},{3,5},{5,3},{7,1},{8,14},{10,12},{12... | collective-permute-start | bytes 737288 | tf_op jit(solution)/shard_map/ppermute | solution.py:227
  105.6 10.7 %all-to-all-start = ((f32[64,1,128]{2,1,0:T(1,128)}), f32[64,1,128]{2,1,0:T(1,128)}, u32[]{:S(2)}, u32[]{:S(2)}) async-start(f32[64,1,128]{2,1,0:T(1,128)} %broadcast_in_dim.115), calls=%async_computation | async-start | bytes 65536 | tf_op jit(solution)/shard_map/all_to_all | solution.py:331
  119.2 6.1 %all-to-all-done = f32[64,1,128]{2,1,0:T(1,128)} async-done(((f32[64,1,128]{2,1,0:T(1,128)}), f32[64,1,128]{2,1,0:T(1,128)}, u32[]{:S(2)}, u32[]{:S(2)}) %all-to-all-start) | async-done | bytes 32800 | tf_op jit(solution)/shard_map/all_to_all | solution.py:331
  126.2 1.8 %collective-permute-start.15 = (f32[20,8,128]{2,1,0:T(8,128)}, f32[20,8,128]{2,1,0:T(8,128)S(1)}, u32[]{:S(2)}, u32[]{:S(2)}) collective-permute-start(f32[20,8,128]{2,1,0:T(8,128)} %copy-done.7), channel_id=1, source_target_pairs={{0,2},{2,0},{4,6},{6,4},{1,3},{3,1},{5,7},{7,5},{8,10},{10,8},{12,... | collective-permute-start | bytes 245768 | tf_op jit(solution)/shard_map/ppermute | solution.py:227
  128.0 2.1 %collective-permute-start.16 = (f32[20,8,128]{2,1,0:T(8,128)}, f32[20,8,128]{2,1,0:T(8,128)S(1)}, u32[]{:S(2)}, u32[]{:S(2)}) collective-permute-start(f32[20,8,128]{2,1,0:T(8,128)} %copy-done.6), channel_id=1, source_target_pairs={{0,4},{2,6},{4,0},{6,2},{1,5},{3,7},{5,1},{7,3},{8,12},{10,14},{12... | collective-permute-start | bytes 245768 | tf_op jit(solution)/shard_map/ppermute | solution.py:227
  130.5 2.2 %collective-permute-start.11 = (f32[40,8,128]{2,1,0:T(8,128)}, f32[40,8,128]{2,1,0:T(8,128)S(1)}, u32[]{:S(2)}, u32[]{:S(2)}) collective-permute-start(f32[40,8,128]{2,1,0:T(8,128)} %copy-done.4), channel_id=1, source_target_pairs={{0,4},{2,6},{4,0},{6,2},{1,5},{3,7},{5,1},{7,3},{8,12},{10,14},{12... | collective-permute-start | bytes 491528 | tf_op jit(solution)/shard_map/ppermute | solution.py:227
  133.5 2.7 %finish.3.refs_8_ = f32[10,3,8,2560]{3,2,1,0:T(8,128)} custom-call(s32[10]{0:T(128)S(1)} %copy-done.2, f32[4,10]{1,0:T(4,128)S(1)} %pad_maximum_fusion.1.weight_ref, f32[3]{0:T(128)S(1)} %slice_divide_fusion.ratio_ref, f32[30,8,128]{2,1,0:T(8,128)S(1)} %get-tuple-element.67.refs_0_, f32[30,8,128]{2,1,0:T(8,128)S(1)} %collective-permute-done.26.refs_1_, ...), custom_call_target="tpu_custom_call" | custom-call | tf_op jit(solution)/shard_map/finish/pallas_call | solution.py:345
  136.9 6.8 %collective-permute-done.12.refs_7_.refs_3_ = f32[40,8,128]{2,1,0:T(8,128)S(1)} collective-permute-done((f32[40,8,128]{2,1,0:T(8,128)S(1)}, f32[40,8,128]{2,1,0:T(8,128)S(1)}, u32[]{:S(2)}, u32[]{:S(2)}) %collective-permute-start.12) | collective-permute-done | bytes 163872 | tf_op jit(solution)/shard_map/ppermute | solution.py:227
  143.7 2.6 %finish.4.refs_8_ = f32[10,3,8,2560]{3,2,1,0:T(8,128)} custom-call(s32[10]{0:T(128)S(1)} %copy-done.2, f32[4,10]{1,0:T(4,128)S(1)} %pad_maximum_fusion.1.weight_ref, f32[3]{0:T(128)S(1)} %slice_divide_fusion.ratio_ref, f32[60,8,128]{2,1,0:T(8,128)S(1)} %get-tuple-element.63.refs_4_.refs_0_, ...), custom_call_target="tpu_custom_call", output_to_operand_aliasing={{}: (11, {})} | custom-call | tf_op jit(solution)/shard_map/finish/pallas_call | solution.py:345
  146.4 2.7 %finish.5 = f32[10,3,8,2560]{3,2,1,0:T(8,128)} custom-call(s32[10]{0:T(128)S(1)} %copy-done.2, f32[4,10]{1,0:T(4,128)S(1)} %pad_maximum_fusion.1.weight_ref, f32[3]{0:T(128)S(1)} %slice_divide_fusion.ratio_ref, f32[40,8,128]{2,1,0:T(8,128)S(1)} %get-tuple-element.50.refs_4_.refs_0_, ...), custom_call_target="tpu_custom_call", output_to_operand_aliasing={{}: (11, {})} | custom-call | tf_op jit(solution)/shard_map/finish/pallas_call | solution.py:345
  (92 shorter events, 23.0 us)
Async XLA Ops:
  9.6 35.6 %collective-permute-start.5 = (f32[60,8,128]{2,1,0:T(8,128)S(1)}, f32[60,8,128]{2,1,0:T(8,128)S(1)}, u32[]{:S(2)}, u32[]{:S(2)}) collective-permute-start(f32[60,8,128]{2,1,0:T(8,128)S(1)} %get-tuple-element.46), channel_id=1, source_target_pairs={{0,2},{2,0},{4,6},{6,4},{1,3},{3,1},{5,7},{7,5},{8,10},{10,8},{12,... | collective-permute-start | bytes 737288 | tf_op jit(solution)/shard_map/ppermute | solution.py:227
  9.7 35.6 %collective-permute-start.6 = (f32[60,8,128]{2,1,0:T(8,128)S(1)}, f32[60,8,128]{2,1,0:T(8,128)S(1)}, u32[]{:S(2)}, u32[]{:S(2)}) collective-permute-start(f32[60,8,128]{2,1,0:T(8,128)S(1)} %get-tuple-element.47), channel_id=1, source_target_pairs={{0,4},{2,6},{4,0},{6,2},{1,5},{3,7},{5,1},{7,3},{8,12},{10,14},{12... | collective-permute-start | bytes 737288 | tf_op jit(solution)/shard_map/ppermute | solution.py:227
  14.2 14.3 %collective-permute-start.18 = (f32[60,8,128]{2,1,0:T(8,128)S(1)}, f32[60,8,128]{2,1,0:T(8,128)S(1)}, u32[]{:S(2)}, u32[]{:S(2)}) collective-permute-start(f32[60,8,128]{2,1,0:T(8,128)S(1)} %get-tuple-element.60), channel_id=1, source_target_pairs={{0,2},{2,0},{4,6},{6,4},{1,3},{3,1},{5,7},{7,5},{8,10},{10,8},{12,... | collective-permute-start | bytes 737288 | tf_op jit(solution)/shard_map/ppermute | solution.py:227
  14.9 21.2 %collective-permute-start.19 = (f32[60,8,128]{2,1,0:T(8,128)S(1)}, f32[60,8,128]{2,1,0:T(8,128)S(1)}, u32[]{:S(2)}, u32[]{:S(2)}) collective-permute-start(f32[60,8,128]{2,1,0:T(8,128)S(1)} %get-tuple-element.61), channel_id=1, source_target_pairs={{0,4},{2,6},{4,0},{6,2},{1,5},{3,7},{5,1},{7,3},{8,12},{10,14},{12... | collective-permute-start | bytes 737288 | tf_op jit(solution)/shard_map/ppermute | solution.py:227
  17.5 18.6 %collective-permute-start.20 = (f32[60,8,128]{2,1,0:T(8,128)S(1)}, f32[60,8,128]{2,1,0:T(8,128)S(1)}, u32[]{:S(2)}, u32[]{:S(2)}) collective-permute-start(f32[60,8,128]{2,1,0:T(8,128)S(1)} %get-tuple-element.62), channel_id=1, source_target_pairs={{0,6},{2,4},{4,2},{6,0},{1,7},{3,5},{5,3},{7,1},{8,14},{10,12},{12... | collective-permute-start | bytes 737288 | tf_op jit(solution)/shard_map/ppermute | solution.py:227
  28.5 18.4 %collective-permute-start.7 = (f32[60,8,128]{2,1,0:T(8,128)S(1)}, f32[60,8,128]{2,1,0:T(8,128)S(1)}, u32[]{:S(2)}, u32[]{:S(2)}) collective-permute-start(f32[60,8,128]{2,1,0:T(8,128)S(1)} %get-tuple-element.48), channel_id=1, source_target_pairs={{0,6},{2,4},{4,2},{6,0},{1,7},{3,5},{5,3},{7,1},{8,14},{10,12},{12... | collective-permute-start | bytes 737288 | tf_op jit(solution)/shard_map/ppermute | solution.py:227
  36.1 45.6 %collective-permute-start.22 = (f32[4,60,8,128]{3,2,1,0:T(8,128)S(1)}, f32[4,60,8,128]{3,2,1,0:T(8,128)S(1)}, u32[]{:S(2)}, u32[]{:S(2)}) collective-permute-start(f32[4,60,8,128]{3,2,1,0:T(8,128)S(1)} %join.5.refs_1_), channel_id=1, source_target_pairs={{0,248},{8,16},{16,8},{24,32},{32,24},{40,48},{48,40},{56,64},{64,... | collective-permute-start | bytes 2949128 | tf_op jit(solution)/shard_map/ppermute | solution.py:227
  44.0 31.4 %collective-permute-start.4 = (f32[4,31,8,128]{3,2,1,0:T(8,128)S(1)}, f32[4,31,8,128]{3,2,1,0:T(8,128)S(1)}, u32[]{:S(2)}, u32[]{:S(2)}) collective-permute-start(f32[4,31,8,128]{3,2,1,0:T(8,128)S(1)} %get-tuple-element.43.refs_1_), channel_id=1, source_target_pairs={{0,248},{8,16},{16,8},{24,32},{32,24},{40,48},{48,40},{56,64},{64,... | collective-permute-start | bytes 1523720 | tf_op jit(solution)/shard_map/ppermute | solution.py:227
  45.2 30.2 %collective-permute-start.3 = (f32[4,31,8,128]{3,2,1,0:T(8,128)S(1)}, f32[4,31,8,128]{3,2,1,0:T(8,128)S(1)}, u32[]{:S(2)}, u32[]{:S(2)}) collective-permute-start(f32[4,31,8,128]{3,2,1,0:T(8,128)S(1)} %get-tuple-element.43.refs_1_), channel_id=1, source_target_pairs={{0,8},{8,0},{16,24},{24,16},{32,40},{40,32},{48,56},{56,48},{64,72... | collective-permute-start | bytes 1523720 | tf_op jit(solution)/shard_map/ppermute | solution.py:227
  45.4 36.6 %collective-permute-start.21 = (f32[4,60,8,128]{3,2,1,0:T(8,128)S(1)}, f32[4,60,8,128]{3,2,1,0:T(8,128)S(1)}, u32[]{:S(2)}, u32[]{:S(2)}) collective-permute-start(f32[4,60,8,128]{3,2,1,0:T(8,128)S(1)} %join.5.refs_1_), channel_id=1, source_target_pairs={{0,8},{8,0},{16,24},{24,16},{32,40},{40,32},{48,56},{56,48},{64,72... | collective-permute-start | bytes 2949128 | tf_op jit(solution)/shard_map/ppermute | solution.py:227
  46.9 51.7 %collective-permute-start.9 = (f32[4,40,8,128]{3,2,1,0:T(8,128)S(1)}, f32[4,40,8,128]{3,2,1,0:T(8,128)S(1)}, u32[]{:S(2)}, u32[]{:S(2)}) collective-permute-start(f32[4,40,8,128]{3,2,1,0:T(8,128)S(1)} %get-tuple-element.49.refs_1_), channel_id=1, source_target_pairs={{0,248},{8,16},{16,8},{24,32},{32,24},{40,48},{48,40},{56,64},{64,... | collective-permute-start | bytes 1966088 | tf_op jit(solution)/shard_map/ppermute | solution.py:227
  75.4 24.5 %collective-permute-start.8 = (f32[4,40,8,128]{3,2,1,0:T(8,128)S(1)}, f32[4,40,8,128]{3,2,1,0:T(8,128)S(1)}, u32[]{:S(2)}, u32[]{:S(2)}) collective-permute-start(f32[4,40,8,128]{3,2,1,0:T(8,128)S(1)} %get-tuple-element.49.refs_1_), channel_id=1, source_target_pairs={{0,8},{8,0},{16,24},{24,16},{32,40},{40,32},{48,56},{56,48},{64,72... | collective-permute-start | bytes 1966088 | tf_op jit(solution)/shard_map/ppermute | solution.py:227
  75.4 21.0 %collective-permute-start.14 = (f32[4,20,8,128]{3,2,1,0:T(8,128)S(1)}, f32[4,20,8,128]{3,2,1,0:T(8,128)S(1)}, u32[]{:S(2)}, u32[]{:S(2)}) collective-permute-start(f32[4,20,8,128]{3,2,1,0:T(8,128)S(1)} %get-tuple-element.54.refs_1_), channel_id=1, source_target_pairs={{0,248},{8,16},{16,8},{24,32},{32,24},{40,48},{48,40},{56,64},{64,... | collective-permute-start | bytes 983048 | tf_op jit(solution)/shard_map/ppermute | solution.py:227
  81.7 16.8 %collective-permute-start.13 = (f32[4,20,8,128]{3,2,1,0:T(8,128)S(1)}, f32[4,20,8,128]{3,2,1,0:T(8,128)S(1)}, u32[]{:S(2)}, u32[]{:S(2)}) collective-permute-start(f32[4,20,8,128]{3,2,1,0:T(8,128)S(1)} %get-tuple-element.54.refs_1_), channel_id=1, source_target_pairs={{0,8},{8,0},{16,24},{24,16},{32,40},{40,32},{48,56},{56,48},{64,72... | collective-permute-start | bytes 983048 | tf_op jit(solution)/shard_map/ppermute | solution.py:227
  82.0 22.2 %collective-permute-start.26 = (f32[30,8,128]{2,1,0:T(8,128)S(1)}, f32[30,8,128]{2,1,0:T(8,128)S(1)}, u32[]{:S(2)}, u32[]{:S(2)}) collective-permute-start(f32[30,8,128]{2,1,0:T(8,128)S(1)} %get-tuple-element.68), channel_id=1, source_target_pairs={{0,2},{2,0},{4,6},{6,4},{1,3},{3,1},{5,7},{7,5},{8,10},{10,8},{12,... | collective-permute-start | bytes 368648 | tf_op jit(solution)/shard_map/ppermute | solution.py:227
  98.6 31.6 %collective-permute-start.23 = (f32[60,8,128]{2,1,0:T(8,128)}, f32[60,8,128]{2,1,0:T(8,128)S(1)}, u32[]{:S(2)}, u32[]{:S(2)}) collective-permute-start(f32[60,8,128]{2,1,0:T(8,128)} %get-tuple-element.64), channel_id=1, source_target_pairs={{0,2},{2,0},{4,6},{6,4},{1,3},{3,1},{5,7},{7,5},{8,10},{10,8},{12,... | collective-permute-start | bytes 737288 | tf_op jit(solution)/shard_map/ppermute | solution.py:227
  98.6 31.9 %collective-permute-start.24 = (f32[60,8,128]{2,1,0:T(8,128)S(1)}, f32[60,8,128]{2,1,0:T(8,128)S(1)}, u32[]{:S(2)}, u32[]{:S(2)}) collective-permute-start(f32[60,8,128]{2,1,0:T(8,128)S(1)} %get-tuple-element.65), channel_id=1, source_target_pairs={{0,4},{2,6},{4,0},{6,2},{1,5},{3,7},{5,1},{7,3},{8,12},{10,14},{12... | collective-permute-start | bytes 737288 | tf_op jit(solution)/shard_map/ppermute | solution.py:227
  99.9 32.8 %collective-permute-start.25 = (f32[60,8,128]{2,1,0:T(8,128)S(1)}, f32[60,8,128]{2,1,0:T(8,128)S(1)}, u32[]{:S(2)}, u32[]{:S(2)}) collective-permute-start(f32[60,8,128]{2,1,0:T(8,128)S(1)} %get-tuple-element.66), channel_id=1, source_target_pairs={{0,6},{2,4},{4,2},{6,0},{1,7},{3,5},{5,3},{7,1},{8,14},{10,12},{12... | collective-permute-start | bytes 737288 | tf_op jit(solution)/shard_map/ppermute | solution.py:227
  104.2 22.0 %collective-permute-start.28 = (f32[30,8,128]{2,1,0:T(8,128)}, f32[30,8,128]{2,1,0:T(8,128)S(1)}, u32[]{:S(2)}, u32[]{:S(2)}) collective-permute-start(f32[30,8,128]{2,1,0:T(8,128)} %get-tuple-element.70), channel_id=1, source_target_pairs={{0,6},{2,4},{4,2},{6,0},{1,7},{3,5},{5,3},{7,1},{8,14},{10,12},{12... | collective-permute-start | bytes 368648 | tf_op jit(solution)/shard_map/ppermute | solution.py:227
  104.8 23.1 %collective-permute-start.10 = (f32[40,8,128]{2,1,0:T(8,128)}, f32[40,8,128]{2,1,0:T(8,128)S(1)}, u32[]{:S(2)}, u32[]{:S(2)}) collective-permute-start(f32[40,8,128]{2,1,0:T(8,128)} %get-tuple-element.51), channel_id=1, source_target_pairs={{0,2},{2,0},{4,6},{6,4},{1,3},{3,1},{5,7},{7,5},{8,10},{10,8},{12,... | collective-permute-start | bytes 491528 | tf_op jit(solution)/shard_map/ppermute | solution.py:227
  105.6 19.8 %all-to-all-start = ((f32[64,1,128]{2,1,0:T(1,128)}), f32[64,1,128]{2,1,0:T(1,128)}, u32[]{:S(2)}, u32[]{:S(2)}) async-start(f32[64,1,128]{2,1,0:T(1,128)} %broadcast_in_dim.115), calls=%async_computation | async-start | bytes 65536 | tf_op jit(solution)/shard_map/all_to_all | solution.py:331
  126.2 20.2 %collective-permute-start.15 = (f32[20,8,128]{2,1,0:T(8,128)}, f32[20,8,128]{2,1,0:T(8,128)S(1)}, u32[]{:S(2)}, u32[]{:S(2)}) collective-permute-start(f32[20,8,128]{2,1,0:T(8,128)} %copy-done.7), channel_id=1, source_target_pairs={{0,2},{2,0},{4,6},{6,4},{1,3},{3,1},{5,7},{7,5},{8,10},{10,8},{12,... | collective-permute-start | bytes 245768 | tf_op jit(solution)/shard_map/ppermute | solution.py:227
  128.0 18.4 %collective-permute-start.16 = (f32[20,8,128]{2,1,0:T(8,128)}, f32[20,8,128]{2,1,0:T(8,128)S(1)}, u32[]{:S(2)}, u32[]{:S(2)}) collective-permute-start(f32[20,8,128]{2,1,0:T(8,128)} %copy-done.6), channel_id=1, source_target_pairs={{0,4},{2,6},{4,0},{6,2},{1,5},{3,7},{5,1},{7,3},{8,12},{10,14},{12... | collective-permute-start | bytes 245768 | tf_op jit(solution)/shard_map/ppermute | solution.py:227
  130.1 16.2 %collective-permute-start.17 = (f32[20,8,128]{2,1,0:T(8,128)}, f32[20,8,128]{2,1,0:T(8,128)S(1)}, u32[]{:S(2)}, u32[]{:S(2)}) collective-permute-start(f32[20,8,128]{2,1,0:T(8,128)} %copy-done.5), channel_id=1, source_target_pairs={{0,6},{2,4},{4,2},{6,0},{1,7},{3,5},{5,3},{7,1},{8,14},{10,12},{12... | collective-permute-start | bytes 245768 | tf_op jit(solution)/shard_map/ppermute | solution.py:227
  (16 other events, 157.5 us)

commit v8 on v7

--- a/solution.py
+++ b/solution.py
@@ -19,10 +19,10 @@
 QUARTER = 5
 TILES = RING * QUARTER
 LON = TILES * LANES
-CHUNKS = ((0, 3), (3, 9), (9, 13), (13, 15))
+CHUNKS = ((0, 4), (4, 11), (11, 15))
 PARTNERS = (2, 1, 3)
-OWN = ((0,), (1,), (2, 3))
-BACK = ((0,), (1,), (2,), (3,))
+OWN = ((0,), (1,), (2,))
+BACK = ((0,), (1,), (2,))
 INFO_CHUNK = 0
 TOGETHER = 5
 VMEM_LIMIT = 12 * 1024 * 1024

time: 149 us -> 137 us (0.919)
  waiting for transfers between devices: 69.7 us -> 59.9 us
  starting transfers between devices: 53.6 us -> 51.4 us
    ppermute x29 -> x24, waiting for transfers between devices: 63.6 us -> 57.2 us  [swap(): lax.ppermute(array, axis, [(i, partner(i)) for i in range(lax.axis_size(a...]
    all_to_all x1, waiting for transfers between devices: 6.15 us -> 2.74 us  [per_device(): spread = lax.all_to_all(spread, parties, 0, 0)]
    pallas_call x4 -> x3, Pallas kernels: 6.45 us -> 5.08 us  [per_device(): pl.pallas_call(partial(column_kernel, batch), out_shape=shapes, in_specs=...]
    ppermute x29 -> x24, starting transfers between devices: 42.9 us -> 41.7 us  [swap(): lax.ppermute(array, axis, [(i, partner(i)) for i in range(lax.axis_size(a...]
    unnamed x20 -> x22, local copies, waits for them, and re-layouts: 4.72 us -> 5.7 us
  transfers between devices with their start and end apart: 30 -> 25, of which waited for: 10 -> 8; matrix products, arithmetic and copies ran while one was open for 3% -> 2% of each run, Pallas kernels for 8% -> 8%
where the time goes in v8:
time: 137 us; the launch traced here: 136 us
  waiting for transfers between devices  59.9 us (44%)
  starting transfers between devices  51.4 us (38%)
  Pallas kernels  15.3 us (11%)
  local copies, waits for them, and re-layouts  6.33 us (5%)
  other arithmetic  3.23 us (2%)
    ppermute x24, waiting for transfers between devices, swap(): lax.ppermute(array, axis, [(i, partner(i)) for i in range(lax.axis_size(a...  57.2 us
    ppermute x24, starting transfers between devices, swap(): lax.ppermute(array, axis, [(i, partner(i)) for i in range(lax.axis_size(a...  41.7 us
    all_to_all x1, starting transfers between devices, per_device(): spread = lax.all_to_all(spread, parties, 0, 0)  9.72 us
    pallas_call x3, Pallas kernels, per_device(): pl.pallas_call(partial(finish_kernel, field), grid=(1,), out_shape=jax.Sh...  8.37 us
    unnamed x22, local copies, waits for them, and re-layouts  5.7 us
    pallas_call x3, Pallas kernels, per_device(): pl.pallas_call(partial(column_kernel, batch), out_shape=shapes, in_specs=...  5.08 us
  transfers between devices with their start and end apart: 25, of which 8 were waited for; matrix products, arithmetic and copies ran while one was open for 2% of the time, Pallas kernels for 8%

profile of v8, /device:TPU:1, one launch (start us, length us, event | category | flops | bytes accessed | tf_op | source)
XLA Modules:
  0.0 136.4 jit_solution(14108843716584330073)
XLA Ops:
  5.2 2.1 %collective-permute-start = (f32[41,8,128]{2,1,0:T(8,128)}, f32[41,8,128]{2,1,0:T(8,128)S(1)}, u32[]{:S(2)}, u32[]{:S(2)}) collective-permute-start(f32[41,8,128]{2,1,0:T(8,128)} %get-tuple-element.33), channel_id=1, source_target_pairs={{0,2},{2,0},{4,6},{6,4},{1,3},{3,1},{5,7},{7,5},{8,10},{10,8},{12,... | collective-permute-start | bytes 503816 | tf_op jit(solution)/shard_map/ppermute | solution.py:227
  7.3 2.6 %collective-permute-start.1 = (f32[41,8,128]{2,1,0:T(8,128)S(1)}, f32[41,8,128]{2,1,0:T(8,128)S(1)}, u32[]{:S(2)}, u32[]{:S(2)}) collective-permute-start(f32[41,8,128]{2,1,0:T(8,128)S(1)} %get-tuple-element.34), channel_id=1, source_target_pairs={{0,4},{2,6},{4,0},{6,2},{1,5},{3,7},{5,1},{7,3},{8,12},{10,14},{12... | collective-permute-start | bytes 503816 | tf_op jit(solution)/shard_map/ppermute | solution.py:227
  10.3 3.8 %collective-permute-start.14 = (f32[40,8,128]{2,1,0:T(8,128)S(1)}, f32[40,8,128]{2,1,0:T(8,128)S(1)}, u32[]{:S(2)}, u32[]{:S(2)}) collective-permute-start(f32[40,8,128]{2,1,0:T(8,128)S(1)} %get-tuple-element.49), channel_id=1, source_target_pairs={{0,4},{2,6},{4,0},{6,2},{1,5},{3,7},{5,1},{7,3},{8,12},{10,14},{12... | collective-permute-start | bytes 491528 | tf_op jit(solution)/shard_map/ppermute | solution.py:227
  14.2 3.4 %collective-permute-done.13.refs_1_ = f32[40,8,128]{2,1,0:T(8,128)S(1)} collective-permute-done((f32[40,8,128]{2,1,0:T(8,128)S(1)}, f32[40,8,128]{2,1,0:T(8,128)S(1)}, u32[]{:S(2)}, u32[]{:S(2)}) %collective-permute-start.13) | collective-permute-done | bytes 163872 | tf_op jit(solution)/shard_map/ppermute | solution.py:227
  17.6 3.7 %collective-permute-start.15 = (f32[40,8,128]{2,1,0:T(8,128)S(1)}, f32[40,8,128]{2,1,0:T(8,128)S(1)}, u32[]{:S(2)}, u32[]{:S(2)}) collective-permute-start(f32[40,8,128]{2,1,0:T(8,128)S(1)} %get-tuple-element.50), channel_id=1, source_target_pairs={{0,6},{2,4},{4,2},{6,0},{1,7},{3,5},{5,3},{7,1},{8,14},{10,12},{12... | collective-permute-start | bytes 491528 | tf_op jit(solution)/shard_map/ppermute | solution.py:227
  21.3 3.3 %collective-permute-done.14.refs_2_ = f32[40,8,128]{2,1,0:T(8,128)S(1)} collective-permute-done((f32[40,8,128]{2,1,0:T(8,128)S(1)}, f32[40,8,128]{2,1,0:T(8,128)S(1)}, u32[]{:S(2)}, u32[]{:S(2)}) %collective-permute-start.14) | collective-permute-done | bytes 163872 | tf_op jit(solution)/shard_map/ppermute | solution.py:227
  24.6 3.0 %collective-permute-done.15.refs_3_ = f32[40,8,128]{2,1,0:T(8,128)S(1)} collective-permute-done((f32[40,8,128]{2,1,0:T(8,128)S(1)}, f32[40,8,128]{2,1,0:T(8,128)S(1)}, u32[]{:S(2)}, u32[]{:S(2)}) %collective-permute-start.15) | collective-permute-done | bytes 163872 | tf_op jit(solution)/shard_map/ppermute | solution.py:227
  28.3 2.4 %collective-permute-start.7 = (f32[70,8,128]{2,1,0:T(8,128)S(1)}, f32[70,8,128]{2,1,0:T(8,128)S(1)}, u32[]{:S(2)}, u32[]{:S(2)}) collective-permute-start(f32[70,8,128]{2,1,0:T(8,128)S(1)} %get-tuple-element.42), channel_id=1, source_target_pairs={{0,6},{2,4},{4,2},{6,0},{1,7},{3,5},{5,3},{7,1},{8,14},{10,12},{12... | collective-permute-start | bytes 860168 | tf_op jit(solution)/shard_map/ppermute | solution.py:227
  30.7 7.9 %collective-permute-start.17 = (f32[4,40,8,128]{3,2,1,0:T(8,128)S(1)}, f32[4,40,8,128]{3,2,1,0:T(8,128)S(1)}, u32[]{:S(2)}, u32[]{:S(2)}) collective-permute-start(f32[4,40,8,128]{3,2,1,0:T(8,128)S(1)} %join.5.refs_1_), channel_id=1, source_target_pairs={{0,248},{8,16},{16,8},{24,32},{32,24},{40,48},{48,40},{56,64},{64,... | collective-permute-start | bytes 1966088 | tf_op jit(solution)/shard_map/ppermute | solution.py:227
  40.2 3.8 %collective-permute-done.7.refs_3_ = f32[70,8,128]{2,1,0:T(8,128)S(1)} collective-permute-done((f32[70,8,128]{2,1,0:T(8,128)S(1)}, f32[70,8,128]{2,1,0:T(8,128)S(1)}, u32[]{:S(2)}, u32[]{:S(2)}) %collective-permute-start.7) | collective-permute-done | bytes 286752 | tf_op jit(solution)/shard_map/ppermute | solution.py:227
  44.1 7.8 %collective-permute-start.9 = (f32[4,70,8,128]{3,2,1,0:T(8,128)S(1)}, f32[4,70,8,128]{3,2,1,0:T(8,128)S(1)}, u32[]{:S(2)}, u32[]{:S(2)}) collective-permute-start(f32[4,70,8,128]{3,2,1,0:T(8,128)S(1)} %join.4.refs_1_), channel_id=1, source_target_pairs={{0,248},{8,16},{16,8},{24,32},{32,24},{40,48},{48,40},{56,64},{64,... | collective-permute-start | bytes 3440648 | tf_op jit(solution)/shard_map/ppermute | solution.py:227
  51.9 14.7 %collective-permute-done.4.refs_2_ = f32[4,41,8,128]{3,2,1,0:T(8,128)S(1)} collective-permute-done((f32[4,41,8,128]{3,2,1,0:T(8,128)S(1)}, f32[4,41,8,128]{3,2,1,0:T(8,128)S(1)}, u32[]{:S(2)}, u32[]{:S(2)}) %collective-permute-start.4) | collective-permute-done | bytes 671776 | tf_op jit(solution)/shard_map/ppermute | solution.py:227
  66.7 1.9 %column.3 = (f32[40,8,128]{2,1,0:T(8,128)S(1)}, f32[40,8,128]{2,1,0:T(8,128)S(1)}, f32[40,8,128]{2,1,0:T(8,128)}, f32[40,8,128]{2,1,0:T(8,128)}, f32[3,4,8,128]{3,2,1,0:T(8,128)S(1)}) custom-call(s32[4,10]{1,0:T(4,128)S(1)} %bitcast.30, f32[4,4,10]{2,1,0:T(4,128)S(1)} %pad_maximum_fusion.weight_ref, f32[4,41,8,128]{3,2,1,0:T(8,128)S(1)} %collective-permute-done.3.refs_0_, ...), custom_call_target="tpu_custom_call" | custom-call | tf_op jit(solution)/shard_map/column/pallas_call | solution.py:296
  69.1 22.1 %collective-permute-done.9.refs_2_ = f32[4,70,8,128]{3,2,1,0:T(8,128)S(1)} collective-permute-done((f32[4,70,8,128]{3,2,1,0:T(8,128)S(1)}, f32[4,70,8,128]{3,2,1,0:T(8,128)S(1)}, u32[]{:S(2)}, u32[]{:S(2)}) %collective-permute-start.9) | collective-permute-done | bytes 1146912 | tf_op jit(solution)/shard_map/ppermute | solution.py:227
  91.4 2.1 %column.4 = (f32[70,8,128]{2,1,0:T(8,128)S(1)}, f32[70,8,128]{2,1,0:T(8,128)}, f32[70,8,128]{2,1,0:T(8,128)}, f32[70,8,128]{2,1,0:T(8,128)S(1)}) custom-call(s32[4,10]{1,0:T(4,128)S(1)} %bitcast.31, f32[4,4,10]{2,1,0:T(4,128)S(1)} %pad_maximum_fusion.weight_ref, f32[4,70,8,128]{3,2,1,0:T(8,128)S(1)} %collective-permute-done.8.refs_0_, ...), custom_call_target="tpu_custom_call" | custom-call | tf_op jit(solution)/shard_map/column/pallas_call | solution.py:296
  94.4 2.9 %collective-permute-start.23 = (f32[40,8,128]{2,1,0:T(8,128)}, f32[40,8,128]{2,1,0:T(8,128)}, u32[]{:S(2)}, u32[]{:S(2)}) collective-permute-start(f32[40,8,128]{2,1,0:T(8,128)} %get-tuple-element.58), channel_id=1, source_target_pairs={{0,6},{2,4},{4,2},{6,0},{1,7},{3,5},{5,3},{7,1},{8,14},{10,12},{12... | collective-permute-start | bytes 491528 | tf_op jit(solution)/shard_map/ppermute | solution.py:227
  98.0 9.7 %all-to-all-start = ((f32[64,1,128]{2,1,0:T(1,128)}), f32[64,1,128]{2,1,0:T(1,128)S(1)}, u32[]{:S(2)}, u32[]{:S(2)}) async-start(f32[64,1,128]{2,1,0:T(1,128)} %broadcast_in_dim.115), calls=%async_computation | async-start | bytes 65536 | tf_op jit(solution)/shard_map/all_to_all | solution.py:331
  108.6 2.0 %collective-permute-start.12 = (f32[70,8,128]{2,1,0:T(8,128)}, f32[70,8,128]{2,1,0:T(8,128)S(1)}, u32[]{:S(2)}, u32[]{:S(2)}) collective-permute-start(f32[70,8,128]{2,1,0:T(8,128)} %copy-done.6), channel_id=1, source_target_pairs={{0,6},{2,4},{4,2},{6,0},{1,7},{3,5},{5,3},{7,1},{8,14},{10,12},{12... | collective-permute-start | bytes 860168 | tf_op jit(solution)/shard_map/ppermute | solution.py:227
  114.3 2.7 %all-to-all-done = f32[64,1,128]{2,1,0:T(1,128)S(1)} async-done(((f32[64,1,128]{2,1,0:T(1,128)}), f32[64,1,128]{2,1,0:T(1,128)S(1)}, u32[]{:S(2)}, u32[]{:S(2)}) %all-to-all-start) | async-done | bytes 32800 | tf_op jit(solution)/shard_map/all_to_all | solution.py:331
  118.7 2.3 %collective-permute-start.20 = (f32[40,8,128]{2,1,0:T(8,128)}, f32[40,8,128]{2,1,0:T(8,128)S(1)}, u32[]{:S(2)}, u32[]{:S(2)}) collective-permute-start(f32[40,8,128]{2,1,0:T(8,128)} %copy-done.7), channel_id=1, source_target_pairs={{0,6},{2,4},{4,2},{6,0},{1,7},{3,5},{5,3},{7,1},{8,14},{10,12},{12... | collective-permute-start | bytes 491528 | tf_op jit(solution)/shard_map/ppermute | solution.py:227
  121.1 6.9 %collective-permute-done.12.refs_7_.refs_3_ = f32[70,8,128]{2,1,0:T(8,128)S(1)} collective-permute-done((f32[70,8,128]{2,1,0:T(8,128)}, f32[70,8,128]{2,1,0:T(8,128)S(1)}, u32[]{:S(2)}, u32[]{:S(2)}) %collective-permute-start.12) | collective-permute-done | bytes 286752 | tf_op jit(solution)/shard_map/ppermute | solution.py:227
  128.0 3.1 %finish.3.refs_4_ = f32[10,3,8,2560]{3,2,1,0:T(8,128)} custom-call(s32[10]{0:T(128)S(1)} %copy-done.4, f32[4,10]{1,0:T(4,128)S(1)} %pad_maximum_fusion.1.weight_ref, f32[3]{0:T(128)S(1)} %slice_divide_fusion.ratio_ref, f32[40,8,128]{2,1,0:T(8,128)S(1)} %get-tuple-element.55.refs_0_, f32[40,8,128]{2,1,0:T(8,128)S(1)} %collective-permute-done.21.refs_1_, ...), custom_call_target="tpu_custom_call" | custom-call | tf_op jit(solution)/shard_map/finish/pallas_call | solution.py:345
  131.1 2.6 %finish.4.refs_8_ = f32[10,3,8,2560]{3,2,1,0:T(8,128)} custom-call(s32[10]{0:T(128)S(1)} %copy-done.4, f32[4,10]{1,0:T(4,128)S(1)} %pad_maximum_fusion.1.weight_ref, f32[3]{0:T(128)S(1)} %slice_divide_fusion.ratio_ref, f32[70,8,128]{2,1,0:T(8,128)S(1)} %get-tuple-element.43.refs_4_.refs_0_, ...), custom_call_target="tpu_custom_call", output_to_operand_aliasing={{}: (7, {})} | custom-call | tf_op jit(solution)/shard_map/finish/pallas_call | solution.py:345
  133.7 2.7 %finish.5 = f32[10,3,8,2560]{3,2,1,0:T(8,128)} custom-call(s32[10]{0:T(128)S(1)} %copy-done.4, f32[4,10]{1,0:T(4,128)S(1)} %pad_maximum_fusion.1.weight_ref, f32[3]{0:T(128)S(1)} %slice_divide_fusion.ratio_ref, f32[70,8,128]{2,1,0:T(8,128)S(1)} %get-tuple-element.43.refs_4_.refs_0_, ...), custom_call_target="tpu_custom_call", output_to_operand_aliasing={{}: (11, {})} | custom-call | tf_op jit(solution)/shard_map/finish/pallas_call | solution.py:345
  (83 shorter events, 16.6 us)
Async XLA Ops:
  5.2 23.1 %collective-permute-start = (f32[41,8,128]{2,1,0:T(8,128)}, f32[41,8,128]{2,1,0:T(8,128)S(1)}, u32[]{:S(2)}, u32[]{:S(2)}) collective-permute-start(f32[41,8,128]{2,1,0:T(8,128)} %get-tuple-element.33), channel_id=1, source_target_pairs={{0,2},{2,0},{4,6},{6,4},{1,3},{3,1},{5,7},{7,5},{8,10},{10,8},{12,... | collective-permute-start | bytes 503816 | tf_op jit(solution)/shard_map/ppermute | solution.py:227
  7.3 23.4 %collective-permute-start.1 = (f32[41,8,128]{2,1,0:T(8,128)S(1)}, f32[41,8,128]{2,1,0:T(8,128)S(1)}, u32[]{:S(2)}, u32[]{:S(2)}) collective-permute-start(f32[41,8,128]{2,1,0:T(8,128)S(1)} %get-tuple-element.34), channel_id=1, source_target_pairs={{0,4},{2,6},{4,0},{6,2},{1,5},{3,7},{5,1},{7,3},{8,12},{10,14},{12... | collective-permute-start | bytes 503816 | tf_op jit(solution)/shard_map/ppermute | solution.py:227
  9.9 28.7 %collective-permute-start.2 = (f32[41,8,128]{2,1,0:T(8,128)S(1)}, f32[41,8,128]{2,1,0:T(8,128)S(1)}, u32[]{:S(2)}, u32[]{:S(2)}) collective-permute-start(f32[41,8,128]{2,1,0:T(8,128)S(1)} %get-tuple-element.35), channel_id=1, source_target_pairs={{0,6},{2,4},{4,2},{6,0},{1,7},{3,5},{5,3},{7,1},{8,14},{10,12},{12... | collective-permute-start | bytes 503816 | tf_op jit(solution)/shard_map/ppermute | solution.py:227
  10.3 14.3 %collective-permute-start.14 = (f32[40,8,128]{2,1,0:T(8,128)S(1)}, f32[40,8,128]{2,1,0:T(8,128)S(1)}, u32[]{:S(2)}, u32[]{:S(2)}) collective-permute-start(f32[40,8,128]{2,1,0:T(8,128)S(1)} %get-tuple-element.49), channel_id=1, source_target_pairs={{0,4},{2,6},{4,0},{6,2},{1,5},{3,7},{5,1},{7,3},{8,12},{10,14},{12... | collective-permute-start | bytes 491528 | tf_op jit(solution)/shard_map/ppermute | solution.py:227
  17.6 10.0 %collective-permute-start.15 = (f32[40,8,128]{2,1,0:T(8,128)S(1)}, f32[40,8,128]{2,1,0:T(8,128)S(1)}, u32[]{:S(2)}, u32[]{:S(2)}) collective-permute-start(f32[40,8,128]{2,1,0:T(8,128)S(1)} %get-tuple-element.50), channel_id=1, source_target_pairs={{0,6},{2,4},{4,2},{6,0},{1,7},{3,5},{5,3},{7,1},{8,14},{10,12},{12... | collective-permute-start | bytes 491528 | tf_op jit(solution)/shard_map/ppermute | solution.py:227
  24.6 15.5 %collective-permute-start.5 = (f32[70,8,128]{2,1,0:T(8,128)S(1)}, f32[70,8,128]{2,1,0:T(8,128)S(1)}, u32[]{:S(2)}, u32[]{:S(2)}) collective-permute-start(f32[70,8,128]{2,1,0:T(8,128)S(1)} %get-tuple-element.40), channel_id=1, source_target_pairs={{0,2},{2,0},{4,6},{6,4},{1,3},{3,1},{5,7},{7,5},{8,10},{10,8},{12,... | collective-permute-start | bytes 860168 | tf_op jit(solution)/shard_map/ppermute | solution.py:227
  27.5 12.6 %collective-permute-start.6 = (f32[70,8,128]{2,1,0:T(8,128)S(1)}, f32[70,8,128]{2,1,0:T(8,128)S(1)}, u32[]{:S(2)}, u32[]{:S(2)}) collective-permute-start(f32[70,8,128]{2,1,0:T(8,128)S(1)} %get-tuple-element.41), channel_id=1, source_target_pairs={{0,4},{2,6},{4,0},{6,2},{1,5},{3,7},{5,1},{7,3},{8,12},{10,14},{12... | collective-permute-start | bytes 860168 | tf_op jit(solution)/shard_map/ppermute | solution.py:227
  28.3 15.7 %collective-permute-start.7 = (f32[70,8,128]{2,1,0:T(8,128)S(1)}, f32[70,8,128]{2,1,0:T(8,128)S(1)}, u32[]{:S(2)}, u32[]{:S(2)}) collective-permute-start(f32[70,8,128]{2,1,0:T(8,128)S(1)} %get-tuple-element.42), channel_id=1, source_target_pairs={{0,6},{2,4},{4,2},{6,0},{1,7},{3,5},{5,3},{7,1},{8,14},{10,12},{12... | collective-permute-start | bytes 860168 | tf_op jit(solution)/shard_map/ppermute | solution.py:227
  30.7 63.7 %collective-permute-start.17 = (f32[4,40,8,128]{3,2,1,0:T(8,128)S(1)}, f32[4,40,8,128]{3,2,1,0:T(8,128)S(1)}, u32[]{:S(2)}, u32[]{:S(2)}) collective-permute-start(f32[4,40,8,128]{3,2,1,0:T(8,128)S(1)} %join.5.refs_1_), channel_id=1, source_target_pairs={{0,248},{8,16},{16,8},{24,32},{32,24},{40,48},{48,40},{56,64},{64,... | collective-permute-start | bytes 1966088 | tf_op jit(solution)/shard_map/ppermute | solution.py:227
  38.8 27.9 %collective-permute-start.4 = (f32[4,41,8,128]{3,2,1,0:T(8,128)S(1)}, f32[4,41,8,128]{3,2,1,0:T(8,128)S(1)}, u32[]{:S(2)}, u32[]{:S(2)}) collective-permute-start(f32[4,41,8,128]{3,2,1,0:T(8,128)S(1)} %get-tuple-element.37.refs_1_), channel_id=1, source_target_pairs={{0,248},{8,16},{16,8},{24,32},{32,24},{40,48},{48,40},{56,64},{64,... | collective-permute-start | bytes 2015240 | tf_op jit(solution)/shard_map/ppermute | solution.py:227
  40.1 26.6 %collective-permute-start.3 = (f32[4,41,8,128]{3,2,1,0:T(8,128)S(1)}, f32[4,41,8,128]{3,2,1,0:T(8,128)S(1)}, u32[]{:S(2)}, u32[]{:S(2)}) collective-permute-start(f32[4,41,8,128]{3,2,1,0:T(8,128)S(1)} %get-tuple-element.37.refs_1_), channel_id=1, source_target_pairs={{0,8},{8,0},{16,24},{24,16},{32,40},{40,32},{48,56},{56,48},{64,72... | collective-permute-start | bytes 2015240 | tf_op jit(solution)/shard_map/ppermute | solution.py:227
  44.1 47.2 %collective-permute-start.9 = (f32[4,70,8,128]{3,2,1,0:T(8,128)S(1)}, f32[4,70,8,128]{3,2,1,0:T(8,128)S(1)}, u32[]{:S(2)}, u32[]{:S(2)}) collective-permute-start(f32[4,70,8,128]{3,2,1,0:T(8,128)S(1)} %join.4.refs_1_), channel_id=1, source_target_pairs={{0,248},{8,16},{16,8},{24,32},{32,24},{40,48},{48,40},{56,64},{64,... | collective-permute-start | bytes 3440648 | tf_op jit(solution)/shard_map/ppermute | solution.py:227
  51.9 39.5 %collective-permute-start.8 = (f32[4,70,8,128]{3,2,1,0:T(8,128)S(1)}, f32[4,70,8,128]{3,2,1,0:T(8,128)S(1)}, u32[]{:S(2)}, u32[]{:S(2)}) collective-permute-start(f32[4,70,8,128]{3,2,1,0:T(8,128)S(1)} %join.4.refs_1_), channel_id=1, source_target_pairs={{0,8},{8,0},{16,24},{24,16},{32,40},{40,32},{48,56},{56,48},{64,72... | collective-permute-start | bytes 3440648 | tf_op jit(solution)/shard_map/ppermute | solution.py:227
  66.7 41.1 %collective-permute-start.16 = (f32[4,40,8,128]{3,2,1,0:T(8,128)S(1)}, f32[4,40,8,128]{3,2,1,0:T(8,128)S(1)}, u32[]{:S(2)}, u32[]{:S(2)}) collective-permute-start(f32[4,40,8,128]{3,2,1,0:T(8,128)S(1)} %join.5.refs_1_), channel_id=1, source_target_pairs={{0,8},{8,0},{16,24},{24,16},{32,40},{40,32},{48,56},{56,48},{64,72... | collective-permute-start | bytes 1966088 | tf_op jit(solution)/shard_map/ppermute | solution.py:227
  68.5 40.1 %collective-permute-start.21 = (f32[40,8,128]{2,1,0:T(8,128)S(1)}, f32[40,8,128]{2,1,0:T(8,128)S(1)}, u32[]{:S(2)}, u32[]{:S(2)}) collective-permute-start(f32[40,8,128]{2,1,0:T(8,128)S(1)} %get-tuple-element.56), channel_id=1, source_target_pairs={{0,2},{2,0},{4,6},{6,4},{1,3},{3,1},{5,7},{7,5},{8,10},{10,8},{12,... | collective-permute-start | bytes 491528 | tf_op jit(solution)/shard_map/ppermute | solution.py:227
  91.2 25.9 %collective-permute-start.22 = (f32[40,8,128]{2,1,0:T(8,128)}, f32[40,8,128]{2,1,0:T(8,128)}, u32[]{:S(2)}, u32[]{:S(2)}) collective-permute-start(f32[40,8,128]{2,1,0:T(8,128)} %get-tuple-element.57), channel_id=1, source_target_pairs={{0,4},{2,6},{4,0},{6,2},{1,5},{3,7},{5,1},{7,3},{8,12},{10,14},{12... | collective-permute-start | bytes 491528 | tf_op jit(solution)/shard_map/ppermute | solution.py:227
  94.2 24.5 %collective-permute-start.10 = (f32[70,8,128]{2,1,0:T(8,128)}, f32[70,8,128]{2,1,0:T(8,128)S(1)}, u32[]{:S(2)}, u32[]{:S(2)}) collective-permute-start(f32[70,8,128]{2,1,0:T(8,128)} %get-tuple-element.44), channel_id=1, source_target_pairs={{0,2},{2,0},{4,6},{6,4},{1,3},{3,1},{5,7},{7,5},{8,10},{10,8},{12,... | collective-permute-start | bytes 860168 | tf_op jit(solution)/shard_map/ppermute | solution.py:227
  94.4 23.1 %collective-permute-start.23 = (f32[40,8,128]{2,1,0:T(8,128)}, f32[40,8,128]{2,1,0:T(8,128)}, u32[]{:S(2)}, u32[]{:S(2)}) collective-permute-start(f32[40,8,128]{2,1,0:T(8,128)} %get-tuple-element.58), channel_id=1, source_target_pairs={{0,6},{2,4},{4,2},{6,0},{1,7},{3,5},{5,3},{7,1},{8,14},{10,12},{12... | collective-permute-start | bytes 491528 | tf_op jit(solution)/shard_map/ppermute | solution.py:227
  98.0 19.0 %all-to-all-start = ((f32[64,1,128]{2,1,0:T(1,128)}), f32[64,1,128]{2,1,0:T(1,128)S(1)}, u32[]{:S(2)}, u32[]{:S(2)}) async-start(f32[64,1,128]{2,1,0:T(1,128)} %broadcast_in_dim.115), calls=%async_computation | async-start | bytes 65536 | tf_op jit(solution)/shard_map/all_to_all | solution.py:331
  107.8 13.4 %collective-permute-start.11 = (f32[70,8,128]{2,1,0:T(8,128)}, f32[70,8,128]{2,1,0:T(8,128)S(1)}, u32[]{:S(2)}, u32[]{:S(2)}) collective-permute-start(f32[70,8,128]{2,1,0:T(8,128)} %get-tuple-element.45), channel_id=1, source_target_pairs={{0,4},{2,6},{4,0},{6,2},{1,5},{3,7},{5,1},{7,3},{8,12},{10,14},{12... | collective-permute-start | bytes 860168 | tf_op jit(solution)/shard_map/ppermute | solution.py:227
  108.6 19.4 %collective-permute-start.12 = (f32[70,8,128]{2,1,0:T(8,128)}, f32[70,8,128]{2,1,0:T(8,128)S(1)}, u32[]{:S(2)}, u32[]{:S(2)}) collective-permute-start(f32[70,8,128]{2,1,0:T(8,128)} %copy-done.6), channel_id=1, source_target_pairs={{0,6},{2,4},{4,2},{6,0},{1,7},{3,5},{5,3},{7,1},{8,14},{10,12},{12... | collective-permute-start | bytes 860168 | tf_op jit(solution)/shard_map/ppermute | solution.py:227
  117.1 16.6 %collective-permute-start.18 = (f32[40,8,128]{2,1,0:T(8,128)}, f32[40,8,128]{2,1,0:T(8,128)S(1)}, u32[]{:S(2)}, u32[]{:S(2)}) collective-permute-start(f32[40,8,128]{2,1,0:T(8,128)} %copy-done.9), channel_id=1, source_target_pairs={{0,2},{2,0},{4,6},{6,4},{1,3},{3,1},{5,7},{7,5},{8,10},{10,8},{12,... | collective-permute-start | bytes 491528 | tf_op jit(solution)/shard_map/ppermute | solution.py:227
  117.5 16.2 %collective-permute-start.19 = (f32[40,8,128]{2,1,0:T(8,128)}, f32[40,8,128]{2,1,0:T(8,128)S(1)}, u32[]{:S(2)}, u32[]{:S(2)}) collective-permute-start(f32[40,8,128]{2,1,0:T(8,128)} %copy-done.8), channel_id=1, source_target_pairs={{0,4},{2,6},{4,0},{6,2},{1,5},{3,7},{5,1},{7,3},{8,12},{10,14},{12... | collective-permute-start | bytes 491528 | tf_op jit(solution)/shard_map/ppermute | solution.py:227
  118.7 15.0 %collective-permute-start.20 = (f32[40,8,128]{2,1,0:T(8,128)}, f32[40,8,128]{2,1,0:T(8,128)S(1)}, u32[]{:S(2)}, u32[]{:S(2)}) collective-permute-start(f32[40,8,128]{2,1,0:T(8,128)} %copy-done.7), channel_id=1, source_target_pairs={{0,6},{2,4},{4,2},{6,0},{1,7},{3,5},{5,3},{7,1},{8,14},{10,12},{12... | collective-permute-start | bytes 491528 | tf_op jit(solution)/shard_map/ppermute | solution.py:227
  (12 other events, 76.2 us)

commit v9 on v5

--- a/solution.py
+++ b/solution.py
@@ -19,12 +19,14 @@
 QUARTER = 5
 TILES = RING * QUARTER
 LON = TILES * LANES
-CHUNKS = ((0, 3), (3, 9), (9, 13), (13, 15))
+CHUNKS = ((0, 4), (4, 11), (11, 15))
 PARTNERS = (2, 1, 3)
-OWN = ((0,), (1,), (2, 3))
-BACK = ((0, 1), (2,), (3,))
+OWN = ((0,), (1,), (2,))
+BACK = ((0,), (1,), (2,))
+SUMS_CHUNK = 0
 INFO_CHUNK = 1
-TOGETHER = 2
+MARKED = (SUMS_CHUNK, INFO_CHUNK)
+TOGETHER = 5
 VMEM_LIMIT = 12 * 1024 * 1024
 
 
@@ -57,7 +59,7 @@
 
 
 def tile_count(chunk):
-    return ROWS * width_of(chunk) + (1 if chunk == INFO_CHUNK else 0)
+    return ROWS * width_of(chunk) + (1 if chunk in MARKED else 0)
 
 
 def batch_tiles(batch):
@@ -86,12 +88,24 @@
 
 
 def pack_first(fields_ref, *piece_refs):
+    sub = lax.broadcasted_iota(jnp.int32, (ROWS, LANES), 0)
+    lane = lax.broadcasted_iota(jnp.int32, (ROWS, LANES), 1)
+    sums_sub = lax.broadcasted_iota(jnp.int32, (8, LANES), 0)
+    sums = jnp.zeros((8, LANES), jnp.float32)
+    for field in range(FIELDS):
+        total = fields_ref[:, field, :, 0:LANES]
+        for tile in range(1, TILES):
+            total = total + fields_ref[:, field, :, tile * LANES : (tile + 1) * LANES]
+        by_row = jnp.sum(jnp.sum(total, axis=1), axis=1, keepdims=True)
+        in_lanes = jnp.sum(jnp.where(sub == lane, by_row, 0.0), axis=0, keepdims=True)
+        sums = jnp.where(sums_sub == field, in_lanes, sums)
     copy_units(fields_ref, OWN[0], piece_refs)
-
-
-def pack_rest(departure_ref, extents_ref, lat_ref, lon_ref, fields_ref, *piece_refs):
-    band = lax.axis_index(LAT)
-    first_row = band * ROWS
+    for ref in piece_refs:
+        ref[batch_tiles(OWN[0]) - 1] = sums
+
+
+def pack_second(departure_ref, extents_ref, lat_ref, lon_ref, fields_ref, *piece_refs):
+    first_row = lax.axis_index(LAT) * ROWS
     group_row = lax.axis_index(LAT[:2]) * GROUP
     low_bound = first_row - extents_ref[0, 0] * ROWS + 1
     high_bound = first_row + ROWS - 3 + extents_ref[0, 1] * ROWS
@@ -107,21 +121,13 @@
         info = jnp.where(here & (info_sub == 1), lat_ref[row], info)
         info = jnp.where(here & (info_sub == 2), lon_ref[row], info)
     info = jnp.where(info_sub == 0, starts.astype(jnp.float32), info)
-    sub = lax.broadcasted_iota(jnp.int32, (ROWS, LANES), 0)
-    lane = lax.broadcasted_iota(jnp.int32, (ROWS, LANES), 1)
-    for field in range(FIELDS):
-        total = fields_ref[:, field, :, 0:LANES]
-        for tile in range(1, TILES):
-            total = total + fields_ref[:, field, :, tile * LANES : (tile + 1) * LANES]
-        by_row = jnp.sum(jnp.sum(total, axis=1), axis=1, keepdims=True)
-        in_lanes = jnp.sum(jnp.where(sub == lane, by_row, 0.0), axis=0, keepdims=True)
-        info = jnp.where(info_sub == 3 + field, in_lanes, info)
-    for number, batch in enumerate(OWN[1:]):
-        refs = piece_refs[number * RING : (number + 1) * RING]
-        copy_units(fields_ref, batch, refs)
-        if INFO_CHUNK in batch:
-            for ref in refs:
-                ref[batch_tiles(batch) - 1] = info
+    copy_units(fields_ref, OWN[1], piece_refs)
+    for ref in piece_refs:
+        ref[batch_tiles(OWN[1]) - 1] = info
+
+
+def pack_third(fields_ref, *piece_refs):
+    copy_units(fields_ref, OWN[2], piece_refs)
 
 
 def join_kernel(batch, *refs):
@@ -143,7 +149,7 @@
     positions = side_places(lax.axis_index(LAT[:2]))
     for chunk, side_refs, rows_ref in zip(batch, sides, rows_refs):
         count = width_of(chunk) * ROWS
-        if chunk == INFO_CHUNK:
+        if chunk == SUMS_CHUNK:
             for side, ref in zip(positions, side_refs):
                 refs[RING][side] = ref[:, count]
         for distance in range(RING):
@@ -250,25 +256,23 @@
 
 def per_device(fields, lat_fraction, lon_fraction, lon_shift, departure_row, extents):
     params = pltpu.CompilerParams(vmem_limit_bytes=VMEM_LIMIT)
-    pieces = [
-        pl.pallas_call(
-            pack_first,
-            out_shape=[tiles(batch_tiles(OWN[0]))] * RING,
-            in_specs=[VMEM],
-            out_specs=[VMEM] * RING,
-            compiler_params=params,
-            name="pack_a",
-        )(fields)
-    ]
-    rest = pl.pallas_call(
-        pack_rest,
-        out_shape=[tiles(batch_tiles(batch)) for batch in OWN[1:] for _ in range(RING)],
-        in_specs=[SMEM] * 4 + [VMEM],
-        out_specs=[VMEM] * (RING * (len(OWN) - 1)),
-        compiler_params=params,
-        name="pack_b",
-    )(departure_row, extents, lat_fraction, lon_fraction, fields)
-    pieces += [rest[number * RING : (number + 1) * RING] for number in range(len(OWN) - 1)]
+    pieces = []
+    packs = (
+        (pack_first, ()),
+        (pack_second, (departure_row, extents, lat_fraction, lon_fraction)),
+        (pack_third, ()),
+    )
+    for number, (kernel, scalars) in enumerate(packs):
+        pieces.append(
+            pl.pallas_call(
+                kernel,
+                out_shape=[tiles(batch_tiles(OWN[number]))] * RING,
+                in_specs=[SMEM] * len(scalars) + [VMEM],
+                out_specs=[VMEM] * RING,
+                compiler_params=params,
+                name="pack",
+            )(*scalars, fields)
+        )
 
     own, inner, outer = {}, {}, {}
     for number, batch in enumerate(OWN):
@@ -293,7 +297,7 @@
 
     gathered = []
     for batch in BACK:
-        shapes = [tiles(column_tiles(batch))] * RING + [tiles(3, RING)] * (INFO_CHUNK in batch)
+        shapes = [tiles(column_tiles(batch))] * RING + [tiles(3, RING)] * (SUMS_CHUNK in batch)
         operands = [part[chunk] for chunk in batch for part in (inner, own, outer)]
         columns = pl.pallas_call(
             partial(column_kernel, batch),
@@ -306,8 +310,8 @@
             compiler_params=params,
             name="column",
         )(ring_start, ring_weight, *operands)
-        if INFO_CHUNK in batch:
-            all_info = columns[RING]
+        if SUMS_CHUNK in batch:
+            all_sums = columns[RING]
         gathered.append(exchange(columns[:RING]))
 
     total_rows = lax.axis_size(LAT) * ROWS
@@ -315,7 +319,7 @@
     bands = across(lax.axis_index(LAT[2]), jnp.arange(RING, dtype=jnp.int32))
     ring_rows = bands[:, None] * ROWS + jnp.arange(ROWS, dtype=jnp.int32)[None]
     area = jnp.cos(math.pi * ((group_row + ring_rows).astype(jnp.float32) + 0.5) / total_rows - math.pi / 2.0)
-    sums = all_info[:, :, 3 : 3 + FIELDS, :ROWS]
+    sums = all_sums[:, :, :FIELDS, :ROWS]
     lon_total = sum(cubic_weights(ring_info[:, 2]))
     before = jnp.sum(area[:, None, :] * sums[1], axis=(0, 2))
     after = jnp.zeros((FIELDS,), jnp.float32)

time: 135 us -> 140 us (1.037)
  waiting for transfers between devices: 47.6 us -> 72.3 us
  starting transfers between devices: 63.1 us -> 42 us
    ppermute x26 -> x24, waiting for transfers between devices: 42.2 us -> 69.1 us  [swap(): lax.ppermute(array, axis, [(i, partner(i)) for i in range(lax.axis_size(a...]
    ppermute x26 -> x24, starting transfers between devices: 53.1 us -> 32.1 us  [swap(): lax.ppermute(array, axis, [(i, partner(i)) for i in range(lax.axis_size(a...]
    all_to_all x1, waiting for transfers between devices: 5.39 us -> 3.17 us  [per_device(): spread = lax.all_to_all(spread, parties, 0, 0)]
    unnamed x20 -> x44, local copies, waits for them, and re-layouts: 5.61 us -> 5.07 us
  transfers between devices with their start and end apart: 27 -> 25, of which waited for: 9 -> 7; matrix products, arithmetic and copies ran while one was open for 2% -> 3% of each run, Pallas kernels for 9% -> 10%
where the time goes in v9:
time: 140 us; the launch traced here: 139 us
  waiting for transfers between devices  72.3 us (52%)
  starting transfers between devices  42 us (30%)
  Pallas kernels  16.1 us (12%)
  local copies, waits for them, and re-layouts  5.7 us (4%)
  other arithmetic  2.99 us (2%)
    ppermute x24, waiting for transfers between devices, swap(): lax.ppermute(array, axis, [(i, partner(i)) for i in range(lax.axis_size(a...  69.1 us
    ppermute x24, starting transfers between devices, swap(): lax.ppermute(array, axis, [(i, partner(i)) for i in range(lax.axis_size(a...  32.1 us
    all_to_all x1, starting transfers between devices, per_device(): spread = lax.all_to_all(spread, parties, 0, 0)  9.89 us
    pallas_call x3, Pallas kernels, per_device(): pl.pallas_call(partial(finish_kernel, field), grid=(1,), out_shape=jax.Sh...  8.37 us
    pallas_call x3, Pallas kernels, per_device(): pl.pallas_call(partial(column_kernel, batch), out_shape=shapes, in_specs=...  5.08 us
    unnamed x44, local copies, waits for them, and re-layouts  5.07 us
    all_to_all x1, waiting for transfers between devices, per_device(): spread = lax.all_to_all(spread, parties, 0, 0)  3.17 us
  transfers between devices with their start and end apart: 25, of which 7 were waited for; matrix products, arithmetic and copies ran while one was open for 3% of the time, Pallas kernels for 10%

profile of v9, /device:TPU:1, one launch (start us, length us, event | category | flops | bytes accessed | tf_op | source)
XLA Modules:
  0.0 139.4 jit_solution(1965038881179705396)
XLA Ops:
  0.0 1.7 %copy-done = f32[10,3,8,2560]{3,2,1,0:T(8,128)S(1)} copy-done((f32[10,3,8,2560]{3,2,1,0:T(8,128)S(1)}, f32[10,3,8,2560]{3,2,1,0:T(8,128)}, u32[]{:S(2)}) %copy-start) | copy-done | bytes 2457624
  1.8 2.2 %collective-permute-start.13 = (f32[40,8,128]{2,1,0:T(8,128)S(1)}, f32[40,8,128]{2,1,0:T(8,128)S(1)}, u32[]{:S(2)}, u32[]{:S(2)}) collective-permute-start(f32[40,8,128]{2,1,0:T(8,128)S(1)} %get-tuple-element.48), channel_id=1, source_target_pairs={{0,2},{2,0},{4,6},{6,4},{1,3},{3,1},{5,7},{7,5},{8,10},{10,8},{12,... | collective-permute-start | bytes 491528 | tf_op jit(solution)/shard_map/ppermute | solution.py:236
  4.0 2.6 %collective-permute-start.14 = (f32[40,8,128]{2,1,0:T(8,128)S(1)}, f32[40,8,128]{2,1,0:T(8,128)S(1)}, u32[]{:S(2)}, u32[]{:S(2)}) collective-permute-start(f32[40,8,128]{2,1,0:T(8,128)S(1)} %get-tuple-element.49), channel_id=1, source_target_pairs={{0,4},{2,6},{4,0},{6,2},{1,5},{3,7},{5,1},{7,3},{8,12},{10,14},{12... | collective-permute-start | bytes 491528 | tf_op jit(solution)/shard_map/ppermute | solution.py:236
  7.6 1.5 %pack.3 = (f32[71,8,128]{2,1,0:T(8,128)S(1)}, f32[71,8,128]{2,1,0:T(8,128)}, f32[71,8,128]{2,1,0:T(8,128)S(1)}, f32[71,8,128]{2,1,0:T(8,128)S(1)}) custom-call(s32[10]{0:T(128)S(1)} %copy-done.6, s32[1,2]{1,0:T(1,128)S(1)} %copy-done.7, f32[10]{0:T(128)S(1)} %copy-done.8, f32[10]{0:T(128)S(1)} %copy-done.5, f32[10,3,8,2560]{3,2,1,0:T(8,128)S(1)} %copy-done.1), custom_call_target="tpu_custom_call" | custom-call | tf_op jit(solution)/shard_map/pack/pallas_call | solution.py:267
  9.1 1.4 %collective-permute-start = (f32[71,8,128]{2,1,0:T(8,128)}, f32[71,8,128]{2,1,0:T(8,128)S(1)}, u32[]{:S(2)}, u32[]{:S(2)}) collective-permute-start(f32[71,8,128]{2,1,0:T(8,128)} %get-tuple-element.33), channel_id=1, source_target_pairs={{0,2},{2,0},{4,6},{6,4},{1,3},{3,1},{5,7},{7,5},{8,10},{10,8},{12,... | collective-permute-start | bytes 872456 | tf_op jit(solution)/shard_map/ppermute | solution.py:236
  10.5 2.5 %collective-permute-start.1 = (f32[71,8,128]{2,1,0:T(8,128)S(1)}, f32[71,8,128]{2,1,0:T(8,128)S(1)}, u32[]{:S(2)}, u32[]{:S(2)}) collective-permute-start(f32[71,8,128]{2,1,0:T(8,128)S(1)} %get-tuple-element.34), channel_id=1, source_target_pairs={{0,4},{2,6},{4,0},{6,2},{1,5},{3,7},{5,1},{7,3},{8,12},{10,14},{12... | collective-permute-start | bytes 872456 | tf_op jit(solution)/shard_map/ppermute | solution.py:236
  14.5 2.1 %collective-permute-done.15.refs_3_ = f32[40,8,128]{2,1,0:T(8,128)S(1)} collective-permute-done((f32[40,8,128]{2,1,0:T(8,128)S(1)}, f32[40,8,128]{2,1,0:T(8,128)S(1)}, u32[]{:S(2)}, u32[]{:S(2)}) %collective-permute-start.15) | collective-permute-done | bytes 163872 | tf_op jit(solution)/shard_map/ppermute | solution.py:236
  18.3 15.2 %collective-permute-done.4.refs_2_ = f32[41,8,128]{2,1,0:T(8,128)S(1)} collective-permute-done((f32[41,8,128]{2,1,0:T(8,128)}, f32[41,8,128]{2,1,0:T(8,128)S(1)}, u32[]{:S(2)}, u32[]{:S(2)}) %collective-permute-start.4) | collective-permute-done | bytes 167968 | tf_op jit(solution)/shard_map/ppermute | solution.py:236
  33.5 7.8 %collective-permute-start.17 = (f32[4,40,8,128]{3,2,1,0:T(8,128)S(1)}, f32[4,40,8,128]{3,2,1,0:T(8,128)S(1)}, u32[]{:S(2)}, u32[]{:S(2)}) collective-permute-start(f32[4,40,8,128]{3,2,1,0:T(8,128)S(1)} %join.5.refs_1_), channel_id=1, source_target_pairs={{0,248},{8,16},{16,8},{24,32},{32,24},{40,48},{48,40},{56,64},{64,... | collective-permute-start | bytes 1966088 | tf_op jit(solution)/shard_map/ppermute | solution.py:236
  41.7 4.7 %collective-permute-start.9 = (f32[4,71,8,128]{3,2,1,0:T(8,128)S(1)}, f32[4,71,8,128]{3,2,1,0:T(8,128)S(1)}, u32[]{:S(2)}, u32[]{:S(2)}) collective-permute-start(f32[4,71,8,128]{3,2,1,0:T(8,128)S(1)} %get-tuple-element.42.refs_1_), channel_id=1, source_target_pairs={{0,248},{8,16},{16,8},{24,32},{32,24},{40,48},{48,40},{56,64},{64,... | collective-permute-start | bytes 3489800 | tf_op jit(solution)/shard_map/ppermute | solution.py:236
  46.6 1.2 select_reduce_fusion.4
  47.9 21.3 %collective-permute-done.7.refs_2_ = f32[4,41,8,128]{3,2,1,0:T(8,128)S(1)} collective-permute-done((f32[4,41,8,128]{3,2,1,0:T(8,128)S(1)}, f32[4,41,8,128]{3,2,1,0:T(8,128)S(1)}, u32[]{:S(2)}, u32[]{:S(2)}) %collective-permute-start.7) | collective-permute-done | bytes 671776 | tf_op jit(solution)/shard_map/ppermute | solution.py:236
  69.2 1.9 %column.3 = (f32[40,8,128]{2,1,0:T(8,128)S(1)}, f32[40,8,128]{2,1,0:T(8,128)S(1)}, f32[40,8,128]{2,1,0:T(8,128)}, f32[40,8,128]{2,1,0:T(8,128)}, f32[3,4,8,128]{3,2,1,0:T(8,128)S(1)}) custom-call(s32[4,10]{1,0:T(4,128)S(1)} %bitcast.30, f32[4,4,10]{2,1,0:T(4,128)S(1)} %pad_maximum_fusion.weight_ref, f32[4,41,8,128]{3,2,1,0:T(8,128)S(1)} %collective-permute-done.6.refs_0_, ...), custom_call_target="tpu_custom_call" | custom-call | tf_op jit(solution)/shard_map/column/pallas_call | solution.py:302
  71.3 22.8 %collective-permute-done.9.refs_2_ = f32[4,71,8,128]{3,2,1,0:T(8,128)S(1)} collective-permute-done((f32[4,71,8,128]{3,2,1,0:T(8,128)S(1)}, f32[4,71,8,128]{3,2,1,0:T(8,128)S(1)}, u32[]{:S(2)}, u32[]{:S(2)}) %collective-permute-start.9) | collective-permute-done | bytes 1163296 | tf_op jit(solution)/shard_map/ppermute | solution.py:236
  95.0 2.1 %column.4 = (f32[70,8,128]{2,1,0:T(8,128)S(1)}, f32[70,8,128]{2,1,0:T(8,128)}, f32[70,8,128]{2,1,0:T(8,128)}, f32[70,8,128]{2,1,0:T(8,128)S(1)}) custom-call(s32[4,10]{1,0:T(4,128)S(1)} %bitcast.31, f32[4,4,10]{2,1,0:T(4,128)S(1)} %pad_maximum_fusion.weight_ref, f32[4,71,8,128]{3,2,1,0:T(8,128)S(1)} %collective-permute-done.8.refs_0_, ...), custom_call_target="tpu_custom_call" | custom-call | tf_op jit(solution)/shard_map/column/pallas_call | solution.py:302
  97.8 2.4 %collective-permute-start.23 = (f32[40,8,128]{2,1,0:T(8,128)}, f32[40,8,128]{2,1,0:T(8,128)}, u32[]{:S(2)}, u32[]{:S(2)}) collective-permute-start(f32[40,8,128]{2,1,0:T(8,128)} %get-tuple-element.58), channel_id=1, source_target_pairs={{0,6},{2,4},{4,2},{6,0},{1,7},{3,5},{5,3},{7,1},{8,14},{10,12},{12... | collective-permute-start | bytes 491528 | tf_op jit(solution)/shard_map/ppermute | solution.py:236
  100.9 9.9 %all-to-all-start = ((f32[64,1,128]{2,1,0:T(1,128)}), f32[64,1,128]{2,1,0:T(1,128)S(1)}, u32[]{:S(2)}, u32[]{:S(2)}) async-start(f32[64,1,128]{2,1,0:T(1,128)} %broadcast_in_dim.115), calls=%async_computation | async-start | bytes 65536 | tf_op jit(solution)/shard_map/all_to_all | solution.py:337
  111.5 1.7 %collective-permute-start.12 = (f32[70,8,128]{2,1,0:T(8,128)}, f32[70,8,128]{2,1,0:T(8,128)S(1)}, u32[]{:S(2)}, u32[]{:S(2)}) collective-permute-start(f32[70,8,128]{2,1,0:T(8,128)} %copy-done.9), channel_id=1, source_target_pairs={{0,6},{2,4},{4,2},{6,0},{1,7},{3,5},{5,3},{7,1},{8,14},{10,12},{12... | collective-permute-start | bytes 860168 | tf_op jit(solution)/shard_map/ppermute | solution.py:236
  117.0 3.2 %all-to-all-done = f32[64,1,128]{2,1,0:T(1,128)S(1)} async-done(((f32[64,1,128]{2,1,0:T(1,128)}), f32[64,1,128]{2,1,0:T(1,128)S(1)}, u32[]{:S(2)}, u32[]{:S(2)}) %all-to-all-start) | async-done | bytes 32800 | tf_op jit(solution)/shard_map/all_to_all | solution.py:337
  121.4 2.7 %collective-permute-start.20 = (f32[40,8,128]{2,1,0:T(8,128)}, f32[40,8,128]{2,1,0:T(8,128)S(1)}, u32[]{:S(2)}, u32[]{:S(2)}) collective-permute-start(f32[40,8,128]{2,1,0:T(8,128)} %copy-done.10), channel_id=1, source_target_pairs={{0,6},{2,4},{4,2},{6,0},{1,7},{3,5},{5,3},{7,1},{8,14},{10,12},{12... | collective-permute-start | bytes 491528 | tf_op jit(solution)/shard_map/ppermute | solution.py:236
  124.2 6.9 %collective-permute-done.12.refs_7_.refs_3_ = f32[70,8,128]{2,1,0:T(8,128)S(1)} collective-permute-done((f32[70,8,128]{2,1,0:T(8,128)}, f32[70,8,128]{2,1,0:T(8,128)S(1)}, u32[]{:S(2)}, u32[]{:S(2)}) %collective-permute-start.12) | collective-permute-done | bytes 286752 | tf_op jit(solution)/shard_map/ppermute | solution.py:236
  131.0 3.1 %finish.3.refs_4_ = f32[10,3,8,2560]{3,2,1,0:T(8,128)} custom-call(s32[10]{0:T(128)S(1)} %copy-done.4, f32[4,10]{1,0:T(4,128)S(1)} %pad_maximum_fusion.1.weight_ref, f32[3]{0:T(128)S(1)} %slice_divide_fusion.ratio_ref, f32[40,8,128]{2,1,0:T(8,128)S(1)} %get-tuple-element.55.refs_0_, f32[40,8,128]{2,1,0:T(8,128)S(1)} %collective-permute-done.21.refs_1_, ...), custom_call_target="tpu_custom_call" | custom-call | tf_op jit(solution)/shard_map/finish/pallas_call | solution.py:351
  134.1 2.6 %finish.4.refs_8_ = f32[10,3,8,2560]{3,2,1,0:T(8,128)} custom-call(s32[10]{0:T(128)S(1)} %copy-done.4, f32[4,10]{1,0:T(4,128)S(1)} %pad_maximum_fusion.1.weight_ref, f32[3]{0:T(128)S(1)} %slice_divide_fusion.ratio_ref, f32[70,8,128]{2,1,0:T(8,128)S(1)} %get-tuple-element.43.refs_4_.refs_0_, ...), custom_call_target="tpu_custom_call", output_to_operand_aliasing={{}: (7, {})} | custom-call | tf_op jit(solution)/shard_map/finish/pallas_call | solution.py:351
  136.8 2.7 %finish.5 = f32[10,3,8,2560]{3,2,1,0:T(8,128)} custom-call(s32[10]{0:T(128)S(1)} %copy-done.4, f32[4,10]{1,0:T(4,128)S(1)} %pad_maximum_fusion.1.weight_ref, f32[3]{0:T(128)S(1)} %slice_divide_fusion.ratio_ref, f32[70,8,128]{2,1,0:T(8,128)S(1)} %get-tuple-element.43.refs_4_.refs_0_, ...), custom_call_target="tpu_custom_call", output_to_operand_aliasing={{}: (11, {})} | custom-call | tf_op jit(solution)/shard_map/finish/pallas_call | solution.py:351
  (104 shorter events, 13.0 us)
Async XLA Ops:
  4.0 9.8 %collective-permute-start.14 = (f32[40,8,128]{2,1,0:T(8,128)S(1)}, f32[40,8,128]{2,1,0:T(8,128)S(1)}, u32[]{:S(2)}, u32[]{:S(2)}) collective-permute-start(f32[40,8,128]{2,1,0:T(8,128)S(1)} %get-tuple-element.49), channel_id=1, source_target_pairs={{0,4},{2,6},{4,0},{6,2},{1,5},{3,7},{5,1},{7,3},{8,12},{10,14},{12... | collective-permute-start | bytes 491528 | tf_op jit(solution)/shard_map/ppermute | solution.py:236
  6.6 9.9 %collective-permute-start.15 = (f32[40,8,128]{2,1,0:T(8,128)S(1)}, f32[40,8,128]{2,1,0:T(8,128)S(1)}, u32[]{:S(2)}, u32[]{:S(2)}) collective-permute-start(f32[40,8,128]{2,1,0:T(8,128)S(1)} %get-tuple-element.50), channel_id=1, source_target_pairs={{0,6},{2,4},{4,2},{6,0},{1,7},{3,5},{5,3},{7,1},{8,14},{10,12},{12... | collective-permute-start | bytes 491528 | tf_op jit(solution)/shard_map/ppermute | solution.py:236
  7.6 9.0 %collective-permute-start.3 = (f32[41,8,128]{2,1,0:T(8,128)S(1)}, f32[41,8,128]{2,1,0:T(8,128)S(1)}, u32[]{:S(2)}, u32[]{:S(2)}) collective-permute-start(f32[41,8,128]{2,1,0:T(8,128)S(1)} %get-tuple-element.38), channel_id=1, source_target_pairs={{0,2},{2,0},{4,6},{6,4},{1,3},{3,1},{5,7},{7,5},{8,10},{10,8},{12,... | collective-permute-start | bytes 503816 | tf_op jit(solution)/shard_map/ppermute | solution.py:236
  9.1 32.4 %collective-permute-start = (f32[71,8,128]{2,1,0:T(8,128)}, f32[71,8,128]{2,1,0:T(8,128)S(1)}, u32[]{:S(2)}, u32[]{:S(2)}) collective-permute-start(f32[71,8,128]{2,1,0:T(8,128)} %get-tuple-element.33), channel_id=1, source_target_pairs={{0,2},{2,0},{4,6},{6,4},{1,3},{3,1},{5,7},{7,5},{8,10},{10,8},{12,... | collective-permute-start | bytes 872456 | tf_op jit(solution)/shard_map/ppermute | solution.py:236
  10.5 31.0 %collective-permute-start.1 = (f32[71,8,128]{2,1,0:T(8,128)S(1)}, f32[71,8,128]{2,1,0:T(8,128)S(1)}, u32[]{:S(2)}, u32[]{:S(2)}) collective-permute-start(f32[71,8,128]{2,1,0:T(8,128)S(1)} %get-tuple-element.34), channel_id=1, source_target_pairs={{0,4},{2,6},{4,0},{6,2},{1,5},{3,7},{5,1},{7,3},{8,12},{10,14},{12... | collective-permute-start | bytes 872456 | tf_op jit(solution)/shard_map/ppermute | solution.py:236
  13.8 27.8 %collective-permute-start.2 = (f32[71,8,128]{2,1,0:T(8,128)S(1)}, f32[71,8,128]{2,1,0:T(8,128)S(1)}, u32[]{:S(2)}, u32[]{:S(2)}) collective-permute-start(f32[71,8,128]{2,1,0:T(8,128)S(1)} %get-tuple-element.35), channel_id=1, source_target_pairs={{0,6},{2,4},{4,2},{6,0},{1,7},{3,5},{5,3},{7,1},{8,14},{10,12},{12... | collective-permute-start | bytes 872456 | tf_op jit(solution)/shard_map/ppermute | solution.py:236
  16.6 16.9 %collective-permute-start.4 = (f32[41,8,128]{2,1,0:T(8,128)}, f32[41,8,128]{2,1,0:T(8,128)S(1)}, u32[]{:S(2)}, u32[]{:S(2)}) collective-permute-start(f32[41,8,128]{2,1,0:T(8,128)} %get-tuple-element.39), channel_id=1, source_target_pairs={{0,4},{2,6},{4,0},{6,2},{1,5},{3,7},{5,1},{7,3},{8,12},{10,14},{12... | collective-permute-start | bytes 503816 | tf_op jit(solution)/shard_map/ppermute | solution.py:236
  16.6 24.7 %collective-permute-start.5 = (f32[41,8,128]{2,1,0:T(8,128)}, f32[41,8,128]{2,1,0:T(8,128)S(1)}, u32[]{:S(2)}, u32[]{:S(2)}) collective-permute-start(f32[41,8,128]{2,1,0:T(8,128)} %get-tuple-element.40), channel_id=1, source_target_pairs={{0,6},{2,4},{4,2},{6,0},{1,7},{3,5},{5,3},{7,1},{8,14},{10,12},{12... | collective-permute-start | bytes 503816 | tf_op jit(solution)/shard_map/ppermute | solution.py:236
  33.5 64.3 %collective-permute-start.17 = (f32[4,40,8,128]{3,2,1,0:T(8,128)S(1)}, f32[4,40,8,128]{3,2,1,0:T(8,128)S(1)}, u32[]{:S(2)}, u32[]{:S(2)}) collective-permute-start(f32[4,40,8,128]{3,2,1,0:T(8,128)S(1)} %join.5.refs_1_), channel_id=1, source_target_pairs={{0,248},{8,16},{16,8},{24,32},{32,24},{40,48},{48,40},{56,64},{64,... | collective-permute-start | bytes 1966088 | tf_op jit(solution)/shard_map/ppermute | solution.py:236
  41.3 27.9 %collective-permute-start.7 = (f32[4,41,8,128]{3,2,1,0:T(8,128)S(1)}, f32[4,41,8,128]{3,2,1,0:T(8,128)S(1)}, u32[]{:S(2)}, u32[]{:S(2)}) collective-permute-start(f32[4,41,8,128]{3,2,1,0:T(8,128)S(1)} %join.4.refs_1_), channel_id=1, source_target_pairs={{0,248},{8,16},{16,8},{24,32},{32,24},{40,48},{48,40},{56,64},{64,... | collective-permute-start | bytes 2015240 | tf_op jit(solution)/shard_map/ppermute | solution.py:236
  41.5 27.8 %collective-permute-start.6 = (f32[4,41,8,128]{3,2,1,0:T(8,128)S(1)}, f32[4,41,8,128]{3,2,1,0:T(8,128)S(1)}, u32[]{:S(2)}, u32[]{:S(2)}) collective-permute-start(f32[4,41,8,128]{3,2,1,0:T(8,128)S(1)} %join.4.refs_1_), channel_id=1, source_target_pairs={{0,8},{8,0},{16,24},{24,16},{32,40},{40,32},{48,56},{56,48},{64,72... | collective-permute-start | bytes 2015240 | tf_op jit(solution)/shard_map/ppermute | solution.py:236
  41.7 52.5 %collective-permute-start.9 = (f32[4,71,8,128]{3,2,1,0:T(8,128)S(1)}, f32[4,71,8,128]{3,2,1,0:T(8,128)S(1)}, u32[]{:S(2)}, u32[]{:S(2)}) collective-permute-start(f32[4,71,8,128]{3,2,1,0:T(8,128)S(1)} %get-tuple-element.42.refs_1_), channel_id=1, source_target_pairs={{0,248},{8,16},{16,8},{24,32},{32,24},{40,48},{48,40},{56,64},{64,... | collective-permute-start | bytes 3489800 | tf_op jit(solution)/shard_map/ppermute | solution.py:236
  46.4 48.6 %collective-permute-start.8 = (f32[4,71,8,128]{3,2,1,0:T(8,128)S(1)}, f32[4,71,8,128]{3,2,1,0:T(8,128)S(1)}, u32[]{:S(2)}, u32[]{:S(2)}) collective-permute-start(f32[4,71,8,128]{3,2,1,0:T(8,128)S(1)} %get-tuple-element.42.refs_1_), channel_id=1, source_target_pairs={{0,8},{8,0},{16,24},{24,16},{32,40},{40,32},{48,56},{56,48},{64,72... | collective-permute-start | bytes 3489800 | tf_op jit(solution)/shard_map/ppermute | solution.py:236
  69.2 41.6 %collective-permute-start.16 = (f32[4,40,8,128]{3,2,1,0:T(8,128)S(1)}, f32[4,40,8,128]{3,2,1,0:T(8,128)S(1)}, u32[]{:S(2)}, u32[]{:S(2)}) collective-permute-start(f32[4,40,8,128]{3,2,1,0:T(8,128)S(1)} %join.5.refs_1_), channel_id=1, source_target_pairs={{0,8},{8,0},{16,24},{24,16},{32,40},{40,32},{48,56},{56,48},{64,72... | collective-permute-start | bytes 1966088 | tf_op jit(solution)/shard_map/ppermute | solution.py:236
  71.1 40.4 %collective-permute-start.21 = (f32[40,8,128]{2,1,0:T(8,128)S(1)}, f32[40,8,128]{2,1,0:T(8,128)S(1)}, u32[]{:S(2)}, u32[]{:S(2)}) collective-permute-start(f32[40,8,128]{2,1,0:T(8,128)S(1)} %get-tuple-element.56), channel_id=1, source_target_pairs={{0,2},{2,0},{4,6},{6,4},{1,3},{3,1},{5,7},{7,5},{8,10},{10,8},{12,... | collective-permute-start | bytes 491528 | tf_op jit(solution)/shard_map/ppermute | solution.py:236
  94.1 26.0 %collective-permute-start.22 = (f32[40,8,128]{2,1,0:T(8,128)}, f32[40,8,128]{2,1,0:T(8,128)}, u32[]{:S(2)}, u32[]{:S(2)}) collective-permute-start(f32[40,8,128]{2,1,0:T(8,128)} %get-tuple-element.57), channel_id=1, source_target_pairs={{0,4},{2,6},{4,0},{6,2},{1,5},{3,7},{5,1},{7,3},{8,12},{10,14},{12... | collective-permute-start | bytes 491528 | tf_op jit(solution)/shard_map/ppermute | solution.py:236
  97.8 23.6 %collective-permute-start.10 = (f32[70,8,128]{2,1,0:T(8,128)}, f32[70,8,128]{2,1,0:T(8,128)S(1)}, u32[]{:S(2)}, u32[]{:S(2)}) collective-permute-start(f32[70,8,128]{2,1,0:T(8,128)} %get-tuple-element.44), channel_id=1, source_target_pairs={{0,2},{2,0},{4,6},{6,4},{1,3},{3,1},{5,7},{7,5},{8,10},{10,8},{12,... | collective-permute-start | bytes 860168 | tf_op jit(solution)/shard_map/ppermute | solution.py:236
  97.8 22.4 %collective-permute-start.23 = (f32[40,8,128]{2,1,0:T(8,128)}, f32[40,8,128]{2,1,0:T(8,128)}, u32[]{:S(2)}, u32[]{:S(2)}) collective-permute-start(f32[40,8,128]{2,1,0:T(8,128)} %get-tuple-element.58), channel_id=1, source_target_pairs={{0,6},{2,4},{4,2},{6,0},{1,7},{3,5},{5,3},{7,1},{8,14},{10,12},{12... | collective-permute-start | bytes 491528 | tf_op jit(solution)/shard_map/ppermute | solution.py:236
  100.9 19.2 %all-to-all-start = ((f32[64,1,128]{2,1,0:T(1,128)}), f32[64,1,128]{2,1,0:T(1,128)S(1)}, u32[]{:S(2)}, u32[]{:S(2)}) async-start(f32[64,1,128]{2,1,0:T(1,128)} %broadcast_in_dim.115), calls=%async_computation | async-start | bytes 65536 | tf_op jit(solution)/shard_map/all_to_all | solution.py:337
  110.8 13.4 %collective-permute-start.11 = (f32[70,8,128]{2,1,0:T(8,128)}, f32[70,8,128]{2,1,0:T(8,128)S(1)}, u32[]{:S(2)}, u32[]{:S(2)}) collective-permute-start(f32[70,8,128]{2,1,0:T(8,128)} %get-tuple-element.45), channel_id=1, source_target_pairs={{0,4},{2,6},{4,0},{6,2},{1,5},{3,7},{5,1},{7,3},{8,12},{10,14},{12... | collective-permute-start | bytes 860168 | tf_op jit(solution)/shard_map/ppermute | solution.py:236
  111.5 19.5 %collective-permute-start.12 = (f32[70,8,128]{2,1,0:T(8,128)}, f32[70,8,128]{2,1,0:T(8,128)S(1)}, u32[]{:S(2)}, u32[]{:S(2)}) collective-permute-start(f32[70,8,128]{2,1,0:T(8,128)} %copy-done.9), channel_id=1, source_target_pairs={{0,6},{2,4},{4,2},{6,0},{1,7},{3,5},{5,3},{7,1},{8,14},{10,12},{12... | collective-permute-start | bytes 860168 | tf_op jit(solution)/shard_map/ppermute | solution.py:236
  120.2 16.6 %collective-permute-start.18 = (f32[40,8,128]{2,1,0:T(8,128)}, f32[40,8,128]{2,1,0:T(8,128)S(1)}, u32[]{:S(2)}, u32[]{:S(2)}) collective-permute-start(f32[40,8,128]{2,1,0:T(8,128)} %copy-done.12), channel_id=1, source_target_pairs={{0,2},{2,0},{4,6},{6,4},{1,3},{3,1},{5,7},{7,5},{8,10},{10,8},{12,... | collective-permute-start | bytes 491528 | tf_op jit(solution)/shard_map/ppermute | solution.py:236
  120.3 16.5 %collective-permute-start.19 = (f32[40,8,128]{2,1,0:T(8,128)}, f32[40,8,128]{2,1,0:T(8,128)S(1)}, u32[]{:S(2)}, u32[]{:S(2)}) collective-permute-start(f32[40,8,128]{2,1,0:T(8,128)} %copy-done.11), channel_id=1, source_target_pairs={{0,4},{2,6},{4,0},{6,2},{1,5},{3,7},{5,1},{7,3},{8,12},{10,14},{12... | collective-permute-start | bytes 491528 | tf_op jit(solution)/shard_map/ppermute | solution.py:236
  121.4 15.4 %collective-permute-start.20 = (f32[40,8,128]{2,1,0:T(8,128)}, f32[40,8,128]{2,1,0:T(8,128)S(1)}, u32[]{:S(2)}, u32[]{:S(2)}) collective-permute-start(f32[40,8,128]{2,1,0:T(8,128)} %copy-done.10), channel_id=1, source_target_pairs={{0,6},{2,4},{4,2},{6,0},{1,7},{3,5},{5,3},{7,1},{8,14},{10,12},{12... | collective-permute-start | bytes 491528 | tf_op jit(solution)/shard_map/ppermute | solution.py:236
  (23 other events, 476.5 us)

commit v10 on v9

--- a/solution.py
+++ b/solution.py
@@ -19,12 +19,13 @@
 QUARTER = 5
 TILES = RING * QUARTER
 LON = TILES * LANES
-CHUNKS = ((0, 4), (4, 11), (11, 15))
+CHUNKS = ((0, 3), (3, 10), (10, 15))
 PARTNERS = (2, 1, 3)
-OWN = ((0,), (1,), (2,))
+EARLY = 0
+OWN = ((1,), (2,))
 BACK = ((0,), (1,), (2,))
 SUMS_CHUNK = 0
-INFO_CHUNK = 1
+INFO_CHUNK = 2
 MARKED = (SUMS_CHUNK, INFO_CHUNK)
 TOGETHER = 5
 VMEM_LIMIT = 12 * 1024 * 1024
@@ -67,27 +68,29 @@
 
 
 def column_tiles(batch):
-    return sum(ROWS * width_of(chunk) for chunk in batch)
-
-
-def copy_units(fields_ref, batch, piece_refs):
+    return sum(ROWS * width_of(chunk) for chunk in batch) + (1 if EARLY in batch else 0)
+
+
+def copy_units(fields_ref, chunk, owner, piece_ref):
+    first, last = CHUNKS[chunk]
+    for unit in range(first, last):
+        field, tile = divmod(unit, QUARTER)
+        start = pl.multiple_of((owner * QUARTER + tile) * LANES, LANES)
+        for row in range(ROWS):
+            piece_ref[row * (last - first) + unit - first] = fields_ref[row, field, :, pl.ds(start, LANES)]
+
+
+def copy_pieces(fields_ref, chunk, piece_refs):
     place = lax.axis_index(LAT[2])
     for distance in range(RING):
-        owner = across(place, distance)
-        base = 0
-        for chunk in batch:
-            first, last = CHUNKS[chunk]
-            for unit in range(first, last):
-                field, tile = divmod(unit, QUARTER)
-                start = pl.multiple_of((owner * QUARTER + tile) * LANES, LANES)
-                for row in range(ROWS):
-                    piece_refs[distance][base + row * (last - first) + unit - first] = fields_ref[
-                        row, field, :, pl.ds(start, LANES)
-                    ]
-            base += tile_count(chunk)
-
-
-def pack_first(fields_ref, *piece_refs):
+        copy_units(fields_ref, chunk, across(place, distance), piece_refs[distance])
+
+
+def pack_plain(fields_ref, *piece_refs):
+    copy_pieces(fields_ref, OWN[0][0], piece_refs)
+
+
+def pack_early(fields_ref, early_ref):
     sub = lax.broadcasted_iota(jnp.int32, (ROWS, LANES), 0)
     lane = lax.broadcasted_iota(jnp.int32, (ROWS, LANES), 1)
     sums_sub = lax.broadcasted_iota(jnp.int32, (8, LANES), 0)
@@ -99,12 +102,12 @@
         by_row = jnp.sum(jnp.sum(total, axis=1), axis=1, keepdims=True)
         in_lanes = jnp.sum(jnp.where(sub == lane, by_row, 0.0), axis=0, keepdims=True)
         sums = jnp.where(sums_sub == field, in_lanes, sums)
-    copy_units(fields_ref, OWN[0], piece_refs)
-    for ref in piece_refs:
-        ref[batch_tiles(OWN[0]) - 1] = sums
-
-
-def pack_second(departure_ref, extents_ref, lat_ref, lon_ref, fields_ref, *piece_refs):
+    copy_pieces(fields_ref, EARLY, [early_ref.at[distance] for distance in range(RING)])
+    for distance in range(RING):
+        early_ref[distance, tile_count(EARLY) - 1] = sums
+
+
+def pack_marked(departure_ref, extents_ref, lat_ref, lon_ref, fields_ref, *piece_refs):
     first_row = lax.axis_index(LAT) * ROWS
     group_row = lax.axis_index(LAT[:2]) * GROUP
     low_bound = first_row - extents_ref[0, 0] * ROWS + 1
@@ -121,13 +124,18 @@
         info = jnp.where(here & (info_sub == 1), lat_ref[row], info)
         info = jnp.where(here & (info_sub == 2), lon_ref[row], info)
     info = jnp.where(info_sub == 0, starts.astype(jnp.float32), info)
-    copy_units(fields_ref, OWN[1], piece_refs)
+    copy_pieces(fields_ref, INFO_CHUNK, piece_refs)
     for ref in piece_refs:
-        ref[batch_tiles(OWN[1]) - 1] = info
-
-
-def pack_third(fields_ref, *piece_refs):
-    copy_units(fields_ref, OWN[2], piece_refs)
+        ref[tile_count(INFO_CHUNK) - 1] = info
+
+
+def bundle_kernel(*refs):
+    count = ROWS * width_of(EARLY)
+    positions = side_places(lax.axis_index(LAT[:2]))
+    for side in range(3):
+        refs[-1][positions[side]] = refs[side][0, count]
+        for distance in range(RING):
+            refs[3 + distance][side * count : (side + 1) * count] = refs[side][distance, :count]
 
 
 def join_kernel(batch, *refs):
@@ -142,20 +150,28 @@
 
 
 def column_kernel(batch, start_ref, weight_ref, *refs):
-    sides = [refs[3 * number : 3 * number + 3] for number in range(len(batch))]
-    refs = refs[3 * len(batch) :]
-    out_refs, rows_refs = refs[:RING], refs[len(refs) - len(batch) :]
+    sides = []
+    for chunk in batch:
+        taken = RING if chunk == EARLY else 3
+        sides.append(refs[:taken])
+        refs = refs[taken:]
+    if EARLY in batch:
+        for out_ref in refs[1 : RING + 1]:
+            out_ref[column_tiles(batch) - 1] = refs[0][...]
+        refs = refs[1:]
+    out_refs, rows_refs = refs[:RING], refs[RING:]
     place = lax.axis_index(LAT[2])
     positions = side_places(lax.axis_index(LAT[:2]))
     for chunk, side_refs, rows_ref in zip(batch, sides, rows_refs):
         count = width_of(chunk) * ROWS
-        if chunk == SUMS_CHUNK:
-            for side, ref in zip(positions, side_refs):
-                refs[RING][side] = ref[:, count]
         for distance in range(RING):
             band = across(place, distance)
-            for side, ref in zip(positions, side_refs):
-                rows_ref[pl.ds((side * RING + band) * count, count)] = ref[distance, :count]
+            for side in range(3):
+                if chunk == EARLY:
+                    block = side_refs[distance][side * count : (side + 1) * count]
+                else:
+                    block = side_refs[side][distance, :count]
+                rows_ref[pl.ds((positions[side] * RING + band) * count, count)] = block
 
     def one_row(row, carry):
         for distance in range(RING):
@@ -256,23 +272,33 @@
 
 def per_device(fields, lat_fraction, lon_fraction, lon_shift, departure_row, extents):
     params = pltpu.CompilerParams(vmem_limit_bytes=VMEM_LIMIT)
-    pieces = []
-    packs = (
-        (pack_first, ()),
-        (pack_second, (departure_row, extents, lat_fraction, lon_fraction)),
-        (pack_third, ()),
-    )
-    for number, (kernel, scalars) in enumerate(packs):
-        pieces.append(
-            pl.pallas_call(
-                kernel,
-                out_shape=[tiles(batch_tiles(OWN[number]))] * RING,
-                in_specs=[SMEM] * len(scalars) + [VMEM],
-                out_specs=[VMEM] * RING,
-                compiler_params=params,
-                name="pack",
-            )(*scalars, fields)
-        )
+
+    def pack(kernel, shapes, *operands):
+        return pl.pallas_call(
+            kernel,
+            out_shape=shapes,
+            in_specs=[SMEM] * (len(operands) - 1) + [VMEM],
+            out_specs=[VMEM] * len(shapes),
+            compiler_params=params,
+            name="pack",
+        )(*operands)
+
+    pieces = [pack(pack_plain, [tiles(batch_tiles(OWN[0]))] * RING, fields)]
+    early = pack(pack_early, [tiles(RING, tile_count(EARLY))], fields)[0]
+    scalars = (departure_row, extents, lat_fraction, lon_fraction)
+    pieces.append(pack(pack_marked, [tiles(batch_tiles(OWN[1]))] * RING, *scalars, fields))
+
+    early_inner, early_outer = both_sides(early)
+    bundles = pl.pallas_call(
+        bundle_kernel,
+        out_shape=[tiles(3 * ROWS * width_of(EARLY))] * RING + [tiles(3)],
+        in_specs=[VMEM] * 3,
+        out_specs=[VMEM] * (RING + 1),
+        compiler_params=params,
+        name="bundle",
+    )(early_inner, early, early_outer)
+    sums = bundles[RING][:, :FIELDS, :ROWS]
+    bundles = exchange(bundles[:RING])
 
     own, inner, outer = {}, {}, {}
     for number, batch in enumerate(OWN):
@@ -295,10 +321,35 @@
     ring_start = ring_info[:, 0].astype(jnp.int32)
     ring_weight = jnp.stack(cubic_weights(ring_info[:, 1]))
 
+    total_rows = lax.axis_size(LAT) * ROWS
+    group_row = lax.axis_index(LAT[:2]) * GROUP
+    place = lax.axis_index(LAT[2])
+    bands = across(place, jnp.arange(RING, dtype=jnp.int32))
+    ring_rows = bands[:, None] * ROWS + jnp.arange(ROWS, dtype=jnp.int32)[None]
+    area = jnp.cos(math.pi * ((group_row + ring_rows).astype(jnp.float32) + 0.5) / total_rows - math.pi / 2.0)
+    lon_total = sum(cubic_weights(ring_info[:, 2]))
+    spots = jnp.arange(3, dtype=jnp.int32)[:, None] * GROUP + ring_rows[0][None]
+    factor = jnp.zeros((3, ROWS), jnp.float32)
+    for step in range(4):
+        hit = (ring_start + step)[None, None] == spots[..., None, None]
+        share = area * lon_total * ring_weight[step]
+        factor = factor + jnp.sum(jnp.where(hit, share[None, None], 0.0), axis=(2, 3))
+    before = jnp.sum(area[0][None] * sums[1], axis=1)
+    after = jnp.sum(factor[:, None, :] * sums, axis=(0, 2))
+    mass = jnp.pad(jnp.concatenate([before, after]), (0, LANES - 2 * FIELDS))
+    parties = (LAT[0], LAT[1], "lev")
+    spread = jnp.broadcast_to(mass[None, None], (lax.axis_size(parties), 1, LANES))
+    spread = lax.all_to_all(spread, parties, 0, 0)
+    column_mass = jnp.broadcast_to(jnp.sum(spread, axis=0), (8, LANES))
+
     gathered = []
     for batch in BACK:
-        shapes = [tiles(column_tiles(batch))] * RING + [tiles(3, RING)] * (SUMS_CHUNK in batch)
-        operands = [part[chunk] for chunk in batch for part in (inner, own, outer)]
+        shapes = [tiles(column_tiles(batch))] * RING
+        operands = []
+        for chunk in batch:
+            operands += bundles if chunk == EARLY else [inner[chunk], own[chunk], outer[chunk]]
+        if EARLY in batch:
+            operands.append(column_mass)
         columns = pl.pallas_call(
             partial(column_kernel, batch),
             out_shape=shapes,
@@ -310,33 +361,10 @@
             compiler_params=params,
             name="column",
         )(ring_start, ring_weight, *operands)
-        if SUMS_CHUNK in batch:
-            all_sums = columns[RING]
-        gathered.append(exchange(columns[:RING]))
-
-    total_rows = lax.axis_size(LAT) * ROWS
-    group_row = lax.axis_index(LAT[:2]) * GROUP
-    bands = across(lax.axis_index(LAT[2]), jnp.arange(RING, dtype=jnp.int32))
-    ring_rows = bands[:, None] * ROWS + jnp.arange(ROWS, dtype=jnp.int32)[None]
-    area = jnp.cos(math.pi * ((group_row + ring_rows).astype(jnp.float32) + 0.5) / total_rows - math.pi / 2.0)
-    sums = all_sums[:, :, :FIELDS, :ROWS]
-    lon_total = sum(cubic_weights(ring_info[:, 2]))
-    before = jnp.sum(area[:, None, :] * sums[1], axis=(0, 2))
-    after = jnp.zeros((FIELDS,), jnp.float32)
-    for side in range(3):
-        spots = side * GROUP + ring_rows
-        factor = jnp.zeros((RING, ROWS), jnp.float32)
-        for step in range(4):
-            hit = (ring_start + step)[None, None] == spots[..., None, None]
-            share = area * lon_total * ring_weight[step]
-            factor = factor + jnp.sum(jnp.where(hit, share[None, None], 0.0), axis=(2, 3))
-        after = after + jnp.sum(factor[:, None, :] * sums[side], axis=(0, 2))
-    mass = jnp.pad(jnp.concatenate([before, after]), (0, LANES - 2 * FIELDS))
-    parties = (LAT[0], LAT[1], "lev")
-    spread = jnp.broadcast_to(mass[None, None], (lax.axis_size(parties), 1, LANES))
-    spread = lax.all_to_all(spread, parties, 0, 0)
-    mass = jnp.sum(spread, axis=(0, 1))
-    ratio = mass[:FIELDS] / mass[FIELDS : 2 * FIELDS]
+        gathered.append(exchange(columns))
+
+    mass = sum(piece[-1, 0, : 2 * FIELDS] for piece in gathered[0])
+    ratio = mass[:FIELDS] / mass[FIELDS:]
     lon_w = jnp.stack(cubic_weights(lon_fraction))
 
     result = None

time: 140 us -> 132 us (0.943)
  waiting for transfers between devices: 72.3 us -> 60.3 us
  starting transfers between devices: 42 us -> 45.7 us
  Pallas kernels: 16.1 us -> 17.8 us
  local copies, waits for them, and re-layouts: 5.7 us -> 4.07 us
    ppermute x24, waiting for transfers between devices: 69.1 us -> 42.2 us  [swap(): lax.ppermute(array, axis, [(i, partner(i)) for i in range(lax.axis_size(a...]
    all_to_all x1, waiting for transfers between devices: 3.17 us -> 18.2 us  [per_device(): spread = lax.all_to_all(spread, parties, 0, 0)]
    ppermute x24, starting transfers between devices: 32.1 us -> 36.4 us  [swap(): lax.ppermute(array, axis, [(i, partner(i)) for i in range(lax.axis_size(a...]
    unnamed x44 -> x18, local copies, waits for them, and re-layouts: 5.07 us -> 3.43 us
    pallas_call x3 -> x4, Pallas kernels: 2.49 us -> 3.69 us  [the longest x3 1.9 us: pack(): pl.pallas_call(kernel, out_shape=shapes, in_specs=[SMEM] * (len(operands)...]
  transfers between devices with their start and end apart: 25 -> 25, of which waited for: 7 -> 13; matrix products, arithmetic and copies ran while one was open for 3% -> 2% of each run, Pallas kernels for 10% -> 11%
where the time goes in v10:
time: 132 us; the launch traced here: 131 us
  waiting for transfers between devices  60.3 us (46%)
  starting transfers between devices  45.7 us (35%)
  Pallas kernels  17.8 us (13%)
  local copies, waits for them, and re-layouts  4.07 us (3%)
  other arithmetic  2.4 us (2%)
    ppermute x24, waiting for transfers between devices, swap(): lax.ppermute(array, axis, [(i, partner(i)) for i in range(lax.axis_size(a...  42.2 us
    ppermute x24, starting transfers between devices, swap(): lax.ppermute(array, axis, [(i, partner(i)) for i in range(lax.axis_size(a...  36.4 us
    all_to_all x1, waiting for transfers between devices, per_device(): spread = lax.all_to_all(spread, parties, 0, 0)  18.2 us
    all_to_all x1, starting transfers between devices, per_device(): spread = lax.all_to_all(spread, parties, 0, 0)  9.36 us
    pallas_call x3, Pallas kernels, per_device(): pl.pallas_call(partial(finish_kernel, field), grid=(1,), out_shape=jax.Sh...  7.92 us
    pallas_call x3, Pallas kernels, per_device(): pl.pallas_call(partial(column_kernel, batch), out_shape=shapes, in_specs=...  5.12 us
    unnamed x18, local copies, waits for them, and re-layouts  3.43 us
  transfers between devices with their start and end apart: 25, of which 13 were waited for; matrix products, arithmetic and copies ran while one was open for 2% of the time, Pallas kernels for 11%

profile of v10, /device:TPU:1, one launch (start us, length us, event | category | flops | bytes accessed | tf_op | source)
XLA Modules:
  0.0 130.5 jit_solution(12710932778452806627)
XLA Ops:
  1.9 8.7 %collective-permute-start.4 = (f32[4,31,8,128]{3,2,1,0:T(8,128)S(1)}, f32[4,31,8,128]{3,2,1,0:T(8,128)S(1)}, u32[]{:S(2)}, u32[]{:S(2)}) collective-permute-start(f32[4,31,8,128]{3,2,1,0:T(8,128)S(1)} %pack.4.refs_1_), channel_id=1, source_target_pairs={{0,248},{8,16},{16,8},{24,32},{32,24},{40,48},{48,40},{56,64},{64,... | collective-permute-start | bytes 1523720 | tf_op jit(solution)/shard_map/ppermute | solution.py:252
  12.7 2.6 %collective-permute-start.1 = (f32[51,8,128]{2,1,0:T(8,128)S(1)}, f32[51,8,128]{2,1,0:T(8,128)S(1)}, u32[]{:S(2)}, u32[]{:S(2)}) collective-permute-start(f32[51,8,128]{2,1,0:T(8,128)S(1)} %get-tuple-element.34), channel_id=1, source_target_pairs={{0,4},{2,6},{4,0},{6,2},{1,5},{3,7},{5,1},{7,3},{8,12},{10,14},{12... | collective-permute-start | bytes 626696 | tf_op jit(solution)/shard_map/ppermute | solution.py:252
  18.6 5.6 %collective-permute-done.1.refs_2_ = f32[51,8,128]{2,1,0:T(8,128)S(1)} collective-permute-done((f32[51,8,128]{2,1,0:T(8,128)S(1)}, f32[51,8,128]{2,1,0:T(8,128)S(1)}, u32[]{:S(2)}, u32[]{:S(2)}) %collective-permute-start.1) | collective-permute-done | bytes 208928 | tf_op jit(solution)/shard_map/ppermute | solution.py:252
  24.5 2.5 %collective-permute-done.2.refs_3_ = f32[51,8,128]{2,1,0:T(8,128)S(1)} collective-permute-done((f32[51,8,128]{2,1,0:T(8,128)S(1)}, f32[51,8,128]{2,1,0:T(8,128)S(1)}, u32[]{:S(2)}, u32[]{:S(2)}) %collective-permute-start.2) | collective-permute-done | bytes 208928 | tf_op jit(solution)/shard_map/ppermute | solution.py:252
  28.2 8.3 %collective-permute-done.17.refs_2_ = f32[70,8,128]{2,1,0:T(8,128)S(1)} collective-permute-done((f32[70,8,128]{2,1,0:T(8,128)}, f32[70,8,128]{2,1,0:T(8,128)S(1)}, u32[]{:S(2)}, u32[]{:S(2)}) %collective-permute-start.17) | collective-permute-done | bytes 286752 | tf_op jit(solution)/shard_map/ppermute | solution.py:252
  36.5 5.4 %collective-permute-done.18.refs_3_ = f32[70,8,128]{2,1,0:T(8,128)S(1)} collective-permute-done((f32[70,8,128]{2,1,0:T(8,128)S(1)}, f32[70,8,128]{2,1,0:T(8,128)S(1)}, u32[]{:S(2)}, u32[]{:S(2)}) %collective-permute-start.18) | collective-permute-done | bytes 286752 | tf_op jit(solution)/shard_map/ppermute | solution.py:252
  43.8 1.8 %bundle.1 = (f32[90,8,128]{2,1,0:T(8,128)S(1)}, f32[90,8,128]{2,1,0:T(8,128)S(1)}, f32[90,8,128]{2,1,0:T(8,128)S(1)}, f32[90,8,128]{2,1,0:T(8,128)}, f32[3,8,128]{2,1,0:T(8,128)S(1)}) custom-call(f32[4,31,8,128]{3,2,1,0:T(8,128)} %collective-permute-done.3.refs_0_, f32[4,31,8,128]{3,2,1,0:T(8,128)S(1)} %pack.4.refs_1_, ...), custom_call_target="tpu_custom_call" | custom-call | tf_op jit(solution)/shard_map/bundle/pallas_call | solution.py:292
  47.8 2.9 %collective-permute-start.7 = (f32[90,8,128]{2,1,0:T(8,128)}, f32[90,8,128]{2,1,0:T(8,128)S(1)}, u32[]{:S(2)}, u32[]{:S(2)}) collective-permute-start(f32[90,8,128]{2,1,0:T(8,128)} %get-tuple-element.40), channel_id=1, source_target_pairs={{0,6},{2,4},{4,2},{6,0},{1,7},{3,5},{5,3},{7,1},{8,14},{10,12},{12... | collective-permute-start | bytes 1105928 | tf_op jit(solution)/shard_map/ppermute | solution.py:252
  50.8 4.0 %collective-permute-done.5.refs_1_ = f32[90,8,128]{2,1,0:T(8,128)S(1)} collective-permute-done((f32[90,8,128]{2,1,0:T(8,128)S(1)}, f32[90,8,128]{2,1,0:T(8,128)S(1)}, u32[]{:S(2)}, u32[]{:S(2)}) %collective-permute-start.5) | collective-permute-done | bytes 368672 | tf_op jit(solution)/shard_map/ppermute | solution.py:252
  54.8 3.7 %collective-permute-start.12 = (f32[4,51,8,128]{3,2,1,0:T(8,128)}, f32[4,51,8,128]{3,2,1,0:T(8,128)}, u32[]{:S(2)}, u32[]{:S(2)}) collective-permute-start(f32[4,51,8,128]{3,2,1,0:T(8,128)} %get-tuple-element.46.refs_1_), channel_id=1, source_target_pairs={{0,248},{8,16},{16,8},{24,32},{32,24},{40,48},{48,40},{56,64},{64,... | collective-permute-start | bytes 2506760 | tf_op jit(solution)/shard_map/ppermute | solution.py:252
  58.5 3.5 %collective-permute-done.6.refs_2_ = f32[90,8,128]{2,1,0:T(8,128)S(1)} collective-permute-done((f32[90,8,128]{2,1,0:T(8,128)S(1)}, f32[90,8,128]{2,1,0:T(8,128)S(1)}, u32[]{:S(2)}, u32[]{:S(2)}) %collective-permute-start.6) | collective-permute-done | bytes 368672 | tf_op jit(solution)/shard_map/ppermute | solution.py:252
  63.9 9.4 %all-to-all-start = ((f32[64,1,128]{2,1,0:T(1,128)}), f32[64,1,128]{2,1,0:T(1,128)S(1)}, u32[]{:S(2)}, u32[]{:S(2)}) async-start(f32[64,1,128]{2,1,0:T(1,128)} %broadcast_in_dim.62), calls=%async_computation | async-start | bytes 65536 | tf_op jit(solution)/shard_map/all_to_all | solution.py:342
  74.0 18.2 %all-to-all-done = f32[64,1,128]{2,1,0:T(1,128)S(1)} async-done(((f32[64,1,128]{2,1,0:T(1,128)}), f32[64,1,128]{2,1,0:T(1,128)S(1)}, u32[]{:S(2)}, u32[]{:S(2)}) %all-to-all-start) | async-done | bytes 32800 | tf_op jit(solution)/shard_map/all_to_all | solution.py:342
  95.4 2.8 %collective-permute-start.10 = (f32[31,8,128]{2,1,0:T(8,128)S(1)}, f32[31,8,128]{2,1,0:T(8,128)S(1)}, u32[]{:S(2)}, u32[]{:S(2)}) collective-permute-start(f32[31,8,128]{2,1,0:T(8,128)S(1)} %get-tuple-element.45), channel_id=1, source_target_pairs={{0,6},{2,4},{4,2},{6,0},{1,7},{3,5},{5,3},{7,1},{8,14},{10,12},{12... | collective-permute-start | bytes 380936 | tf_op jit(solution)/shard_map/ppermute | solution.py:252
  98.2 1.9 %column.5 = (f32[70,8,128]{2,1,0:T(8,128)S(1)}, f32[70,8,128]{2,1,0:T(8,128)S(1)}, f32[70,8,128]{2,1,0:T(8,128)S(1)}, f32[70,8,128]{2,1,0:T(8,128)S(1)}) custom-call(s32[4,10]{1,0:T(4,128)S(1)} %bitcast.26, f32[4,4,10]{2,1,0:T(4,128)S(1)} %pad_maximum_fusion.weight_ref, f32[4,70,8,128]{3,2,1,0:T(8,128)} %collective-permute-done.19.refs_0_, ...), custom_call_target="tpu_custom_call" | custom-call | tf_op jit(solution)/shard_map/column/pallas_call | solution.py:353
  101.4 1.8 %collective-permute-start.22 = (f32[70,8,128]{2,1,0:T(8,128)S(1)}, f32[70,8,128]{2,1,0:T(8,128)S(1)}, u32[]{:S(2)}, u32[]{:S(2)}) collective-permute-start(f32[70,8,128]{2,1,0:T(8,128)S(1)} %get-tuple-element.57), channel_id=1, source_target_pairs={{0,4},{2,6},{4,0},{6,2},{1,5},{3,7},{5,1},{7,3},{8,12},{10,14},{12... | collective-permute-start | bytes 860168 | tf_op jit(solution)/shard_map/ppermute | solution.py:252
  104.1 2.3 %collective-permute-start.23 = (f32[70,8,128]{2,1,0:T(8,128)S(1)}, f32[70,8,128]{2,1,0:T(8,128)S(1)}, u32[]{:S(2)}, u32[]{:S(2)}) collective-permute-start(f32[70,8,128]{2,1,0:T(8,128)S(1)} %get-tuple-element.58), channel_id=1, source_target_pairs={{0,6},{2,4},{4,2},{6,0},{1,7},{3,5},{5,3},{7,1},{8,14},{10,12},{12... | collective-permute-start | bytes 860168 | tf_op jit(solution)/shard_map/ppermute | solution.py:252
  106.3 2.1 %column.4 = (f32[50,8,128]{2,1,0:T(8,128)S(1)}, f32[50,8,128]{2,1,0:T(8,128)S(1)}, f32[50,8,128]{2,1,0:T(8,128)S(1)}, f32[50,8,128]{2,1,0:T(8,128)S(1)}) custom-call(s32[4,10]{1,0:T(4,128)S(1)} %bitcast.27, f32[4,4,10]{2,1,0:T(4,128)S(1)} %pad_maximum_fusion.weight_ref, f32[4,51,8,128]{3,2,1,0:T(8,128)} %collective-permute-done.11.refs_0_, ...), custom_call_target="tpu_custom_call" | custom-call | tf_op jit(solution)/shard_map/column/pallas_call | solution.py:353
  110.2 2.3 %collective-permute-start.15 = (f32[50,8,128]{2,1,0:T(8,128)S(1)}, f32[50,8,128]{2,1,0:T(8,128)S(1)}, u32[]{:S(2)}, u32[]{:S(2)}) collective-permute-start(f32[50,8,128]{2,1,0:T(8,128)S(1)} %get-tuple-element.50), channel_id=1, source_target_pairs={{0,6},{2,4},{4,2},{6,0},{1,7},{3,5},{5,3},{7,1},{8,14},{10,12},{12... | collective-permute-start | bytes 614408 | tf_op jit(solution)/shard_map/ppermute | solution.py:252
  113.1 7.6 %collective-permute-done.23.refs_7_.refs_3_ = f32[70,8,128]{2,1,0:T(8,128)S(1)} collective-permute-done((f32[70,8,128]{2,1,0:T(8,128)S(1)}, f32[70,8,128]{2,1,0:T(8,128)S(1)}, u32[]{:S(2)}, u32[]{:S(2)}) %collective-permute-start.23) | collective-permute-done | bytes 286752 | tf_op jit(solution)/shard_map/ppermute | solution.py:252
  120.7 2.6 %finish.3.refs_4_ = f32[10,3,8,2560]{3,2,1,0:T(8,128)} custom-call(s32[10]{0:T(128)S(1)} %copy-done.4, f32[4,10]{1,0:T(4,128)S(1)} %pad_maximum_fusion.1.weight_ref, f32[3]{0:T(128)S(1)} %fusion.31.ratio_ref, f32[31,8,128]{2,1,0:T(8,128)S(1)} %get-tuple-element.42.refs_0_, f32[31,8,128]{2,1,0:T(8,128)S(1)} %collective-permute-done.8.refs_1_, ...), custom_call_target="tpu_custom_call" | custom-call | tf_op jit(solution)/shard_map/finish/pallas_call | solution.py:379
  123.3 2.6 %finish.4.refs_4_ = f32[10,3,8,2560]{3,2,1,0:T(8,128)} custom-call(s32[10]{0:T(128)S(1)} %copy-done.4, f32[4,10]{1,0:T(4,128)S(1)} %pad_maximum_fusion.1.weight_ref, f32[3]{0:T(128)S(1)} %fusion.31.ratio_ref, f32[70,8,128]{2,1,0:T(8,128)S(1)} %get-tuple-element.55.refs_4_.refs_0_, ...), custom_call_target="tpu_custom_call", output_to_operand_aliasing={{}: (7, {})} | custom-call | tf_op jit(solution)/shard_map/finish/pallas_call | solution.py:379
  126.0 1.9 %collective-permute-done.15.refs_3_ = f32[50,8,128]{2,1,0:T(8,128)S(1)} collective-permute-done((f32[50,8,128]{2,1,0:T(8,128)S(1)}, f32[50,8,128]{2,1,0:T(8,128)S(1)}, u32[]{:S(2)}, u32[]{:S(2)}) %collective-permute-start.15) | collective-permute-done | bytes 204832 | tf_op jit(solution)/shard_map/ppermute | solution.py:252
  127.9 2.6 %finish.5 = f32[10,3,8,2560]{3,2,1,0:T(8,128)} custom-call(s32[10]{0:T(128)S(1)} %copy-done.4, f32[4,10]{1,0:T(4,128)S(1)} %pad_maximum_fusion.1.weight_ref, f32[3]{0:T(128)S(1)} %fusion.31.ratio_ref, f32[50,8,128]{2,1,0:T(8,128)S(1)} %get-tuple-element.47.refs_0_, ...), custom_call_target="tpu_custom_call", output_to_operand_aliasing={{}: (7, {})} | custom-call | tf_op jit(solution)/shard_map/finish/pallas_call | solution.py:379
  (80 shorter events, 23.4 us)
Async XLA Ops:
  1.9 41.9 %collective-permute-start.4 = (f32[4,31,8,128]{3,2,1,0:T(8,128)S(1)}, f32[4,31,8,128]{3,2,1,0:T(8,128)S(1)}, u32[]{:S(2)}, u32[]{:S(2)}) collective-permute-start(f32[4,31,8,128]{3,2,1,0:T(8,128)S(1)} %pack.4.refs_1_), channel_id=1, source_target_pairs={{0,248},{8,16},{16,8},{24,32},{32,24},{40,48},{48,40},{56,64},{64,... | collective-permute-start | bytes 1523720 | tf_op jit(solution)/shard_map/ppermute | solution.py:252
  10.6 33.3 %collective-permute-start.3 = (f32[4,31,8,128]{3,2,1,0:T(8,128)S(1)}, f32[4,31,8,128]{3,2,1,0:T(8,128)}, u32[]{:S(2)}, u32[]{:S(2)}) collective-permute-start(f32[4,31,8,128]{3,2,1,0:T(8,128)S(1)} %pack.4.refs_1_), channel_id=1, source_target_pairs={{0,8},{8,0},{16,24},{24,16},{32,40},{40,32},{48,56},{56,48},{64,72... | collective-permute-start | bytes 1523720 | tf_op jit(solution)/shard_map/ppermute | solution.py:252
  11.3 6.0 %collective-permute-start = (f32[51,8,128]{2,1,0:T(8,128)S(1)}, f32[51,8,128]{2,1,0:T(8,128)S(1)}, u32[]{:S(2)}, u32[]{:S(2)}) collective-permute-start(f32[51,8,128]{2,1,0:T(8,128)S(1)} %get-tuple-element.33), channel_id=1, source_target_pairs={{0,2},{2,0},{4,6},{6,4},{1,3},{3,1},{5,7},{7,5},{8,10},{10,8},{12,... | collective-permute-start | bytes 626696 | tf_op jit(solution)/shard_map/ppermute | solution.py:252
  12.7 11.4 %collective-permute-start.1 = (f32[51,8,128]{2,1,0:T(8,128)S(1)}, f32[51,8,128]{2,1,0:T(8,128)S(1)}, u32[]{:S(2)}, u32[]{:S(2)}) collective-permute-start(f32[51,8,128]{2,1,0:T(8,128)S(1)} %get-tuple-element.34), channel_id=1, source_target_pairs={{0,4},{2,6},{4,0},{6,2},{1,5},{3,7},{5,1},{7,3},{8,12},{10,14},{12... | collective-permute-start | bytes 626696 | tf_op jit(solution)/shard_map/ppermute | solution.py:252
  15.3 11.7 %collective-permute-start.2 = (f32[51,8,128]{2,1,0:T(8,128)S(1)}, f32[51,8,128]{2,1,0:T(8,128)S(1)}, u32[]{:S(2)}, u32[]{:S(2)}) collective-permute-start(f32[51,8,128]{2,1,0:T(8,128)S(1)} %get-tuple-element.35), channel_id=1, source_target_pairs={{0,6},{2,4},{4,2},{6,0},{1,7},{3,5},{5,3},{7,1},{8,14},{10,12},{12... | collective-permute-start | bytes 626696 | tf_op jit(solution)/shard_map/ppermute | solution.py:252
  17.3 10.9 %collective-permute-start.16 = (f32[70,8,128]{2,1,0:T(8,128)}, f32[70,8,128]{2,1,0:T(8,128)S(1)}, u32[]{:S(2)}, u32[]{:S(2)}) collective-permute-start(f32[70,8,128]{2,1,0:T(8,128)} %get-tuple-element.52), channel_id=1, source_target_pairs={{0,2},{2,0},{4,6},{6,4},{1,3},{3,1},{5,7},{7,5},{8,10},{10,8},{12,... | collective-permute-start | bytes 860168 | tf_op jit(solution)/shard_map/ppermute | solution.py:252
  24.2 12.3 %collective-permute-start.17 = (f32[70,8,128]{2,1,0:T(8,128)}, f32[70,8,128]{2,1,0:T(8,128)S(1)}, u32[]{:S(2)}, u32[]{:S(2)}) collective-permute-start(f32[70,8,128]{2,1,0:T(8,128)} %get-tuple-element.53), channel_id=1, source_target_pairs={{0,4},{2,6},{4,0},{6,2},{1,5},{3,7},{5,1},{7,3},{8,12},{10,14},{12... | collective-permute-start | bytes 860168 | tf_op jit(solution)/shard_map/ppermute | solution.py:252
  27.0 14.9 %collective-permute-start.18 = (f32[70,8,128]{2,1,0:T(8,128)S(1)}, f32[70,8,128]{2,1,0:T(8,128)S(1)}, u32[]{:S(2)}, u32[]{:S(2)}) collective-permute-start(f32[70,8,128]{2,1,0:T(8,128)S(1)} %get-tuple-element.54), channel_id=1, source_target_pairs={{0,6},{2,4},{4,2},{6,0},{1,7},{3,5},{5,3},{7,1},{8,14},{10,12},{12... | collective-permute-start | bytes 860168 | tf_op jit(solution)/shard_map/ppermute | solution.py:252
  42.0 52.4 %collective-permute-start.20 = (f32[4,70,8,128]{3,2,1,0:T(8,128)S(1)}, f32[4,70,8,128]{3,2,1,0:T(8,128)S(1)}, u32[]{:S(2)}, u32[]{:S(2)}) collective-permute-start(f32[4,70,8,128]{3,2,1,0:T(8,128)S(1)} %join.3.refs_1_), channel_id=1, source_target_pairs={{0,248},{8,16},{16,8},{24,32},{32,24},{40,48},{48,40},{56,64},{64,... | collective-permute-start | bytes 3440648 | tf_op jit(solution)/shard_map/ppermute | solution.py:252
  43.1 52.3 %collective-permute-start.19 = (f32[4,70,8,128]{3,2,1,0:T(8,128)S(1)}, f32[4,70,8,128]{3,2,1,0:T(8,128)}, u32[]{:S(2)}, u32[]{:S(2)}) collective-permute-start(f32[4,70,8,128]{3,2,1,0:T(8,128)S(1)} %join.3.refs_1_), channel_id=1, source_target_pairs={{0,8},{8,0},{16,24},{24,16},{32,40},{40,32},{48,56},{56,48},{64,72... | collective-permute-start | bytes 3440648 | tf_op jit(solution)/shard_map/ppermute | solution.py:252
  46.4 8.4 %collective-permute-start.5 = (f32[90,8,128]{2,1,0:T(8,128)S(1)}, f32[90,8,128]{2,1,0:T(8,128)S(1)}, u32[]{:S(2)}, u32[]{:S(2)}) collective-permute-start(f32[90,8,128]{2,1,0:T(8,128)S(1)} %get-tuple-element.38), channel_id=1, source_target_pairs={{0,2},{2,0},{4,6},{6,4},{1,3},{3,1},{5,7},{7,5},{8,10},{10,8},{12,... | collective-permute-start | bytes 1105928 | tf_op jit(solution)/shard_map/ppermute | solution.py:252
  46.4 15.7 %collective-permute-start.6 = (f32[90,8,128]{2,1,0:T(8,128)S(1)}, f32[90,8,128]{2,1,0:T(8,128)S(1)}, u32[]{:S(2)}, u32[]{:S(2)}) collective-permute-start(f32[90,8,128]{2,1,0:T(8,128)S(1)} %get-tuple-element.39), channel_id=1, source_target_pairs={{0,4},{2,6},{4,0},{6,2},{1,5},{3,7},{5,1},{7,3},{8,12},{10,14},{12... | collective-permute-start | bytes 1105928 | tf_op jit(solution)/shard_map/ppermute | solution.py:252
  47.8 44.4 %collective-permute-start.7 = (f32[90,8,128]{2,1,0:T(8,128)}, f32[90,8,128]{2,1,0:T(8,128)S(1)}, u32[]{:S(2)}, u32[]{:S(2)}) collective-permute-start(f32[90,8,128]{2,1,0:T(8,128)} %get-tuple-element.40), channel_id=1, source_target_pairs={{0,6},{2,4},{4,2},{6,0},{1,7},{3,5},{5,3},{7,1},{8,14},{10,12},{12... | collective-permute-start | bytes 1105928 | tf_op jit(solution)/shard_map/ppermute | solution.py:252
  54.8 51.5 %collective-permute-start.12 = (f32[4,51,8,128]{3,2,1,0:T(8,128)}, f32[4,51,8,128]{3,2,1,0:T(8,128)}, u32[]{:S(2)}, u32[]{:S(2)}) collective-permute-start(f32[4,51,8,128]{3,2,1,0:T(8,128)} %get-tuple-element.46.refs_1_), channel_id=1, source_target_pairs={{0,248},{8,16},{16,8},{24,32},{32,24},{40,48},{48,40},{56,64},{64,... | collective-permute-start | bytes 2506760 | tf_op jit(solution)/shard_map/ppermute | solution.py:252
  62.0 44.3 %collective-permute-start.11 = (f32[4,51,8,128]{3,2,1,0:T(8,128)}, f32[4,51,8,128]{3,2,1,0:T(8,128)}, u32[]{:S(2)}, u32[]{:S(2)}) collective-permute-start(f32[4,51,8,128]{3,2,1,0:T(8,128)} %get-tuple-element.46.refs_1_), channel_id=1, source_target_pairs={{0,8},{8,0},{16,24},{24,16},{32,40},{40,32},{48,56},{56,48},{64,72... | collective-permute-start | bytes 2506760 | tf_op jit(solution)/shard_map/ppermute | solution.py:252
  63.9 28.2 %all-to-all-start = ((f32[64,1,128]{2,1,0:T(1,128)}), f32[64,1,128]{2,1,0:T(1,128)S(1)}, u32[]{:S(2)}, u32[]{:S(2)}) async-start(f32[64,1,128]{2,1,0:T(1,128)} %broadcast_in_dim.62), calls=%async_computation | async-start | bytes 65536 | tf_op jit(solution)/shard_map/all_to_all | solution.py:342
  94.4 7.1 %collective-permute-start.9 = (f32[31,8,128]{2,1,0:T(8,128)S(1)}, f32[31,8,128]{2,1,0:T(8,128)S(1)}, u32[]{:S(2)}, u32[]{:S(2)}) collective-permute-start(f32[31,8,128]{2,1,0:T(8,128)S(1)} %get-tuple-element.44), channel_id=1, source_target_pairs={{0,4},{2,6},{4,0},{6,2},{1,5},{3,7},{5,1},{7,3},{8,12},{10,14},{12... | collective-permute-start | bytes 380936 | tf_op jit(solution)/shard_map/ppermute | solution.py:252
  95.4 8.7 %collective-permute-start.10 = (f32[31,8,128]{2,1,0:T(8,128)S(1)}, f32[31,8,128]{2,1,0:T(8,128)S(1)}, u32[]{:S(2)}, u32[]{:S(2)}) collective-permute-start(f32[31,8,128]{2,1,0:T(8,128)S(1)} %get-tuple-element.45), channel_id=1, source_target_pairs={{0,6},{2,4},{4,2},{6,0},{1,7},{3,5},{5,3},{7,1},{8,14},{10,12},{12... | collective-permute-start | bytes 380936 | tf_op jit(solution)/shard_map/ppermute | solution.py:252
  100.1 10.1 %collective-permute-start.21 = (f32[70,8,128]{2,1,0:T(8,128)S(1)}, f32[70,8,128]{2,1,0:T(8,128)S(1)}, u32[]{:S(2)}, u32[]{:S(2)}) collective-permute-start(f32[70,8,128]{2,1,0:T(8,128)S(1)} %get-tuple-element.56), channel_id=1, source_target_pairs={{0,2},{2,0},{4,6},{6,4},{1,3},{3,1},{5,7},{7,5},{8,10},{10,8},{12,... | collective-permute-start | bytes 860168 | tf_op jit(solution)/shard_map/ppermute | solution.py:252
  101.4 11.7 %collective-permute-start.22 = (f32[70,8,128]{2,1,0:T(8,128)S(1)}, f32[70,8,128]{2,1,0:T(8,128)S(1)}, u32[]{:S(2)}, u32[]{:S(2)}) collective-permute-start(f32[70,8,128]{2,1,0:T(8,128)S(1)} %get-tuple-element.57), channel_id=1, source_target_pairs={{0,4},{2,6},{4,0},{6,2},{1,5},{3,7},{5,1},{7,3},{8,12},{10,14},{12... | collective-permute-start | bytes 860168 | tf_op jit(solution)/shard_map/ppermute | solution.py:252
  104.1 16.6 %collective-permute-start.23 = (f32[70,8,128]{2,1,0:T(8,128)S(1)}, f32[70,8,128]{2,1,0:T(8,128)S(1)}, u32[]{:S(2)}, u32[]{:S(2)}) collective-permute-start(f32[70,8,128]{2,1,0:T(8,128)S(1)} %get-tuple-element.58), channel_id=1, source_target_pairs={{0,6},{2,4},{4,2},{6,0},{1,7},{3,5},{5,3},{7,1},{8,14},{10,12},{12... | collective-permute-start | bytes 860168 | tf_op jit(solution)/shard_map/ppermute | solution.py:252
  108.5 17.5 %collective-permute-start.13 = (f32[50,8,128]{2,1,0:T(8,128)S(1)}, f32[50,8,128]{2,1,0:T(8,128)S(1)}, u32[]{:S(2)}, u32[]{:S(2)}) collective-permute-start(f32[50,8,128]{2,1,0:T(8,128)S(1)} %get-tuple-element.48), channel_id=1, source_target_pairs={{0,2},{2,0},{4,6},{6,4},{1,3},{3,1},{5,7},{7,5},{8,10},{10,8},{12,... | collective-permute-start | bytes 614408 | tf_op jit(solution)/shard_map/ppermute | solution.py:252
  108.6 17.4 %collective-permute-start.14 = (f32[50,8,128]{2,1,0:T(8,128)S(1)}, f32[50,8,128]{2,1,0:T(8,128)S(1)}, u32[]{:S(2)}, u32[]{:S(2)}) collective-permute-start(f32[50,8,128]{2,1,0:T(8,128)S(1)} %get-tuple-element.49), channel_id=1, source_target_pairs={{0,4},{2,6},{4,0},{6,2},{1,5},{3,7},{5,1},{7,3},{8,12},{10,14},{12... | collective-permute-start | bytes 614408 | tf_op jit(solution)/shard_map/ppermute | solution.py:252
  110.2 17.7 %collective-permute-start.15 = (f32[50,8,128]{2,1,0:T(8,128)S(1)}, f32[50,8,128]{2,1,0:T(8,128)S(1)}, u32[]{:S(2)}, u32[]{:S(2)}) collective-permute-start(f32[50,8,128]{2,1,0:T(8,128)S(1)} %get-tuple-element.50), channel_id=1, source_target_pairs={{0,6},{2,4},{4,2},{6,0},{1,7},{3,5},{5,3},{7,1},{8,14},{10,12},{12... | collective-permute-start | bytes 614408 | tf_op jit(solution)/shard_map/ppermute | solution.py:252
  (10 other events, 76.3 us)

commit v11 on v10

--- a/solution.py
+++ b/solution.py
@@ -20,10 +20,10 @@
 TILES = RING * QUARTER
 LON = TILES * LANES
 CHUNKS = ((0, 3), (3, 10), (10, 15))
-PARTNERS = (2, 1, 3)
+PARTNERS = (1, 3, 2)
 EARLY = 0
 OWN = ((1,), (2,))
-BACK = ((0,), (1,), (2,))
+BACK = ((0, 1), (2,))
 SUMS_CHUNK = 0
 INFO_CHUNK = 2
 MARKED = (SUMS_CHUNK, INFO_CHUNK)
@@ -68,7 +68,7 @@
 
 
 def column_tiles(batch):
-    return sum(ROWS * width_of(chunk) for chunk in batch) + (1 if EARLY in batch else 0)
+    return sum(ROWS * width_of(chunk) for chunk in batch)
 
 
 def copy_units(fields_ref, chunk, owner, piece_ref):
@@ -130,12 +130,10 @@
 
 
 def bundle_kernel(*refs):
-    count = ROWS * width_of(EARLY)
-    positions = side_places(lax.axis_index(LAT[:2]))
-    for side in range(3):
-        refs[-1][positions[side]] = refs[side][0, count]
-        for distance in range(RING):
-            refs[3 + distance][side * count : (side + 1) * count] = refs[side][distance, :count]
+    count = tile_count(EARLY)
+    for distance in range(RING):
+        for side in range(3):
+            refs[3 + distance][side * count : (side + 1) * count] = refs[side][distance]
 
 
 def join_kernel(batch, *refs):
@@ -155,20 +153,19 @@
         taken = RING if chunk == EARLY else 3
         sides.append(refs[:taken])
         refs = refs[taken:]
-    if EARLY in batch:
-        for out_ref in refs[1 : RING + 1]:
-            out_ref[column_tiles(batch) - 1] = refs[0][...]
-        refs = refs[1:]
-    out_refs, rows_refs = refs[:RING], refs[RING:]
+    out_refs, rows_refs = refs[:RING], refs[len(refs) - len(batch) :]
     place = lax.axis_index(LAT[2])
     positions = side_places(lax.axis_index(LAT[:2]))
     for chunk, side_refs, rows_ref in zip(batch, sides, rows_refs):
         count = width_of(chunk) * ROWS
+        span = tile_count(chunk)
         for distance in range(RING):
             band = across(place, distance)
             for side in range(3):
                 if chunk == EARLY:
-                    block = side_refs[distance][side * count : (side + 1) * count]
+                    ref, base = side_refs[distance], side * span
+                    block = ref[base : base + count]
+                    refs[RING][positions[side], distance] = ref[base + count]
                 else:
                     block = side_refs[side][distance, :count]
                 rows_ref[pl.ds((positions[side] * RING + band) * count, count)] = block
@@ -291,14 +288,13 @@
     early_inner, early_outer = both_sides(early)
     bundles = pl.pallas_call(
         bundle_kernel,
-        out_shape=[tiles(3 * ROWS * width_of(EARLY))] * RING + [tiles(3)],
+        out_shape=[tiles(3 * tile_count(EARLY))] * RING,
         in_specs=[VMEM] * 3,
-        out_specs=[VMEM] * (RING + 1),
+        out_specs=[VMEM] * RING,
         compiler_params=params,
         name="bundle",
     )(early_inner, early, early_outer)
-    sums = bundles[RING][:, :FIELDS, :ROWS]
-    bundles = exchange(bundles[:RING])
+    bundles = exchange(bundles)
 
     own, inner, outer = {}, {}, {}
     for number, batch in enumerate(OWN):
@@ -321,35 +317,12 @@
     ring_start = ring_info[:, 0].astype(jnp.int32)
     ring_weight = jnp.stack(cubic_weights(ring_info[:, 1]))
 
-    total_rows = lax.axis_size(LAT) * ROWS
-    group_row = lax.axis_index(LAT[:2]) * GROUP
-    place = lax.axis_index(LAT[2])
-    bands = across(place, jnp.arange(RING, dtype=jnp.int32))
-    ring_rows = bands[:, None] * ROWS + jnp.arange(ROWS, dtype=jnp.int32)[None]
-    area = jnp.cos(math.pi * ((group_row + ring_rows).astype(jnp.float32) + 0.5) / total_rows - math.pi / 2.0)
-    lon_total = sum(cubic_weights(ring_info[:, 2]))
-    spots = jnp.arange(3, dtype=jnp.int32)[:, None] * GROUP + ring_rows[0][None]
-    factor = jnp.zeros((3, ROWS), jnp.float32)
-    for step in range(4):
-        hit = (ring_start + step)[None, None] == spots[..., None, None]
-        share = area * lon_total * ring_weight[step]
-        factor = factor + jnp.sum(jnp.where(hit, share[None, None], 0.0), axis=(2, 3))
-    before = jnp.sum(area[0][None] * sums[1], axis=1)
-    after = jnp.sum(factor[:, None, :] * sums, axis=(0, 2))
-    mass = jnp.pad(jnp.concatenate([before, after]), (0, LANES - 2 * FIELDS))
-    parties = (LAT[0], LAT[1], "lev")
-    spread = jnp.broadcast_to(mass[None, None], (lax.axis_size(parties), 1, LANES))
-    spread = lax.all_to_all(spread, parties, 0, 0)
-    column_mass = jnp.broadcast_to(jnp.sum(spread, axis=0), (8, LANES))
-
     gathered = []
     for batch in BACK:
-        shapes = [tiles(column_tiles(batch))] * RING
+        shapes = [tiles(column_tiles(batch))] * RING + [tiles(3, RING)] * (SUMS_CHUNK in batch)
         operands = []
         for chunk in batch:
             operands += bundles if chunk == EARLY else [inner[chunk], own[chunk], outer[chunk]]
-        if EARLY in batch:
-            operands.append(column_mass)
         columns = pl.pallas_call(
             partial(column_kernel, batch),
             out_shape=shapes,
@@ -361,10 +334,33 @@
             compiler_params=params,
             name="column",
         )(ring_start, ring_weight, *operands)
-        gathered.append(exchange(columns))
-
-    mass = sum(piece[-1, 0, : 2 * FIELDS] for piece in gathered[0])
-    ratio = mass[:FIELDS] / mass[FIELDS:]
+        if SUMS_CHUNK in batch:
+            all_sums = columns[RING]
+        gathered.append(exchange(columns[:RING]))
+
+    total_rows = lax.axis_size(LAT) * ROWS
+    group_row = lax.axis_index(LAT[:2]) * GROUP
+    bands = across(lax.axis_index(LAT[2]), jnp.arange(RING, dtype=jnp.int32))
+    ring_rows = bands[:, None] * ROWS + jnp.arange(ROWS, dtype=jnp.int32)[None]
+    area = jnp.cos(math.pi * ((group_row + ring_rows).astype(jnp.float32) + 0.5) / total_rows - math.pi / 2.0)
+    sums = all_sums[:, :, :FIELDS, :ROWS]
+    lon_total = sum(cubic_weights(ring_info[:, 2]))
+    before = jnp.sum(area[:, None, :] * sums[1], axis=(0, 2))
+    after = jnp.zeros((FIELDS,), jnp.float32)
+    for side in range(3):
+        spots = side * GROUP + ring_rows
+        factor = jnp.zeros((RING, ROWS), jnp.float32)
+        for step in range(4):
+            hit = (ring_start + step)[None, None] == spots[..., None, None]
+            share = area * lon_total * ring_weight[step]
+            factor = factor + jnp.sum(jnp.where(hit, share[None, None], 0.0), axis=(2, 3))
+        after = after + jnp.sum(factor[:, None, :] * sums[side], axis=(0, 2))
+    mass = jnp.pad(jnp.concatenate([before, after]), (0, LANES - 2 * FIELDS))
+    parties = (LAT[0], LAT[1], "lev")
+    spread = jnp.broadcast_to(mass[None, None], (lax.axis_size(parties), 1, LANES))
+    spread = lax.all_to_all(spread, parties, 0, 0)
+    mass = jnp.sum(spread, axis=(0, 1))
+    ratio = mass[:FIELDS] / mass[FIELDS : 2 * FIELDS]
     lon_w = jnp.stack(cubic_weights(lon_fraction))
 
     result = None

time: 132 us -> 112 us (0.85)
  waiting for transfers between devices: 60.3 us -> 49.9 us
  starting transfers between devices: 45.7 us -> 39 us
  Pallas kernels: 17.8 us -> 15 us
    all_to_all x1, waiting for transfers between devices: 18.2 us -> 3.57 us  [per_device(): spread = lax.all_to_all(spread, parties, 0, 0)]
    ppermute x24 -> x21, starting transfers between devices: 36.4 us -> 29.8 us  [swap(): lax.ppermute(array, axis, [(i, partner(i)) for i in range(lax.axis_size(a...]
    ppermute x24 -> x21, waiting for transfers between devices: 42.2 us -> 46.3 us  [swap(): lax.ppermute(array, axis, [(i, partner(i)) for i in range(lax.axis_size(a...]
    pallas_call x1, Pallas kernels: 1.79 us -> 0.1 us  [per_device(): pl.pallas_call(bundle_kernel, out_shape=[tiles(3 * tile_count(EARLY))] *...]
    unnamed x18 -> x20, local copies, waits for them, and re-layouts: 3.43 us -> 3.99 us
    pallas_call x3 -> x2, Pallas kernels: 5.12 us -> 4.96 us  [per_device(): pl.pallas_call(partial(column_kernel, batch), out_shape=shapes, in_specs=...]
  transfers between devices with their start and end apart: 25 -> 22, of which waited for: 13 -> 11; matrix products, arithmetic and copies ran while one was open for 2% -> 3% of each run, Pallas kernels for 11% -> 11%
where the time goes in v11:
time: 112 us; the launch traced here: 111 us
  waiting for transfers between devices  49.9 us (45%)
  starting transfers between devices  39 us (35%)
  Pallas kernels  15 us (13%)
  local copies, waits for them, and re-layouts  4.63 us (4%)
  other arithmetic  2.58 us (2%)
    ppermute x21, waiting for transfers between devices, swap(): lax.ppermute(array, axis, [(i, partner(i)) for i in range(lax.axis_size(a...  46.3 us
    ppermute x21, starting transfers between devices, swap(): lax.ppermute(array, axis, [(i, partner(i)) for i in range(lax.axis_size(a...  29.8 us
    all_to_all x1, starting transfers between devices, per_device(): spread = lax.all_to_all(spread, parties, 0, 0)  9.14 us
    pallas_call x3, Pallas kernels, per_device(): pl.pallas_call(partial(finish_kernel, field), grid=(1,), out_shape=jax.Sh...  7.92 us
    pallas_call x2, Pallas kernels, per_device(): pl.pallas_call(partial(column_kernel, batch), out_shape=shapes, in_specs=...  4.96 us
    unnamed x20, local copies, waits for them, and re-layouts  3.99 us
    all_to_all x1, waiting for transfers between devices, per_device(): spread = lax.all_to_all(spread, parties, 0, 0)  3.57 us
  transfers between devices with their start and end apart: 22, of which 11 were waited for; matrix products, arithmetic and copies ran while one was open for 3% of the time, Pallas kernels for 11%

profile of v11, /device:TPU:1, one launch (start us, length us, event | category | flops | bytes accessed | tf_op | source)
XLA Modules:
  0.0 111.2 jit_solution(16210385963556626152)
XLA Ops:
  0.0 1.7 %copy-done = f32[10,3,8,2560]{3,2,1,0:T(8,128)S(1)} copy-done((f32[10,3,8,2560]{3,2,1,0:T(8,128)S(1)}, f32[10,3,8,2560]{3,2,1,0:T(8,128)}, u32[]{:S(2)}) %copy-start) | copy-done | bytes 2457624
  1.9 8.7 %collective-permute-start.4 = (f32[4,31,8,128]{3,2,1,0:T(8,128)S(1)}, f32[4,31,8,128]{3,2,1,0:T(8,128)S(1)}, u32[]{:S(2)}, u32[]{:S(2)}) collective-permute-start(f32[4,31,8,128]{3,2,1,0:T(8,128)S(1)} %pack.4.refs_1_), channel_id=1, source_target_pairs={{0,248},{8,16},{16,8},{24,32},{32,24},{40,48},{48,40},{56,64},{64,... | collective-permute-start | bytes 1523720 | tf_op jit(solution)/shard_map/ppermute | solution.py:249
  11.3 1.4 %collective-permute-start = (f32[51,8,128]{2,1,0:T(8,128)S(1)}, f32[51,8,128]{2,1,0:T(8,128)S(1)}, u32[]{:S(2)}, u32[]{:S(2)}) collective-permute-start(f32[51,8,128]{2,1,0:T(8,128)S(1)} %get-tuple-element.29), channel_id=1, source_target_pairs={{0,2},{2,0},{4,6},{6,4},{1,3},{3,1},{5,7},{7,5},{8,10},{10,8},{12,... | collective-permute-start | bytes 626696 | tf_op jit(solution)/shard_map/ppermute | solution.py:249
  12.7 2.6 %collective-permute-start.1 = (f32[51,8,128]{2,1,0:T(8,128)S(1)}, f32[51,8,128]{2,1,0:T(8,128)S(1)}, u32[]{:S(2)}, u32[]{:S(2)}) collective-permute-start(f32[51,8,128]{2,1,0:T(8,128)S(1)} %get-tuple-element.30), channel_id=1, source_target_pairs={{0,4},{2,6},{4,0},{6,2},{1,5},{3,7},{5,1},{7,3},{8,12},{10,14},{12... | collective-permute-start | bytes 626696 | tf_op jit(solution)/shard_map/ppermute | solution.py:249
  18.5 5.7 %collective-permute-done.1.refs_2_ = f32[51,8,128]{2,1,0:T(8,128)S(1)} collective-permute-done((f32[51,8,128]{2,1,0:T(8,128)S(1)}, f32[51,8,128]{2,1,0:T(8,128)S(1)}, u32[]{:S(2)}, u32[]{:S(2)}) %collective-permute-start.1) | collective-permute-done | bytes 208928 | tf_op jit(solution)/shard_map/ppermute | solution.py:249
  24.5 2.5 %collective-permute-done.2.refs_3_ = f32[51,8,128]{2,1,0:T(8,128)S(1)} collective-permute-done((f32[51,8,128]{2,1,0:T(8,128)S(1)}, f32[51,8,128]{2,1,0:T(8,128)S(1)}, u32[]{:S(2)}, u32[]{:S(2)}) %collective-permute-start.2) | collective-permute-done | bytes 208928 | tf_op jit(solution)/shard_map/ppermute | solution.py:249
  28.9 7.6 %collective-permute-done.9.refs_2_ = f32[70,8,128]{2,1,0:T(8,128)S(1)} collective-permute-done((f32[70,8,128]{2,1,0:T(8,128)}, f32[70,8,128]{2,1,0:T(8,128)S(1)}, u32[]{:S(2)}, u32[]{:S(2)}) %collective-permute-start.9) | collective-permute-done | bytes 286752 | tf_op jit(solution)/shard_map/ppermute | solution.py:249
  36.5 6.1 %collective-permute-done.10.refs_3_ = f32[70,8,128]{2,1,0:T(8,128)S(1)} collective-permute-done((f32[70,8,128]{2,1,0:T(8,128)}, f32[70,8,128]{2,1,0:T(8,128)S(1)}, u32[]{:S(2)}, u32[]{:S(2)}) %collective-permute-start.10) | collective-permute-done | bytes 286752 | tf_op jit(solution)/shard_map/ppermute | solution.py:249
  45.2 1.4 %collective-permute-start.6 = (f32[93,8,128]{2,1,0:T(8,128)S(1)}, f32[93,8,128]{2,1,0:T(8,128)S(1)}, u32[]{:S(2)}, u32[]{:S(2)}) collective-permute-start(f32[93,8,128]{2,1,0:T(8,128)S(1)} %get-tuple-element.35), channel_id=1, source_target_pairs={{0,4},{2,6},{4,0},{6,2},{1,5},{3,7},{5,1},{7,3},{8,12},{10,14},{12... | collective-permute-start | bytes 1142792 | tf_op jit(solution)/shard_map/ppermute | solution.py:249
  46.5 2.5 %collective-permute-start.7 = (f32[93,8,128]{2,1,0:T(8,128)S(1)}, f32[93,8,128]{2,1,0:T(8,128)S(1)}, u32[]{:S(2)}, u32[]{:S(2)}) collective-permute-start(f32[93,8,128]{2,1,0:T(8,128)S(1)} %get-tuple-element.36), channel_id=1, source_target_pairs={{0,6},{2,4},{4,2},{6,0},{1,7},{3,5},{5,3},{7,1},{8,14},{10,12},{12... | collective-permute-start | bytes 1142792 | tf_op jit(solution)/shard_map/ppermute | solution.py:249
  49.1 4.8 %collective-permute-done.5.refs_1_ = f32[93,8,128]{2,1,0:T(8,128)S(1)} collective-permute-done((f32[93,8,128]{2,1,0:T(8,128)S(1)}, f32[93,8,128]{2,1,0:T(8,128)S(1)}, u32[]{:S(2)}, u32[]{:S(2)}) %collective-permute-start.5) | collective-permute-done | bytes 380960 | tf_op jit(solution)/shard_map/ppermute | solution.py:249
  53.9 4.0 %collective-permute-start.14 = (f32[4,51,8,128]{3,2,1,0:T(8,128)S(1)}, f32[4,51,8,128]{3,2,1,0:T(8,128)S(1)}, u32[]{:S(2)}, u32[]{:S(2)}) collective-permute-start(f32[4,51,8,128]{3,2,1,0:T(8,128)S(1)} %get-tuple-element.42.refs_1_), channel_id=1, source_target_pairs={{0,248},{8,16},{16,8},{24,32},{32,24},{40,48},{48,40},{56,64},{64,... | collective-permute-start | bytes 2506760 | tf_op jit(solution)/shard_map/ppermute | solution.py:249
  57.9 4.2 %collective-permute-done.6.refs_2_ = f32[93,8,128]{2,1,0:T(8,128)S(1)} collective-permute-done((f32[93,8,128]{2,1,0:T(8,128)S(1)}, f32[93,8,128]{2,1,0:T(8,128)S(1)}, u32[]{:S(2)}, u32[]{:S(2)}) %collective-permute-start.6) | collective-permute-done | bytes 380960 | tf_op jit(solution)/shard_map/ppermute | solution.py:249
  63.2 8.6 %collective-permute-done.12.refs_6_ = f32[4,70,8,128]{3,2,1,0:T(8,128)S(1)} collective-permute-done((f32[4,70,8,128]{3,2,1,0:T(8,128)S(1)}, f32[4,70,8,128]{3,2,1,0:T(8,128)S(1)}, u32[]{:S(2)}, u32[]{:S(2)}) %collective-permute-start.12) | collective-permute-done | bytes 1146912 | tf_op jit(solution)/shard_map/ppermute | solution.py:249
  71.8 2.6 %column.2 = (f32[100,8,128]{2,1,0:T(8,128)S(1)}, f32[100,8,128]{2,1,0:T(8,128)}, f32[100,8,128]{2,1,0:T(8,128)}, f32[100,8,128]{2,1,0:T(8,128)}, f32[3,4,8,128]{3,2,1,0:T(8,128)S(1)}) custom-call(s32[4,10]{1,0:T(4,128)S(1)} %bitcast.30, f32[4,4,10]{2,1,0:T(4,128)S(1)} %pad_maximum_fusion.weight_ref, f32[93,8,128]{2,1,0:T(8,128)S(1)} %get-tuple-element.33.refs_0_, ...), custom_call_target="tpu_custom_call" | custom-call | tf_op jit(solution)/shard_map/column/pallas_call | solution.py:326
  75.7 2.5 %collective-permute-start.20 = (f32[100,8,128]{2,1,0:T(8,128)}, f32[100,8,128]{2,1,0:T(8,128)S(1)}, u32[]{:S(2)}, u32[]{:S(2)}) collective-permute-start(f32[100,8,128]{2,1,0:T(8,128)} %get-tuple-element.50), channel_id=1, source_target_pairs={{0,6},{2,4},{4,2},{6,0},{1,7},{3,5},{5,3},{7,1},{8,14},{10,12},{12... | collective-permute-start | bytes 1228808 | tf_op jit(solution)/shard_map/ppermute | solution.py:249
  79.1 9.1 %all-to-all-start = ((f32[64,1,128]{2,1,0:T(1,128)}), f32[64,1,128]{2,1,0:T(1,128)}, u32[]{:S(2)}, u32[]{:S(2)}) async-start(f32[64,1,128]{2,1,0:T(1,128)} %broadcast_in_dim.115), calls=%async_computation | async-start | bytes 65536 | tf_op jit(solution)/shard_map/all_to_all | solution.py:361
  88.3 1.4 %collective-permute-done.14.refs_2_ = f32[4,51,8,128]{3,2,1,0:T(8,128)S(1)} collective-permute-done((f32[4,51,8,128]{3,2,1,0:T(8,128)S(1)}, f32[4,51,8,128]{3,2,1,0:T(8,128)S(1)}, u32[]{:S(2)}, u32[]{:S(2)}) %collective-permute-start.14) | collective-permute-done | bytes 835616 | tf_op jit(solution)/shard_map/ppermute | solution.py:249
  89.7 2.4 %column.3 = (f32[50,8,128]{2,1,0:T(8,128)S(1)}, f32[50,8,128]{2,1,0:T(8,128)}, f32[50,8,128]{2,1,0:T(8,128)}, f32[50,8,128]{2,1,0:T(8,128)S(1)}) custom-call(s32[4,10]{1,0:T(4,128)S(1)} %bitcast.31, f32[4,4,10]{2,1,0:T(4,128)S(1)} %pad_maximum_fusion.weight_ref, f32[4,51,8,128]{3,2,1,0:T(8,128)} %collective-permute-done.13.refs_0_, ...), custom_call_target="tpu_custom_call" | custom-call | tf_op jit(solution)/shard_map/column/pallas_call | solution.py:326
  94.1 3.6 %all-to-all-done = f32[64,1,128]{2,1,0:T(1,128)} async-done(((f32[64,1,128]{2,1,0:T(1,128)}), f32[64,1,128]{2,1,0:T(1,128)}, u32[]{:S(2)}, u32[]{:S(2)}) %all-to-all-start) | async-done | bytes 32800 | tf_op jit(solution)/shard_map/all_to_all | solution.py:361
  98.6 2.6 %finish.3.refs_4_ = f32[10,3,8,2560]{3,2,1,0:T(8,128)} custom-call(s32[10]{0:T(128)S(1)} %copy-done.4, f32[4,10]{1,0:T(4,128)S(1)} %pad_maximum_fusion.1.weight_ref, f32[3]{0:T(128)S(1)} %slice_divide_fusion.ratio_ref, f32[100,8,128]{2,1,0:T(8,128)S(1)} %get-tuple-element.47.refs_0_, f32[100,8,128]{2,1,0:T(8,128)S(1)} %collective-permute-done.18.refs_1_, ...), custom_call_target="tpu_custom_call" | custom-call | tf_op jit(solution)/shard_map/finish/pallas_call | solution.py:375
  101.3 2.6 %finish.4.refs_4_ = f32[10,3,8,2560]{3,2,1,0:T(8,128)} custom-call(s32[10]{0:T(128)S(1)} %copy-done.4, f32[4,10]{1,0:T(4,128)S(1)} %pad_maximum_fusion.1.weight_ref, f32[3]{0:T(128)S(1)} %slice_divide_fusion.ratio_ref, f32[100,8,128]{2,1,0:T(8,128)S(1)} %get-tuple-element.47.refs_0_, ...), custom_call_target="tpu_custom_call", output_to_operand_aliasing={{}: (7, {})} | custom-call | tf_op jit(solution)/shard_map/finish/pallas_call | solution.py:375
  103.9 4.7 %collective-permute-done.17.refs_3_ = f32[50,8,128]{2,1,0:T(8,128)S(1)} collective-permute-done((f32[50,8,128]{2,1,0:T(8,128)}, f32[50,8,128]{2,1,0:T(8,128)S(1)}, u32[]{:S(2)}, u32[]{:S(2)}) %collective-permute-start.17) | collective-permute-done | bytes 204832 | tf_op jit(solution)/shard_map/ppermute | solution.py:249
  108.6 2.6 %finish.5 = f32[10,3,8,2560]{3,2,1,0:T(8,128)} custom-call(s32[10]{0:T(128)S(1)} %copy-done.4, f32[4,10]{1,0:T(4,128)S(1)} %pad_maximum_fusion.1.weight_ref, f32[3]{0:T(128)S(1)} %slice_divide_fusion.ratio_ref, f32[50,8,128]{2,1,0:T(8,128)S(1)} %get-tuple-element.43.refs_0_, ...), custom_call_target="tpu_custom_call", output_to_operand_aliasing={{}: (7, {})} | custom-call | tf_op jit(solution)/shard_map/finish/pallas_call | solution.py:375
  (73 shorter events, 15.2 us)
Async XLA Ops:
  1.7 8.9 %copy-start.8 = (f32[10]{0:T(128)S(1)}, f32[10]{0:T(128)}, u32[]{:S(2)}) copy-start(f32[10]{0:T(128)} %lat_ref.1) | copy-start | bytes 124
  1.9 43.0 %collective-permute-start.4 = (f32[4,31,8,128]{3,2,1,0:T(8,128)S(1)}, f32[4,31,8,128]{3,2,1,0:T(8,128)S(1)}, u32[]{:S(2)}, u32[]{:S(2)}) collective-permute-start(f32[4,31,8,128]{3,2,1,0:T(8,128)S(1)} %pack.4.refs_1_), channel_id=1, source_target_pairs={{0,248},{8,16},{16,8},{24,32},{32,24},{40,48},{48,40},{56,64},{64,... | collective-permute-start | bytes 1523720 | tf_op jit(solution)/shard_map/ppermute | solution.py:249
  10.6 34.4 %collective-permute-start.3 = (f32[4,31,8,128]{3,2,1,0:T(8,128)S(1)}, f32[4,31,8,128]{3,2,1,0:T(8,128)S(1)}, u32[]{:S(2)}, u32[]{:S(2)}) collective-permute-start(f32[4,31,8,128]{3,2,1,0:T(8,128)S(1)} %pack.4.refs_1_), channel_id=1, source_target_pairs={{0,8},{8,0},{16,24},{24,16},{32,40},{40,32},{48,56},{56,48},{64,72... | collective-permute-start | bytes 1523720 | tf_op jit(solution)/shard_map/ppermute | solution.py:249
  11.3 5.9 %collective-permute-start = (f32[51,8,128]{2,1,0:T(8,128)S(1)}, f32[51,8,128]{2,1,0:T(8,128)S(1)}, u32[]{:S(2)}, u32[]{:S(2)}) collective-permute-start(f32[51,8,128]{2,1,0:T(8,128)S(1)} %get-tuple-element.29), channel_id=1, source_target_pairs={{0,2},{2,0},{4,6},{6,4},{1,3},{3,1},{5,7},{7,5},{8,10},{10,8},{12,... | collective-permute-start | bytes 626696 | tf_op jit(solution)/shard_map/ppermute | solution.py:249
  12.7 11.4 %collective-permute-start.1 = (f32[51,8,128]{2,1,0:T(8,128)S(1)}, f32[51,8,128]{2,1,0:T(8,128)S(1)}, u32[]{:S(2)}, u32[]{:S(2)}) collective-permute-start(f32[51,8,128]{2,1,0:T(8,128)S(1)} %get-tuple-element.30), channel_id=1, source_target_pairs={{0,4},{2,6},{4,0},{6,2},{1,5},{3,7},{5,1},{7,3},{8,12},{10,14},{12... | collective-permute-start | bytes 626696 | tf_op jit(solution)/shard_map/ppermute | solution.py:249
  15.3 11.7 %collective-permute-start.2 = (f32[51,8,128]{2,1,0:T(8,128)S(1)}, f32[51,8,128]{2,1,0:T(8,128)S(1)}, u32[]{:S(2)}, u32[]{:S(2)}) collective-permute-start(f32[51,8,128]{2,1,0:T(8,128)S(1)} %get-tuple-element.31), channel_id=1, source_target_pairs={{0,6},{2,4},{4,2},{6,0},{1,7},{3,5},{5,3},{7,1},{8,14},{10,12},{12... | collective-permute-start | bytes 626696 | tf_op jit(solution)/shard_map/ppermute | solution.py:249
  17.2 11.7 %collective-permute-start.8 = (f32[70,8,128]{2,1,0:T(8,128)}, f32[70,8,128]{2,1,0:T(8,128)S(1)}, u32[]{:S(2)}, u32[]{:S(2)}) collective-permute-start(f32[70,8,128]{2,1,0:T(8,128)} %get-tuple-element.38), channel_id=1, source_target_pairs={{0,2},{2,0},{4,6},{6,4},{1,3},{3,1},{5,7},{7,5},{8,10},{10,8},{12,... | collective-permute-start | bytes 860168 | tf_op jit(solution)/shard_map/ppermute | solution.py:249
  24.2 12.3 %collective-permute-start.9 = (f32[70,8,128]{2,1,0:T(8,128)}, f32[70,8,128]{2,1,0:T(8,128)S(1)}, u32[]{:S(2)}, u32[]{:S(2)}) collective-permute-start(f32[70,8,128]{2,1,0:T(8,128)} %get-tuple-element.39), channel_id=1, source_target_pairs={{0,4},{2,6},{4,0},{6,2},{1,5},{3,7},{5,1},{7,3},{8,12},{10,14},{12... | collective-permute-start | bytes 860168 | tf_op jit(solution)/shard_map/ppermute | solution.py:249
  27.7 14.9 %collective-permute-start.10 = (f32[70,8,128]{2,1,0:T(8,128)}, f32[70,8,128]{2,1,0:T(8,128)S(1)}, u32[]{:S(2)}, u32[]{:S(2)}) collective-permute-start(f32[70,8,128]{2,1,0:T(8,128)} %get-tuple-element.40), channel_id=1, source_target_pairs={{0,6},{2,4},{4,2},{6,0},{1,7},{3,5},{5,3},{7,1},{8,14},{10,12},{12... | collective-permute-start | bytes 860168 | tf_op jit(solution)/shard_map/ppermute | solution.py:249
  42.7 29.1 %collective-permute-start.12 = (f32[4,70,8,128]{3,2,1,0:T(8,128)S(1)}, f32[4,70,8,128]{3,2,1,0:T(8,128)S(1)}, u32[]{:S(2)}, u32[]{:S(2)}) collective-permute-start(f32[4,70,8,128]{3,2,1,0:T(8,128)S(1)} %join.3.refs_5_), channel_id=1, source_target_pairs={{0,248},{8,16},{16,8},{24,32},{32,24},{40,48},{48,40},{56,64},{64,... | collective-permute-start | bytes 3440648 | tf_op jit(solution)/shard_map/ppermute | solution.py:249
  43.7 28.1 %collective-permute-start.11 = (f32[4,70,8,128]{3,2,1,0:T(8,128)S(1)}, f32[4,70,8,128]{3,2,1,0:T(8,128)S(1)}, u32[]{:S(2)}, u32[]{:S(2)}) collective-permute-start(f32[4,70,8,128]{3,2,1,0:T(8,128)S(1)} %join.3.refs_5_), channel_id=1, source_target_pairs={{0,8},{8,0},{16,24},{24,16},{32,40},{40,32},{48,56},{56,48},{64,72... | collective-permute-start | bytes 3440648 | tf_op jit(solution)/shard_map/ppermute | solution.py:249
  45.1 8.8 %collective-permute-start.5 = (f32[93,8,128]{2,1,0:T(8,128)S(1)}, f32[93,8,128]{2,1,0:T(8,128)S(1)}, u32[]{:S(2)}, u32[]{:S(2)}) collective-permute-start(f32[93,8,128]{2,1,0:T(8,128)S(1)} %get-tuple-element.34), channel_id=1, source_target_pairs={{0,2},{2,0},{4,6},{6,4},{1,3},{3,1},{5,7},{7,5},{8,10},{10,8},{12,... | collective-permute-start | bytes 1142792 | tf_op jit(solution)/shard_map/ppermute | solution.py:249
  45.2 16.9 %collective-permute-start.6 = (f32[93,8,128]{2,1,0:T(8,128)S(1)}, f32[93,8,128]{2,1,0:T(8,128)S(1)}, u32[]{:S(2)}, u32[]{:S(2)}) collective-permute-start(f32[93,8,128]{2,1,0:T(8,128)S(1)} %get-tuple-element.35), channel_id=1, source_target_pairs={{0,4},{2,6},{4,0},{6,2},{1,5},{3,7},{5,1},{7,3},{8,12},{10,14},{12... | collective-permute-start | bytes 1142792 | tf_op jit(solution)/shard_map/ppermute | solution.py:249
  46.5 16.7 %collective-permute-start.7 = (f32[93,8,128]{2,1,0:T(8,128)S(1)}, f32[93,8,128]{2,1,0:T(8,128)S(1)}, u32[]{:S(2)}, u32[]{:S(2)}) collective-permute-start(f32[93,8,128]{2,1,0:T(8,128)S(1)} %get-tuple-element.36), channel_id=1, source_target_pairs={{0,6},{2,4},{4,2},{6,0},{1,7},{3,5},{5,3},{7,1},{8,14},{10,12},{12... | collective-permute-start | bytes 1142792 | tf_op jit(solution)/shard_map/ppermute | solution.py:249
  53.9 35.8 %collective-permute-start.14 = (f32[4,51,8,128]{3,2,1,0:T(8,128)S(1)}, f32[4,51,8,128]{3,2,1,0:T(8,128)S(1)}, u32[]{:S(2)}, u32[]{:S(2)}) collective-permute-start(f32[4,51,8,128]{3,2,1,0:T(8,128)S(1)} %get-tuple-element.42.refs_1_), channel_id=1, source_target_pairs={{0,248},{8,16},{16,8},{24,32},{32,24},{40,48},{48,40},{56,64},{64,... | collective-permute-start | bytes 2506760 | tf_op jit(solution)/shard_map/ppermute | solution.py:249
  62.1 27.5 %collective-permute-start.13 = (f32[4,51,8,128]{3,2,1,0:T(8,128)S(1)}, f32[4,51,8,128]{3,2,1,0:T(8,128)}, u32[]{:S(2)}, u32[]{:S(2)}) collective-permute-start(f32[4,51,8,128]{3,2,1,0:T(8,128)S(1)} %get-tuple-element.42.refs_1_), channel_id=1, source_target_pairs={{0,8},{8,0},{16,24},{24,16},{32,40},{40,32},{48,56},{56,48},{64,72... | collective-permute-start | bytes 2506760 | tf_op jit(solution)/shard_map/ppermute | solution.py:249
  74.3 24.3 %copy-start.4 = (s32[10]{0:T(128)S(1)}, s32[10]{0:T(128)}, u32[]{:S(2)}) copy-start(s32[10]{0:T(128)} %shift_ref.5) | copy-start | bytes 124
  74.3 24.1 %collective-permute-start.18 = (f32[100,8,128]{2,1,0:T(8,128)}, f32[100,8,128]{2,1,0:T(8,128)S(1)}, u32[]{:S(2)}, u32[]{:S(2)}) collective-permute-start(f32[100,8,128]{2,1,0:T(8,128)} %get-tuple-element.48), channel_id=1, source_target_pairs={{0,2},{2,0},{4,6},{6,4},{1,3},{3,1},{5,7},{7,5},{8,10},{10,8},{12,... | collective-permute-start | bytes 1228808 | tf_op jit(solution)/shard_map/ppermute | solution.py:249
  74.3 24.3 %collective-permute-start.19 = (f32[100,8,128]{2,1,0:T(8,128)}, f32[100,8,128]{2,1,0:T(8,128)S(1)}, u32[]{:S(2)}, u32[]{:S(2)}) collective-permute-start(f32[100,8,128]{2,1,0:T(8,128)} %get-tuple-element.49), channel_id=1, source_target_pairs={{0,4},{2,6},{4,0},{6,2},{1,5},{3,7},{5,1},{7,3},{8,12},{10,14},{12... | collective-permute-start | bytes 1228808 | tf_op jit(solution)/shard_map/ppermute | solution.py:249
  75.7 23.0 %collective-permute-start.20 = (f32[100,8,128]{2,1,0:T(8,128)}, f32[100,8,128]{2,1,0:T(8,128)S(1)}, u32[]{:S(2)}, u32[]{:S(2)}) collective-permute-start(f32[100,8,128]{2,1,0:T(8,128)} %get-tuple-element.50), channel_id=1, source_target_pairs={{0,6},{2,4},{4,2},{6,0},{1,7},{3,5},{5,3},{7,1},{8,14},{10,12},{12... | collective-permute-start | bytes 1228808 | tf_op jit(solution)/shard_map/ppermute | solution.py:249
  79.1 18.5 %all-to-all-start = ((f32[64,1,128]{2,1,0:T(1,128)}), f32[64,1,128]{2,1,0:T(1,128)}, u32[]{:S(2)}, u32[]{:S(2)}) async-start(f32[64,1,128]{2,1,0:T(1,128)} %broadcast_in_dim.115), calls=%async_computation | async-start | bytes 65536 | tf_op jit(solution)/shard_map/all_to_all | solution.py:361
  92.8 11.1 %collective-permute-start.15 = (f32[50,8,128]{2,1,0:T(8,128)}, f32[50,8,128]{2,1,0:T(8,128)S(1)}, u32[]{:S(2)}, u32[]{:S(2)}) collective-permute-start(f32[50,8,128]{2,1,0:T(8,128)} %get-tuple-element.44), channel_id=1, source_target_pairs={{0,2},{2,0},{4,6},{6,4},{1,3},{3,1},{5,7},{7,5},{8,10},{10,8},{12,... | collective-permute-start | bytes 614408 | tf_op jit(solution)/shard_map/ppermute | solution.py:249
  92.8 11.1 %collective-permute-start.16 = (f32[50,8,128]{2,1,0:T(8,128)}, f32[50,8,128]{2,1,0:T(8,128)S(1)}, u32[]{:S(2)}, u32[]{:S(2)}) collective-permute-start(f32[50,8,128]{2,1,0:T(8,128)} %get-tuple-element.45), channel_id=1, source_target_pairs={{0,4},{2,6},{4,0},{6,2},{1,5},{3,7},{5,1},{7,3},{8,12},{10,14},{12... | collective-permute-start | bytes 614408 | tf_op jit(solution)/shard_map/ppermute | solution.py:249
  98.4 10.2 %collective-permute-start.17 = (f32[50,8,128]{2,1,0:T(8,128)}, f32[50,8,128]{2,1,0:T(8,128)S(1)}, u32[]{:S(2)}, u32[]{:S(2)}) collective-permute-start(f32[50,8,128]{2,1,0:T(8,128)} %copy-done.9), channel_id=1, source_target_pairs={{0,6},{2,4},{4,2},{6,0},{1,7},{3,5},{5,3},{7,1},{8,14},{10,12},{12... | collective-permute-start | bytes 614408 | tf_op jit(solution)/shard_map/ppermute | solution.py:249
  (8 other events, 39.5 us)
